TPU v7x, 32 devices: a whole 2x2x4 slice. The times are simulated.
32 devices in a mesh: dp: 8 (over z, x), seq: 4 (over y, core).
Axes of the slice: x: 2, y: 2, z: 4, core: 2. Of those that a mesh axis runs over, the one named last changes fastest.
Arguments:
- tokens: bfloat16 [16, 2048, 768], P('dp', 'seq'), may hold values from -6 to 6
- segment_ids: int32 [16, 2048], P('dp'), may hold values from 0 to 3, never falling along the last dimension, each value on 1 to 1024 neighbouring positions
- w_query: float32 [768, 768], P('dp'), may hold values from -0.3125 to 0.3125
- w_key: float32 [768, 768], P('dp'), may hold values from -0.3125 to 0.3125
- w_value: float32 [768, 768], P('dp'), may hold values from -0.21875 to 0.21875
- w_output: float32 [768, 768], P('dp'), may hold values from -0.875 to 0.875
- b_query: float32 [768], P('dp'), may hold values from -3 to 3
- b_value: float32 [768], P('dp'), may hold values from -3 to 3
- b_output: float32 [768], P('dp'), may hold values from -3 to 3
- first_gain: float32 [768], P('dp'), may hold values from 0.5 to 1.5
- first_shift: float32 [768], P('dp'), may hold values from -3 to 3
- w_inner: float32 [768, 3072], P('dp'), may hold values from -0.21875 to 0.21875
- b_inner: float32 [3072], P('dp'), may hold values from -3 to 3
- w_outer: float32 [3072, 768], P('dp'), may hold values from -0.109375 to 0.109375
- b_outer: float32 [768], P('dp'), may hold values from -3 to 3
- second_gain: float32 [768], P('dp'), may hold values from 0.5 to 1.5
- second_shift: float32 [768], P('dp'), may hold values from -3 to 3
- cotangent: bfloat16 [16, 2048, 768], P('dp', 'seq'), may hold values from -6 to 6
Outputs:
- mixed: bfloat16 [16, 2048, 768], P('dp', 'seq')
- grad_tokens: float32 [16, 2048, 768], P('dp', 'seq')
- grad_w_query: float32 [768, 768], P('dp')
- grad_w_key: float32 [768, 768], P('dp')
- grad_w_value: float32 [768, 768], P('dp')
- grad_w_output: float32 [768, 768], P('dp')
- grad_b_query: float32 [768], P('dp')
- grad_b_value: float32 [768], P('dp')
- grad_b_output: float32 [768], P('dp')
- grad_first_gain: float32 [768], P('dp')
- grad_first_shift: float32 [768], P('dp')
- grad_w_inner: float32 [768, 3072], P('dp')
- grad_b_inner: float32 [3072], P('dp')
- grad_w_outer: float32 [3072, 768], P('dp')
- grad_b_outer: float32 [768], P('dp')
- grad_second_gain: float32 [768], P('dp')
- grad_second_shift: float32 [768], P('dp')
Inputs may be any that keep to these rules, and one draw needn't show every extreme that they name: `segment_ids`: within each sequence the segment numbers never fall, and each of the 4 numbers covers 1 to 1024 positions.
All inputs are finite; a program needn't handle non-finite values.
Results may differ from a plain program's by a relative error of at most 0.017.
The roundings to bfloat16 on the way count: a program that leaves them out, or rounds other values in their place, can miss the bound.
Values may be sent and summed in bfloat16 or wider, within the bound.
A program may use at most 192 MiB of HBM per device.

v0:
```python
import jax
import jax.numpy as jnp
from jax import lax
from jax.experimental import pallas as pl
from jax.experimental.pallas import tpu as pltpu
from jax.sharding import Mesh
from jax.sharding import PartitionSpec as P

BLK = 256
BIG = -1.0e9
DOCUMENTS = 4


def dot_nn(a, b):
    return jnp.dot(a, b, preferred_element_type=jnp.float32)


def part_rows(place_ref, part, rows):
    return pl.ds(pl.multiple_of(place_ref[part], 128), rows)


def find_bounds(segment_ref, bound_ref):
    length = segment_ref.shape[0]
    bound_ref[0] = 0
    bound_ref[DOCUMENTS] = length
    for d in range(1, DOCUMENTS):

        def halve(_, span):
            low, high = span
            middle = (low + high) // 2
            below = segment_ref[jnp.minimum(middle, length - 1)] < d
            inside = low < high
            return (
                jnp.where(jnp.logical_and(inside, below), middle + 1, low),
                jnp.where(jnp.logical_and(inside, jnp.logical_not(below)), middle, high),
            )

        low, _ = lax.fori_loop(0, length.bit_length(), halve, (0, length))
        bound_ref[d] = low


def find_window(segment_ref, bound_ref, qb):
    length = segment_ref.shape[0]
    first = segment_ref[qb * BLK]
    last = segment_ref[qb * BLK + BLK - 1]
    start = bound_ref[first] // 128 * 128
    count = (bound_ref[last + 1] - start + BLK - 1) // BLK
    return jnp.minimum(start, length - count * BLK), count


def make_marks(row_ref, mark_query, mark_key):
    length = mark_query.shape[0]
    step = 512
    for b in range(length // step):
        rows = slice(b * step, (b + 1) * step)
        column = jnp.broadcast_to(row_ref[0:1, rows], (128, step)).T
        lane = lax.broadcasted_iota(jnp.int32, (step, 128), 1) % 64
        same = lane == column
        mark_query[rows, :] = jnp.where(same, 1.0, 0.0).astype(jnp.bfloat16)
        apart = jnp.logical_and(lane < DOCUMENTS, jnp.logical_not(same))
        mark_key[rows, :] = jnp.where(apart, BIG, 0.0).astype(jnp.bfloat16)


def forward_kernel(
    place_ref, segment_ref, qkv_ref, row_ref, mine_ref, other_ref, lse_ref, q2, k2, vt, acc, top, tot, keep, mark_query, mark_key, bound_ref
):
    length = qkv_ref.shape[0]
    blocks = length // BLK
    part = length // 4

    @pl.when(pl.program_id(0) == 0)
    def _():
        find_bounds(segment_ref, bound_ref)
        make_marks(row_ref, mark_query, mark_key)

    low = lax.broadcasted_iota(jnp.int32, (part, 128), 1) < 64
    for b in range(4):
        src = part_rows(place_ref, b, part)
        dst = slice(b * part, (b + 1) * part)
        q, k = qkv_ref[src, 0:128], qkv_ref[src, 128:256]
        ohq, nohk = mark_query[dst, :], mark_key[dst, :]
        q2[0, :, dst] = jnp.where(low, q, ohq).T
        q2[1, :, dst] = jnp.where(low, ohq, q).T
        k2[0, dst, :] = jnp.where(low, k, nohk)
        k2[1, dst, :] = jnp.where(low, nohk, k)
        vt[:, dst] = qkv_ref[src, 256:384].T
    lse_ref[...] = jnp.zeros_like(lse_ref)

    def row(qb, _):
        qs = pl.ds(pl.multiple_of(qb * BLK, BLK), BLK)
        start, count = find_window(segment_ref, bound_ref, qb)
        top[...] = jnp.full_like(top, -1.0e30)

        def span(i):
            return pl.ds(pl.multiple_of(start + i * BLK, 128), BLK)

        def fold(tile, function):
            return function(tile.reshape(BLK // 8, 8, BLK), axis=0)

        def highest(i):
            for h in range(2):
                st = dot_nn(k2[h, span(i), :], q2[h, :, qs])
                keep[h, pl.ds(pl.multiple_of(i * BLK, BLK), BLK), :] = st
                top[h] = jnp.maximum(top[h], fold(st, jnp.max))

        def weigh(i, largest):
            for h in range(2):
                rows = slice(64 * h, 64 * h + 64)
                st = keep[h, pl.ds(pl.multiple_of(i * BLK, BLK), BLK), :]
                p = jnp.exp(st - largest[h])
                tot[h] = tot[h] + fold(p, jnp.sum)
                acc[rows, :] = acc[rows, :] + dot_nn(vt[rows, span(i)], p.astype(jnp.bfloat16))

        def paired(step):
            def two(i, _):
                step(2 * i)
                step(2 * i + 1)
                return 0

            lax.fori_loop(0, count // 2, two, 0)

            @pl.when(count % 2 == 1)
            def _():
                step(count - 1)

        paired(highest)
        largest = [jnp.max(top[h], axis=0, keepdims=True) for h in range(2)]
        acc[...] = jnp.zeros_like(acc)
        tot[...] = jnp.zeros_like(tot)
        paired(lambda i: weigh(i, largest))
        for h in range(2):
            rows = slice(64 * h, 64 * h + 64)
            total = jnp.sum(tot[h], axis=0, keepdims=True)
            acc[rows, :] = acc[rows, :] / total
            lse_ref[h : h + 1, qs] = largest[h] + jnp.log(total)
        where = place_ref[qb * BLK // part] + qb * BLK % part
        result = acc[...].T.astype(jnp.bfloat16)

        @pl.when(where < 2 * part)
        def _():
            mine_ref[pl.ds(pl.multiple_of(where, BLK), BLK), :] = result

        @pl.when(where >= 2 * part)
        def _():
            other_ref[pl.ds(pl.multiple_of(where - 2 * part, BLK), BLK), :] = result

        return 0

    lax.fori_loop(0, blocks, row, 0)


def attention(place, segments, qkv):
    length, width = qkv.shape
    pairs = width // 384
    rows = length // 2
    return pl.pallas_call(
        forward_kernel,
        out_shape=(
            jax.ShapeDtypeStruct((rows, pairs * 128), jnp.bfloat16),
            jax.ShapeDtypeStruct((rows, pairs * 128), jnp.bfloat16),
            jax.ShapeDtypeStruct((pairs * 8, length), jnp.float32),
        ),
        grid_spec=pltpu.PrefetchScalarGridSpec(
            num_scalar_prefetch=2,
            grid=(pairs,),
            in_specs=[
                pl.BlockSpec((length, 384), lambda p, *_: (0, p)),
                pl.BlockSpec((1, length), lambda p, *_: (0, 0)),
            ],
            out_specs=[
                pl.BlockSpec((rows, 128), lambda p, *_: (0, p)),
                pl.BlockSpec((rows, 128), lambda p, *_: (0, p)),
                pl.BlockSpec((8, length), lambda p, *_: (p, 0)),
            ],
            scratch_shapes=[
                pltpu.VMEM((2, 128, length), jnp.bfloat16),
                pltpu.VMEM((2, length, 128), jnp.bfloat16),
                pltpu.VMEM((128, length), jnp.bfloat16),
                pltpu.VMEM((128, BLK), jnp.float32),
                pltpu.VMEM((2, 8, BLK), jnp.float32),
                pltpu.VMEM((2, 8, BLK), jnp.float32),
                pltpu.VMEM((2, length, BLK), jnp.float32),
                pltpu.VMEM((length, 128), jnp.bfloat16),
                pltpu.VMEM((length, 128), jnp.bfloat16),
                pltpu.SMEM((DOCUMENTS + 1,), jnp.int32),
            ],
        ),
        compiler_params=pltpu.CompilerParams(dimension_semantics=("arbitrary",), vmem_limit_bytes=60 << 20),
        cost_estimate=pl.CostEstimate(flops=pairs * 8_000_000_000, bytes_accessed=pairs * 3_000_000, transcendentals=pairs * 4_000_000),
        name="attention_forward",
    )(place, segments, qkv, segments.reshape(1, length))


def backward_kernel(
    place_ref,
    segment_ref,
    qkv_ref,
    ctx_mine_ref,
    ctx_other_ref,
    do_mine_ref,
    do_other_ref,
    lse_ref,
    row_ref,
    out_ref,
    sum_ref,
    q2,
    k2,
    q0,
    d0,
    dt,
    v0,
    kt,
    dk,
    dv,
    dqt,
    delta,
    mark_query,
    mark_key,
    bound_ref,
):
    length = qkv_ref.shape[0]
    blocks = length // BLK
    part = length // 4

    @pl.when(pl.program_id(0) == 0)
    def _():
        find_bounds(segment_ref, bound_ref)
        make_marks(row_ref, mark_query, mark_key)

    low = lax.broadcasted_iota(jnp.int32, (part, 128), 1) < 64

    def prepare(b, do, ctx):
        src = part_rows(place_ref, b, part)
        dst = slice(b * part, (b + 1) * part)
        q, k = qkv_ref[src, 0:128], qkv_ref[src, 128:256]
        zero = jnp.zeros_like(q)
        ohq, nohk = mark_query[dst, :], mark_key[dst, :]
        q2[0, :, dst] = jnp.where(low, q, ohq).T
        q2[1, :, dst] = jnp.where(low, ohq, q).T
        k2[0, dst, :] = jnp.where(low, k, nohk)
        k2[1, dst, :] = jnp.where(low, nohk, k)
        q0[0, dst, :] = jnp.where(low, q, zero)
        q0[1, dst, :] = jnp.where(low, zero, q)
        d0[0, dst, :] = jnp.where(low, do, zero)
        d0[1, dst, :] = jnp.where(low, zero, do)
        dt[0, :, dst] = jnp.where(low, do, zero).T
        dt[1, :, dst] = jnp.where(low, zero, do).T
        v0[dst, :] = qkv_ref[src, 256:384]
        kt[:, dst] = k.T
        prod = (do.astype(jnp.float32) * ctx.astype(jnp.float32)).T
        delta[0:1, dst] = jnp.sum(prod[0:64], axis=0, keepdims=True)
        delta[1:2, dst] = jnp.sum(prod[64:128], axis=0, keepdims=True)

    for b in range(4):

        @pl.when(place_ref[b] < 2 * part)
        def _():
            rows = part_rows(place_ref, b, part)
            prepare(b, do_mine_ref[rows, :], ctx_mine_ref[rows, :])

        @pl.when(place_ref[b] >= 2 * part)
        def _():
            rows = pl.ds(pl.multiple_of(place_ref[b] - 2 * part, 128), part)
            prepare(b, do_other_ref[rows, :], ctx_other_ref[rows, :])

    dk[...] = jnp.zeros_like(dk)
    dv[...] = jnp.zeros_like(dv)
    dqt[...] = jnp.zeros_like(dqt)

    def row(qb, _):
        qs = pl.ds(pl.multiple_of(qb * BLK, BLK), BLK)
        start, count = find_window(segment_ref, bound_ref, qb)

        def tile(i):
            ks = pl.ds(pl.multiple_of(start + i * BLK, 128), BLK)
            for h in range(2):
                rows = slice(64 * h, 64 * h + 64)
                st = dot_nn(k2[h, ks, :], q2[h, :, qs])
                w = jnp.exp(st - lse_ref[h : h + 1, qs])
                gw = dot_nn(v0[ks, :], dt[h, :, qs])
                ds = (w * (gw - delta[h : h + 1, qs])).astype(jnp.bfloat16)
                dv[ks, :] += dot_nn(w.astype(jnp.bfloat16), d0[h, qs, :])
                dk[ks, :] += dot_nn(ds, q0[h, qs, :])
                dqt[rows, qs] += dot_nn(kt[rows, ks], ds)

        def two(i, _):
            tile(2 * i)
            tile(2 * i + 1)
            return 0

        lax.fori_loop(0, count // 2, two, 0)

        @pl.when(count % 2 == 1)
        def _():
            tile(count - 1)

        return 0

    lax.fori_loop(0, blocks, row, 0)
    sums = [jnp.zeros((1, 128), jnp.float32) for _ in range(3)]
    for b in range(4):
        dst = part_rows(place_ref, b, part)
        src = slice(b * part, (b + 1) * part)
        pieces = ((dqt[:, src].T * 0.125).astype(jnp.bfloat16), dk[src, :].astype(jnp.bfloat16), dv[src, :].astype(jnp.bfloat16))
        for i, piece in enumerate(pieces):
            out_ref[dst, 128 * i : 128 * i + 128] = piece
            sums[i] = sums[i] + jnp.sum(piece.astype(jnp.float32), axis=0, keepdims=True)
    sum_ref[...] = jnp.zeros_like(sum_ref)
    for i in range(3):
        sum_ref[0:1, 128 * i : 128 * i + 128] = sums[i]


def attention_back(place, segments, qkv, ctx_mine, ctx_other, do_all, do_other, lse):
    length, width = qkv.shape
    pairs = width // 384
    rows = length // 2
    half = lambda: pltpu.VMEM((2, length, 128), jnp.bfloat16)
    turned = lambda: pltpu.VMEM((2, 128, length), jnp.bfloat16)
    column = pl.BlockSpec((rows, 128), lambda p, *_: (0, p))
    return pl.pallas_call(
        backward_kernel,
        out_shape=(
            jax.ShapeDtypeStruct((length, width), jnp.bfloat16),
            jax.ShapeDtypeStruct((pairs * 8, 384), jnp.float32),
        ),
        grid_spec=pltpu.PrefetchScalarGridSpec(
            num_scalar_prefetch=2,
            grid=(pairs,),
            in_specs=[
                pl.BlockSpec((length, 384), lambda p, *_: (0, p)),
                column,
                column,
                pl.BlockSpec((rows, 128), lambda p, place, seg: (0, place[4] * pairs + p)),
                column,
                pl.BlockSpec((8, length), lambda p, *_: (p, 0)),
                pl.BlockSpec((1, length), lambda p, *_: (0, 0)),
            ],
            out_specs=[
                pl.BlockSpec((length, 384), lambda p, *_: (0, p)),
                pl.BlockSpec((8, 384), lambda p, *_: (p, 0)),
            ],
            scratch_shapes=[
                turned(),
                half(),
                half(),
                half(),
                turned(),
                pltpu.VMEM((length, 128), jnp.bfloat16),
                pltpu.VMEM((128, length), jnp.bfloat16),
                pltpu.VMEM((length, 128), jnp.float32),
                pltpu.VMEM((length, 128), jnp.float32),
                pltpu.VMEM((128, length), jnp.float32),
                pltpu.VMEM((8, length), jnp.float32),
                pltpu.VMEM((length, 128), jnp.bfloat16),
                pltpu.VMEM((length, 128), jnp.bfloat16),
                pltpu.SMEM((DOCUMENTS + 1,), jnp.int32),
            ],
        ),
        compiler_params=pltpu.CompilerParams(dimension_semantics=("arbitrary",), vmem_limit_bytes=60 << 20),
        cost_estimate=pl.CostEstimate(flops=pairs * 20_000_000_000, bytes_accessed=pairs * 5_000_000, transcendentals=pairs * 4_000_000),
        name="attention_backward",
    )(place, segments, qkv, ctx_mine, ctx_other, do_all, do_other, lse, segments.reshape(1, length))


MESH_ID = pl.DeviceIdType.MESH


def place_of():
    return tuple(lax.axis_index(name) for name in ("z", "x", "y", "core"))


def sizes_of():
    return lax.axis_size("z"), lax.axis_size("x")


def partner(**moved):
    z, x, y, core = place_of()
    return (moved.get("z", z), moved.get("x", x), moved.get("y", y), moved.get("core", core))


def greet(with_grid):
    z, x, y, core = place_of()
    size_z, size_x = sizes_of()
    peers = [partner(y=1 - y), partner(core=1 - core)]
    if with_grid:
        peers += [partner(z=lax.rem(z + k, size_z)) for k in range(1, size_z)]
        peers += [partner(x=lax.rem(x + j, size_x)) for j in range(1, size_x)]
    barrier = pltpu.get_barrier_semaphore()
    for peer in peers:
        pl.semaphore_signal(barrier, inc=1, device_id=peer, device_id_type=MESH_ID)
    pl.semaphore_wait(barrier, len(peers))


def remote(src, dst, send, recv, peer):
    return pltpu.make_async_remote_copy(
        src_ref=src, dst_ref=dst, send_sem=send, recv_sem=recv, device_id=peer, device_id_type=MESH_ID
    )


def entry_kernel(size_z, size_x, count, *refs):
    tokens, wq, wk, wv = refs[:4]
    vectors = refs[4 : 4 + count]
    tokens_all, weights_all, vectors_all = refs[4 + count : 7 + count]
    raw = refs[7 + count : 7 + 2 * count]
    stage, wbuf, pack, vpack, local_sem, load_sem, tsend, trecv, zsend, zrecv, xsend, xrecv = refs[7 + 2 * count :]
    z, x, y, core = place_of()
    half = pack.shape[1] // 3
    pairs = half // 128
    me = z * size_x + x

    mine = pl.ds(pl.multiple_of(core * half, 128), half)
    loads = [pltpu.make_async_copy(w.at[:, mine], wbuf.at[i], load_sem.at[i]) for i, w in enumerate((wq, wk, wv))]
    loads += [pltpu.make_async_copy(v, r, load_sem.at[3 + i]) for i, (v, r) in enumerate(zip(vectors, raw))]
    for load in loads:
        load.start()
    load = pltpu.make_async_copy(tokens.at[y], stage, local_sem.at[0])
    load.start()
    vpack[...] = jnp.zeros_like(vpack)
    for copy in loads:
        copy.wait()
    for i, vector in enumerate(raw):
        vpack[i : i + 1, 0 : vector.shape[1]] = vector[...].astype(jnp.bfloat16).astype(jnp.float32)
    for i in range(3):
        for p in range(pairs):
            pack[:, (3 * p + i) * 128 : (3 * p + i + 1) * 128] = wbuf[i, :, p * 128 : (p + 1) * 128].astype(jnp.bfloat16)
    greet(True)
    across = remote(tokens.at[1 - y], tokens_all.at[1], tsend.at[0], trecv.at[0], partner(y=1 - y))
    across.start()
    along = []
    for k in range(1, size_z):
        peer = partner(z=lax.rem(z + k, size_z))
        along.append(
            (
                remote(pack, weights_all.at[me], zsend.at[0, k - 1], zrecv.at[0, k - 1], peer),
                remote(vpack, vectors_all.at[me], zsend.at[1, k - 1], zrecv.at[1, k - 1], peer),
            )
        )
    beside = remote(tokens.at[y], tokens_all.at[2], tsend.at[1], trecv.at[1], partner(core=1 - core))
    sideways = []

    def forward(k, weights_src, vectors_src):
        slot = lax.rem(z - k + size_z, size_z) * size_x + x
        for j in range(1, size_x):
            peer = partner(x=lax.rem(x + j, size_x))
            first = remote(weights_src, weights_all.at[slot], xsend.at[0, k, j - 1], xrecv.at[0, k, j - 1], peer)
            second = remote(vectors_src, vectors_all.at[slot], xsend.at[1, k, j - 1], xrecv.at[1, k, j - 1], peer)
            first.start()
            second.start()
            sideways.append((first, second))

    forward(0, pack, vpack)
    for first, second in along:
        first.start()
        second.start()
    beside.start()
    keep_weights = pltpu.make_async_copy(pack, weights_all.at[me], local_sem.at[1])
    keep_vectors = pltpu.make_async_copy(vpack, vectors_all.at[me], local_sem.at[2])
    keep_weights.start()
    keep_vectors.start()
    load.wait()
    keep_tokens = pltpu.make_async_copy(stage, tokens_all.at[0], local_sem.at[3])
    keep_tokens.start()
    order = sorted(range(1, size_z), key=lambda k: min(k, size_z - k))
    for k in order:
        first, second = along[k - 1]
        first.wait_recv()
        second.wait_recv()
        slot = lax.rem(z - k + size_z, size_z) * size_x + x
        forward(k, weights_all.at[slot], vectors_all.at[slot])
    across.wait_recv()
    onward = remote(tokens_all.at[1], tokens_all.at[3], tsend.at[2], trecv.at[2], partner(core=1 - core))
    onward.start()
    for first, second in sideways:
        first.wait()
        second.wait()
    for first, second in along:
        first.wait_send()
        second.wait_send()
    across.wait_send()
    beside.wait()
    onward.wait()
    keep_weights.wait()
    keep_vectors.wait()
    keep_tokens.wait()


def entry(size_z, size_x, tokens, wq, wk, wv, vectors):
    _, part, width = tokens.shape
    rows = wq.shape[0]
    lanes = wq.shape[1] // 2 * 3
    longest = max(v.shape[0] for v in vectors)
    shards = size_z * size_x
    anywhere = pl.BlockSpec(memory_space=pl.ANY)
    dma = pltpu.SemaphoreType.DMA
    return pl.pallas_call(
        lambda *refs: entry_kernel(size_z, size_x, len(vectors), *refs),
        out_shape=(
            jax.ShapeDtypeStruct((4, part, width), tokens.dtype),
            jax.ShapeDtypeStruct((shards, rows, lanes), jnp.bfloat16),
            jax.ShapeDtypeStruct((shards, 16, longest), jnp.float32),
        ),
        in_specs=[anywhere] * (4 + len(vectors)),
        out_specs=(anywhere, anywhere, anywhere),
        scratch_shapes=[pltpu.VMEM((1, v.shape[0]), v.dtype) for v in vectors]
        + [
            pltpu.VMEM((part, width), tokens.dtype),
            pltpu.VMEM((3, rows, lanes // 3), wq.dtype),
            pltpu.VMEM((rows, lanes), jnp.bfloat16),
            pltpu.VMEM((16, longest), jnp.float32),
            dma((4,)),
            dma((3 + len(vectors),)),
            dma((3,)),
            dma((3,)),
            dma((2, size_z - 1)),
            dma((2, size_z - 1)),
            dma((2, size_z, max(size_x - 1, 1))),
            dma((2, size_z, max(size_x - 1, 1))),
        ],
        compiler_params=pltpu.CompilerParams(collective_id=0, has_side_effects=True, vmem_limit_bytes=20 << 20),
        name="entry",
    )(tokens, wq, wk, wv, *[v.reshape(1, -1) for v in vectors])


def exit_kernel(size_z, size_x, terms, output_term, vector_terms, own_rows, other_rows, *refs):
    token_grads, grad_query, grad_key, grad_value, grad_output, vector_sums = refs[:6]
    refs = refs[6:]
    recv_rows, send_rows, far_rows, odd, xbuf, xvec, zout, zvout, zbuf, zvec, ybuf, yvec, cbuf, cvec = refs[:14]
    tsend, trecv, osend, orecv, xsend, xrecv, zsend, zrecv, ysend, yrecv, csend, crecv = refs[14:]
    z, x, y, core = place_of()
    shards, rows, lanes = terms.shape
    half = output_term.shape[2] // 2
    pairs = half // 128
    part = token_grads.shape[1]
    mine = pl.ds(pl.multiple_of(core * half, 128), half)
    theirs = pl.ds(pl.multiple_of((1 - core) * half, 128), half)
    order = sorted(range(size_z), key=lambda k: -min(k, size_z - k))
    greet(True)

    outputs = remote(output_term.at[:, :, theirs], odd, osend, orecv, partner(core=1 - core))
    outputs.start()
    halves = remote(other_rows, recv_rows, tsend.at[0], trecv.at[0], partner(core=1 - core))
    halves.start()
    sideways = {}

    def send_side(n, k, src, dst):
        for j in range(1, size_x):
            column = lax.rem(x + j, size_x)
            slot = lax.rem(z + k, size_z) * size_x + column
            if n == 1:
                odd[slot] = (odd[slot].astype(jnp.float32) + output_term[slot, :, mine].astype(jnp.float32)).astype(jnp.bfloat16)
            move = remote(src.at[slot], dst(j), xsend.at[n, k, j - 1], xrecv.at[n, k, j - 1], partner(x=column))
            move.start()
            sideways.setdefault((k, j), []).append(move)

    for k in order:
        send_side(0, k, terms, lambda j: xbuf.at[j - 1, k, :, 0:lanes])
        send_side(2, k, vector_terms, lambda j: xvec.at[j - 1, k])
        if k == order[0]:
            outputs.wait()
        send_side(1, k, odd, lambda j: xbuf.at[j - 1, k, :, lanes : lanes + half])

    halves.wait()
    for i in (1, 0):
        block = slice(i * part, (i + 1) * part)
        summed = own_rows[block, :] + recv_rows[block, :].astype(jnp.float32)
        if i == 1:
            send_rows[...] = summed.astype(jnp.bfloat16)
            back = remote(send_rows, far_rows, tsend.at[1], trecv.at[1], partner(y=1 - y))
            back.start()
        else:
            token_grads[y] = summed

    along = {}
    kept = None
    for k in order:
        target = lax.rem(z + k, size_z)
        slot = target * size_x + x
        total = terms[slot].astype(jnp.float32)
        total_out = odd[slot].astype(jnp.float32) + output_term[slot, :, mine].astype(jnp.float32)
        total_vec = vector_terms[slot]
        for j in range(1, size_x):
            for move in sideways[k, j]:
                move.wait()
            total = total + xbuf[j - 1, k, :, 0:lanes].astype(jnp.float32)
            total_out = total_out + xbuf[j - 1, k, :, lanes : lanes + half].astype(jnp.float32)
            total_vec = total_vec + xvec[j - 1, k]
        if k == 0:
            kept = (total, total_out, total_vec)
            continue
        zout[k - 1, :, 0:lanes] = total.astype(jnp.bfloat16)
        zout[k - 1, :, lanes : lanes + half] = total_out.astype(jnp.bfloat16)
        zvout[k - 1] = total_vec
        peer = partner(z=target)
        moves = (
            remote(zout.at[k - 1], zbuf.at[k - 1], zsend.at[0, k - 1], zrecv.at[0, k - 1], peer),
            remote(zvout.at[k - 1], zvec.at[k - 1], zsend.at[1, k - 1], zrecv.at[1, k - 1], peer),
        )
        for move in moves:
            move.start()
        along[k] = moves

    total, total_out, total_vec = kept
    for k in reversed(order):
        if k == 0:
            continue
        for move in along[k]:
            move.wait()
        total = total + zbuf[k - 1, :, 0:lanes].astype(jnp.float32)
        total_out = total_out + zbuf[k - 1, :, lanes : lanes + half].astype(jnp.float32)
        total_vec = total_vec + zvec[k - 1]
    ybuf[0, :, 0:lanes] = total.astype(jnp.bfloat16)
    ybuf[0, :, lanes : lanes + half] = total_out.astype(jnp.bfloat16)
    yvec[0] = total_vec
    moves = (
        remote(ybuf.at[0], ybuf.at[1], ysend.at[0], yrecv.at[0], partner(y=1 - y)),
        remote(yvec.at[0], yvec.at[1], ysend.at[1], yrecv.at[1], partner(y=1 - y)),
    )
    for move in moves:
        move.start()
    for move in moves:
        move.wait()
    cbuf[0] = ybuf[0].astype(jnp.float32) + ybuf[1].astype(jnp.float32)
    cvec[0] = yvec[0] + yvec[1]
    moves = (
        remote(cbuf.at[0], cbuf.at[1], csend.at[0], crecv.at[0], partner(core=1 - core)),
        remote(cvec.at[0], cvec.at[1], csend.at[1], crecv.at[1], partner(core=1 - core)),
    )
    for move in moves:
        move.start()
    back.wait()
    token_grads[1 - y] = far_rows[...].astype(jnp.float32)
    for move in moves:
        move.wait()
    for i in range(2):
        owner = core if i == 0 else 1 - core
        for p in range(pairs):
            place = pl.ds(pl.multiple_of(owner * half + p * 128, 128), 128)
            for n, out in enumerate((grad_query, grad_key, grad_value)):
                out[:, place] = cbuf[i, :, (3 * p + n) * 128 : (3 * p + n + 1) * 128]
        grad_output[:, pl.ds(pl.multiple_of(owner * half, 128), half)] = cbuf[i, :, lanes : lanes + half]
    vector_sums[...] = cvec[0] + cvec[1]


def exit_call(size_z, size_x, terms, output_term, vector_terms, own_rows, other_rows):
    shards, rows, lanes = terms.shape
    width = output_term.shape[2]
    half = width // 2
    part = own_rows.shape[0] // 2
    vrows, vlanes = vector_terms.shape[1:]
    vmem = pl.BlockSpec(memory_space=pltpu.VMEM)
    dma = pltpu.SemaphoreType.DMA
    full = lanes + half
    side = max(size_x - 1, 1)
    low, high = jnp.bfloat16, jnp.float32
    matrix = jax.ShapeDtypeStruct((rows, width), high)
    return pl.pallas_call(
        lambda *refs: exit_kernel(size_z, size_x, *refs),
        out_shape=(
            jax.ShapeDtypeStruct((2, part, width), high),
            matrix,
            matrix,
            matrix,
            matrix,
            jax.ShapeDtypeStruct((vrows, vlanes), high),
        ),
        in_specs=[vmem] * 5,
        out_specs=(vmem,) * 6,
        scratch_shapes=[
            pltpu.VMEM((2 * part, width), low),
            pltpu.VMEM((part, width), low),
            pltpu.VMEM((part, width), low),
            pltpu.VMEM((shards, rows, half), low),
            pltpu.VMEM((side, size_z, rows, full), low),
            pltpu.VMEM((side, size_z, vrows, vlanes), high),
            pltpu.VMEM((size_z - 1, rows, full), low),
            pltpu.VMEM((size_z - 1, vrows, vlanes), high),
            pltpu.VMEM((size_z - 1, rows, full), low),
            pltpu.VMEM((size_z - 1, vrows, vlanes), high),
            pltpu.VMEM((2, rows, full), low),
            pltpu.VMEM((2, vrows, vlanes), high),
            pltpu.VMEM((2, rows, full), high),
            pltpu.VMEM((2, vrows, vlanes), high),
            dma((2,)),
            dma((2,)),
            dma,
            dma,
            dma((3, size_z, side)),
            dma((3, size_z, side)),
            dma((2, size_z - 1)),
            dma((2, size_z - 1)),
            dma((2,)),
            dma((2,)),
            dma((2,)),
            dma((2,)),
        ],
        compiler_params=pltpu.CompilerParams(collective_id=1, has_side_effects=True, vmem_limit_bytes=60 << 20),
        name="exit",
    )(terms, output_term, vector_terms, own_rows, other_rows)


def finish_kernel(inner, outer, grad_inner, grad_outer, ybuf, yvuf, cbuf, cvuf, ysend, yrecv, csend, crecv):
    z, x, y, core = place_of()
    greet(False)
    moves = (
        remote(inner, ybuf, ysend.at[0], yrecv.at[0], partner(y=1 - y)),
        remote(outer, yvuf, ysend.at[1], yrecv.at[1], partner(y=1 - y)),
    )
    for move in moves:
        move.start()
    sources = ((inner, ybuf, cbuf, grad_inner), (outer, yvuf, cvuf, grad_outer))
    onward = []
    for i, (own, far, swap_buf, out) in enumerate(sources):
        moves[i].wait()
        swap_buf[0] = own[...].astype(jnp.float32) + far[...].astype(jnp.float32)
        move = remote(swap_buf.at[0], swap_buf.at[1], csend.at[i], crecv.at[i], partner(core=1 - core))
        move.start()
        onward.append(move)
    for i, (own, far, swap_buf, out) in enumerate(sources):
        onward[i].wait()
        rows = own.shape[0]
        first = core == 0
        out[0:rows, :] = jnp.where(first, swap_buf[0], swap_buf[1])
        out[rows : 2 * rows, :] = jnp.where(first, swap_buf[1], swap_buf[0])


def finish(inner, outer):
    vmem = pl.BlockSpec(memory_space=pltpu.VMEM)
    dma = pltpu.SemaphoreType.DMA
    low, high = jnp.bfloat16, jnp.float32
    return pl.pallas_call(
        finish_kernel,
        out_shape=tuple(jax.ShapeDtypeStruct((2 * a.shape[0], a.shape[1]), high) for a in (inner, outer)),
        in_specs=[vmem] * 2,
        out_specs=(vmem,) * 2,
        scratch_shapes=[
            pltpu.VMEM(inner.shape, low),
            pltpu.VMEM(outer.shape, low),
            pltpu.VMEM((2,) + inner.shape, high),
            pltpu.VMEM((2,) + outer.shape, high),
            dma((2,)),
            dma((2,)),
            dma((2,)),
            dma((2,)),
        ],
        compiler_params=pltpu.CompilerParams(collective_id=2, has_side_effects=True, vmem_limit_bytes=30 << 20),
        name="finish",
    )(inner, outer)


HD = 64
EPS = 1e-12
ROOT_HALF = 0.7071067811865476
INV_ROOT_TAU = 0.3989422804014327


def lowered(piece):
    return piece.astype(jnp.bfloat16)


def widen(piece):
    return piece.astype(jnp.float32)


def matmul(left, right):
    return jnp.dot(left, right, preferred_element_type=jnp.float32)


def matmul_tn(left, right):
    return lax.dot_general(
        left, right, (((0,), (0,)), ((), ())), preferred_element_type=jnp.float32
    )


def matmul_nt(left, right):
    return lax.dot_general(
        left, right, (((1,), (1,)), ((), ())), preferred_element_type=jnp.float32
    )


def normalize(hidden, norm_gain, norm_shift):
    centred = hidden - jnp.mean(hidden, axis=-1, keepdims=True)
    reciprocal = lax.rsqrt(jnp.mean(centred * centred, axis=-1, keepdims=True) + EPS)
    normed = centred * reciprocal
    return (normed * norm_gain + norm_shift, normed, reciprocal)


def normalize_back(upstream, normed, reciprocal, norm_gain):
    scaled = upstream * norm_gain
    result = reciprocal * (
        scaled
        - jnp.mean(scaled, axis=-1, keepdims=True)
        - normed * jnp.mean(scaled * normed, axis=-1, keepdims=True)
    )
    return (result, jnp.sum(upstream * normed, axis=0), jnp.sum(upstream, axis=0))


def gelu_value(values_in):
    return 0.5 * values_in * (1.0 + lax.erf(values_in * ROOT_HALF))


def gelu_slope(values_in):
    return (
        0.5 * (1.0 + lax.erf(values_in * ROOT_HALF))
        + values_in * jnp.exp(-0.5 * values_in * values_in) * INV_ROOT_TAU
    )


def swap(piece, axis):
    return lax.ppermute(piece, axis, [(0, 1), (1, 0)])


def pick(piece, index, axis=0):
    return lax.dynamic_index_in_dim(piece, index, axis, keepdims=False)


def in_order(first_is_zero, own, other, axis):
    return jnp.where(
        first_is_zero,
        jnp.concatenate([own, other], axis),
        jnp.concatenate([other, own], axis),
    )


def body(
    tokens,
    segment_ids,
    w_query,
    w_key,
    w_value,
    w_output,
    b_query,
    b_value,
    b_output,
    first_gain,
    first_shift,
    w_inner,
    b_inner,
    w_outer,
    b_outer,
    second_gain,
    second_shift,
    cotangent,
):
    core, y = lax.axis_index("core"), lax.axis_index("y")
    size_z, size_x = lax.axis_size("z"), lax.axis_size("x")
    shards = size_z * size_x
    everyone = ("z", "x", "core")
    sequences, part, width = tokens.shape
    half = width // 2
    pairs = half // 128
    hidden = w_inner.shape[1]
    local = 2 * part
    own_rows = w_query.shape[0]
    lanes = 3 * half

    stack = hidden // width

    def core_rows(matrix):
        rows = matrix.shape[0] // 2
        return lowered(lax.dynamic_slice_in_dim(matrix, core * rows, rows, 0))

    def side_by_side(matrix, groups):
        rows = matrix.shape[0] // groups // stack
        return matrix.reshape(groups, stack, rows, width).transpose(0, 2, 1, 3).reshape(groups * rows, hidden)

    def stacked(matrix, groups):
        rows = matrix.shape[0] // groups
        return matrix.reshape(groups, rows, stack, width).transpose(0, 2, 1, 3).reshape(groups * rows * stack, width)

    pieces = (core_rows(w_inner), core_rows(w_output), side_by_side(core_rows(w_outer), 1))
    dense = lax.all_gather(jnp.concatenate(pieces, axis=1), everyone, axis=0, tiled=True)
    full_inner, full_output = dense[:, :hidden], dense[:, hidden : hidden + width]
    full_outer = stacked(dense[:, hidden + width :], 2 * shards)

    vectors = (b_query, b_value, b_output, first_gain, first_shift, b_inner, b_outer, second_gain, second_shift)
    sizes = [v.shape[0] for v in vectors]
    tokens_all, early, vectors_all = entry(size_z, size_x, tokens, w_query, w_key, w_value, vectors)
    inputs_all = tokens_all.reshape(4 * part, width)
    full_early = early.reshape(width, lanes)
    inputs = inputs_all[:local]
    cotangent_mine = pick(cotangent, y)
    cotangent_arrived = swap(pick(cotangent, 1 - y), "y")
    bias_query, bias_value, bias_output, gain_first, shift_first, bias_inner, bias_outer, gain_second, shift_second = [
        vectors_all[:, i, :size].reshape(shards * size) for i, size in enumerate(sizes)
    ]
    heads_query = lax.dynamic_slice_in_dim(bias_query, core * half, half).reshape(pairs, 1, 128)
    heads_value = lax.dynamic_slice_in_dim(bias_value, core * half, half).reshape(pairs, 1, 128)
    bias_all = jnp.concatenate([heads_query, jnp.zeros_like(heads_query), heads_value], axis=1).reshape(lanes)
    scale = jnp.tile(jnp.concatenate([jnp.full((128,), HD ** (-0.5)), jnp.ones((256,))]), pairs)
    projected = lowered((matmul(inputs_all, full_early) + bias_all) * scale)

    spot = jnp.arange(5, dtype=jnp.int32)
    place = jnp.where(spot < 4, ((spot % 2 != core) * 2 + (spot // 2 != y) * 1) * part, core)
    segments = pick(segment_ids, y)
    context_mine, context_other, logsum = attention(place, segments, projected)
    context = in_order(core == 0, context_mine, swap(context_other, "core"), 1)

    attended = matmul(context, full_output) + bias_output
    first, first_normed, first_recip = normalize(widen(inputs) + attended, gain_first, shift_first)
    first_low = lowered(first)
    inner = matmul(first_low, full_inner) + bias_inner
    active = lowered(gelu_value(inner))
    outer = matmul(active, full_outer) + bias_outer
    mixed, second_normed, second_recip = normalize(first + outer, gain_second, shift_second)
    mixed = lowered(mixed)

    upstream = widen(jnp.concatenate([cotangent_mine, cotangent_arrived], axis=0))
    pre_second, grad_second_gain, grad_second_shift = normalize_back(upstream, second_normed, second_recip, gain_second)
    grad_outer = lowered(pre_second)
    grad_b_outer = jnp.sum(widen(grad_outer), axis=0)
    outer_term = side_by_side(lowered(matmul_tn(active, grad_outer)), 2 * shards)
    grad_inner = lowered(matmul_nt(grad_outer, full_outer) * gelu_slope(inner))
    grad_b_inner = jnp.sum(widen(grad_inner), axis=0)
    inner_term = lowered(matmul_tn(first_low, grad_inner))
    both_done = lax.psum_scatter(jnp.concatenate([inner_term, outer_term], axis=1), everyone, scatter_dimension=0, tiled=True)
    inner_done, outer_done = both_done[:, :hidden], stacked(both_done[:, hidden:], 1)
    grad_first = pre_second + matmul_nt(grad_inner, full_inner)
    pre_first, grad_first_gain, grad_first_shift = normalize_back(grad_first, first_normed, first_recip, gain_first)
    grad_attended = lowered(pre_first)
    grad_b_output = jnp.sum(widen(grad_attended), axis=0)
    grad_w_output = lowered(matmul_tn(context, grad_attended))
    grad_context = lowered(matmul_nt(grad_attended, full_output))
    context_send = lax.dynamic_slice_in_dim(grad_context, (1 - core) * half, half, 1)
    upstream_other = swap(context_send, "core")
    mixed_out = in_order(y == 0, mixed[None, :part], swap(mixed[part:], "y")[None], 0)

    grads, sums = attention_back(place, segments, projected, context_mine, context_other, grad_context, upstream_other, logsum)
    grad_early = lowered(matmul_tn(inputs_all, grads)).reshape(shards, own_rows, lanes)
    own_partial = pre_first + matmul_nt(grads[:local], full_early)
    other_partial = lowered(matmul_nt(grads[local:], full_early))
    sums = sums.reshape(pairs, 8, 3, 128)[:, 0]
    blank = jnp.zeros((width,), jnp.float32)
    grad_b_query = lax.dynamic_update_slice(blank, sums[:, 0].reshape(half), (core * half,))
    grad_b_value = lax.dynamic_update_slice(blank, sums[:, 2].reshape(half), (core * half,))
    vector_grads = (
        grad_b_query,
        grad_b_value,
        grad_b_output,
        grad_first_gain,
        grad_first_shift,
        grad_b_inner,
        grad_b_outer,
        grad_second_gain,
        grad_second_shift,
    )
    longest = vectors_all.shape[2]
    rows = [jnp.pad(v.reshape(shards, 1, -1), ((0, 0), (0, 0), (0, longest - v.shape[0] // shards))) for v in vector_grads]
    rows.append(jnp.zeros((shards, vectors_all.shape[1] - len(rows), longest), jnp.float32))
    vector_terms = jnp.concatenate(rows, axis=1)
    grad_tokens, grad_query, grad_key, grad_value, grad_output, vector_sums = exit_call(
        size_z, size_x, grad_early, grad_w_output.reshape(shards, own_rows, width), vector_terms, own_partial, other_partial
    )
    grad_inner_full, grad_outer_full = finish(inner_done, outer_done)
    done = [vector_sums[i, :size] for i, size in enumerate(sizes)]
    return (
        mixed_out,
        grad_tokens,
        grad_query,
        grad_key,
        grad_value,
        grad_output,
        done[0],
        done[1],
        done[2],
        done[3],
        done[4],
        grad_inner_full,
        done[5],
        grad_outer_full,
        done[6],
        done[7],
        done[8],
    )


def solution(mesh):
    outer, inner = mesh.devices.shape
    size_z = 1
    while size_z * size_z < outer:
        size_z *= 2
    split = Mesh(mesh.devices.reshape(size_z, outer // size_z, inner // 2, 2), ("z", "x", "y", "core"))
    dp, seq = ("z", "x"), ("y", "core")
    activation, matrix, vector = P(dp, seq, None), P(dp, None), P(dp)
    return jax.shard_map(
        body,
        mesh=split,
        in_specs=(
            activation,
            matrix,
            matrix,
            matrix,
            matrix,
            matrix,
            vector,
            vector,
            vector,
            vector,
            vector,
            matrix,
            vector,
            matrix,
            vector,
            vector,
            vector,
            activation,
        ),
        out_specs=(
            activation,
            activation,
            matrix,
            matrix,
            matrix,
            matrix,
            vector,
            vector,
            vector,
            vector,
            vector,
            matrix,
            vector,
            matrix,
            vector,
            vector,
            vector,
        ),
        check_vma=False,
    )
```

profile of v0, /device:TPU:0, one launch (start us, length us, event | category | flops | bytes accessed | tf_op | source)
XLA Modules:
  0.0 423.4 jit_solution(11497198483780251028)
XLA Ops:
  12.0 41.7 %entry.1 = (bf16[4,512,768]{2,1,0:T(8,128)(2,1)S(1)}, bf16[8,96,1152]{2,1,0:T(8,128)(2,1)S(1)}, f32[8,16,384]{2,1,0:T(8,128)S(1)}) custom-call(bf16[2,512,768]{2,1,0:T(8,128)(2,1)S(1)} %copy-done.2, f32[96,768]{1,0:T(8,128)S(1)} %copy-done.6, f32[96,768]{1,0:T(8,128)S(1)} %copy-done.7, f32[96,768]{1,0:T(8,128)S(1)} %copy-done.8, f32[1,96]{1,0:T(1,128)S(1)} %bitcast.80, ...), custom_call_target="tpu_custom_call" | custom-call | tf_op jit(solution)/shard_map/entry/pallas_call | solution.py:495
  58.3 9.1 %multiply_convert_fusion.1.qkv_ref = bf16[2048,1152]{1,0:T(8,128)(2,1)} fusion(bf16[2048,768]{1,0:T(8,128)(2,1)} %bitcast.78, bf16[768,1152]{1,0:T(8,128)(2,1)} %bitcast.88, f32[1152]{0:T(1024)S(1)} %mul.163, f32[1152]{0:T(1024)S(1)} %add.153), kind=kOutput, calls=%fused_computation.11 | convolution fusion | flops 3630956544 | bytes 9643008 | tf_op jit(solution)/shard_map/dot_general | solution.py:765
  67.4 34.9 %attention_forward.1 = (bf16[1024,384]{1,0:T(8,128)(2,1)}, bf16[1024,384]{1,0:T(8,128)(2,1)}, f32[24,2048]{1,0:T(8,128)}) custom-call(s32[5]{0:T(128)} %compare_select_fusion.1.place_ref, s32[2048]{0:T(1024)} %bitcast.107, bf16[2048,1152]{1,0:T(8,128)(2,1)} %multiply_convert_fusion.1.qkv_ref, s32[1,2048]{1,0:T(1,128)} %constant_dynamic-slice_fusion.1.row_ref), custom_call_target="tpu_custom_call" | custom-call | flops 24000000000 | bytes 9000000 | tf_op jit(solution)/shard_map/attention_forward/pallas_call | solution.py:156
  105.1 7.0 %collective-permute-start.2 = (bf16[512,768]{1,0:T(8,128)(2,1)}, bf16[512,768]{1,0:T(8,128)(2,1)}, u32[]{:S(2)}, u32[]{:S(2)}) collective-permute-start(bf16[512,768]{1,0:T(8,128)(2,1)} %get-tuple-element.73), channel_id=1, source_target_pairs={{0,2},{2,0},{1,3},{3,1},{4,6},{6,4},{5,7},{7,5},{8,10},{10,8},{9,1... | collective-permute-start | bytes 2359304 | tf_op jit(solution)/shard_map/ppermute | solution.py:809
  113.8 3.2 all-gather.2.cloned.1.call-done
  116.9 4.2 %fusion.45 = (f32[1024]{0:T(1024)S(1)}, f32[1024,768]{1,0:T(8,128)S(1)}) fusion(f32[768]{0:T(1024)S(1)} %add.158, bf16[768,6912]{1,0:T(8,128)(2,1)} %all-gather.2.cloned.1.call-done, bf16[1024,384]{1,0:T(8,128)(2,1)} %collective-permute-done, bf16[1024,384]{1,0:T(8,128)(2,1)} %get-tuple-element.36.ctx_mine_ref, pred[]{:T(512)S(6)} %eq.9, ...), kind=kOutput, calls=%fused_computation.114 | convolution fusion | flops 1218182144 | bytes 7478273 | tf_op jit(solution)/shard_map/dot_general | solution.py:765
  121.7 4.9 %slice.127 = bf16[768,3072]{1,0:T(8,128)(2,1)} slice(bf16[768,6912]{1,0:T(8,128)(2,1)} %all-gather.2.cloned.1.call-done), slice={[0:768], [3840:6912]} | slice | bytes 9437184 | tf_op jit(solution)/shard_map/slice | solution.py:873
  126.6 9.7 %reshape.202 = bf16[16,48,4,768]{3,2,1,0:T(4,128)(2,1)} reshape(bf16[768,3072]{1,0:T(8,128)(2,1)} %slice.127) | data formatting | bytes 9437184 | tf_op jit(solution)/shard_map/reshape | solution.py:868
  136.3 3.2 copy.45
  139.6 11.0 %multiply_convert_fusion = (bf16[1024,3072]{1,0:T(8,128)(2,1)S(1)}, f32[1024,3072]{1,0:T(8,128)}) fusion(f32[3072]{0:T(1024)S(1)} %bitcast.105, bf16[768,6912]{1,0:T(8,128)(2,1)} %all-gather.2.cloned.1.call-done, f32[1024,768]{1,0:T(8,128)S(1)} %get-tuple-element.87, f32[768]{0:T(1024)S(1)} %add.163, f32[768]{0:T(1024)S(1)} %mul.171, ...), kind=kOutput, calls=%fused_computation.8 | convolution fusion | flops 4854644736 | bytes 26765312 | tf_op jit(solution)/shard_map/dot_general | solution.py:765
  150.6 5.4 %fusion.46 = (f32[1024]{0:T(1024)S(1)}, f32[1024,768]{1,0:T(8,128)S(1)}) fusion(f32[768]{0:T(1024)S(1)} %add.170, bf16[1024,3072]{1,0:T(8,128)(2,1)S(1)} %get-tuple-element.88, bf16[3072,768]{1,0:T(8,128)(2,1)S(1)} %bitcast.94, f32[768]{0:T(1024)S(1)} %add.163, f32[768]{0:T(1024)S(1)} %mul.171, f32[1024]{0:T(1024)S(1)} %add_rsqrt_fusion.1, ...), kind=kOutput, calls=%fused_computation.115 | convolution fusion | flops 4837342208 | bytes 17323008 | tf_op jit(solution)/shard_map/dot_general | solution.py:765
  159.5 3.0 convert_reduce_fusion.2
  162.5 5.8 %convolution_convert_fusion = bf16[3072,768]{1,0:T(8,128)(2,1)S(1)} fusion(bf16[1024,3072]{1,0:T(8,128)(2,1)S(1)} %get-tuple-element.88, f32[1024,768]{1,0:T(8,128)S(1)} %get-tuple-element.68), kind=kOutput, calls=%fused_computation.12 | convolution fusion | flops 4834983936 | bytes 14155776 | tf_op jit(solution)/shard_map/dot_general | solution.py:769
  168.2 11.7 %convert_reduce_fusion = (f32[3072]{0:T(1024)S(1)}, bf16[1024,3072]{1,0:T(8,128)(2,1)S(1)}) fusion(f32[1024,3072]{1,0:T(8,128)} %get-tuple-element.89, f32[3072]{0:T(1024)S(1)} %bitcast.106, bf16[3072,768]{1,0:T(8,128)(2,1)S(1)} %bitcast.95, f32[1024,768]{1,0:T(8,128)S(1)} %get-tuple-element.68), kind=kOutput, calls=%fused_computation.7 | convolution fusion | flops 4873516032 | bytes 26763264 | tf_op jit(solution)/shard_map/dot_general | solution.py:775
  183.5 6.3 %convolution_convert_fusion.1 = bf16[768,3072]{1,0:T(8,128)(2,1)S(1)} fusion(bf16[1024,3072]{1,0:T(8,128)(2,1)S(1)} %get-tuple-element.94, f32[1024,768]{1,0:T(8,128)S(1)} %get-tuple-element.87, f32[768]{0:T(1024)S(1)} %add.163, f32[768]{0:T(1024)S(1)} %mul.171, f32[1024]{0:T(1024)S(1)} %add_rsqrt_fusion.1, f32[1024]{0:T(1024)S(1)} %broadcast_multiply_fusion.5), kind=kOutput, calls=%fused_computation.13 | convolution fusion | flops 4838129664 | bytes 14170112 | tf_op jit(solution)/shard_map/dot_general | solution.py:769
  189.8 4.0 pad_maximum_fusion
  193.8 10.2 %multiply_reduce_fusion = (f32[768]{0:T(1024)S(1)}, f32[1024]{0:T(1024)S(1)}, f32[1024]{0:T(1024)S(1)}, f32[768]{0:T(1024)S(1)}, f32[1024,768]{1,0:T(8,128)S(1)}) fusion(f32[1024,768]{1,0:T(8,128)S(1)} %get-tuple-element.87, f32[1024]{0:T(1024)S(1)} %add_rsqrt_fusion.1, f32[1024]{0:T(1024)S(1)} %broadcast_multiply_fusion.5, f32[768]{0:T(1024)S(1)} %mul.171, ...), kind=kOutput, calls=%fused_computation.31 | convolution fusion | flops 4839698432 | bytes 20472832 | tf_op jit(solution)/shard_map/dot_general | solution.py:775
  214.6 6.0 %convolution_convert_fusion.4 = bf16[768,768]{1,0:T(8,128)(2,1)} fusion(bf16[1024,384]{1,0:T(8,128)(2,1)} %collective-permute-done, bf16[1024,384]{1,0:T(8,128)(2,1)} %get-tuple-element.36.ctx_mine_ref, pred[]{:T(512)S(6)} %eq.9, f32[1024,768]{1,0:T(8,128)} %copy-done.23), kind=kOutput, calls=%fused_computation.55 | convolution fusion | flops 1216413696 | bytes 5898241 | tf_op jit(solution)/shard_map/dot_general | solution.py:769
  220.6 58.6 %attention_backward.1 = (bf16[2048,1152]{1,0:T(8,128)(2,1)}, f32[24,384]{1,0:T(8,128)}) custom-call(s32[5]{0:T(128)} %compare_select_fusion.1.place_ref, s32[2048]{0:T(1024)} %bitcast.108, bf16[2048,1152]{1,0:T(8,128)(2,1)} %multiply_convert_fusion.1.qkv_ref, bf16[1024,384]{1,0:T(8,128)(2,1)} %get-tuple-element.36.ctx_mine_ref, ...), custom_call_target="tpu_custom_call" | custom-call | flops 60000002048 | bytes 15000000 | tf_op jit(solution)/shard_map/attention_backward/pallas_call | solution.py:320
  280.4 5.2 %fusion.28.refs_4_ = bf16[1024,768]{1,0:T(8,128)(2,1)} fusion(bf16[768,1152]{1,0:T(8,128)(2,1)S(1)} %bitcast.89, bf16[2048,1152]{1,0:T(8,128)(2,1)} %get-tuple-element.39), kind=kOutput, calls=%fused_computation.50 | convolution fusion | flops 1812725760 | bytes 5701632 | tf_op jit(solution)/shard_map/dot_general | solution.py:775
  285.6 5.5 %convolution_convert_fusion.2 = bf16[768,1152]{1,0:T(8,128)(2,1)} fusion(bf16[2048,768]{1,0:T(8,128)(2,1)S(1)} %bitcast.79, bf16[2048,1152]{1,0:T(8,128)(2,1)S(1)} %copy-done.34), kind=kOutput, calls=%fused_computation.24 | convolution fusion | flops 3624763392 | bytes 9633792 | tf_op jit(solution)/shard_map/dot_general | solution.py:769
  292.8 6.5 %fusion.25.refs_3_ = f32[1024,768]{1,0:T(8,128)} fusion(f32[1024,768]{1,0:T(8,128)} %copy-done.23, bf16[768,1152]{1,0:T(8,128)(2,1)S(1)} %bitcast.90, bf16[2048,1152]{1,0:T(8,128)(2,1)} %get-tuple-element.39), kind=kOutput, calls=%fused_computation.49 | convolution fusion | flops 1812725760 | bytes 10420224 | tf_op jit(solution)/shard_map/dot_general | solution.py:775
  299.3 82.2 %exit.1 = (f32[2,512,768]{2,1,0:T(8,128)}, f32[96,768]{1,0:T(8,128)}, f32[96,768]{1,0:T(8,128)}, f32[96,768]{1,0:T(8,128)}, f32[96,768]{1,0:T(8,128)}, /*index=5*/f32[16,384]{1,0:T(8,128)}) custom-call(bf16[8,96,1152]{2,1,0:T(8,128)(2,1)} %bitcast.97, bf16[8,96,768]{2,1,0:T(8,128)(2,1)} %bitcast.102, f32[8,16,384]{2,1,0:T(8,128)} %concatenate.34.refs_2_, ...), custom_call_target="tpu_custom_call" | custom-call | tf_op jit(solution)/shard_map/exit/pallas_call | solution.py:656
  392.0 17.5 %finish.1 = (f32[96,3072]{1,0:T(8,128)S(1)}, f32[384,768]{1,0:T(8,128)S(1)}) custom-call(bf16[48,3072]{1,0:T(8,128)(2,1)S(1)} %get-tuple-element.77.inner, bf16[192,768]{1,0:T(8,128)(2,1)S(1)} %bitcast.77), custom_call_target="tpu_custom_call" | custom-call | tf_op jit(solution)/shard_map/finish/pallas_call | solution.py:730
  (166 shorter events, 51.4 us)
Async XLA Ops:
  7.2 4.6 %copy-start.32 = (f32[384]{0:T(512)S(1)}, f32[384]{0:T(512)}, u32[]{:S(2)}) copy-start(f32[384]{0:T(512)} %constant.84.clone.1) | copy-start | bytes 4612
  7.2 4.6 %copy-start.31 = (f32[384]{0:T(512)S(1)}, f32[384]{0:T(512)}, u32[]{:S(2)}) copy-start(f32[384]{0:T(512)} %param.30) | copy-start | bytes 4612
  7.2 4.7 %copy-start.2 = (bf16[2,512,768]{2,1,0:T(8,128)(2,1)S(1)}, bf16[2,512,768]{2,1,0:T(8,128)(2,1)}, u32[]{:S(2)}) copy-start(bf16[2,512,768]{2,1,0:T(8,128)(2,1)} %refs_0_.1) | copy-start | bytes 4718596
  7.2 4.7 %copy-start.6 = (f32[96,768]{1,0:T(8,128)S(1)}, f32[96,768]{1,0:T(8,128)}, u32[]{:S(2)}) copy-start(f32[96,768]{1,0:T(8,128)} %refs_1_.1) | copy-start | bytes 884740
  7.3 4.7 %copy-start.7 = (f32[96,768]{1,0:T(8,128)S(1)}, f32[96,768]{1,0:T(8,128)}, u32[]{:S(2)}) copy-start(f32[96,768]{1,0:T(8,128)} %refs_2_.1) | copy-start | bytes 884740
  7.3 4.7 %copy-start.9 = (f32[96]{0:T(128)S(1)}, f32[96]{0:T(128)}, u32[]{:S(2)}) copy-start(f32[96]{0:T(128)} %param.24) | copy-start | bytes 1156
  7.3 4.7 %copy-start.10 = (f32[96]{0:T(128)S(1)}, f32[96]{0:T(128)}, u32[]{:S(2)}) copy-start(f32[96]{0:T(128)} %param.25) | copy-start | bytes 1156
  7.3 4.7 %copy-start.11 = (f32[96]{0:T(128)S(1)}, f32[96]{0:T(128)}, u32[]{:S(2)}) copy-start(f32[96]{0:T(128)} %param.26) | copy-start | bytes 1156
  7.3 4.7 %copy-start.12 = (f32[96]{0:T(128)S(1)}, f32[96]{0:T(128)}, u32[]{:S(2)}) copy-start(f32[96]{0:T(128)} %param.27) | copy-start | bytes 1156
  7.3 109.6 %all-gather.2.cloned.1.call-start = ((), (), s32[]{:S(2)}) async-start(), calls=%async_computation.1 | async-start | bytes 11280384 | tf_op jit(solution)/shard_map/all_gather | solution.py:871
  8.6 49.1 %copy-start.30 = (s32[2,2048]{1,0:T(2,128)S(1)}, s32[2,2048]{1,0:T(2,128)}, u32[]{:S(2)}) copy-start(s32[2,2048]{1,0:T(2,128)} %param.19) | copy-start | bytes 49156
  11.8 375.5 %reduce-scatter.2.cloned.1.call-start = ((), (), s32[]{:S(2)}) async-start(), calls=%async_computation.2 | async-start | bytes 10027008 | tf_op jit(solution)/shard_map/reduce_scatter | solution.py:915
  102.3 9.8 %copy-start.4 = (bf16[4,512,768]{2,1,0:T(8,128)(2,1)S(1)}, bf16[4,512,768]{2,1,0:T(8,128)(2,1)}, u32[]{:S(2)}) copy-start(bf16[4,512,768]{2,1,0:T(8,128)(2,1)} %copy-done.3) | copy-start | bytes 9437188
  102.3 11.5 %collective-permute-start = (bf16[1024,384]{1,0:T(8,128)(2,1)}, bf16[1024,384]{1,0:T(8,128)(2,1)}, u32[]{:S(2)}, u32[]{:S(2)}) collective-permute-start(bf16[1024,384]{1,0:T(8,128)(2,1)} %get-tuple-element.37.ctx_other_ref), channel_id=1, source_target_pairs={{0,1},{1,0},{2,3},{3,2},{4,5},{5,4},{6,7},{7,6},{8,9},{9,8},{10,11... | collective-permute-start | bytes 2359304 | tf_op jit(solution)/shard_map/ppermute | solution.py:809
  105.1 51.4 %collective-permute-start.2 = (bf16[512,768]{1,0:T(8,128)(2,1)}, bf16[512,768]{1,0:T(8,128)(2,1)}, u32[]{:S(2)}, u32[]{:S(2)}) collective-permute-start(bf16[512,768]{1,0:T(8,128)(2,1)} %get-tuple-element.73), channel_id=1, source_target_pairs={{0,2},{2,0},{1,3},{3,1},{4,6},{6,4},{5,7},{7,5},{8,10},{10,8},{9,1... | collective-permute-start | bytes 2359304 | tf_op jit(solution)/shard_map/ppermute | solution.py:809
  162.5 5.8 %copy-start.21 = (f32[1024,768]{1,0:T(8,128)}, f32[1024,768]{1,0:T(8,128)S(1)}, u32[]{:S(2)}) copy-start(f32[1024,768]{1,0:T(8,128)S(1)} %get-tuple-element.68) | copy-start | bytes 9437188
  210.9 9.6 %collective-permute-start.3 = (bf16[1024,384]{1,0:T(8,128)(2,1)S(1)}, bf16[1024,384]{1,0:T(8,128)(2,1)}, u32[]{:S(2)}, u32[]{:S(2)}) collective-permute-start(bf16[1024,384]{1,0:T(8,128)(2,1)S(1)} %constant_dynamic-slice_fusion), channel_id=1, source_target_pairs={{0,1},{1,0},{2,3},{3,2},{4,5},{5,4},{6,7},{7,6},{8,9},{9,8},{10,11... | collective-permute-start | bytes 2359304 | tf_op jit(solution)/shard_map/ppermute | solution.py:809
  212.5 170.5 %collective-permute-start.1 = (bf16[512,768]{1,0:T(8,128)(2,1)}, bf16[512,768]{1,0:T(8,128)(2,1)}, u32[]{:S(2)}, u32[]{:S(2)}) collective-permute-start(bf16[512,768]{1,0:T(8,128)(2,1)} %get-tuple-element.75), channel_id=1, source_target_pairs={{0,2},{2,0},{1,3},{3,1},{4,6},{6,4},{5,7},{7,5},{8,10},{10,8},{9,1... | collective-permute-start | bytes 2359304 | tf_op jit(solution)/shard_map/ppermute | solution.py:809
  220.5 59.8 %copy-start.18 = (bf16[8,96,1152]{2,1,0:T(8,128)(2,1)S(1)}, bf16[8,96,1152]{2,1,0:T(8,128)(2,1)}, u32[]{:S(2)}) copy-start(bf16[8,96,1152]{2,1,0:T(8,128)(2,1)} %copy-done.17) | copy-start | bytes 5308420
  280.4 5.2 %copy-start.5 = (bf16[4,512,768]{2,1,0:T(8,128)(2,1)S(1)}, bf16[4,512,768]{2,1,0:T(8,128)(2,1)}, u32[]{:S(2)}) copy-start(bf16[4,512,768]{2,1,0:T(8,128)(2,1)} %copy-done.3) | copy-start | bytes 9437188
  280.4 5.2 %copy-start.34 = (bf16[2048,1152]{1,0:T(8,128)(2,1)S(1)}, bf16[2048,1152]{1,0:T(8,128)(2,1)}, u32[]{:S(2)}) copy-start(bf16[2048,1152]{1,0:T(8,128)(2,1)} %get-tuple-element.39) | copy-start | bytes 14155780
  299.3 83.7 %copy-start.24 = (bf16[1,512,768]{2,1,0:T(8,128)(2,1)S(1)}, bf16[1,512,768]{2,1,0:T(8,128)(2,1)}, u32[]{:S(2)}) copy-start(bf16[1,512,768]{2,1,0:T(8,128)(2,1)} %get-tuple-element.74) | copy-start | bytes 2359300
  381.6 28.0 %copy-start.22 = (f32[2,512,768]{2,1,0:T(8,128)S(1)}, f32[2,512,768]{2,1,0:T(8,128)}, u32[]{:S(2)}) copy-start(f32[2,512,768]{2,1,0:T(8,128)} %get-tuple-element.115) | copy-start | bytes 9437188
  411.3 4.9 %copy-start.1 = (f32[384,768]{1,0:T(8,128)S(1)}, f32[384,768]{1,0:T(8,128)}, u32[]{:S(2)}) copy-start(f32[384,768]{1,0:T(8,128)} %param.31) | copy-start | bytes 3538948
  (17 other events, 44.3 us)
Sparse Core Ops, SparseCore 0:
  11.9 105.0 all-gather.1
  193.9 124.8 reduce-scatter.1
where the time goes:
time: 432 us; the launch traced here: 423 us
  Pallas kernels  235 us (54%)
  matrix products  89.7 us (21%)
  local copies, waits for them, and re-layouts  55.7 us (13%)
  other arithmetic  15.8 us (4%)
  between operations  15.2 us (4%)
  starting transfers between devices  8.84 us (2%)
    pallas_call x1, Pallas kernels, exit_call(): pl.pallas_call(lambda *refs: exit_kernel(size_z, size_x, *refs), out_shap...  82.2 us
    pallas_call x1, Pallas kernels, attention_back(): pl.pallas_call(backward_kernel, out_shape=(jax.ShapeDtypeStruct((length,...  58.6 us
    pallas_call x1, Pallas kernels, entry(): pl.pallas_call(lambda *refs: entry_kernel(size_z, size_x, len(vectors), *...  41.7 us
    dot_general x5, matrix products, matmul_nt(): lax.dot_general(left, right, (((1,), (1,)), ((), ())), preferred_element_...  36.4 us
    pallas_call x1, Pallas kernels, attention(): pl.pallas_call(forward_kernel, out_shape=(jax.ShapeDtypeStruct((rows, pai...  34.9 us
    dot_general x4, matrix products, matmul(): return jnp.dot(left, right, preferred_element_type=jnp.float32)  29.8 us
    dot_general x4, matrix products, matmul_tn(): lax.dot_general(left, right, (((0,), (0,)), ((), ())), preferred_element_...  23.5 us
    pallas_call x1, Pallas kernels, finish(): pl.pallas_call(finish_kernel, out_shape=tuple((jax.ShapeDtypeStruct((2 *...  17.5 us
  transfers between devices with their start and end apart: 6, of which 1 were waited for; matrix products, arithmetic and copies ran while one was open for 24% of the time, Pallas kernels for 51%

commit v1 on v0

--- a/solution.py
+++ b/solution.py
@@ -5,6 +5,12 @@
 from jax.experimental.pallas import tpu as pltpu
 from jax.sharding import Mesh
 from jax.sharding import PartitionSpec as P
+
+
+HD = 64
+EPS = 1e-12
+ROOT_HALF = 0.7071067811865476
+INV_ROOT_TAU = 0.3989422804014327
 
 BLK = 256
 BIG = -1.0e9
@@ -310,7 +316,7 @@
         sum_ref[0:1, 128 * i : 128 * i + 128] = sums[i]
 
 
-def attention_back(place, segments, qkv, ctx_mine, ctx_other, do_all, do_other, lse):
+def attention_back(place, segments, qkv, ctx_mine, ctx_other, do_mine, do_other, lse):
     length, width = qkv.shape
     pairs = width // 384
     rows = length // 2
@@ -330,7 +336,7 @@
                 pl.BlockSpec((length, 384), lambda p, *_: (0, p)),
                 column,
                 column,
-                pl.BlockSpec((rows, 128), lambda p, place, seg: (0, place[4] * pairs + p)),
+                column,
                 column,
                 pl.BlockSpec((8, length), lambda p, *_: (p, 0)),
                 pl.BlockSpec((1, length), lambda p, *_: (0, 0)),
@@ -359,7 +365,7 @@
         compiler_params=pltpu.CompilerParams(dimension_semantics=("arbitrary",), vmem_limit_bytes=60 << 20),
         cost_estimate=pl.CostEstimate(flops=pairs * 20_000_000_000, bytes_accessed=pairs * 5_000_000, transcendentals=pairs * 4_000_000),
         name="attention_backward",
-    )(place, segments, qkv, ctx_mine, ctx_other, do_all, do_other, lse, segments.reshape(1, length))
+    )(place, segments, qkv, ctx_mine, ctx_other, do_mine, do_other, lse, segments.reshape(1, length))
 
 
 MESH_ID = pl.DeviceIdType.MESH
@@ -747,10 +753,302 @@
     )(inner, outer)
 
 
-HD = 64
-EPS = 1e-12
-ROOT_HALF = 0.7071067811865476
-INV_ROOT_TAU = 0.3989422804014327
+TILE = 256
+CHUNK = 768
+
+
+def dot_nt(a, b):
+    return lax.dot_general(a, b, (((1,), (1,)), ((), ())), preferred_element_type=jnp.float32)
+
+
+def row_mean(value):
+    return jnp.sum(value, axis=-1, keepdims=True) * (1.0 / value.shape[-1])
+
+
+def standardize(hidden):
+    centred = hidden - row_mean(hidden)
+    reciprocal = lax.rsqrt(row_mean(centred * centred) + EPS)
+    return centred * reciprocal, reciprocal
+
+
+def column_sum(value):
+    return jnp.sum(value.reshape(value.shape[0] // 8, 8, value.shape[1]), axis=0)
+
+
+def dense_kernel(
+    direct,
+    pieces,
+    where_ref,
+    tokens_ref,
+    mine_ref,
+    other_ref,
+    cot_ref,
+    cot_far_ref,
+    vectors_ref,
+    bias_inner_ref,
+    weights_hbm,
+    outer_hbm,
+    mixed_ref,
+    pre_first_ref,
+    grad_mine_ref,
+    grad_other_ref,
+    sums_ref,
+    inner_sum_ref,
+    grad_output_ref,
+    terms_hbm,
+    outer_terms_hbm,
+    w_output,
+    w_inner,
+    w_outer,
+    a_output,
+    a_inner,
+    a_outer,
+    stage,
+    context,
+    first_low,
+    turned_low,
+    normed,
+    first,
+    slope,
+    active,
+    work,
+    load_sem,
+    outer_sem,
+    store_sem,
+):
+    step, steps = pl.program_id(0), pl.num_programs(0)
+    core = where_ref[0]
+    width, hidden = w_inner.shape
+    half = width // 2
+    chunks = hidden // CHUNK
+    rows = width // pieces
+    ratio = hidden // width
+
+    def load_outer(start):
+        if not direct:
+            copy = pltpu.make_async_copy(outer_hbm, w_outer, outer_sem)
+            copy.start() if start else copy.wait()
+            return
+
+        if not start:
+            pltpu.make_async_copy(w_outer, w_outer, outer_sem).wait()
+            return
+
+        def piece(s, _):
+            for q in range(ratio):
+                src = weights_hbm.at[
+                    pl.ds(pl.multiple_of(s * rows, rows), rows), pl.ds(hidden + width + q * width, width)
+                ]
+                dst = w_outer.at[pl.ds(pl.multiple_of((s * ratio + q) * rows, rows), rows), :]
+                pltpu.make_async_copy(src, dst, outer_sem).start()
+            return 0
+
+        lax.fori_loop(0, pieces, piece, 0)
+
+    loads = (
+        pltpu.make_async_copy(weights_hbm.at[:, pl.ds(hidden, width)], w_output, load_sem.at[0]),
+        pltpu.make_async_copy(weights_hbm.at[:, pl.ds(0, hidden)], w_inner, load_sem.at[1]),
+    )
+
+    @pl.when(step == 0)
+    def _():
+        for load in loads:
+            load.start()
+        load_outer(True)
+        a_output[...] = jnp.zeros_like(a_output)
+        a_inner[...] = jnp.zeros_like(a_inner)
+        a_outer[...] = jnp.zeros_like(a_outer)
+        sums_ref[...] = jnp.zeros_like(sums_ref)
+        inner_sum_ref[...] = jnp.zeros_like(inner_sum_ref)
+
+    def vector(i):
+        return vectors_ref[i : i + 1, :]
+
+    def add_sum(i, value):
+        sums_ref[8 * i : 8 * i + 8, :] += column_sum(value)
+
+    context[:, pl.ds(pl.multiple_of(core * half, 128), half)] = mine_ref[...]
+    context[:, pl.ds(pl.multiple_of((1 - core) * half, 128), half)] = other_ref[...]
+
+    @pl.when(step == 0)
+    def _():
+        loads[0].wait()
+
+    hidden_rows = tokens_ref[...].astype(jnp.float32) + (dot_nn(context[...], w_output[...]) + vector(0))
+    normed[...], first_recip = standardize(hidden_rows)
+    first[...] = normed[...] * vector(1) + vector(2)
+    first_low[...] = first[...].astype(jnp.bfloat16)
+    turned_low[...] = first_low[...].T
+    work[...] = jnp.broadcast_to(vector(3), work.shape)
+
+    @pl.when(step == 0)
+    def _():
+        loads[1].wait()
+        load_outer(False)
+
+    def part(c):
+        return pl.ds(pl.multiple_of(c * CHUNK, CHUNK), CHUNK)
+
+    def forward(c, _):
+        u = dot_nn(first_low[...], w_inner[:, part(c)]) + bias_inner_ref[0:1, part(c)]
+        cdf = 0.5 * (1.0 + lax.erf(u * ROOT_HALF))
+        slope[:, part(c)] = cdf + u * jnp.exp(-0.5 * u * u) * INV_ROOT_TAU
+        active[:, part(c)] = (u * cdf).astype(jnp.bfloat16)
+        work[...] += dot_nn(active[:, part(c)], w_outer[part(c), :])
+        return 0
+
+    lax.fori_loop(0, chunks, forward, 0)
+    second, second_recip = standardize(first[...] + work[...])
+    mixed_ref[...] = (second * vector(4) + vector(5)).astype(jnp.bfloat16)
+    upstream = jnp.where(step < steps // 2, cot_ref[0], cot_far_ref[...]).astype(jnp.float32)
+    add_sum(0, upstream * second)
+    add_sum(1, upstream)
+    scaled = upstream * vector(4)
+    pre_second = second_recip * (scaled - row_mean(scaled) - second * row_mean(scaled * second))
+    grad_outer = pre_second.astype(jnp.bfloat16)
+    add_sum(2, grad_outer.astype(jnp.float32))
+    work[...] = pre_second
+    stage[0, 0:TILE, :] = grad_outer
+
+    def backward(c, _):
+        grad_out = stage[0, 0:TILE, :]
+        grad = dot_nt(grad_out, w_outer[part(c), :])
+        grad_inner = (grad * slope[:, part(c)]).astype(jnp.bfloat16)
+        inner_sum_ref[:, part(c)] += column_sum(grad_inner.astype(jnp.float32))
+        a_outer[part(c), :] += dot_nn(active[:, part(c)].T, grad_out)
+        a_inner[:, part(c)] += dot_nn(turned_low[...], grad_inner)
+        work[...] += dot_nt(grad_inner, w_inner[:, part(c)])
+        return 0
+
+    lax.fori_loop(0, chunks, backward, 0)
+    grad_first = work[...]
+    add_sum(3, grad_first * normed[...])
+    add_sum(4, grad_first)
+    scaled = grad_first * vector(1)
+    pre_first = first_recip * (scaled - row_mean(scaled) - normed[...] * row_mean(scaled * normed[...]))
+    pre_first_ref[...] = pre_first
+    grad_attended = pre_first.astype(jnp.bfloat16)
+    add_sum(5, grad_attended.astype(jnp.float32))
+    a_output[...] += dot_nn(context[...].T, grad_attended)
+    context[...] = dot_nt(grad_attended, w_output[...]).astype(jnp.bfloat16)
+    grad_mine_ref[...] = context[:, pl.ds(pl.multiple_of(core * half, 128), half)]
+    grad_other_ref[...] = context[:, pl.ds(pl.multiple_of((1 - core) * half, 128), half)]
+
+    @pl.when(step == steps - 1)
+    def _():
+        grad_output_ref[...] = a_output[...].astype(jnp.bfloat16)
+
+        def inner_copy(c, slot):
+            return pltpu.make_async_copy(stage.at[slot], terms_hbm.at[:, part(c)], store_sem.at[slot])
+
+        def outer_wait(slot):
+            pltpu.make_async_copy(stage.at[slot], stage.at[slot], store_sem.at[slot]).wait()
+
+        def outer_start(c, slot):
+            if not direct:
+                pltpu.make_async_copy(stage.at[slot], outer_terms_hbm.at[part(c), :], store_sem.at[slot]).start()
+                return
+            groups = CHUNK // (rows * ratio)
+            for s in range(groups):
+                for q in range(ratio):
+                    src = stage.at[slot, pl.ds((s * ratio + q) * rows, rows), :]
+                    dst = terms_hbm.at[
+                        pl.ds(pl.multiple_of((c * groups + s) * rows, rows), rows), pl.ds(hidden + q * width, width)
+                    ]
+                    pltpu.make_async_copy(src, dst, store_sem.at[slot]).start()
+
+        for c in range(chunks):
+            if c > 0:
+                inner_copy(c - 1, 0).wait()
+                outer_wait(1)
+            stage[0] = a_inner[:, part(c)].astype(jnp.bfloat16)
+            inner_copy(c, 0).start()
+            stage[1] = a_outer[part(c), :].astype(jnp.bfloat16)
+            outer_start(c, 1)
+        inner_copy(chunks - 1, 0).wait()
+        outer_wait(1)
+
+
+def dense_layer(where, tokens, mine, other, cotangent, cotangent_far, vectors, bias_inner, weights, outer, pieces, direct):
+    local, half = mine.shape
+    width = 2 * half
+    hidden = bias_inner.shape[1]
+    steps = local // TILE
+    rows = width // pieces
+    low, high = jnp.bfloat16, jnp.float32
+    tile = pl.BlockSpec((TILE, width), lambda t, *_: (t, 0))
+    half_tile = pl.BlockSpec((TILE, half), lambda t, *_: (t, 0))
+    anywhere = pl.BlockSpec(memory_space=pl.ANY)
+    halfway = steps // 2
+
+    def whole(shape):
+        return pl.BlockSpec(shape, lambda t, *_: (0, 0))
+
+    terms_shape = (width, 2 * hidden if direct else hidden)
+    outer_shape = (8, 128) if direct else (hidden, width)
+    return pl.pallas_call(
+        lambda *refs: dense_kernel(direct, pieces, *refs),
+        out_shape=(
+            jax.ShapeDtypeStruct((local, width), low),
+            jax.ShapeDtypeStruct((local, width), high),
+            jax.ShapeDtypeStruct((local, half), low),
+            jax.ShapeDtypeStruct((local, half), low),
+            jax.ShapeDtypeStruct((48, width), high),
+            jax.ShapeDtypeStruct((8, hidden), high),
+            jax.ShapeDtypeStruct((width, width), low),
+            jax.ShapeDtypeStruct(terms_shape, low),
+            jax.ShapeDtypeStruct(outer_shape, low),
+        ),
+        grid_spec=pltpu.PrefetchScalarGridSpec(
+            num_scalar_prefetch=1,
+            grid=(steps,),
+            in_specs=[
+                tile,
+                half_tile,
+                half_tile,
+                pl.BlockSpec((1, TILE, width), lambda t, where: (where[1], jnp.minimum(t, halfway - 1), 0)),
+                pl.BlockSpec((TILE, width), lambda t, *_: (jnp.maximum(t - halfway, 0), 0)),
+                whole((8, width)),
+                whole((1, hidden)),
+                anywhere,
+                anywhere,
+            ],
+            out_specs=[
+                tile,
+                tile,
+                half_tile,
+                half_tile,
+                whole((48, width)),
+                whole((8, hidden)),
+                whole((width, width)),
+                anywhere,
+                anywhere,
+            ],
+            scratch_shapes=[
+                pltpu.VMEM((width, width), low),
+                pltpu.VMEM((width, hidden), low),
+                pltpu.VMEM((hidden, width), low),
+                pltpu.VMEM((width, width), high),
+                pltpu.VMEM((width, hidden), high),
+                pltpu.VMEM((hidden, width), high),
+                pltpu.VMEM((2, width, CHUNK), low),
+                pltpu.VMEM((TILE, width), low),
+                pltpu.VMEM((TILE, width), low),
+                pltpu.VMEM((width, TILE), low),
+                pltpu.VMEM((TILE, width), high),
+                pltpu.VMEM((TILE, width), high),
+                pltpu.VMEM((TILE, hidden), high),
+                pltpu.VMEM((TILE, hidden), low),
+                pltpu.VMEM((TILE, width), high),
+                pltpu.SemaphoreType.DMA((2,)),
+                pltpu.SemaphoreType.DMA,
+                pltpu.SemaphoreType.DMA((2,)),
+            ],
+        ),
+        compiler_params=pltpu.CompilerParams(dimension_semantics=("arbitrary",), vmem_limit_bytes=66_000_000),
+        cost_estimate=pl.CostEstimate(flops=32_000_000_000, bytes_accessed=40_000_000, transcendentals=6_000_000),
+        name="dense_layer",
+    )(where, tokens, mine, other, cotangent, cotangent_far, vectors, bias_inner, weights, outer)
 
 
 def lowered(piece):
@@ -774,34 +1072,6 @@
 def matmul_nt(left, right):
     return lax.dot_general(
         left, right, (((1,), (1,)), ((), ())), preferred_element_type=jnp.float32
-    )
-
-
-def normalize(hidden, norm_gain, norm_shift):
-    centred = hidden - jnp.mean(hidden, axis=-1, keepdims=True)
-    reciprocal = lax.rsqrt(jnp.mean(centred * centred, axis=-1, keepdims=True) + EPS)
-    normed = centred * reciprocal
-    return (normed * norm_gain + norm_shift, normed, reciprocal)
-
-
-def normalize_back(upstream, normed, reciprocal, norm_gain):
-    scaled = upstream * norm_gain
-    result = reciprocal * (
-        scaled
-        - jnp.mean(scaled, axis=-1, keepdims=True)
-        - normed * jnp.mean(scaled * normed, axis=-1, keepdims=True)
-    )
-    return (result, jnp.sum(upstream * normed, axis=0), jnp.sum(upstream, axis=0))
-
-
-def gelu_value(values_in):
-    return 0.5 * values_in * (1.0 + lax.erf(values_in * ROOT_HALF))
-
-
-def gelu_slope(values_in):
-    return (
-        0.5 * (1.0 + lax.erf(values_in * ROOT_HALF))
-        + values_in * jnp.exp(-0.5 * values_in * values_in) * INV_ROOT_TAU
     )
 
 
@@ -869,17 +1139,19 @@
 
     pieces = (core_rows(w_inner), core_rows(w_output), side_by_side(core_rows(w_outer), 1))
     dense = lax.all_gather(jnp.concatenate(pieces, axis=1), everyone, axis=0, tiled=True)
-    full_inner, full_output = dense[:, :hidden], dense[:, hidden : hidden + width]
-    full_outer = stacked(dense[:, hidden + width :], 2 * shards)
+    pieces_count = 2 * shards
+    direct = (width // pieces_count) % 16 == 0
+    if direct:
+        full_outer = dense
+    else:
+        full_outer = stacked(dense[:, hidden + width :], pieces_count)
 
     vectors = (b_query, b_value, b_output, first_gain, first_shift, b_inner, b_outer, second_gain, second_shift)
     sizes = [v.shape[0] for v in vectors]
     tokens_all, early, vectors_all = entry(size_z, size_x, tokens, w_query, w_key, w_value, vectors)
     inputs_all = tokens_all.reshape(4 * part, width)
     full_early = early.reshape(width, lanes)
-    inputs = inputs_all[:local]
-    cotangent_mine = pick(cotangent, y)
-    cotangent_arrived = swap(pick(cotangent, 1 - y), "y")
+    cotangent_far = swap(pick(cotangent, 1 - y), "y")
     bias_query, bias_value, bias_output, gain_first, shift_first, bias_inner, bias_outer, gain_second, shift_second = [
         vectors_all[:, i, :size].reshape(shards * size) for i, size in enumerate(sizes)
     ]
@@ -893,38 +1165,35 @@
     place = jnp.where(spot < 4, ((spot % 2 != core) * 2 + (spot // 2 != y) * 1) * part, core)
     segments = pick(segment_ids, y)
     context_mine, context_other, logsum = attention(place, segments, projected)
-    context = in_order(core == 0, context_mine, swap(context_other, "core"), 1)
-
-    attended = matmul(context, full_output) + bias_output
-    first, first_normed, first_recip = normalize(widen(inputs) + attended, gain_first, shift_first)
-    first_low = lowered(first)
-    inner = matmul(first_low, full_inner) + bias_inner
-    active = lowered(gelu_value(inner))
-    outer = matmul(active, full_outer) + bias_outer
-    mixed, second_normed, second_recip = normalize(first + outer, gain_second, shift_second)
-    mixed = lowered(mixed)
-
-    upstream = widen(jnp.concatenate([cotangent_mine, cotangent_arrived], axis=0))
-    pre_second, grad_second_gain, grad_second_shift = normalize_back(upstream, second_normed, second_recip, gain_second)
-    grad_outer = lowered(pre_second)
-    grad_b_outer = jnp.sum(widen(grad_outer), axis=0)
-    outer_term = side_by_side(lowered(matmul_tn(active, grad_outer)), 2 * shards)
-    grad_inner = lowered(matmul_nt(grad_outer, full_outer) * gelu_slope(inner))
-    grad_b_inner = jnp.sum(widen(grad_inner), axis=0)
-    inner_term = lowered(matmul_tn(first_low, grad_inner))
-    both_done = lax.psum_scatter(jnp.concatenate([inner_term, outer_term], axis=1), everyone, scatter_dimension=0, tiled=True)
+    norms = jnp.stack([bias_output, gain_first, shift_first, bias_outer, gain_second, shift_second])
+    norms = jnp.concatenate([norms, jnp.zeros((2, width), jnp.float32)], axis=0)
+    mixed, pre_first, upstream_mine, upstream_send, dense_sums, inner_sums, grad_w_output, terms, outer_terms = dense_layer(
+        jnp.stack([core, y]).astype(jnp.int32),
+        inputs_all,
+        context_mine,
+        swap(context_other, "core"),
+        cotangent,
+        cotangent_far,
+        norms,
+        bias_inner.reshape(1, hidden),
+        dense,
+        full_outer,
+        pieces_count,
+        direct,
+    )
+    if not direct:
+        terms = jnp.concatenate([terms, side_by_side(outer_terms, pieces_count)], axis=1)
+    both_done = lax.psum_scatter(terms, everyone, scatter_dimension=0, tiled=True)
     inner_done, outer_done = both_done[:, :hidden], stacked(both_done[:, hidden:], 1)
-    grad_first = pre_second + matmul_nt(grad_inner, full_inner)
-    pre_first, grad_first_gain, grad_first_shift = normalize_back(grad_first, first_normed, first_recip, gain_first)
-    grad_attended = lowered(pre_first)
-    grad_b_output = jnp.sum(widen(grad_attended), axis=0)
-    grad_w_output = lowered(matmul_tn(context, grad_attended))
-    grad_context = lowered(matmul_nt(grad_attended, full_output))
-    context_send = lax.dynamic_slice_in_dim(grad_context, (1 - core) * half, half, 1)
-    upstream_other = swap(context_send, "core")
+    upstream_other = swap(upstream_send, "core")
+    dense_sums = jnp.sum(dense_sums.reshape(6, 8, width), axis=1)
+    grad_second_gain, grad_second_shift, grad_b_outer, grad_first_gain, grad_first_shift, grad_b_output = [
+        dense_sums[i] for i in range(6)
+    ]
+    grad_b_inner = jnp.sum(inner_sums, axis=0)
     mixed_out = in_order(y == 0, mixed[None, :part], swap(mixed[part:], "y")[None], 0)
 
-    grads, sums = attention_back(place, segments, projected, context_mine, context_other, grad_context, upstream_other, logsum)
+    grads, sums = attention_back(place, segments, projected, context_mine, context_other, upstream_mine, upstream_other, logsum)
     grad_early = lowered(matmul_tn(inputs_all, grads)).reshape(shards, own_rows, lanes)
     own_partial = pre_first + matmul_nt(grads[:local], full_early)
     other_partial = lowered(matmul_nt(grads[local:], full_early))

time: 432 us -> 410 us (0.949); the launches traced: 423 us -> 409 us
  Pallas kernels: 235 us -> 311 us
  matrix products: 89.7 us -> 25.4 us
  local copies, waits for them, and re-layouts: 55.7 us -> 28.7 us
  waiting for transfers between devices: 3.22 us -> 17.6 us
  starting transfers between devices: 8.84 us -> 0.51 us
  other arithmetic: 15.8 us -> 10.6 us
    pallas_call x0 -> x1, Pallas kernels: none -> 66.7 us  [dense_layer(): pl.pallas_call(lambda *refs: dense_kernel(direct, pieces, *refs), out_sha...]
    dot_general x5 -> x2, matrix products: 36.4 us -> 10.8 us  [matmul_nt(): lax.dot_general(left, right, (((1,), (1,)), ((), ())), preferred_element_...]
    dot_general x4 -> x1, matrix products: 29.8 us -> 9.09 us  [matmul(): return jnp.dot(left, right, preferred_element_type=jnp.float32)]
    dot_general x4 -> x1, matrix products: 23.5 us -> 5.5 us  [matmul_tn(): lax.dot_general(left, right, (((0,), (0,)), ((), ())), preferred_element_...]
    ppermute x4, waiting for transfers between devices: 0.01 us -> 17.6 us  [swap(): return lax.ppermute(piece, axis, [(0, 1), (1, 0)])]
    pallas_call x1, Pallas kernels: 58.6 us -> 71.8 us  [attention_back(): pl.pallas_call(backward_kernel, out_shape=(jax.ShapeDtypeStruct((length,...]
    pallas_call x1, Pallas kernels: 82.2 us -> 69.7 us  [exit_call(): pl.pallas_call(lambda *refs: exit_kernel(size_z, size_x, *refs), out_shap...]
    reshape x3 -> x2, local copies, waits for them, and re-layouts: 12.6 us -> 2.88 us  [stacked(): matrix.reshape(groups, rows, stack, width).transpose(0, 2, 1, 3)]
  transfers between devices with their start and end apart: 6 -> 6, of which waited for: 1 -> 1; matrix products, arithmetic and copies ran while one was open for 24% -> 11% of each run, Pallas kernels for 51% -> 56%
where the time goes in v1:
time: 410 us; the launch traced here: 409 us
  Pallas kernels  311 us (76%)
  local copies, waits for them, and re-layouts  28.7 us (7%)
  matrix products  25.4 us (6%)
  waiting for transfers between devices  17.6 us (4%)
  between operations  14.7 us (4%)
  other arithmetic  10.6 us (3%)
    pallas_call x1, Pallas kernels, attention_back(): pl.pallas_call(backward_kernel, out_shape=(jax.ShapeDtypeStruct((length,...  71.8 us
    pallas_call x1, Pallas kernels, exit_call(): pl.pallas_call(lambda *refs: exit_kernel(size_z, size_x, *refs), out_shap...  69.7 us
    pallas_call x1, Pallas kernels, dense_layer(): pl.pallas_call(lambda *refs: dense_kernel(direct, pieces, *refs), out_sha...  66.7 us
    pallas_call x1, Pallas kernels, attention(): pl.pallas_call(forward_kernel, out_shape=(jax.ShapeDtypeStruct((rows, pai...  43.9 us
    pallas_call x1, Pallas kernels, entry(): pl.pallas_call(lambda *refs: entry_kernel(size_z, size_x, len(vectors), *...  41.6 us
    ppermute x4, waiting for transfers between devices, swap(): return lax.ppermute(piece, axis, [(0, 1), (1, 0)])  17.6 us
    pallas_call x1, Pallas kernels, finish(): pl.pallas_call(finish_kernel, out_shape=tuple((jax.ShapeDtypeStruct((2 *...  17.5 us
    unnamed x75, local copies, waits for them, and re-layouts  11.3 us
  transfers between devices with their start and end apart: 6, of which 1 were waited for; matrix products, arithmetic and copies ran while one was open for 11% of the time, Pallas kernels for 56%

profile of v1, /device:TPU:0, one launch (start us, length us, event | category | flops | bytes accessed | tf_op | source)
XLA Modules:
  0.0 408.8 jit_solution(14201611763722739931)
XLA Ops:
  7.3 1.1 dynamic-slice_convert_fusion.1
  8.6 1.2 dynamic-slice_convert_fusion
  11.1 41.6 %entry.1 = (bf16[4,512,768]{2,1,0:T(8,128)(2,1)S(1)}, bf16[8,96,1152]{2,1,0:T(8,128)(2,1)S(1)}, f32[8,16,384]{2,1,0:T(8,128)S(1)}) custom-call(bf16[2,512,768]{2,1,0:T(8,128)(2,1)S(1)} %copy-done.2, f32[96,768]{1,0:T(8,128)S(1)} %copy-done.3, f32[96,768]{1,0:T(8,128)S(1)} %copy-done.4, f32[96,768]{1,0:T(8,128)S(1)} %copy-done.5, f32[1,96]{1,0:T(1,128)S(1)} %bitcast.64, ...), custom_call_target="tpu_custom_call" | custom-call | tf_op jit(solution)/shard_map/entry/pallas_call | solution.py:501
  52.8 1.7 copy-done.14
  54.5 1.2 copy-done.16
  57.4 9.1 %multiply_convert_fusion.qkv_ref = bf16[2048,1152]{1,0:T(8,128)(2,1)} fusion(bf16[2048,768]{1,0:T(8,128)(2,1)} %bitcast.72, bf16[768,1152]{1,0:T(8,128)(2,1)} %bitcast.75, f32[1152]{0:T(1024)S(1)} %mul.32, f32[1152]{0:T(1024)S(1)} %add.67), kind=kOutput, calls=%fused_computation | convolution fusion | flops 3630956544 | bytes 9643008 | tf_op jit(solution)/shard_map/dot_general | solution.py:1063
  66.5 43.9 %attention_forward.1 = (bf16[1024,384]{1,0:T(8,128)(2,1)}, bf16[1024,384]{1,0:T(8,128)(2,1)}, f32[24,2048]{1,0:T(8,128)}) custom-call(s32[5]{0:T(128)} %compare_select_fusion.1.place_ref, s32[2048]{0:T(1024)} %bitcast.86, bf16[2048,1152]{1,0:T(8,128)(2,1)} %multiply_convert_fusion.qkv_ref, s32[1,2048]{1,0:T(1,128)} %constant_dynamic-slice_fusion.row_ref), custom_call_target="tpu_custom_call" | custom-call | flops 24000000000 | bytes 9000000 | tf_op jit(solution)/shard_map/attention_forward/pallas_call | solution.py:162
  112.9 17.6 %collective-permute-done.1.refs_5_ = bf16[512,768]{1,0:T(8,128)(2,1)S(1)} collective-permute-done((bf16[512,768]{1,0:T(8,128)(2,1)S(1)}, bf16[512,768]{1,0:T(8,128)(2,1)S(1)}, u32[]{:S(2)}, u32[]{:S(2)}) %collective-permute-start.1) | collective-permute-done | bytes 786464 | tf_op jit(solution)/shard_map/ppermute | solution.py:1079
  131.4 66.7 %dense_layer.1 = (bf16[1024,768]{1,0:T(8,128)(2,1)}, f32[1024,768]{1,0:T(8,128)}, bf16[1024,384]{1,0:T(8,128)(2,1)}, bf16[1024,384]{1,0:T(8,128)(2,1)}, f32[48,7...) custom-call(s32[2]{0:T(128)} %pad_add_fusion.refs_0_, ...), custom_call_target="tpu_custom_call" | custom-call | flops 32000000000 | bytes 40000000 | tf_op jit(solution)/shard_map/dense_layer/pallas_call | solution.py:989
  201.1 71.8 %attention_backward.1 = (bf16[2048,1152]{1,0:T(8,128)(2,1)}, f32[24,384]{1,0:T(8,128)}) custom-call(s32[5]{0:T(128)} %compare_select_fusion.1.place_ref, s32[2048]{0:T(1024)} %bitcast.87, bf16[2048,1152]{1,0:T(8,128)(2,1)} %multiply_convert_fusion.qkv_ref, bf16[1024,384]{1,0:T(8,128)(2,1)} %get-tuple-element.44.refs_2_.ctx_mine_ref, ...), custom_call_target="tpu_custom_call" | custom-call | flops 60000002048 | bytes 15000000 | tf_op jit(solution)/shard_map/attention_backward/pallas_call | solution.py:326
  273.9 5.7 %fusion.2 = f32[1024,768]{1,0:T(8,128)} fusion(bf16[768,1152]{1,0:T(8,128)(2,1)S(1)} %bitcast.76, bf16[2048,1152]{1,0:T(8,128)(2,1)} %get-tuple-element.50), kind=kOutput, calls=%fused_computation.4 | convolution fusion | flops 1811939328 | bytes 7274496 | tf_op jit(solution)/shard_map/dot_general | solution.py:1073
  279.7 5.5 %convolution_convert_fusion = bf16[768,1152]{1,0:T(8,128)(2,1)} fusion(bf16[2048,768]{1,0:T(8,128)(2,1)S(1)} %bitcast.74, bf16[2048,1152]{1,0:T(8,128)(2,1)S(1)} %copy-done.32), kind=kOutput, calls=%fused_computation.1 | convolution fusion | flops 3624763392 | bytes 9633792 | tf_op jit(solution)/shard_map/dot_general | solution.py:1067
  285.6 5.1 %add.73.refs_3_ = f32[1024,768]{1,0:T(8,128)} add(f32[1024,768]{1,0:T(8,128)} %get-tuple-element.55, f32[1024,768]{1,0:T(8,128)} %fusion.2) | non-fusion elementwise | flops 786432 | bytes 9437184 | tf_op jit(solution)/shard_map/add | solution.py:1198
  290.7 1.5 concatenate.23.refs_2_
  292.1 5.1 %fusion.4.refs_4_ = bf16[1024,768]{1,0:T(8,128)(2,1)} fusion(bf16[768,1152]{1,0:T(8,128)(2,1)S(1)} %bitcast.77, bf16[2048,1152]{1,0:T(8,128)(2,1)} %get-tuple-element.50), kind=kOutput, calls=%fused_computation.6 | convolution fusion | flops 1812725760 | bytes 5701632 | tf_op jit(solution)/shard_map/dot_general | solution.py:1073
  297.2 69.7 %exit.1 = (f32[2,512,768]{2,1,0:T(8,128)}, f32[96,768]{1,0:T(8,128)}, f32[96,768]{1,0:T(8,128)}, f32[96,768]{1,0:T(8,128)}, f32[96,768]{1,0:T(8,128)}, /*index=5*/f32[16,384]{1,0:T(8,128)}) custom-call(bf16[8,96,1152]{2,1,0:T(8,128)(2,1)} %bitcast.78, bf16[8,96,768]{2,1,0:T(8,128)(2,1)} %bitcast.82, f32[8,16,384]{2,1,0:T(8,128)} %concatenate.23.refs_2_, ...), custom_call_target="tpu_custom_call" | custom-call | tf_op jit(solution)/shard_map/exit/pallas_call | solution.py:662
  366.9 1.3 slice_reduce_fusion.16
  368.2 3.4 maximum_select_fusion
  371.7 1.5 slice_bitcast_fusion.1
  373.1 1.8 fusion.9
  375.0 1.9 reshape.132
  377.8 17.5 %finish.1 = (f32[96,3072]{1,0:T(8,128)S(1)}, f32[384,768]{1,0:T(8,128)S(1)}) custom-call(bf16[48,3072]{1,0:T(8,128)(2,1)S(1)} %get-tuple-element.84.inner, bf16[192,768]{1,0:T(8,128)(2,1)S(1)} %bitcast.63), custom_call_target="tpu_custom_call" | custom-call | tf_op jit(solution)/shard_map/finish/pallas_call | solution.py:736
  395.4 1.7 copy.60
  399.9 1.0 copy.65
  (141 shorter events, 15.5 us)
Async XLA Ops:
  7.2 123.3 %all-gather.2.cloned.1.call-start = ((), (), s32[]{:S(2)}) async-start(), calls=%async_computation.1 | async-start | bytes 11280384 | tf_op jit(solution)/shard_map/all_gather | solution.py:1141
  8.4 2.6 copy-start.28
  8.4 2.6 copy-start.2
  8.5 2.6 copy-start.3
  8.5 2.6 copy-start.4
  8.5 2.6 copy-start.5
  8.5 2.6 copy-start.6
  8.5 2.6 copy-start.7
  8.5 2.6 copy-start.8
  10.9 45.4 %copy-start.29 = (f32[384]{0:T(512)S(1)}, f32[384]{0:T(512)}, u32[]{:S(2)}) copy-start(f32[384]{0:T(512)} %constant.68.clone.1) | copy-start | bytes 4612
  10.9 45.9 %copy-start.27 = (s32[2,2048]{1,0:T(2,128)S(1)}, s32[2,2048]{1,0:T(2,128)}, u32[]{:S(2)}) copy-start(s32[2,2048]{1,0:T(2,128)} %param.19) | copy-start | bytes 49156
  11.0 362.2 %reduce-scatter.2.cloned.1.call-start = ((), (), s32[]{:S(2)}) async-start(), calls=%async_computation.2 | async-start | bytes 10027008 | tf_op jit(solution)/shard_map/reduce_scatter | solution.py:1186
  66.5 43.9 %copy-start.20 = (bf16[2,512,768]{2,1,0:T(8,128)(2,1)S(1)}, bf16[2,512,768]{2,1,0:T(8,128)(2,1)}, u32[]{:S(2)}) copy-start(bf16[2,512,768]{2,1,0:T(8,128)(2,1)} %refs_4_.1) | copy-start | bytes 4718596
  110.4 2.5 collective-permute-start
  110.5 20.0 %collective-permute-start.1 = (bf16[512,768]{1,0:T(8,128)(2,1)S(1)}, bf16[512,768]{1,0:T(8,128)(2,1)S(1)}, u32[]{:S(2)}, u32[]{:S(2)}) collective-permute-start(bf16[512,768]{1,0:T(8,128)(2,1)S(1)} %dynamic-slice_bitcast_fusion), channel_id=1, source_target_pairs={{0,2},{2,0},{1,3},{3,1},{4,6},{6,4},{5,7},{7,5},{8,10},{10,8},{9,1... | collective-permute-start | bytes 2359304 | tf_op jit(solution)/shard_map/ppermute | solution.py:1079
  112.9 17.6 %copy-start.30 = (bf16[1024,384]{1,0:T(8,128)(2,1)}, bf16[1024,384]{1,0:T(8,128)(2,1)S(1)}, u32[]{:S(2)}) copy-start(bf16[1024,384]{1,0:T(8,128)(2,1)S(1)} %collective-permute-done.refs_3_) | copy-start | bytes 2359300
  198.2 2.8 copy-start.26
  198.2 2.9 collective-permute-start.3
  200.6 167.6 %collective-permute-start.2 = (bf16[512,768]{1,0:T(8,128)(2,1)S(1)}, bf16[512,768]{1,0:T(8,128)(2,1)}, u32[]{:S(2)}, u32[]{:S(2)}) collective-permute-start(bf16[512,768]{1,0:T(8,128)(2,1)S(1)} %get-tuple-element.82), channel_id=1, source_target_pairs={{0,2},{2,0},{1,3},{3,1},{4,6},{6,4},{5,7},{7,5},{8,10},{10,8},{9,1... | collective-permute-start | bytes 2359304 | tf_op jit(solution)/shard_map/ppermute | solution.py:1079
  201.1 72.9 %copy-start.17 = (bf16[8,96,1152]{2,1,0:T(8,128)(2,1)S(1)}, bf16[8,96,1152]{2,1,0:T(8,128)(2,1)}, u32[]{:S(2)}) copy-start(bf16[8,96,1152]{2,1,0:T(8,128)(2,1)} %copy-done.16) | copy-start | bytes 5308420
  273.9 5.8 %copy-start.15 = (bf16[4,512,768]{2,1,0:T(8,128)(2,1)S(1)}, bf16[4,512,768]{2,1,0:T(8,128)(2,1)}, u32[]{:S(2)}) copy-start(bf16[4,512,768]{2,1,0:T(8,128)(2,1)} %copy-done.14) | copy-start | bytes 9437188
  273.9 5.8 %copy-start.32 = (bf16[2048,1152]{1,0:T(8,128)(2,1)S(1)}, bf16[2048,1152]{1,0:T(8,128)(2,1)}, u32[]{:S(2)}) copy-start(bf16[2048,1152]{1,0:T(8,128)(2,1)} %get-tuple-element.50) | copy-start | bytes 14155780
  368.2 27.1 %copy-start.18 = (f32[2,512,768]{2,1,0:T(8,128)S(1)}, f32[2,512,768]{2,1,0:T(8,128)}, u32[]{:S(2)}) copy-start(f32[2,512,768]{2,1,0:T(8,128)} %get-tuple-element.111) | copy-start | bytes 9437188
  395.4 3.1 copy-start.22
  (15 other events, 28.5 us)
Sparse Core Ops, SparseCore 0:
  11.1 104.9 all-gather.1
  198.3 144.6 reduce-scatter.1

commit v2 on v0

--- a/solution.py
+++ b/solution.py
@@ -5,6 +5,12 @@
 from jax.experimental.pallas import tpu as pltpu
 from jax.sharding import Mesh
 from jax.sharding import PartitionSpec as P
+
+
+HD = 64
+EPS = 1e-12
+ROOT_HALF = 0.7071067811865476
+INV_ROOT_TAU = 0.3989422804014327
 
 BLK = 256
 BIG = -1.0e9
@@ -48,15 +54,28 @@
     return jnp.minimum(start, length - count * BLK), count
 
 
+def each_tile(count, step):
+    def two(i, _):
+        step(i * (2 * BLK), 2 * BLK)
+        return 0
+
+    lax.fori_loop(0, count // 2, two, 0)
+
+    @pl.when(count % 2 == 1)
+    def _():
+        step((count - 1) * BLK, BLK)
+
+
 def make_marks(row_ref, mark_query, mark_key):
-    length = mark_query.shape[0]
+    length = mark_key.shape[0]
     step = 512
     for b in range(length // step):
         rows = slice(b * step, (b + 1) * step)
         column = jnp.broadcast_to(row_ref[0:1, rows], (128, step)).T
         lane = lax.broadcasted_iota(jnp.int32, (step, 128), 1) % 64
         same = lane == column
-        mark_query[rows, :] = jnp.where(same, 1.0, 0.0).astype(jnp.bfloat16)
+        line = lax.broadcasted_iota(jnp.int32, (128, step), 0) % 64
+        mark_query[:, rows] = jnp.where(line == row_ref[0:1, rows], 1.0, 0.0).astype(jnp.bfloat16)
         apart = jnp.logical_and(lane < DOCUMENTS, jnp.logical_not(same))
         mark_key[rows, :] = jnp.where(apart, BIG, 0.0).astype(jnp.bfloat16)
 
@@ -77,10 +96,12 @@
     for b in range(4):
         src = part_rows(place_ref, b, part)
         dst = slice(b * part, (b + 1) * part)
-        q, k = qkv_ref[src, 0:128], qkv_ref[src, 128:256]
-        ohq, nohk = mark_query[dst, :], mark_key[dst, :]
-        q2[0, :, dst] = jnp.where(low, q, ohq).T
-        q2[1, :, dst] = jnp.where(low, ohq, q).T
+        k, nohk = qkv_ref[src, 128:256], mark_key[dst, :]
+        turned = qkv_ref[src, 0:128].T
+        q2[0, 0:64, dst] = turned[0:64]
+        q2[0, 64:128, dst] = mark_query[64:128, dst]
+        q2[1, 0:64, dst] = mark_query[0:64, dst]
+        q2[1, 64:128, dst] = turned[64:128]
         k2[0, dst, :] = jnp.where(low, k, nohk)
         k2[1, dst, :] = jnp.where(low, nohk, k)
         vt[:, dst] = qkv_ref[src, 256:384].T
@@ -91,43 +112,33 @@
         start, count = find_window(segment_ref, bound_ref, qb)
         top[...] = jnp.full_like(top, -1.0e30)
 
-        def span(i):
-            return pl.ds(pl.multiple_of(start + i * BLK, 128), BLK)
-
         def fold(tile, function):
-            return function(tile.reshape(BLK // 8, 8, BLK), axis=0)
-
-        def highest(i):
+            return function(tile.reshape(tile.shape[0] // 8, 8, BLK), axis=0)
+
+        def highest(first, size):
+            keys = pl.ds(pl.multiple_of(start + first, 128), size)
             for h in range(2):
-                st = dot_nn(k2[h, span(i), :], q2[h, :, qs])
-                keep[h, pl.ds(pl.multiple_of(i * BLK, BLK), BLK), :] = st
+                st = dot_nn(k2[h, keys, :], q2[h, :, qs])
+                keep[h, pl.ds(pl.multiple_of(first, BLK), size), :] = st
                 top[h] = jnp.maximum(top[h], fold(st, jnp.max))
 
-        def weigh(i, largest):
+        def weigh(first, size, largest):
+            keys = pl.ds(pl.multiple_of(start + first, 128), size)
             for h in range(2):
                 rows = slice(64 * h, 64 * h + 64)
-                st = keep[h, pl.ds(pl.multiple_of(i * BLK, BLK), BLK), :]
+                st = keep[h, pl.ds(pl.multiple_of(first, BLK), size), :]
                 p = jnp.exp(st - largest[h])
                 tot[h] = tot[h] + fold(p, jnp.sum)
-                acc[rows, :] = acc[rows, :] + dot_nn(vt[rows, span(i)], p.astype(jnp.bfloat16))
+                acc[rows, :] = acc[rows, :] + dot_nn(vt[rows, keys], p.astype(jnp.bfloat16))
 
         def paired(step):
-            def two(i, _):
-                step(2 * i)
-                step(2 * i + 1)
-                return 0
-
-            lax.fori_loop(0, count // 2, two, 0)
-
-            @pl.when(count % 2 == 1)
-            def _():
-                step(count - 1)
+            each_tile(count, step)
 
         paired(highest)
         largest = [jnp.max(top[h], axis=0, keepdims=True) for h in range(2)]
         acc[...] = jnp.zeros_like(acc)
         tot[...] = jnp.zeros_like(tot)
-        paired(lambda i: weigh(i, largest))
+        paired(lambda first, size: weigh(first, size, largest))
         for h in range(2):
             rows = slice(64 * h, 64 * h + 64)
             total = jnp.sum(tot[h], axis=0, keepdims=True)
@@ -180,7 +191,7 @@
                 pltpu.VMEM((2, 8, BLK), jnp.float32),
                 pltpu.VMEM((2, 8, BLK), jnp.float32),
                 pltpu.VMEM((2, length, BLK), jnp.float32),
-                pltpu.VMEM((length, 128), jnp.bfloat16),
+                pltpu.VMEM((128, length), jnp.bfloat16),
                 pltpu.VMEM((length, 128), jnp.bfloat16),
                 pltpu.SMEM((DOCUMENTS + 1,), jnp.int32),
             ],
@@ -234,20 +245,27 @@
         dst = slice(b * part, (b + 1) * part)
         q, k = qkv_ref[src, 0:128], qkv_ref[src, 128:256]
         zero = jnp.zeros_like(q)
-        ohq, nohk = mark_query[dst, :], mark_key[dst, :]
-        q2[0, :, dst] = jnp.where(low, q, ohq).T
-        q2[1, :, dst] = jnp.where(low, ohq, q).T
+        nohk = mark_key[dst, :]
+        turned = q.T
+        q2[0, 0:64, dst] = turned[0:64]
+        q2[0, 64:128, dst] = mark_query[64:128, dst]
+        q2[1, 0:64, dst] = mark_query[0:64, dst]
+        q2[1, 64:128, dst] = turned[64:128]
         k2[0, dst, :] = jnp.where(low, k, nohk)
         k2[1, dst, :] = jnp.where(low, nohk, k)
         q0[0, dst, :] = jnp.where(low, q, zero)
         q0[1, dst, :] = jnp.where(low, zero, q)
         d0[0, dst, :] = jnp.where(low, do, zero)
         d0[1, dst, :] = jnp.where(low, zero, do)
-        dt[0, :, dst] = jnp.where(low, do, zero).T
-        dt[1, :, dst] = jnp.where(low, zero, do).T
+        turned = do.T
+        blank = jnp.zeros((64, part), jnp.bfloat16)
+        dt[0, 0:64, dst] = turned[0:64]
+        dt[0, 64:128, dst] = blank
+        dt[1, 0:64, dst] = blank
+        dt[1, 64:128, dst] = turned[64:128]
         v0[dst, :] = qkv_ref[src, 256:384]
         kt[:, dst] = k.T
-        prod = (do.astype(jnp.float32) * ctx.astype(jnp.float32)).T
+        prod = turned.astype(jnp.float32) * ctx.T.astype(jnp.float32)
         delta[0:1, dst] = jnp.sum(prod[0:64], axis=0, keepdims=True)
         delta[1:2, dst] = jnp.sum(prod[64:128], axis=0, keepdims=True)
 
@@ -271,29 +289,22 @@
         qs = pl.ds(pl.multiple_of(qb * BLK, BLK), BLK)
         start, count = find_window(segment_ref, bound_ref, qb)
 
-        def tile(i):
-            ks = pl.ds(pl.multiple_of(start + i * BLK, 128), BLK)
+        def tile(first, size):
+            ks = pl.ds(pl.multiple_of(start + first, 128), size)
+            weights, grads = [], []
             for h in range(2):
-                rows = slice(64 * h, 64 * h + 64)
                 st = dot_nn(k2[h, ks, :], q2[h, :, qs])
                 w = jnp.exp(st - lse_ref[h : h + 1, qs])
                 gw = dot_nn(v0[ks, :], dt[h, :, qs])
-                ds = (w * (gw - delta[h : h + 1, qs])).astype(jnp.bfloat16)
-                dv[ks, :] += dot_nn(w.astype(jnp.bfloat16), d0[h, qs, :])
-                dk[ks, :] += dot_nn(ds, q0[h, qs, :])
-                dqt[rows, qs] += dot_nn(kt[rows, ks], ds)
-
-        def two(i, _):
-            tile(2 * i)
-            tile(2 * i + 1)
-            return 0
-
-        lax.fori_loop(0, count // 2, two, 0)
-
-        @pl.when(count % 2 == 1)
-        def _():
-            tile(count - 1)
-
+                weights.append(w.astype(jnp.bfloat16))
+                grads.append((w * (gw - delta[h : h + 1, qs])).astype(jnp.bfloat16))
+            dv[ks, :] += dot_nn(jnp.concatenate(weights, axis=1), jnp.concatenate([d0[0, qs, :], d0[1, qs, :]], axis=0))
+            dk[ks, :] += dot_nn(jnp.concatenate(grads, axis=1), jnp.concatenate([q0[0, qs, :], q0[1, qs, :]], axis=0))
+            for h in range(2):
+                rows = slice(64 * h, 64 * h + 64)
+                dqt[rows, qs] += dot_nn(kt[rows, ks], grads[h])
+
+        each_tile(count, tile)
         return 0
 
     lax.fori_loop(0, blocks, row, 0)
@@ -310,7 +321,7 @@
         sum_ref[0:1, 128 * i : 128 * i + 128] = sums[i]
 
 
-def attention_back(place, segments, qkv, ctx_mine, ctx_other, do_all, do_other, lse):
+def attention_back(place, segments, qkv, ctx_mine, ctx_other, do_mine, do_other, lse):
     length, width = qkv.shape
     pairs = width // 384
     rows = length // 2
@@ -330,7 +341,7 @@
                 pl.BlockSpec((length, 384), lambda p, *_: (0, p)),
                 column,
                 column,
-                pl.BlockSpec((rows, 128), lambda p, place, seg: (0, place[4] * pairs + p)),
+                column,
                 column,
                 pl.BlockSpec((8, length), lambda p, *_: (p, 0)),
                 pl.BlockSpec((1, length), lambda p, *_: (0, 0)),
@@ -351,7 +362,7 @@
                 pltpu.VMEM((length, 128), jnp.float32),
                 pltpu.VMEM((128, length), jnp.float32),
                 pltpu.VMEM((8, length), jnp.float32),
-                pltpu.VMEM((length, 128), jnp.bfloat16),
+                pltpu.VMEM((128, length), jnp.bfloat16),
                 pltpu.VMEM((length, 128), jnp.bfloat16),
                 pltpu.SMEM((DOCUMENTS + 1,), jnp.int32),
             ],
@@ -359,7 +370,305 @@
         compiler_params=pltpu.CompilerParams(dimension_semantics=("arbitrary",), vmem_limit_bytes=60 << 20),
         cost_estimate=pl.CostEstimate(flops=pairs * 20_000_000_000, bytes_accessed=pairs * 5_000_000, transcendentals=pairs * 4_000_000),
         name="attention_backward",
-    )(place, segments, qkv, ctx_mine, ctx_other, do_all, do_other, lse, segments.reshape(1, length))
+    )(place, segments, qkv, ctx_mine, ctx_other, do_mine, do_other, lse, segments.reshape(1, length))
+
+
+TILE = 256
+CHUNK = 768
+
+
+def dot_nt(a, b):
+    return lax.dot_general(a, b, (((1,), (1,)), ((), ())), preferred_element_type=jnp.float32)
+
+
+def row_mean(value):
+    return jnp.sum(value, axis=-1, keepdims=True) * (1.0 / value.shape[-1])
+
+
+def standardize(hidden):
+    centred = hidden - row_mean(hidden)
+    reciprocal = lax.rsqrt(row_mean(centred * centred) + EPS)
+    return centred * reciprocal, reciprocal
+
+
+def column_sum(value):
+    return jnp.sum(value.reshape(value.shape[0] // 8, 8, value.shape[1]), axis=0)
+
+
+def dense_kernel(
+    direct,
+    pieces,
+    where_ref,
+    tokens_ref,
+    mine_ref,
+    other_ref,
+    cot_ref,
+    cot_far_ref,
+    vectors_ref,
+    bias_inner_ref,
+    weights_hbm,
+    outer_hbm,
+    mixed_ref,
+    pre_first_ref,
+    grad_mine_ref,
+    grad_other_ref,
+    sums_ref,
+    inner_sum_ref,
+    grad_output_ref,
+    terms_hbm,
+    outer_terms_hbm,
+    w_output,
+    w_inner,
+    w_outer,
+    a_output,
+    a_inner,
+    a_outer,
+    stage,
+    context,
+    first_low,
+    turned_low,
+    normed,
+    first,
+    slope,
+    active,
+    work,
+    load_sem,
+    outer_sem,
+    store_sem,
+):
+    step, steps = pl.program_id(0), pl.num_programs(0)
+    core = where_ref[0]
+    width, hidden = w_inner.shape
+    half = width // 2
+    chunks = hidden // CHUNK
+    rows = width // pieces
+    ratio = hidden // width
+
+    def load_outer(start):
+        if not direct:
+            copy = pltpu.make_async_copy(outer_hbm, w_outer, outer_sem)
+            copy.start() if start else copy.wait()
+            return
+
+        if not start:
+            pltpu.make_async_copy(w_outer, w_outer, outer_sem).wait()
+            return
+
+        def piece(s, _):
+            for q in range(ratio):
+                src = weights_hbm.at[
+                    pl.ds(pl.multiple_of(s * rows, rows), rows), pl.ds(hidden + width + q * width, width)
+                ]
+                dst = w_outer.at[pl.ds(pl.multiple_of((s * ratio + q) * rows, rows), rows), :]
+                pltpu.make_async_copy(src, dst, outer_sem).start()
+            return 0
+
+        lax.fori_loop(0, pieces, piece, 0)
+
+    loads = (
+        pltpu.make_async_copy(weights_hbm.at[:, pl.ds(hidden, width)], w_output, load_sem.at[0]),
+        pltpu.make_async_copy(weights_hbm.at[:, pl.ds(0, hidden)], w_inner, load_sem.at[1]),
+    )
+
+    @pl.when(step == 0)
+    def _():
+        for load in loads:
+            load.start()
+        load_outer(True)
+        a_output[...] = jnp.zeros_like(a_output)
+        a_inner[...] = jnp.zeros_like(a_inner)
+        a_outer[...] = jnp.zeros_like(a_outer)
+        sums_ref[...] = jnp.zeros_like(sums_ref)
+        inner_sum_ref[...] = jnp.zeros_like(inner_sum_ref)
+
+    def vector(i):
+        return vectors_ref[i : i + 1, :]
+
+    def add_sum(i, value):
+        sums_ref[8 * i : 8 * i + 8, :] += column_sum(value)
+
+    context[:, pl.ds(pl.multiple_of(core * half, 128), half)] = mine_ref[...]
+    context[:, pl.ds(pl.multiple_of((1 - core) * half, 128), half)] = other_ref[...]
+
+    @pl.when(step == 0)
+    def _():
+        loads[0].wait()
+
+    hidden_rows = tokens_ref[...].astype(jnp.float32) + (dot_nn(context[...], w_output[...]) + vector(0))
+    normed[...], first_recip = standardize(hidden_rows)
+    first[...] = normed[...] * vector(1) + vector(2)
+    first_low[...] = first[...].astype(jnp.bfloat16)
+    turned_low[...] = first_low[...].T
+    work[...] = jnp.broadcast_to(vector(3), work.shape)
+
+    @pl.when(step == 0)
+    def _():
+        loads[1].wait()
+        load_outer(False)
+
+    def part(c):
+        return pl.ds(pl.multiple_of(c * CHUNK, CHUNK), CHUNK)
+
+    def forward(c, _):
+        u = dot_nn(first_low[...], w_inner[:, part(c)]) + bias_inner_ref[0:1, part(c)]
+        cdf = 0.5 * (1.0 + lax.erf(u * ROOT_HALF))
+        slope[:, part(c)] = cdf + u * jnp.exp(-0.5 * u * u) * INV_ROOT_TAU
+        active[:, part(c)] = (u * cdf).astype(jnp.bfloat16)
+        work[...] += dot_nn(active[:, part(c)], w_outer[part(c), :])
+        return 0
+
+    lax.fori_loop(0, chunks, forward, 0)
+    second, second_recip = standardize(first[...] + work[...])
+    mixed_ref[...] = (second * vector(4) + vector(5)).astype(jnp.bfloat16)
+    upstream = jnp.where(step < steps // 2, cot_ref[0], cot_far_ref[...]).astype(jnp.float32)
+    add_sum(0, upstream * second)
+    add_sum(1, upstream)
+    scaled = upstream * vector(4)
+    pre_second = second_recip * (scaled - row_mean(scaled) - second * row_mean(scaled * second))
+    grad_outer = pre_second.astype(jnp.bfloat16)
+    add_sum(2, grad_outer.astype(jnp.float32))
+    work[...] = pre_second
+    stage[0, 0:TILE, :] = grad_outer
+
+    def backward(c, _):
+        grad_out = stage[0, 0:TILE, :]
+        grad = dot_nt(grad_out, w_outer[part(c), :])
+        grad_inner = (grad * slope[:, part(c)]).astype(jnp.bfloat16)
+        inner_sum_ref[:, part(c)] += column_sum(grad_inner.astype(jnp.float32))
+        a_outer[part(c), :] += dot_nn(active[:, part(c)].T, grad_out)
+        a_inner[:, part(c)] += dot_nn(turned_low[...], grad_inner)
+        work[...] += dot_nt(grad_inner, w_inner[:, part(c)])
+        return 0
+
+    lax.fori_loop(0, chunks, backward, 0)
+    grad_first = work[...]
+    add_sum(3, grad_first * normed[...])
+    add_sum(4, grad_first)
+    scaled = grad_first * vector(1)
+    pre_first = first_recip * (scaled - row_mean(scaled) - normed[...] * row_mean(scaled * normed[...]))
+    pre_first_ref[...] = pre_first
+    grad_attended = pre_first.astype(jnp.bfloat16)
+    add_sum(5, grad_attended.astype(jnp.float32))
+    a_output[...] += dot_nn(context[...].T, grad_attended)
+    context[...] = dot_nt(grad_attended, w_output[...]).astype(jnp.bfloat16)
+    grad_mine_ref[...] = context[:, pl.ds(pl.multiple_of(core * half, 128), half)]
+    grad_other_ref[...] = context[:, pl.ds(pl.multiple_of((1 - core) * half, 128), half)]
+
+    @pl.when(step == steps - 1)
+    def _():
+        grad_output_ref[...] = a_output[...].astype(jnp.bfloat16)
+
+        def inner_copy(c, slot):
+            return pltpu.make_async_copy(stage.at[slot], terms_hbm.at[:, part(c)], store_sem.at[slot])
+
+        def outer_wait(slot):
+            pltpu.make_async_copy(stage.at[slot], stage.at[slot], store_sem.at[slot]).wait()
+
+        def outer_start(c, slot):
+            if not direct:
+                pltpu.make_async_copy(stage.at[slot], outer_terms_hbm.at[part(c), :], store_sem.at[slot]).start()
+                return
+            groups = CHUNK // (rows * ratio)
+            for s in range(groups):
+                for q in range(ratio):
+                    src = stage.at[slot, pl.ds((s * ratio + q) * rows, rows), :]
+                    dst = terms_hbm.at[
+                        pl.ds(pl.multiple_of((c * groups + s) * rows, rows), rows), pl.ds(hidden + q * width, width)
+                    ]
+                    pltpu.make_async_copy(src, dst, store_sem.at[slot]).start()
+
+        for c in range(chunks):
+            if c > 0:
+                inner_copy(c - 1, 0).wait()
+                outer_wait(1)
+            stage[0] = a_inner[:, part(c)].astype(jnp.bfloat16)
+            inner_copy(c, 0).start()
+            stage[1] = a_outer[part(c), :].astype(jnp.bfloat16)
+            outer_start(c, 1)
+        inner_copy(chunks - 1, 0).wait()
+        outer_wait(1)
+
+
+def dense_layer(where, tokens, mine, other, cotangent, cotangent_far, vectors, bias_inner, weights, outer, pieces, direct):
+    local, half = mine.shape
+    width = 2 * half
+    hidden = bias_inner.shape[1]
+    steps = local // TILE
+    rows = width // pieces
+    low, high = jnp.bfloat16, jnp.float32
+    tile = pl.BlockSpec((TILE, width), lambda t, *_: (t, 0))
+    half_tile = pl.BlockSpec((TILE, half), lambda t, *_: (t, 0))
+    anywhere = pl.BlockSpec(memory_space=pl.ANY)
+    halfway = steps // 2
+
+    def whole(shape):
+        return pl.BlockSpec(shape, lambda t, *_: (0, 0))
+
+    terms_shape = (width, 2 * hidden if direct else hidden)
+    outer_shape = (8, 128) if direct else (hidden, width)
+    return pl.pallas_call(
+        lambda *refs: dense_kernel(direct, pieces, *refs),
+        out_shape=(
+            jax.ShapeDtypeStruct((local, width), low),
+            jax.ShapeDtypeStruct((local, width), high),
+            jax.ShapeDtypeStruct((local, half), low),
+            jax.ShapeDtypeStruct((local, half), low),
+            jax.ShapeDtypeStruct((48, width), high),
+            jax.ShapeDtypeStruct((8, hidden), high),
+            jax.ShapeDtypeStruct((width, width), low),
+            jax.ShapeDtypeStruct(terms_shape, low),
+            jax.ShapeDtypeStruct(outer_shape, low),
+        ),
+        grid_spec=pltpu.PrefetchScalarGridSpec(
+            num_scalar_prefetch=1,
+            grid=(steps,),
+            in_specs=[
+                tile,
+                half_tile,
+                half_tile,
+                pl.BlockSpec((1, TILE, width), lambda t, where: (where[1], jnp.minimum(t, halfway - 1), 0)),
+                pl.BlockSpec((TILE, width), lambda t, *_: (jnp.maximum(t - halfway, 0), 0)),
+                whole((8, width)),
+                whole((1, hidden)),
+                anywhere,
+                anywhere,
+            ],
+            out_specs=[
+                tile,
+                tile,
+                half_tile,
+                half_tile,
+                whole((48, width)),
+                whole((8, hidden)),
+                whole((width, width)),
+                anywhere,
+                anywhere,
+            ],
+            scratch_shapes=[
+                pltpu.VMEM((width, width), low),
+                pltpu.VMEM((width, hidden), low),
+                pltpu.VMEM((hidden, width), low),
+                pltpu.VMEM((width, width), high),
+                pltpu.VMEM((width, hidden), high),
+                pltpu.VMEM((hidden, width), high),
+                pltpu.VMEM((2, width, CHUNK), low),
+                pltpu.VMEM((TILE, width), low),
+                pltpu.VMEM((TILE, width), low),
+                pltpu.VMEM((width, TILE), low),
+                pltpu.VMEM((TILE, width), high),
+                pltpu.VMEM((TILE, width), high),
+                pltpu.VMEM((TILE, hidden), high),
+                pltpu.VMEM((TILE, hidden), low),
+                pltpu.VMEM((TILE, width), high),
+                pltpu.SemaphoreType.DMA((2,)),
+                pltpu.SemaphoreType.DMA,
+                pltpu.SemaphoreType.DMA((2,)),
+            ],
+        ),
+        compiler_params=pltpu.CompilerParams(dimension_semantics=("arbitrary",), vmem_limit_bytes=66_000_000),
+        cost_estimate=pl.CostEstimate(flops=32_000_000_000, bytes_accessed=40_000_000, transcendentals=6_000_000),
+        name="dense_layer",
+    )(where, tokens, mine, other, cotangent, cotangent_far, vectors, bias_inner, weights, outer)
 
 
 MESH_ID = pl.DeviceIdType.MESH
@@ -398,11 +707,11 @@
 
 
 def entry_kernel(size_z, size_x, count, *refs):
-    tokens, wq, wk, wv = refs[:4]
-    vectors = refs[4 : 4 + count]
-    tokens_all, weights_all, vectors_all = refs[4 + count : 7 + count]
-    raw = refs[7 + count : 7 + 2 * count]
-    stage, wbuf, pack, vpack, local_sem, load_sem, tsend, trecv, zsend, zrecv, xsend, xrecv = refs[7 + 2 * count :]
+    tokens, cotangent, wq, wk, wv = refs[:5]
+    vectors = refs[5 : 5 + count]
+    tokens_all, cotangent_far, weights_all, vectors_all = refs[5 + count : 9 + count]
+    raw = refs[9 + count : 9 + 2 * count]
+    stage, wbuf, pack, vpack, local_sem, load_sem, tsend, trecv, zsend, zrecv, xsend, xrecv = refs[9 + 2 * count :]
     z, x, y, core = place_of()
     half = pack.shape[1] // 3
     pairs = half // 128
@@ -470,6 +779,8 @@
     across.wait_recv()
     onward = remote(tokens_all.at[1], tokens_all.at[3], tsend.at[2], trecv.at[2], partner(core=1 - core))
     onward.start()
+    later = remote(cotangent.at[1 - y], cotangent_far, tsend.at[3], trecv.at[3], partner(y=1 - y))
+    later.start()
     for first, second in sideways:
         first.wait()
         second.wait()
@@ -479,12 +790,13 @@
     across.wait_send()
     beside.wait()
     onward.wait()
+    later.wait()
     keep_weights.wait()
     keep_vectors.wait()
     keep_tokens.wait()
 
 
-def entry(size_z, size_x, tokens, wq, wk, wv, vectors):
+def entry(size_z, size_x, tokens, cotangent, wq, wk, wv, vectors):
     _, part, width = tokens.shape
     rows = wq.shape[0]
     lanes = wq.shape[1] // 2 * 3
@@ -496,11 +808,12 @@
         lambda *refs: entry_kernel(size_z, size_x, len(vectors), *refs),
         out_shape=(
             jax.ShapeDtypeStruct((4, part, width), tokens.dtype),
+            jax.ShapeDtypeStruct((part, width), cotangent.dtype),
             jax.ShapeDtypeStruct((shards, rows, lanes), jnp.bfloat16),
             jax.ShapeDtypeStruct((shards, 16, longest), jnp.float32),
         ),
-        in_specs=[anywhere] * (4 + len(vectors)),
-        out_specs=(anywhere, anywhere, anywhere),
+        in_specs=[anywhere] * (5 + len(vectors)),
+        out_specs=(anywhere,) * 4,
         scratch_shapes=[pltpu.VMEM((1, v.shape[0]), v.dtype) for v in vectors]
         + [
             pltpu.VMEM((part, width), tokens.dtype),
@@ -509,8 +822,8 @@
             pltpu.VMEM((16, longest), jnp.float32),
             dma((4,)),
             dma((3 + len(vectors),)),
-            dma((3,)),
-            dma((3,)),
+            dma((4,)),
+            dma((4,)),
             dma((2, size_z - 1)),
             dma((2, size_z - 1)),
             dma((2, size_z, max(size_x - 1, 1))),
@@ -518,57 +831,174 @@
         ],
         compiler_params=pltpu.CompilerParams(collective_id=0, has_side_effects=True, vmem_limit_bytes=20 << 20),
         name="entry",
-    )(tokens, wq, wk, wv, *[v.reshape(1, -1) for v in vectors])
-
-
-def exit_kernel(size_z, size_x, terms, output_term, vector_terms, own_rows, other_rows, *refs):
-    token_grads, grad_query, grad_key, grad_value, grad_output, vector_sums = refs[:6]
-    refs = refs[6:]
-    recv_rows, send_rows, far_rows, odd, xbuf, xvec, zout, zvout, zbuf, zvec, ybuf, yvec, cbuf, cvec = refs[:14]
-    tsend, trecv, osend, orecv, xsend, xrecv, zsend, zrecv, ysend, yrecv, csend, crecv = refs[14:]
+    )(tokens, cotangent, wq, wk, wv, *[v.reshape(1, -1) for v in vectors])
+
+
+def exit_kernel(
+    size_z,
+    size_x,
+    direct,
+    grads_hbm,
+    inputs_hbm,
+    weights_hbm,
+    base_hbm,
+    terms_hbm,
+    output_term,
+    vector_terms,
+    dense_hbm,
+    token_grads,
+    grad_query,
+    grad_key,
+    grad_value,
+    grad_output,
+    grad_inner,
+    grad_outer,
+    vector_sums,
+    grads,
+    inputs,
+    turned,
+    weights,
+    base,
+    terms,
+    other_rows,
+    recv_rows,
+    send_rows,
+    far_rows,
+    odd,
+    dense_own,
+    dense_far,
+    dense_core,
+    xbuf,
+    xvec,
+    zout,
+    zvout,
+    zbuf,
+    zvec,
+    ybuf,
+    yvec,
+    cbuf,
+    cvec,
+    load_sem,
+    tsend,
+    trecv,
+    osend,
+    orecv,
+    dsend,
+    drecv,
+    xsend,
+    xrecv,
+    zsend,
+    zrecv,
+    ysend,
+    yrecv,
+    csend,
+    crecv,
+):
     z, x, y, core = place_of()
     shards, rows, lanes = terms.shape
-    half = output_term.shape[2] // 2
+    width = grads_hbm.shape[1] * 2 // 3
+    half = width // 2
     pairs = half // 128
+    hidden = grad_inner.shape[1]
     part = token_grads.shape[1]
+    local = 2 * part
     mine = pl.ds(pl.multiple_of(core * half, 128), half)
     theirs = pl.ds(pl.multiple_of((1 - core) * half, 128), half)
     order = sorted(range(size_z), key=lambda k: -min(k, size_z - k))
+    loads = [
+        pltpu.make_async_copy(src, dst, load_sem.at[i])
+        for i, (src, dst) in enumerate(
+            (
+                (inputs_hbm, inputs),
+                (grads_hbm, grads),
+                (weights_hbm, weights),
+                (base_hbm, base),
+                (dense_hbm, dense_own),
+            )
+            + (() if direct else ((terms_hbm, terms),))
+        )
+    ]
+    for load in loads:
+        load.start()
     greet(True)
 
     outputs = remote(output_term.at[:, :, theirs], odd, osend, orecv, partner(core=1 - core))
     outputs.start()
-    halves = remote(other_rows, recv_rows, tsend.at[0], trecv.at[0], partner(core=1 - core))
-    halves.start()
+    dense_move = remote(dense_hbm, dense_far, dsend.at[0], drecv.at[0], partner(y=1 - y))
+    dense_move.start()
     sideways = {}
 
-    def send_side(n, k, src, dst):
+    def send_side(n, k, src, dst, lane=None):
         for j in range(1, size_x):
             column = lax.rem(x + j, size_x)
             slot = lax.rem(z + k, size_z) * size_x + column
-            if n == 1:
-                odd[slot] = (odd[slot].astype(jnp.float32) + output_term[slot, :, mine].astype(jnp.float32)).astype(jnp.bfloat16)
-            move = remote(src.at[slot], dst(j), xsend.at[n, k, j - 1], xrecv.at[n, k, j - 1], partner(x=column))
+            view = src.at[slot] if lane is None else src.at[slot, :, lane]
+            move = remote(view, dst(j), xsend.at[n, k, j - 1], xrecv.at[n, k, j - 1], partner(x=column))
             move.start()
             sideways.setdefault((k, j), []).append(move)
 
     for k in order:
-        send_side(0, k, terms, lambda j: xbuf.at[j - 1, k, :, 0:lanes])
-        send_side(2, k, vector_terms, lambda j: xvec.at[j - 1, k])
-        if k == order[0]:
-            outputs.wait()
-        send_side(1, k, odd, lambda j: xbuf.at[j - 1, k, :, lanes : lanes + half])
-
+        send_side(0, k, vector_terms, lambda j: xvec.at[j - 1, k])
+    loads[0].wait()
+    if direct:
+        for b in range(4):
+            turned[:, b * part : (b + 1) * part] = inputs[b * part : (b + 1) * part, :].T
+    loads[1].wait()
+    group = min(shards, 4)
+    for p in range(pairs):
+        block = slice(p * 384, (p + 1) * 384)
+        if direct:
+
+            def some(m, _):
+                value = dot_nn(turned[pl.ds(pl.multiple_of(m * group * rows, group * rows), group * rows), :], grads[:, block])
+                terms[pl.ds(m * group, group), :, block] = value.reshape(group, rows, 384).astype(jnp.bfloat16)
+                return 0
+
+            lax.fori_loop(0, shards // group, some, 0)
+        elif p == 0:
+            loads[5].wait()
+        for k in order:
+            send_side(1 + p, k, terms, lambda j: xbuf.at[j - 1, k, :, block], block)
+    outputs.wait()
+    for k in order:
+        for j in range(1, size_x):
+            slot = lax.rem(z + k, size_z) * size_x + lax.rem(x + j, size_x)
+            odd[slot] = (odd[slot].astype(jnp.float32) + output_term[slot, :, mine].astype(jnp.float32)).astype(jnp.bfloat16)
+        send_side(1 + pairs, k, odd, lambda j: xbuf.at[j - 1, k, :, lanes : lanes + half])
+
+    loads[2].wait()
+    strip = 256
+
+    def product(first):
+        at = pl.ds(pl.multiple_of(first, strip), strip)
+        return dot_nt(grads[at, :], weights[...])
+
+    def other_strip(i, _):
+        other_rows[pl.ds(pl.multiple_of(i * strip, strip), strip), :] = product(local + i * strip).astype(jnp.bfloat16)
+        return 0
+
+    lax.fori_loop(0, local // strip, other_strip, 0)
+    halves = remote(other_rows, recv_rows, tsend.at[0], trecv.at[0], partner(core=1 - core))
+    halves.start()
+    loads[3].wait()
+
+    def own_strip(i, _):
+        at = pl.ds(pl.multiple_of(i * strip, strip), strip)
+        base[at, :] = base[at, :] + product(i * strip)
+        return 0
+
+    lax.fori_loop(0, local // strip, own_strip, 0)
     halves.wait()
-    for i in (1, 0):
-        block = slice(i * part, (i + 1) * part)
-        summed = own_rows[block, :] + recv_rows[block, :].astype(jnp.float32)
-        if i == 1:
-            send_rows[...] = summed.astype(jnp.bfloat16)
-            back = remote(send_rows, far_rows, tsend.at[1], trecv.at[1], partner(y=1 - y))
-            back.start()
-        else:
-            token_grads[y] = summed
+    send_rows[...] = (base[part:local, :] + recv_rows[part:local, :].astype(jnp.float32)).astype(jnp.bfloat16)
+    back = remote(send_rows, far_rows, tsend.at[1], trecv.at[1], partner(y=1 - y))
+    back.start()
+    token_grads[y] = base[0:part, :] + recv_rows[0:part, :].astype(jnp.float32)
+
+    loads[4].wait()
+    dense_move.wait()
+    dense_core[0] = dense_own[...].astype(jnp.float32) + dense_far[...].astype(jnp.float32)
+    dense_swap = remote(dense_core.at[0], dense_core.at[1], dsend.at[1], drecv.at[1], partner(core=1 - core))
+    dense_swap.start()
 
     along = {}
     kept = None
@@ -599,6 +1029,17 @@
             move.start()
         along[k] = moves
 
+    dense_swap.wait()
+    first = core == 0
+    ratio = hidden // width
+    count = dense_own.shape[0]
+    for i in range(2):
+        piece = jnp.where(first, dense_core[i], dense_core[1 - i])
+        grad_inner[i * count : (i + 1) * count, :] = piece[:, 0:hidden]
+        for q in range(ratio):
+            at = (i * ratio + q) * count
+            grad_outer[at : at + count, :] = piece[:, hidden + q * width : hidden + (q + 1) * width]
+
     total, total_out, total_vec = kept
     for k in reversed(order):
         if k == 0:
@@ -617,6 +1058,8 @@
     )
     for move in moves:
         move.start()
+    back.wait()
+    token_grads[1 - y] = far_rows[...].astype(jnp.float32)
     for move in moves:
         move.wait()
     cbuf[0] = ybuf[0].astype(jnp.float32) + ybuf[1].astype(jnp.float32)
@@ -627,8 +1070,6 @@
     )
     for move in moves:
         move.start()
-    back.wait()
-    token_grads[1 - y] = far_rows[...].astype(jnp.float32)
     for move in moves:
         move.wait()
     for i in range(2):
@@ -641,35 +1082,51 @@
     vector_sums[...] = cvec[0] + cvec[1]
 
 
-def exit_call(size_z, size_x, terms, output_term, vector_terms, own_rows, other_rows):
-    shards, rows, lanes = terms.shape
-    width = output_term.shape[2]
+def exit_call(size_z, size_x, direct, hidden, grads, inputs, weights, base, terms, output_term, vector_terms, dense):
+    shards, rows, width = output_term.shape
+    lanes = grads.shape[1]
     half = width // 2
-    part = own_rows.shape[0] // 2
+    pairs = half // 128
+    length = inputs.shape[0]
+    local = length // 2
+    part = local // 2
     vrows, vlanes = vector_terms.shape[1:]
-    vmem = pl.BlockSpec(memory_space=pltpu.VMEM)
+    count = dense.shape[0]
+    vmem, anywhere = pl.BlockSpec(memory_space=pltpu.VMEM), pl.BlockSpec(memory_space=pl.ANY)
     dma = pltpu.SemaphoreType.DMA
     full = lanes + half
     side = max(size_x - 1, 1)
     low, high = jnp.bfloat16, jnp.float32
     matrix = jax.ShapeDtypeStruct((rows, width), high)
     return pl.pallas_call(
-        lambda *refs: exit_kernel(size_z, size_x, *refs),
+        lambda *refs: exit_kernel(size_z, size_x, direct, *refs),
         out_shape=(
             jax.ShapeDtypeStruct((2, part, width), high),
             matrix,
             matrix,
             matrix,
             matrix,
+            jax.ShapeDtypeStruct((2 * count, hidden), high),
+            jax.ShapeDtypeStruct((2 * count * hidden // width, width), high),
             jax.ShapeDtypeStruct((vrows, vlanes), high),
         ),
-        in_specs=[vmem] * 5,
-        out_specs=(vmem,) * 6,
+        in_specs=[anywhere] * 5 + [vmem] * 2 + [anywhere],
+        out_specs=(vmem,) * 8,
         scratch_shapes=[
-            pltpu.VMEM((2 * part, width), low),
+            pltpu.VMEM((length, lanes), low),
+            pltpu.VMEM((length, width), low),
+            pltpu.VMEM((width, length) if direct else (16, 128), low),
+            pltpu.VMEM((width, lanes), low),
+            pltpu.VMEM((local, width), high),
+            pltpu.VMEM((shards, rows, lanes), low),
+            pltpu.VMEM((local, width), low),
+            pltpu.VMEM((local, width), low),
             pltpu.VMEM((part, width), low),
             pltpu.VMEM((part, width), low),
             pltpu.VMEM((shards, rows, half), low),
+            pltpu.VMEM(dense.shape, low),
+            pltpu.VMEM(dense.shape, low),
+            pltpu.VMEM((2,) + dense.shape, high),
             pltpu.VMEM((side, size_z, rows, full), low),
             pltpu.VMEM((side, size_z, vrows, vlanes), high),
             pltpu.VMEM((size_z - 1, rows, full), low),
@@ -680,12 +1137,15 @@
             pltpu.VMEM((2, vrows, vlanes), high),
             pltpu.VMEM((2, rows, full), high),
             pltpu.VMEM((2, vrows, vlanes), high),
+            dma((6,)),
             dma((2,)),
             dma((2,)),
             dma,
             dma,
-            dma((3, size_z, side)),
-            dma((3, size_z, side)),
+            dma((2,)),
+            dma((2,)),
+            dma((2 + pairs, size_z, side)),
+            dma((2 + pairs, size_z, side)),
             dma((2, size_z - 1)),
             dma((2, size_z - 1)),
             dma((2,)),
@@ -693,64 +1153,9 @@
             dma((2,)),
             dma((2,)),
         ],
-        compiler_params=pltpu.CompilerParams(collective_id=1, has_side_effects=True, vmem_limit_bytes=60 << 20),
+        compiler_params=pltpu.CompilerParams(collective_id=1, has_side_effects=True, vmem_limit_bytes=66_000_000),
         name="exit",
-    )(terms, output_term, vector_terms, own_rows, other_rows)
-
-
-def finish_kernel(inner, outer, grad_inner, grad_outer, ybuf, yvuf, cbuf, cvuf, ysend, yrecv, csend, crecv):
-    z, x, y, core = place_of()
-    greet(False)
-    moves = (
-        remote(inner, ybuf, ysend.at[0], yrecv.at[0], partner(y=1 - y)),
-        remote(outer, yvuf, ysend.at[1], yrecv.at[1], partner(y=1 - y)),
-    )
-    for move in moves:
-        move.start()
-    sources = ((inner, ybuf, cbuf, grad_inner), (outer, yvuf, cvuf, grad_outer))
-    onward = []
-    for i, (own, far, swap_buf, out) in enumerate(sources):
-        moves[i].wait()
-        swap_buf[0] = own[...].astype(jnp.float32) + far[...].astype(jnp.float32)
-        move = remote(swap_buf.at[0], swap_buf.at[1], csend.at[i], crecv.at[i], partner(core=1 - core))
-        move.start()
-        onward.append(move)
-    for i, (own, far, swap_buf, out) in enumerate(sources):
-        onward[i].wait()
-        rows = own.shape[0]
-        first = core == 0
-        out[0:rows, :] = jnp.where(first, swap_buf[0], swap_buf[1])
-        out[rows : 2 * rows, :] = jnp.where(first, swap_buf[1], swap_buf[0])
-
-
-def finish(inner, outer):
-    vmem = pl.BlockSpec(memory_space=pltpu.VMEM)
-    dma = pltpu.SemaphoreType.DMA
-    low, high = jnp.bfloat16, jnp.float32
-    return pl.pallas_call(
-        finish_kernel,
-        out_shape=tuple(jax.ShapeDtypeStruct((2 * a.shape[0], a.shape[1]), high) for a in (inner, outer)),
-        in_specs=[vmem] * 2,
-        out_specs=(vmem,) * 2,
-        scratch_shapes=[
-            pltpu.VMEM(inner.shape, low),
-            pltpu.VMEM(outer.shape, low),
-            pltpu.VMEM((2,) + inner.shape, high),
-            pltpu.VMEM((2,) + outer.shape, high),
-            dma((2,)),
-            dma((2,)),
-            dma((2,)),
-            dma((2,)),
-        ],
-        compiler_params=pltpu.CompilerParams(collective_id=2, has_side_effects=True, vmem_limit_bytes=30 << 20),
-        name="finish",
-    )(inner, outer)
-
-
-HD = 64
-EPS = 1e-12
-ROOT_HALF = 0.7071067811865476
-INV_ROOT_TAU = 0.3989422804014327
+    )(grads, inputs, weights, base, terms, output_term, vector_terms, dense)
 
 
 def lowered(piece):
@@ -774,34 +1179,6 @@
 def matmul_nt(left, right):
     return lax.dot_general(
         left, right, (((1,), (1,)), ((), ())), preferred_element_type=jnp.float32
-    )
-
-
-def normalize(hidden, norm_gain, norm_shift):
-    centred = hidden - jnp.mean(hidden, axis=-1, keepdims=True)
-    reciprocal = lax.rsqrt(jnp.mean(centred * centred, axis=-1, keepdims=True) + EPS)
-    normed = centred * reciprocal
-    return (normed * norm_gain + norm_shift, normed, reciprocal)
-
-
-def normalize_back(upstream, normed, reciprocal, norm_gain):
-    scaled = upstream * norm_gain
-    result = reciprocal * (
-        scaled
-        - jnp.mean(scaled, axis=-1, keepdims=True)
-        - normed * jnp.mean(scaled * normed, axis=-1, keepdims=True)
-    )
-    return (result, jnp.sum(upstream * normed, axis=0), jnp.sum(upstream, axis=0))
-
-
-def gelu_value(values_in):
-    return 0.5 * values_in * (1.0 + lax.erf(values_in * ROOT_HALF))
-
-
-def gelu_slope(values_in):
-    return (
-        0.5 * (1.0 + lax.erf(values_in * ROOT_HALF))
-        + values_in * jnp.exp(-0.5 * values_in * values_in) * INV_ROOT_TAU
     )
 
 
@@ -869,17 +1246,18 @@
 
     pieces = (core_rows(w_inner), core_rows(w_output), side_by_side(core_rows(w_outer), 1))
     dense = lax.all_gather(jnp.concatenate(pieces, axis=1), everyone, axis=0, tiled=True)
-    full_inner, full_output = dense[:, :hidden], dense[:, hidden : hidden + width]
-    full_outer = stacked(dense[:, hidden + width :], 2 * shards)
+    pieces_count = 2 * shards
+    direct = (width // pieces_count) % 16 == 0
+    if direct:
+        full_outer = dense
+    else:
+        full_outer = stacked(dense[:, hidden + width :], pieces_count)
 
     vectors = (b_query, b_value, b_output, first_gain, first_shift, b_inner, b_outer, second_gain, second_shift)
     sizes = [v.shape[0] for v in vectors]
-    tokens_all, early, vectors_all = entry(size_z, size_x, tokens, w_query, w_key, w_value, vectors)
+    tokens_all, cotangent_far, early, vectors_all = entry(size_z, size_x, tokens, cotangent, w_query, w_key, w_value, vectors)
     inputs_all = tokens_all.reshape(4 * part, width)
     full_early = early.reshape(width, lanes)
-    inputs = inputs_all[:local]
-    cotangent_mine = pick(cotangent, y)
-    cotangent_arrived = swap(pick(cotangent, 1 - y), "y")
     bias_query, bias_value, bias_output, gain_first, shift_first, bias_inner, bias_outer, gain_second, shift_second = [
         vectors_all[:, i, :size].reshape(shards * size) for i, size in enumerate(sizes)
     ]
@@ -893,41 +1271,38 @@
     place = jnp.where(spot < 4, ((spot % 2 != core) * 2 + (spot // 2 != y) * 1) * part, core)
     segments = pick(segment_ids, y)
     context_mine, context_other, logsum = attention(place, segments, projected)
-    context = in_order(core == 0, context_mine, swap(context_other, "core"), 1)
-
-    attended = matmul(context, full_output) + bias_output
-    first, first_normed, first_recip = normalize(widen(inputs) + attended, gain_first, shift_first)
-    first_low = lowered(first)
-    inner = matmul(first_low, full_inner) + bias_inner
-    active = lowered(gelu_value(inner))
-    outer = matmul(active, full_outer) + bias_outer
-    mixed, second_normed, second_recip = normalize(first + outer, gain_second, shift_second)
-    mixed = lowered(mixed)
-
-    upstream = widen(jnp.concatenate([cotangent_mine, cotangent_arrived], axis=0))
-    pre_second, grad_second_gain, grad_second_shift = normalize_back(upstream, second_normed, second_recip, gain_second)
-    grad_outer = lowered(pre_second)
-    grad_b_outer = jnp.sum(widen(grad_outer), axis=0)
-    outer_term = side_by_side(lowered(matmul_tn(active, grad_outer)), 2 * shards)
-    grad_inner = lowered(matmul_nt(grad_outer, full_outer) * gelu_slope(inner))
-    grad_b_inner = jnp.sum(widen(grad_inner), axis=0)
-    inner_term = lowered(matmul_tn(first_low, grad_inner))
-    both_done = lax.psum_scatter(jnp.concatenate([inner_term, outer_term], axis=1), everyone, scatter_dimension=0, tiled=True)
-    inner_done, outer_done = both_done[:, :hidden], stacked(both_done[:, hidden:], 1)
-    grad_first = pre_second + matmul_nt(grad_inner, full_inner)
-    pre_first, grad_first_gain, grad_first_shift = normalize_back(grad_first, first_normed, first_recip, gain_first)
-    grad_attended = lowered(pre_first)
-    grad_b_output = jnp.sum(widen(grad_attended), axis=0)
-    grad_w_output = lowered(matmul_tn(context, grad_attended))
-    grad_context = lowered(matmul_nt(grad_attended, full_output))
-    context_send = lax.dynamic_slice_in_dim(grad_context, (1 - core) * half, half, 1)
-    upstream_other = swap(context_send, "core")
+    norms = jnp.stack([bias_output, gain_first, shift_first, bias_outer, gain_second, shift_second])
+    norms = jnp.concatenate([norms, jnp.zeros((2, width), jnp.float32)], axis=0)
+    mixed, pre_first, upstream_mine, upstream_send, dense_sums, inner_sums, grad_w_output, terms, outer_terms = dense_layer(
+        jnp.stack([core, y]).astype(jnp.int32),
+        inputs_all,
+        context_mine,
+        swap(context_other, "core"),
+        cotangent,
+        cotangent_far,
+        norms,
+        bias_inner.reshape(1, hidden),
+        dense,
+        full_outer,
+        pieces_count,
+        direct,
+    )
+    if not direct:
+        terms = jnp.concatenate([terms, side_by_side(outer_terms, pieces_count)], axis=1)
+    both_done = lax.psum_scatter(terms, everyone, scatter_dimension=0, tiled=True)
+    upstream_other = swap(upstream_send, "core")
+    dense_sums = jnp.sum(dense_sums.reshape(6, 8, width), axis=1)
+    grad_second_gain, grad_second_shift, grad_b_outer, grad_first_gain, grad_first_shift, grad_b_output = [
+        dense_sums[i] for i in range(6)
+    ]
+    grad_b_inner = jnp.sum(inner_sums, axis=0)
     mixed_out = in_order(y == 0, mixed[None, :part], swap(mixed[part:], "y")[None], 0)
 
-    grads, sums = attention_back(place, segments, projected, context_mine, context_other, grad_context, upstream_other, logsum)
-    grad_early = lowered(matmul_tn(inputs_all, grads)).reshape(shards, own_rows, lanes)
-    own_partial = pre_first + matmul_nt(grads[:local], full_early)
-    other_partial = lowered(matmul_nt(grads[local:], full_early))
+    grads, sums = attention_back(place, segments, projected, context_mine, context_other, upstream_mine, upstream_other, logsum)
+    if direct:
+        grad_early = grads
+    else:
+        grad_early = lowered(matmul_tn(inputs_all, grads)).reshape(shards, own_rows, lanes)
     sums = sums.reshape(pairs, 8, 3, 128)[:, 0]
     blank = jnp.zeros((width,), jnp.float32)
     grad_b_query = lax.dynamic_update_slice(blank, sums[:, 0].reshape(half), (core * half,))
@@ -947,10 +1322,20 @@
     rows = [jnp.pad(v.reshape(shards, 1, -1), ((0, 0), (0, 0), (0, longest - v.shape[0] // shards))) for v in vector_grads]
     rows.append(jnp.zeros((shards, vectors_all.shape[1] - len(rows), longest), jnp.float32))
     vector_terms = jnp.concatenate(rows, axis=1)
-    grad_tokens, grad_query, grad_key, grad_value, grad_output, vector_sums = exit_call(
-        size_z, size_x, grad_early, grad_w_output.reshape(shards, own_rows, width), vector_terms, own_partial, other_partial
+    grad_tokens, grad_query, grad_key, grad_value, grad_output, grad_inner_full, grad_outer_full, vector_sums = exit_call(
+        size_z,
+        size_x,
+        direct,
+        hidden,
+        grads,
+        inputs_all,
+        full_early,
+        pre_first,
+        grad_early,
+        grad_w_output.reshape(shards, own_rows, width),
+        vector_terms,
+        both_done,
     )
-    grad_inner_full, grad_outer_full = finish(inner_done, outer_done)
     done = [vector_sums[i, :size] for i, size in enumerate(sizes)]
     return (
         mixed_out,

time: 432 us -> 405 us (0.938)
  matrix products: 89.7 us -> 7.82 us
  waiting for transfers between devices: 3.22 us -> 70.4 us
  Pallas kernels: 235 us -> 274 us
  local copies, waits for them, and re-layouts: 55.7 us -> 29 us
  other arithmetic: 15.8 us -> 3.51 us
  starting transfers between devices: 8.84 us -> 1.3 us
    reduce_scatter x1, waiting for transfers between devices: 0.01 us -> 69.9 us  [body(): lax.psum_scatter(terms, everyone, scatter_dimension=0, tiled=True)]
    dot_general x9 -> x0, matrix products: 60 us -> none  [the longest x5 36.4 us: matmul_nt(): lax.dot_general(left, right, (((1,), (1,)), ((), ())), preferred_element_...]
    pallas_call x2, Pallas kernels: 99.7 us -> 133 us  [the longest x1 66.5 us: dense_layer(): pl.pallas_call(lambda *refs: dense_kernel(direct, pieces, *refs), out_sha...]
    dot_general x4 -> x1, matrix products: 29.8 us -> 7.82 us  [matmul(): return jnp.dot(left, right, preferred_element_type=jnp.float32)]
    reshape x3 -> x0, local copies, waits for them, and re-layouts: 12.6 us -> none  [stacked(): matrix.reshape(groups, rows, stack, width).transpose(0, 2, 1, 3)]
    slice x3 -> x1, local copies, waits for them, and re-layouts: 7.94 us -> 0.05 us  [body(): dense_sums[i]]
    pallas_call x1, Pallas kernels: 58.6 us -> 50.9 us  [attention_back(): pl.pallas_call(backward_kernel, out_shape=(jax.ShapeDtypeStruct((length,...]
    pallas_call x1, Pallas kernels: 41.7 us -> 49.4 us  [entry(): pl.pallas_call(lambda *refs: entry_kernel(size_z, size_x, len(vectors), *...]
  transfers between devices with their start and end apart: 6 -> 5, of which waited for: 1 -> 2; matrix products, arithmetic and copies ran while one was open for 24% -> 4% of each run, Pallas kernels for 51% -> 35%
where the time goes in v2:
time: 405 us; the launch traced here: 401 us
  Pallas kernels  274 us (68%)
  waiting for transfers between devices  70.4 us (17%)
  local copies, waits for them, and re-layouts  29 us (7%)
  between operations  14.5 us (4%)
  matrix products  7.82 us (2%)
    reduce_scatter x1, waiting for transfers between devices, body(): lax.psum_scatter(terms, everyone, scatter_dimension=0, tiled=True)  69.9 us
    pallas_call x1, Pallas kernels, dense_layer(): pl.pallas_call(lambda *refs: dense_kernel(direct, pieces, *refs), out_sha...  66.5 us
    pallas_call x1, Pallas kernels, exit_call(): pl.pallas_call(lambda *refs: exit_kernel(size_z, size_x, direct, *refs),...  66.2 us
    pallas_call x1, Pallas kernels, attention_back(): pl.pallas_call(backward_kernel, out_shape=(jax.ShapeDtypeStruct((length,...  50.9 us
    pallas_call x1, Pallas kernels, entry(): pl.pallas_call(lambda *refs: entry_kernel(size_z, size_x, len(vectors), *...  49.4 us
    pallas_call x1, Pallas kernels, attention(): pl.pallas_call(forward_kernel, out_shape=(jax.ShapeDtypeStruct((rows, pai...  40.9 us
    unnamed x71, local copies, waits for them, and re-layouts  16.7 us
  transfers between devices with their start and end apart: 5, of which 2 were waited for; matrix products, arithmetic and copies ran while one was open for 4% of the time, Pallas kernels for 35%

profile of v2, /device:TPU:0, one launch (start us, length us, event | category | flops | bytes accessed | tf_op | source)
XLA Modules:
  0.0 400.6 jit_solution(7229280741982768807)
XLA Ops:
  7.3 1.1 dynamic-slice_convert_fusion.1
  8.4 1.1 dynamic-slice_convert_fusion
  9.9 0.9 pad_maximum_fusion
  10.9 1.4 copy-done.4
  12.3 1.4 copy-done.5
  13.8 1.0 copy-done.7
  14.7 1.0 copy-done.8
  15.7 49.4 %entry.1 = (bf16[4,512,768]{2,1,0:T(8,128)(2,1)S(1)}, bf16[512,768]{1,0:T(8,128)(2,1)S(1)}, bf16[8,96,1152]{2,1,0:T(8,128)(2,1)S(1)}, f32[8,16,384]{2,1,0:T(8,128)S(1)}) custom-call(bf16[2,512,768]{2,1,0:T(8,128)(2,1)S(1)} %copy-done.4, bf16[2,512,768]{2,1,0:T(8,128)(2,1)S(1)} %copy-done.5, f32[96,768]{1,0:T(8,128)S(1)} %copy-done.6, ...), custom_call_target="tpu_custom_call" | custom-call | tf_op jit(solution)/shard_map/entry/pallas_call | solution.py:807
  65.1 1.2 copy-done.3
  66.3 0.9 copy-done.18
  69.6 7.8 %multiply_convert_fusion.qkv_ref = bf16[2048,1152]{1,0:T(8,128)(2,1)} fusion(bf16[2048,768]{1,0:T(8,128)(2,1)S(1)} %bitcast.53, bf16[768,1152]{1,0:T(8,128)(2,1)} %bitcast.56, f32[1152]{0:T(1024)S(1)} %mul.32, f32[1152]{0:T(1024)S(1)} %add.59), kind=kOutput, calls=%fused_computation | convolution fusion | flops 3630956544 | bytes 9643008 | tf_op jit(solution)/shard_map/dot_general | solution.py:1170
  77.4 40.9 %attention_forward.1 = (bf16[1024,384]{1,0:T(8,128)(2,1)}, bf16[1024,384]{1,0:T(8,128)(2,1)}, f32[24,2048]{1,0:T(8,128)}) custom-call(s32[5]{0:T(128)} %compare_select_fusion.1.place_ref, s32[2048]{0:T(1024)} %bitcast.74, bf16[2048,1152]{1,0:T(8,128)(2,1)} %multiply_convert_fusion.qkv_ref, s32[1,2048]{1,0:T(1,128)} %constant_dynamic-slice_fusion.row_ref), custom_call_target="tpu_custom_call" | custom-call | flops 24000000000 | bytes 9000000 | tf_op jit(solution)/shard_map/attention_forward/pallas_call | solution.py:167
  118.4 1.5 slice.95
  121.6 66.5 %dense_layer.1 = (bf16[1024,768]{1,0:T(8,128)(2,1)}, f32[1024,768]{1,0:T(8,128)}, bf16[1024,384]{1,0:T(8,128)(2,1)}, bf16[1024,384]{1,0:T(8,128)(2,1)}, f32[48,7...) custom-call(s32[2]{0:T(128)} %pad_add_fusion.refs_0_, ...), custom_call_target="tpu_custom_call" | custom-call | flops 32000000000 | bytes 40000000 | tf_op jit(solution)/shard_map/dense_layer/pallas_call | solution.py:609
  191.1 50.9 %attention_backward.1 = (bf16[2048,1152]{1,0:T(8,128)(2,1)}, f32[24,384]{1,0:T(8,128)}) custom-call(s32[5]{0:T(128)} %compare_select_fusion.1.place_ref, s32[2048]{0:T(1024)} %bitcast.75, bf16[2048,1152]{1,0:T(8,128)(2,1)} %multiply_convert_fusion.qkv_ref, bf16[1024,384]{1,0:T(8,128)(2,1)} %get-tuple-element.45.refs_2_.ctx_mine_ref, ...), custom_call_target="tpu_custom_call" | custom-call | flops 60000002048 | bytes 15000000 | tf_op jit(solution)/shard_map/attention_backward/pallas_call | solution.py:331
  243.2 1.5 concatenate.23.refs_6_
  244.7 1.4 maximum_select_fusion
  246.1 69.9 %reduce-scatter.2.cloned.1.call-done.refs_7_ = bf16[48,6144]{1,0:T(8,128)(2,1)} async-done(((bf16[768,6144]{1,0:T(8,128)(2,1)}), bf16[48,6144]{1,0:T(8,128)(2,1)}) %reduce-scatter.2.cloned.1.call-update) | async-done | bytes 589840 | tf_op jit(solution)/shard_map/reduce_scatter | solution.py:1292
  315.9 66.2 %exit.1 = (f32[2,512,768]{2,1,0:T(8,128)}, f32[96,768]{1,0:T(8,128)}, f32[96,768]{1,0:T(8,128)}, f32[96,768]{1,0:T(8,128)}, f32[96,768]{1,0:T(8,128)}, /*index=5...) custom-call(bf16[2048,1152]{1,0:T(8,128)(2,1)} %get-tuple-element.52.refs_0_.refs_4_, ...), custom_call_target="tpu_custom_call" | custom-call | tf_op jit(solution)/shard_map/exit/pallas_call | solution.py:1101
  382.2 1.5 slice_bitcast_fusion.1
  383.7 1.3 slice_reduce_fusion.16
  385.0 3.8 copy.59
  391.7 1.0 copy.64
  392.7 1.0 copy.65
  (126 shorter events, 11.4 us)
Async XLA Ops:
  7.2 114.4 %all-gather.2.cloned.1.call-start = ((), (), s32[]{:S(2)}) async-start(), calls=%async_computation.1 | async-start | bytes 11280384 | tf_op jit(solution)/shard_map/all_gather | solution.py:1248
  9.5 1.3 copy-start.29
  9.5 1.3 copy-start.6
  9.6 1.3 copy-start.10
  9.6 1.3 copy-start.11
  9.6 1.3 copy-start.12
  9.6 1.3 copy-start.13
  10.8 305.2 %reduce-scatter.2.cloned.1.call-start = ((), (), s32[]{:S(2)}) async-start(), calls=%async_computation.2 | async-start | bytes 10027008 | tf_op jit(solution)/shard_map/reduce_scatter | solution.py:1292
  10.9 1.4 copy-start.4
  12.3 1.4 copy-start.5
  15.7 52.8 %copy-start.30 = (f32[384]{0:T(512)S(1)}, f32[384]{0:T(512)}, u32[]{:S(2)}) copy-start(f32[384]{0:T(512)} %constant.62.clone.1) | copy-start | bytes 4612
  15.7 53.3 %copy-start.28 = (s32[2,2048]{1,0:T(2,128)S(1)}, s32[2,2048]{1,0:T(2,128)}, u32[]{:S(2)}) copy-start(s32[2,2048]{1,0:T(2,128)} %param.19) | copy-start | bytes 49156
  67.2 10.2 %copy-start.2 = (bf16[4,512,768]{2,1,0:T(8,128)(2,1)}, bf16[4,512,768]{2,1,0:T(8,128)(2,1)S(1)}, u32[]{:S(2)}) copy-start(bf16[4,512,768]{2,1,0:T(8,128)(2,1)S(1)} %get-tuple-element.42) | copy-start | bytes 9437188
  118.4 3.2 collective-permute-start
  188.2 1.5 copy-start.19
  188.2 2.8 collective-permute-start.2
  189.8 54.9 %collective-permute-start.1 = (bf16[512,768]{1,0:T(8,128)(2,1)S(1)}, bf16[512,768]{1,0:T(8,128)(2,1)S(1)}, u32[]{:S(2)}, u32[]{:S(2)}) collective-permute-start(bf16[512,768]{1,0:T(8,128)(2,1)S(1)} %get-tuple-element.84), channel_id=1, source_target_pairs={{0,2},{2,0},{1,3},{3,1},{4,6},{6,4},{5,7},{7,5},{8,10},{10,8},{9,1... | collective-permute-start | bytes 2359304 | tf_op jit(solution)/shard_map/ppermute | solution.py:1186
  385.0 3.8 copy-start.25
  385.0 4.6 %copy-start.24 = (f32[96,768]{1,0:T(8,128)S(1)}, f32[96,768]{1,0:T(8,128)}, u32[]{:S(2)}) copy-start(f32[96,768]{1,0:T(8,128)} %get-tuple-element.113) | copy-start | bytes 884740
  385.0 5.3 %copy-start.23 = (f32[96,768]{1,0:T(8,128)S(1)}, f32[96,768]{1,0:T(8,128)}, u32[]{:S(2)}) copy-start(f32[96,768]{1,0:T(8,128)} %get-tuple-element.114) | copy-start | bytes 884740
  388.8 2.2 copy-start.22
  388.8 2.9 copy-start.21
  391.0 1.7 copy-start.20
  391.7 2.0 copy-start.1
  (12 other events, 12.9 us)
Sparse Core Ops, SparseCore 0:
  10.9 110.2 all-gather.1
  188.3 127.5 reduce-scatter.1

commit v3 on v1

v3 whole, which is shorter than its diff:
```python
import jax
import jax.numpy as jnp
from jax import lax
from jax.experimental import pallas as pl
from jax.experimental.pallas import tpu as pltpu
from jax.sharding import Mesh
from jax.sharding import PartitionSpec as P


HD = 64
EPS = 1e-12
ROOT_HALF = 0.7071067811865476
INV_ROOT_TAU = 0.3989422804014327

BLK = 256
BIG = -1.0e9
DOCUMENTS = 4


def dot_nn(a, b):
    return jnp.dot(a, b, preferred_element_type=jnp.float32)


def part_rows(place_ref, part, rows):
    return pl.ds(pl.multiple_of(place_ref[part], 128), rows)


def find_bounds(segment_ref, bound_ref):
    length = segment_ref.shape[0]
    bound_ref[0] = 0
    bound_ref[DOCUMENTS] = length
    for d in range(1, DOCUMENTS):

        def halve(_, span):
            low, high = span
            middle = (low + high) // 2
            below = segment_ref[jnp.minimum(middle, length - 1)] < d
            inside = low < high
            return (
                jnp.where(jnp.logical_and(inside, below), middle + 1, low),
                jnp.where(jnp.logical_and(inside, jnp.logical_not(below)), middle, high),
            )

        low, _ = lax.fori_loop(0, length.bit_length(), halve, (0, length))
        bound_ref[d] = low


def find_window(segment_ref, bound_ref, qb):
    length = segment_ref.shape[0]
    first = segment_ref[qb * BLK]
    last = segment_ref[qb * BLK + BLK - 1]
    start = bound_ref[first] // 128 * 128
    count = (bound_ref[last + 1] - start + BLK - 1) // BLK
    return jnp.minimum(start, length - count * BLK), count


def each_tile(count, step):
    def two(i, _):
        step(i * (2 * BLK), 2 * BLK)
        return 0

    lax.fori_loop(0, count // 2, two, 0)

    @pl.when(count % 2 == 1)
    def _():
        step((count - 1) * BLK, BLK)


def make_marks(row_ref, mark_query, mark_key):
    length = mark_key.shape[0]
    step = 512
    for b in range(length // step):
        rows = slice(b * step, (b + 1) * step)
        column = jnp.broadcast_to(row_ref[0:1, rows], (128, step)).T
        lane = lax.broadcasted_iota(jnp.int32, (step, 128), 1) % 64
        same = lane == column
        line = lax.broadcasted_iota(jnp.int32, (128, step), 0) % 64
        mark_query[:, rows] = jnp.where(line == row_ref[0:1, rows], 1.0, 0.0).astype(jnp.bfloat16)
        apart = jnp.logical_and(lane < DOCUMENTS, jnp.logical_not(same))
        mark_key[rows, :] = jnp.where(apart, BIG, 0.0).astype(jnp.bfloat16)


def forward_kernel(
    place_ref, segment_ref, qkv_ref, row_ref, mine_ref, other_ref, lse_ref, q2, k2, vt, acc, top, tot, keep, mark_query, mark_key, bound_ref
):
    length = qkv_ref.shape[0]
    blocks = length // BLK
    part = length // 4

    @pl.when(pl.program_id(0) == 0)
    def _():
        find_bounds(segment_ref, bound_ref)
        make_marks(row_ref, mark_query, mark_key)

    low = lax.broadcasted_iota(jnp.int32, (part, 128), 1) < 64
    for b in range(4):
        src = part_rows(place_ref, b, part)
        dst = slice(b * part, (b + 1) * part)
        k, nohk = qkv_ref[src, 128:256], mark_key[dst, :]
        turned = qkv_ref[src, 0:128].T
        q2[0, 0:64, dst] = turned[0:64]
        q2[0, 64:128, dst] = mark_query[64:128, dst]
        q2[1, 0:64, dst] = mark_query[0:64, dst]
        q2[1, 64:128, dst] = turned[64:128]
        k2[0, dst, :] = jnp.where(low, k, nohk)
        k2[1, dst, :] = jnp.where(low, nohk, k)
        vt[:, dst] = qkv_ref[src, 256:384].T
    lse_ref[...] = jnp.zeros_like(lse_ref)

    def row(qb, _):
        qs = pl.ds(pl.multiple_of(qb * BLK, BLK), BLK)
        start, count = find_window(segment_ref, bound_ref, qb)
        top[...] = jnp.full_like(top, -1.0e30)

        def fold(tile, function):
            return function(tile.reshape(tile.shape[0] // 8, 8, BLK), axis=0)

        def highest(first, size):
            keys = pl.ds(pl.multiple_of(start + first, 128), size)
            for h in range(2):
                st = dot_nn(k2[h, keys, :], q2[h, :, qs])
                keep[h, pl.ds(pl.multiple_of(first, BLK), size), :] = st
                top[h] = jnp.maximum(top[h], fold(st, jnp.max))

        def weigh(first, size, largest):
            keys = pl.ds(pl.multiple_of(start + first, 128), size)
            for h in range(2):
                rows = slice(64 * h, 64 * h + 64)
                st = keep[h, pl.ds(pl.multiple_of(first, BLK), size), :]
                p = jnp.exp(st - largest[h])
                tot[h] = tot[h] + fold(p, jnp.sum)
                acc[rows, :] = acc[rows, :] + dot_nn(vt[rows, keys], p.astype(jnp.bfloat16))

        def paired(step):
            each_tile(count, step)

        paired(highest)
        largest = [jnp.max(top[h], axis=0, keepdims=True) for h in range(2)]
        acc[...] = jnp.zeros_like(acc)
        tot[...] = jnp.zeros_like(tot)
        paired(lambda first, size: weigh(first, size, largest))
        for h in range(2):
            rows = slice(64 * h, 64 * h + 64)
            total = jnp.sum(tot[h], axis=0, keepdims=True)
            acc[rows, :] = acc[rows, :] / total
            lse_ref[h : h + 1, qs] = largest[h] + jnp.log(total)
        where = place_ref[qb * BLK // part] + qb * BLK % part
        result = acc[...].T.astype(jnp.bfloat16)

        @pl.when(where < 2 * part)
        def _():
            mine_ref[pl.ds(pl.multiple_of(where, BLK), BLK), :] = result

        @pl.when(where >= 2 * part)
        def _():
            other_ref[pl.ds(pl.multiple_of(where - 2 * part, BLK), BLK), :] = result

        return 0

    lax.fori_loop(0, blocks, row, 0)


def attention(place, segments, qkv):
    length, width = qkv.shape
    pairs = width // 384
    rows = length // 2
    return pl.pallas_call(
        forward_kernel,
        out_shape=(
            jax.ShapeDtypeStruct((rows, pairs * 128), jnp.bfloat16),
            jax.ShapeDtypeStruct((rows, pairs * 128), jnp.bfloat16),
            jax.ShapeDtypeStruct((pairs * 8, length), jnp.float32),
        ),
        grid_spec=pltpu.PrefetchScalarGridSpec(
            num_scalar_prefetch=2,
            grid=(pairs,),
            in_specs=[
                pl.BlockSpec((length, 384), lambda p, *_: (0, p)),
                pl.BlockSpec((1, length), lambda p, *_: (0, 0)),
            ],
            out_specs=[
                pl.BlockSpec((rows, 128), lambda p, *_: (0, p)),
                pl.BlockSpec((rows, 128), lambda p, *_: (0, p)),
                pl.BlockSpec((8, length), lambda p, *_: (p, 0)),
            ],
            scratch_shapes=[
                pltpu.VMEM((2, 128, length), jnp.bfloat16),
                pltpu.VMEM((2, length, 128), jnp.bfloat16),
                pltpu.VMEM((128, length), jnp.bfloat16),
                pltpu.VMEM((128, BLK), jnp.float32),
                pltpu.VMEM((2, 8, BLK), jnp.float32),
                pltpu.VMEM((2, 8, BLK), jnp.float32),
                pltpu.VMEM((2, length, BLK), jnp.float32),
                pltpu.VMEM((128, length), jnp.bfloat16),
                pltpu.VMEM((length, 128), jnp.bfloat16),
                pltpu.SMEM((DOCUMENTS + 1,), jnp.int32),
            ],
        ),
        compiler_params=pltpu.CompilerParams(dimension_semantics=("arbitrary",), vmem_limit_bytes=60 << 20),
        cost_estimate=pl.CostEstimate(flops=pairs * 8_000_000_000, bytes_accessed=pairs * 3_000_000, transcendentals=pairs * 4_000_000),
        name="attention_forward",
    )(place, segments, qkv, segments.reshape(1, length))


def backward_kernel(
    place_ref,
    segment_ref,
    qkv_ref,
    ctx_mine_ref,
    ctx_other_ref,
    do_mine_ref,
    do_other_ref,
    lse_ref,
    row_ref,
    out_ref,
    sum_ref,
    q2,
    k2,
    q0,
    d0,
    dt,
    v0,
    kt,
    dk,
    dv,
    dqt,
    delta,
    mark_query,
    mark_key,
    bound_ref,
):
    length = qkv_ref.shape[0]
    blocks = length // BLK
    part = length // 4

    @pl.when(pl.program_id(0) == 0)
    def _():
        find_bounds(segment_ref, bound_ref)
        make_marks(row_ref, mark_query, mark_key)

    low = lax.broadcasted_iota(jnp.int32, (part, 128), 1) < 64

    def prepare(b, do, ctx):
        src = part_rows(place_ref, b, part)
        dst = slice(b * part, (b + 1) * part)
        q, k = qkv_ref[src, 0:128], qkv_ref[src, 128:256]
        zero = jnp.zeros_like(q)
        nohk = mark_key[dst, :]
        turned = q.T
        q2[0, 0:64, dst] = turned[0:64]
        q2[0, 64:128, dst] = mark_query[64:128, dst]
        q2[1, 0:64, dst] = mark_query[0:64, dst]
        q2[1, 64:128, dst] = turned[64:128]
        k2[0, dst, :] = jnp.where(low, k, nohk)
        k2[1, dst, :] = jnp.where(low, nohk, k)
        q0[0, dst, :] = jnp.where(low, q, zero)
        q0[1, dst, :] = jnp.where(low, zero, q)
        d0[0, dst, :] = jnp.where(low, do, zero)
        d0[1, dst, :] = jnp.where(low, zero, do)
        turned = do.T
        blank = jnp.zeros((64, part), jnp.bfloat16)
        dt[0, 0:64, dst] = turned[0:64]
        dt[0, 64:128, dst] = blank
        dt[1, 0:64, dst] = blank
        dt[1, 64:128, dst] = turned[64:128]
        v0[dst, :] = qkv_ref[src, 256:384]
        kt[:, dst] = k.T
        prod = turned.astype(jnp.float32) * ctx.T.astype(jnp.float32)
        delta[0:1, dst] = jnp.sum(prod[0:64], axis=0, keepdims=True)
        delta[1:2, dst] = jnp.sum(prod[64:128], axis=0, keepdims=True)

    for b in range(4):

        @pl.when(place_ref[b] < 2 * part)
        def _():
            rows = part_rows(place_ref, b, part)
            prepare(b, do_mine_ref[rows, :], ctx_mine_ref[rows, :])

        @pl.when(place_ref[b] >= 2 * part)
        def _():
            rows = pl.ds(pl.multiple_of(place_ref[b] - 2 * part, 128), part)
            prepare(b, do_other_ref[rows, :], ctx_other_ref[rows, :])

    dk[...] = jnp.zeros_like(dk)
    dv[...] = jnp.zeros_like(dv)
    dqt[...] = jnp.zeros_like(dqt)

    def row(qb, _):
        qs = pl.ds(pl.multiple_of(qb * BLK, BLK), BLK)
        start, count = find_window(segment_ref, bound_ref, qb)

        def tile(first, size):
            ks = pl.ds(pl.multiple_of(start + first, 128), size)
            weights, grads = [], []
            for h in range(2):
                st = dot_nn(k2[h, ks, :], q2[h, :, qs])
                w = jnp.exp(st - lse_ref[h : h + 1, qs])
                gw = dot_nn(v0[ks, :], dt[h, :, qs])
                weights.append(w.astype(jnp.bfloat16))
                grads.append((w * (gw - delta[h : h + 1, qs])).astype(jnp.bfloat16))
            dv[ks, :] += dot_nn(jnp.concatenate(weights, axis=1), jnp.concatenate([d0[0, qs, :], d0[1, qs, :]], axis=0))
            dk[ks, :] += dot_nn(jnp.concatenate(grads, axis=1), jnp.concatenate([q0[0, qs, :], q0[1, qs, :]], axis=0))
            for h in range(2):
                rows = slice(64 * h, 64 * h + 64)
                dqt[rows, qs] += dot_nn(kt[rows, ks], grads[h])

        each_tile(count, tile)
        return 0

    lax.fori_loop(0, blocks, row, 0)
    sums = [jnp.zeros((1, 128), jnp.float32) for _ in range(3)]
    for b in range(4):
        dst = part_rows(place_ref, b, part)
        src = slice(b * part, (b + 1) * part)
        pieces = ((dqt[:, src].T * 0.125).astype(jnp.bfloat16), dk[src, :].astype(jnp.bfloat16), dv[src, :].astype(jnp.bfloat16))
        for i, piece in enumerate(pieces):
            out_ref[dst, 128 * i : 128 * i + 128] = piece
            sums[i] = sums[i] + jnp.sum(piece.astype(jnp.float32), axis=0, keepdims=True)
    sum_ref[...] = jnp.zeros_like(sum_ref)
    for i in range(3):
        sum_ref[0:1, 128 * i : 128 * i + 128] = sums[i]


def attention_back(place, segments, qkv, ctx_mine, ctx_other, do_mine, do_other, lse):
    length, width = qkv.shape
    pairs = width // 384
    rows = length // 2
    half = lambda: pltpu.VMEM((2, length, 128), jnp.bfloat16)
    turned = lambda: pltpu.VMEM((2, 128, length), jnp.bfloat16)
    column = pl.BlockSpec((rows, 128), lambda p, *_: (0, p))
    return pl.pallas_call(
        backward_kernel,
        out_shape=(
            jax.ShapeDtypeStruct((length, width), jnp.bfloat16),
            jax.ShapeDtypeStruct((pairs * 8, 384), jnp.float32),
        ),
        grid_spec=pltpu.PrefetchScalarGridSpec(
            num_scalar_prefetch=2,
            grid=(pairs,),
            in_specs=[
                pl.BlockSpec((length, 384), lambda p, *_: (0, p)),
                column,
                column,
                column,
                column,
                pl.BlockSpec((8, length), lambda p, *_: (p, 0)),
                pl.BlockSpec((1, length), lambda p, *_: (0, 0)),
            ],
            out_specs=[
                pl.BlockSpec((length, 384), lambda p, *_: (0, p)),
                pl.BlockSpec((8, 384), lambda p, *_: (p, 0)),
            ],
            scratch_shapes=[
                turned(),
                half(),
                half(),
                half(),
                turned(),
                pltpu.VMEM((length, 128), jnp.bfloat16),
                pltpu.VMEM((128, length), jnp.bfloat16),
                pltpu.VMEM((length, 128), jnp.float32),
                pltpu.VMEM((length, 128), jnp.float32),
                pltpu.VMEM((128, length), jnp.float32),
                pltpu.VMEM((8, length), jnp.float32),
                pltpu.VMEM((128, length), jnp.bfloat16),
                pltpu.VMEM((length, 128), jnp.bfloat16),
                pltpu.SMEM((DOCUMENTS + 1,), jnp.int32),
            ],
        ),
        compiler_params=pltpu.CompilerParams(dimension_semantics=("arbitrary",), vmem_limit_bytes=60 << 20),
        cost_estimate=pl.CostEstimate(flops=pairs * 20_000_000_000, bytes_accessed=pairs * 5_000_000, transcendentals=pairs * 4_000_000),
        name="attention_backward",
    )(place, segments, qkv, ctx_mine, ctx_other, do_mine, do_other, lse, segments.reshape(1, length))


MESH_ID = pl.DeviceIdType.MESH


def place_of():
    return tuple(lax.axis_index(name) for name in ("z", "x", "y", "core"))


def sizes_of():
    return lax.axis_size("z"), lax.axis_size("x")


def partner(**moved):
    z, x, y, core = place_of()
    return (moved.get("z", z), moved.get("x", x), moved.get("y", y), moved.get("core", core))


def greet(with_grid):
    z, x, y, core = place_of()
    size_z, size_x = sizes_of()
    peers = [partner(y=1 - y), partner(core=1 - core)]
    if with_grid:
        peers += [partner(z=lax.rem(z + k, size_z)) for k in range(1, size_z)]
        peers += [partner(x=lax.rem(x + j, size_x)) for j in range(1, size_x)]
    barrier = pltpu.get_barrier_semaphore()
    for peer in peers:
        pl.semaphore_signal(barrier, inc=1, device_id=peer, device_id_type=MESH_ID)
    pl.semaphore_wait(barrier, len(peers))


def remote(src, dst, send, recv, peer):
    return pltpu.make_async_remote_copy(
        src_ref=src, dst_ref=dst, send_sem=send, recv_sem=recv, device_id=peer, device_id_type=MESH_ID
    )


def entry_kernel(size_z, size_x, count, *refs):
    tokens, cotangent, wq, wk, wv = refs[:5]
    vectors = refs[5 : 5 + count]
    tokens_all, cotangent_all, weights_all, vectors_all = refs[5 + count : 9 + count]
    raw = refs[9 + count : 9 + 2 * count]
    stage, cot_stage, wbuf, pack, vpack, local_sem, load_sem, tsend, trecv, zsend, zrecv, xsend, xrecv = refs[9 + 2 * count :]
    z, x, y, core = place_of()
    half = pack.shape[1] // 3
    pairs = half // 128
    me = z * size_x + x

    mine = pl.ds(pl.multiple_of(core * half, 128), half)
    loads = [pltpu.make_async_copy(w.at[:, mine], wbuf.at[i], load_sem.at[i]) for i, w in enumerate((wq, wk, wv))]
    loads += [pltpu.make_async_copy(v, r, load_sem.at[3 + i]) for i, (v, r) in enumerate(zip(vectors, raw))]
    for load in loads:
        load.start()
    load = pltpu.make_async_copy(tokens.at[y], stage, local_sem.at[0])
    load.start()
    cot_load = pltpu.make_async_copy(cotangent.at[y], cot_stage, local_sem.at[4])
    cot_load.start()
    vpack[...] = jnp.zeros_like(vpack)
    for copy in loads:
        copy.wait()
    for i, vector in enumerate(raw):
        vpack[i : i + 1, 0 : vector.shape[1]] = vector[...].astype(jnp.bfloat16).astype(jnp.float32)
    for i in range(3):
        for p in range(pairs):
            pack[:, (3 * p + i) * 128 : (3 * p + i + 1) * 128] = wbuf[i, :, p * 128 : (p + 1) * 128].astype(jnp.bfloat16)
    greet(True)
    across = remote(tokens.at[1 - y], tokens_all.at[1], tsend.at[0], trecv.at[0], partner(y=1 - y))
    across.start()
    along = []
    for k in range(1, size_z):
        peer = partner(z=lax.rem(z + k, size_z))
        along.append(
            (
                remote(pack, weights_all.at[me], zsend.at[0, k - 1], zrecv.at[0, k - 1], peer),
                remote(vpack, vectors_all.at[me], zsend.at[1, k - 1], zrecv.at[1, k - 1], peer),
            )
        )
    beside = remote(tokens.at[y], tokens_all.at[2], tsend.at[1], trecv.at[1], partner(core=1 - core))
    sideways = []

    def forward(k, weights_src, vectors_src):
        slot = lax.rem(z - k + size_z, size_z) * size_x + x
        for j in range(1, size_x):
            peer = partner(x=lax.rem(x + j, size_x))
            first = remote(weights_src, weights_all.at[slot], xsend.at[0, k, j - 1], xrecv.at[0, k, j - 1], peer)
            second = remote(vectors_src, vectors_all.at[slot], xsend.at[1, k, j - 1], xrecv.at[1, k, j - 1], peer)
            first.start()
            second.start()
            sideways.append((first, second))

    forward(0, pack, vpack)
    for first, second in along:
        first.start()
        second.start()
    beside.start()
    keep_weights = pltpu.make_async_copy(pack, weights_all.at[me], local_sem.at[1])
    keep_vectors = pltpu.make_async_copy(vpack, vectors_all.at[me], local_sem.at[2])
    keep_weights.start()
    keep_vectors.start()
    load.wait()
    keep_tokens = pltpu.make_async_copy(stage, tokens_all.at[0], local_sem.at[3])
    keep_tokens.start()
    cot_load.wait()
    keep_cot = pltpu.make_async_copy(cot_stage, cotangent_all.at[0], local_sem.at[5])
    keep_cot.start()
    order = sorted(range(1, size_z), key=lambda k: min(k, size_z - k))
    for k in order:
        first, second = along[k - 1]
        first.wait_recv()
        second.wait_recv()
        slot = lax.rem(z - k + size_z, size_z) * size_x + x
        forward(k, weights_all.at[slot], vectors_all.at[slot])
    across.wait_recv()
    onward = remote(tokens_all.at[1], tokens_all.at[3], tsend.at[2], trecv.at[2], partner(core=1 - core))
    onward.start()
    later = remote(cotangent.at[1 - y], cotangent_all.at[1], tsend.at[3], trecv.at[3], partner(y=1 - y))
    later.start()
    for first, second in sideways:
        first.wait()
        second.wait()
    for first, second in along:
        first.wait_send()
        second.wait_send()
    across.wait_send()
    beside.wait()
    onward.wait()
    later.wait()
    keep_weights.wait()
    keep_vectors.wait()
    keep_tokens.wait()
    keep_cot.wait()


def entry(size_z, size_x, tokens, cotangent, wq, wk, wv, vectors):
    _, part, width = tokens.shape
    rows = wq.shape[0]
    lanes = wq.shape[1] // 2 * 3
    longest = max(v.shape[0] for v in vectors)
    shards = size_z * size_x
    anywhere = pl.BlockSpec(memory_space=pl.ANY)
    dma = pltpu.SemaphoreType.DMA
    return pl.pallas_call(
        lambda *refs: entry_kernel(size_z, size_x, len(vectors), *refs),
        out_shape=(
            jax.ShapeDtypeStruct((4, part, width), tokens.dtype),
            jax.ShapeDtypeStruct((2, part, width), cotangent.dtype),
            jax.ShapeDtypeStruct((shards, rows, lanes), jnp.bfloat16),
            jax.ShapeDtypeStruct((shards, 16, longest), jnp.float32),
        ),
        in_specs=[anywhere] * (5 + len(vectors)),
        out_specs=(anywhere,) * 4,
        scratch_shapes=[pltpu.VMEM((1, v.shape[0]), v.dtype) for v in vectors]
        + [
            pltpu.VMEM((part, width), tokens.dtype),
            pltpu.VMEM((part, width), cotangent.dtype),
            pltpu.VMEM((3, rows, lanes // 3), wq.dtype),
            pltpu.VMEM((rows, lanes), jnp.bfloat16),
            pltpu.VMEM((16, longest), jnp.float32),
            dma((6,)),
            dma((3 + len(vectors),)),
            dma((4,)),
            dma((4,)),
            dma((2, size_z - 1)),
            dma((2, size_z - 1)),
            dma((2, size_z, max(size_x - 1, 1))),
            dma((2, size_z, max(size_x - 1, 1))),
        ],
        compiler_params=pltpu.CompilerParams(collective_id=0, has_side_effects=True, vmem_limit_bytes=20 << 20),
        name="entry",
    )(tokens, cotangent, wq, wk, wv, *[v.reshape(1, -1) for v in vectors])


def exit_kernel(size_z, size_x, shapes, *refs):
    z, x, y, core = place_of()
    names = list(shapes)
    grads_hbm, inputs_hbm, weights_hbm, base_hbm, output_term, vector_terms = refs[:6]
    inner_in = refs[6 : 6 + size_z]
    outer_in = refs[6 + size_z : 6 + size_z + size_x]
    refs = refs[6 + size_z + size_x :]
    token_grads, grad_query, grad_key, grad_value, grad_output, grad_inner, grad_outer, vector_sums = refs[:8]
    grads, inputs, turned, weights, base, terms, other_rows, recv_rows, send_rows, far_rows, odd = refs[8:19]
    inner_buf, outer_buf = refs[19:21]
    load_sem, tsend, trecv, osend, orecv = refs[21:26]
    refs = refs[26:]
    xin, xsend, xrecv, xout = {}, {}, {}, {}
    zout, zin, zsend, zrecv = {}, {}, {}, {}
    ybuf, ysend, yrecv, cbuf, csend, crecv = {}, {}, {}, {}, {}, {}
    refs = list(refs)
    for name in names:
        ybuf[name], ysend[name], yrecv[name], cbuf[name], csend[name], crecv[name] = [refs.pop(0) for _ in range(6)]
        if name != "outer":
            xin[name], xsend[name], xrecv[name] = [refs.pop(0) for _ in range(3)]
        if name != "inner":
            zout[name], zin[name], zsend[name], zrecv[name] = [refs.pop(0) for _ in range(4)]
    xout["inner"] = refs.pop(0)

    shards, rows, lanes = terms.shape
    half = lanes // 3
    width = 2 * half
    pairs = half // 128
    hidden = grad_inner.shape[1]
    part = token_grads.shape[1]
    local = 2 * part
    low, high = jnp.bfloat16, jnp.float32
    mine = pl.ds(pl.multiple_of(core * half, 128), half)
    theirs = pl.ds(pl.multiple_of((1 - core) * half, 128), half)
    order = sorted(range(size_z), key=lambda k: -min(k, size_z - k))
    far_order = [k for k in order if k > 0]
    columns = [lax.rem(x + j, size_x) for j in range(size_x)]

    def slot_of(k, j):
        return lax.rem(z + k, size_z) * size_x + columns[j]

    loads = {}
    for i, src in enumerate(inner_in):
        loads["inner", i] = pltpu.make_async_copy(src, inner_buf.at[i], load_sem.at[i])
    for i, src in enumerate(outer_in):
        loads["outer", i] = pltpu.make_async_copy(src, outer_buf.at[i], load_sem.at[size_z + i])
    for i, (name, src, dst) in enumerate(
        (("inputs", inputs_hbm, inputs), ("grads", grads_hbm, grads), ("weights", weights_hbm, weights), ("base", base_hbm, base))
    ):
        loads[name] = pltpu.make_async_copy(src, dst, load_sem.at[size_z + size_x + i])
    for load in loads.values():
        load.start()
    greet(True)

    core_peer, y_peer = partner(core=1 - core), partner(y=1 - y)
    outputs = remote(output_term.at[:, :, theirs], odd, osend, orecv, core_peer)
    outputs.start()
    sideways = {}
    along = {}
    kept = {}

    def send_x(name, n, k, j, src, dst):
        move = remote(src, dst, xsend[name].at[n, k, j - 1], xrecv[name].at[n, k, j - 1], partner(x=columns[j]))
        move.start()
        sideways.setdefault((name, k, j), []).append(move)

    def send_z(name, k):
        move = remote(
            zout[name].at[k - 1],
            zin[name].at[k - 1],
            zsend[name].at[k - 1],
            zrecv[name].at[k - 1],
            partner(z=lax.rem(z + k, size_z)),
        )
        move.start()
        along[name, k] = move

    for k in order:
        for j in range(1, size_x):
            send_x("vec", 0, k, j, vector_terms.at[slot_of(k, j)], xin["vec"].at[j - 1, k])

    for i in range(size_z):
        loads["inner", i].wait()
    for j in range(size_x):
        total = inner_buf[0, columns[j]].astype(high)
        for i in range(1, size_z):
            total = total + inner_buf[i, columns[j]].astype(high)
        if j == 0:
            kept["inner"] = total
        else:
            xout["inner"][j - 1] = total.astype(low)
            send_x("inner", 0, 0, j, xout["inner"].at[j - 1], xin["inner"].at[j - 1, 0])

    for i in range(size_x):
        loads["outer", i].wait()
    for k in order:
        target = lax.rem(z + k, size_z)
        total = outer_buf[0, target].astype(high)
        for i in range(1, size_x):
            total = total + outer_buf[i, target].astype(high)
        if k == 0:
            kept["outer"] = total
        else:
            zout["outer"][k - 1] = total.astype(low)
            send_z("outer", k)

    loads["inputs"].wait()
    for b in range(4):
        turned[:, b * part : (b + 1) * part] = inputs[b * part : (b + 1) * part, :].T
    loads["grads"].wait()
    group = 4
    for p in range(pairs):
        block = slice(p * 384, (p + 1) * 384)

        def some(m, _):
            value = dot_nn(turned[pl.ds(pl.multiple_of(m * group * rows, group * rows), group * rows), :], grads[:, block])
            terms[pl.ds(m * group, group), :, block] = value.reshape(group, rows, 384).astype(low)
            return 0

        lax.fori_loop(0, shards // group, some, 0)
        for k in order:
            for j in range(1, size_x):
                send_x("qkv", p, k, j, terms.at[slot_of(k, j), :, block], xin["qkv"].at[j - 1, k, :, block])

    loads["weights"].wait()
    strip = 256

    def product(first):
        at = pl.ds(pl.multiple_of(first, strip), strip)
        return dot_nt(grads[at, :], weights[...])

    def other_strip(i, _):
        other_rows[pl.ds(pl.multiple_of(i * strip, strip), strip), :] = product(local + i * strip).astype(low)
        return 0

    lax.fori_loop(0, local // strip, other_strip, 0)
    halves = remote(other_rows, recv_rows, tsend.at[0], trecv.at[0], core_peer)
    halves.start()
    outputs.wait()
    for k in order:
        for j in range(1, size_x):
            slot = slot_of(k, j)
            odd[slot] = (odd[slot].astype(high) + output_term[slot, :, mine].astype(high)).astype(low)
            send_x("out", 0, k, j, odd.at[slot], xin["out"].at[j - 1, k])
    loads["base"].wait()

    def own_strip(i, _):
        at = pl.ds(pl.multiple_of(i * strip, strip), strip)
        base[at, :] = base[at, :] + product(i * strip)
        return 0

    lax.fori_loop(0, local // strip, own_strip, 0)
    halves.wait()
    send_rows[...] = (base[part:local, :] + recv_rows[part:local, :].astype(high)).astype(low)
    back = remote(send_rows, far_rows, tsend.at[1], trecv.at[1], y_peer)
    back.start()
    token_grads[y] = base[0:part, :] + recv_rows[0:part, :].astype(high)

    across = {}
    swapped = {}

    def step_y(name):
        move = remote(ybuf[name].at[0], ybuf[name].at[1], ysend[name], yrecv[name], y_peer)
        move.start()
        across[name] = move

    def step_core(name):
        across[name].wait()
        cbuf[name][0] = ybuf[name][0].astype(high) + ybuf[name][1].astype(high)
        move = remote(cbuf[name].at[0], cbuf[name].at[1], csend[name], crecv[name], core_peer)
        move.start()
        swapped[name] = move

    def finish_x(name):
        for k in order:
            slot = slot_of(k, 0)
            if name == "qkv":
                total = terms[slot].astype(high)
            elif name == "out":
                total = odd[slot].astype(high) + output_term[slot, :, mine].astype(high)
            else:
                total = vector_terms[slot]
            for j in range(1, size_x):
                for move in sideways[name, k, j]:
                    move.wait()
                total = total + xin[name][j - 1, k].astype(high)
            if k == 0:
                kept[name] = total
            else:
                zout[name][k - 1] = total.astype(zout[name].dtype)
                send_z(name, k)

    def finish_z(name):
        total = kept[name]
        for k in far_order:
            along[name, k].wait()
            total = total + zin[name][k - 1].astype(high)
        ybuf[name][0] = total.astype(ybuf[name].dtype)
        step_y(name)

    total = kept["inner"]
    for j in range(1, size_x):
        for move in sideways["inner", 0, j]:
            move.wait()
        total = total + xin["inner"][j - 1, 0].astype(high)
    ybuf["inner"][0] = total.astype(low)
    step_y("inner")
    finish_x("vec")
    finish_x("qkv")
    finish_z("outer")
    step_core("inner")
    finish_x("out")
    finish_z("vec")
    step_core("outer")
    finish_z("qkv")
    finish_z("out")
    back.wait()
    token_grads[1 - y] = far_rows[...].astype(high)
    step_core("vec")

    def finish_core(name):
        swapped[name].wait()
        return cbuf[name]

    buf = finish_core("inner")
    chunks = hidden // CHUNK
    for i in range(2):
        owner = core if i == 0 else 1 - core
        for c in range(chunks):
            place = pl.ds(pl.multiple_of(c * CHUNK + owner * half, 128), half)
            grad_inner[:, place] = buf[i, :, c * half : (c + 1) * half]
    buf = finish_core("outer")
    for i in range(2):
        owner = core if i == 0 else 1 - core
        grad_outer[:, pl.ds(pl.multiple_of(owner * half, 128), half)] = buf[i]
    step_core("qkv")
    step_core("out")
    buf = finish_core("vec")
    vector_sums[...] = buf[0] + buf[1]
    buf = finish_core("qkv")
    for i in range(2):
        owner = core if i == 0 else 1 - core
        for p in range(pairs):
            place = pl.ds(pl.multiple_of(owner * half + p * 128, 128), 128)
            for n, out in enumerate((grad_query, grad_key, grad_value)):
                out[:, place] = buf[i, :, (3 * p + n) * 128 : (3 * p + n + 1) * 128]
    buf = finish_core("out")
    for i in range(2):
        owner = core if i == 0 else 1 - core
        grad_output[:, pl.ds(pl.multiple_of(owner * half, 128), half)] = buf[i]


def exit_call(size_z, size_x, grads, inputs, weights, base, output_term, vector_terms, inner_terms, outer_terms):
    shards, rows, width = output_term.shape
    lanes = grads.shape[1]
    half = width // 2
    pairs = half // 128
    length = inputs.shape[0]
    local = length // 2
    part = local // 2
    long = outer_terms[0].shape[1]
    hidden = 2 * inner_terms[0].shape[2]
    vmem, anywhere = pl.BlockSpec(memory_space=pltpu.VMEM), pl.BlockSpec(memory_space=pl.ANY)
    dma = pltpu.SemaphoreType.DMA
    side = size_x - 1
    low, high = jnp.bfloat16, jnp.float32
    shapes = {
        "vec": (vector_terms.shape[1:], high, 1),
        "qkv": ((rows, lanes), low, pairs),
        "out": ((rows, half), low, 1),
        "inner": ((rows, hidden // 2), low, 1),
        "outer": ((long, half), low, 1),
    }
    scratch = [
        pltpu.VMEM((length, lanes), low),
        pltpu.VMEM((length, width), low),
        pltpu.VMEM((width, length), low),
        pltpu.VMEM((width, lanes), low),
        pltpu.VMEM((local, width), high),
        pltpu.VMEM((shards, rows, lanes), low),
        pltpu.VMEM((local, width), low),
        pltpu.VMEM((local, width), low),
        pltpu.VMEM((part, width), low),
        pltpu.VMEM((part, width), low),
        pltpu.VMEM((shards, rows, half), low),
        pltpu.VMEM((size_z,) + inner_terms[0].shape, low),
        pltpu.VMEM((size_x,) + outer_terms[0].shape, low),
        dma((size_z + size_x + 4,)),
        dma((2,)),
        dma((2,)),
        dma,
        dma,
    ]
    for name, (shape, kind, sends) in shapes.items():
        scratch += [pltpu.VMEM((2,) + shape, kind), dma, dma, pltpu.VMEM((2,) + shape, high), dma, dma]
        stages = 1 if name == "inner" else size_z
        if name != "outer":
            scratch += [pltpu.VMEM((side, stages) + shape, kind), dma((sends, stages, side)), dma((sends, stages, side))]
        if name != "inner":
            scratch += [pltpu.VMEM((size_z - 1,) + shape, kind)] * 2 + [dma((size_z - 1,))] * 2
    scratch.append(pltpu.VMEM((side, rows, hidden // 2), low))
    matrix = jax.ShapeDtypeStruct((rows, width), high)
    return pl.pallas_call(
        lambda *refs: exit_kernel(size_z, size_x, shapes, *refs),
        out_shape=(
            jax.ShapeDtypeStruct((2, part, width), high),
            matrix,
            matrix,
            matrix,
            matrix,
            jax.ShapeDtypeStruct((rows, hidden), high),
            jax.ShapeDtypeStruct((long, width), high),
            jax.ShapeDtypeStruct(vector_terms.shape[1:], high),
        ),
        in_specs=[anywhere] * 4 + [vmem] * 2 + [anywhere] * (size_z + size_x),
        out_specs=(vmem,) * 8,
        scratch_shapes=scratch,
        compiler_params=pltpu.CompilerParams(collective_id=1, has_side_effects=True, vmem_limit_bytes=67_000_000),
        name="exit",
    )(grads, inputs, weights, base, output_term, vector_terms, *inner_terms, *outer_terms)


TILE = 256
CHUNK = 768


def dot_nt(a, b):
    return lax.dot_general(a, b, (((1,), (1,)), ((), ())), preferred_element_type=jnp.float32)


def row_mean(value):
    return jnp.sum(value, axis=-1, keepdims=True) * (1.0 / value.shape[-1])


def standardize(hidden):
    centred = hidden - row_mean(hidden)
    reciprocal = lax.rsqrt(row_mean(centred * centred) + EPS)
    return centred * reciprocal, reciprocal


def column_sum(value):
    return jnp.sum(value.reshape(value.shape[0] // 8, 8, value.shape[1]), axis=0)


def dense_kernel(
    size_z,
    size_x,
    tokens_ref,
    mine_ref,
    other_ref,
    cot_ref,
    vectors_ref,
    bias_inner_ref,
    weights_hbm,
    *refs,
):
    mixed_ref, pre_first_ref, grad_mine_ref, grad_other_ref, sums_ref, inner_sum_ref, grad_output_ref = refs[:7]
    inner_terms = refs[7 : 7 + size_z]
    outer_terms = refs[7 + size_z : 7 + size_z + size_x]
    refs = refs[7 + size_z + size_x :]
    w_output, w_inner, w_outer, a_output, a_inner, a_outer, grad_out_buf = refs[:7]
    context, first_low, turned_low, normed, first, slope, active, work = refs[7:15]
    send_inner, send_outer, recv_inner, recv_outer, load_sem, outer_sem, send_sem, recv_sem, store_sem = refs[15:]
    step, steps = pl.program_id(0), pl.num_programs(0)
    core_here = lax.axis_index("core")
    width, hidden = w_inner.shape
    half = width // 2
    chunks = hidden // CHUNK
    shards = size_z * size_x
    pieces = 2 * shards
    rows = width // pieces
    ratio = hidden // width
    z, x, y, _ = place_of()
    twin = partner(core=1 - lax.axis_index("core"))

    def load_outer(start):
        if not start:
            pltpu.make_async_copy(w_outer, w_outer, outer_sem).wait()
            return

        def piece(s, _):
            for q in range(ratio):
                src = weights_hbm.at[
                    pl.ds(pl.multiple_of(s * rows, rows), rows), pl.ds(hidden + width + q * width, width)
                ]
                dst = w_outer.at[pl.ds(pl.multiple_of((s * ratio + q) * rows, rows), rows), :]
                pltpu.make_async_copy(src, dst, outer_sem).start()
            return 0

        lax.fori_loop(0, pieces, piece, 0)

    loads = (
        pltpu.make_async_copy(weights_hbm.at[:, pl.ds(hidden, width)], w_output, load_sem.at[0]),
        pltpu.make_async_copy(weights_hbm.at[:, pl.ds(0, hidden)], w_inner, load_sem.at[1]),
    )

    @pl.when(step == 0)
    def _():
        barrier = pltpu.get_barrier_semaphore()
        pl.semaphore_signal(barrier, inc=1, device_id=twin, device_id_type=MESH_ID)
        pl.semaphore_wait(barrier, 1)
        for load in loads:
            load.start()
        load_outer(True)
        a_output[...] = jnp.zeros_like(a_output)
        a_inner[...] = jnp.zeros_like(a_inner)
        a_outer[...] = jnp.zeros_like(a_outer)
        sums_ref[...] = jnp.zeros_like(sums_ref)
        inner_sum_ref[...] = jnp.zeros_like(inner_sum_ref)

    def vector(i):
        return vectors_ref[i : i + 1, :]

    def add_sum(i, value):
        sums_ref[8 * i : 8 * i + 8, :] += column_sum(value)

    context[:, pl.ds(pl.multiple_of(core_here * half, 128), half)] = mine_ref[...]
    context[:, pl.ds(pl.multiple_of((1 - core_here) * half, 128), half)] = other_ref[...]

    @pl.when(step == 0)
    def _():
        loads[0].wait()

    hidden_rows = tokens_ref[...].astype(jnp.float32) + (dot_nn(context[...], w_output[...]) + vector(0))
    normed[...], first_recip = standardize(hidden_rows)
    first[...] = normed[...] * vector(1) + vector(2)
    first_low[...] = first[...].astype(jnp.bfloat16)
    turned_low[...] = first_low[...].T
    work[...] = jnp.broadcast_to(vector(3), work.shape)

    @pl.when(step == 0)
    def _():
        loads[1].wait()
        load_outer(False)

    def part(c):
        return pl.ds(pl.multiple_of(c * CHUNK, CHUNK), CHUNK)

    def exchange(c):
        return (
            remote(send_inner.at[c], recv_inner.at[c], send_sem.at[0, c], recv_sem.at[0, c], twin),
            remote(send_outer.at[c], recv_outer.at[c], send_sem.at[1, c], recv_sem.at[1, c], twin),
        )

    def forward(c, _):
        u = dot_nn(first_low[...], w_inner[:, part(c)]) + bias_inner_ref[0:1, part(c)]
        cdf = 0.5 * (1.0 + lax.erf(u * ROOT_HALF))
        slope[:, part(c)] = cdf + u * jnp.exp(-0.5 * u * u) * INV_ROOT_TAU
        active[:, part(c)] = (u * cdf).astype(jnp.bfloat16)
        work[...] += dot_nn(active[:, part(c)], w_outer[part(c), :])
        return 0

    lax.fori_loop(0, chunks, forward, 0)
    second, second_recip = standardize(first[...] + work[...])
    mixed_ref[...] = (second * vector(4) + vector(5)).astype(jnp.bfloat16)
    upstream = cot_ref[...].astype(jnp.float32)
    add_sum(0, upstream * second)
    add_sum(1, upstream)
    scaled = upstream * vector(4)
    pre_second = second_recip * (scaled - row_mean(scaled) - second * row_mean(scaled * second))
    grad_outer = pre_second.astype(jnp.bfloat16)
    add_sum(2, grad_outer.astype(jnp.float32))
    work[...] = pre_second
    grad_out_buf[...] = grad_outer

    def backward(c, _):
        grad_out = grad_out_buf[...]
        grad = dot_nt(grad_out, w_outer[part(c), :])
        grad_inner = (grad * slope[:, part(c)]).astype(jnp.bfloat16)
        inner_sum_ref[:, part(c)] += column_sum(grad_inner.astype(jnp.float32))
        a_outer[part(c), :] += dot_nn(active[:, part(c)].T, grad_out)
        a_inner[:, part(c)] += dot_nn(turned_low[...], grad_inner)
        work[...] += dot_nt(grad_inner, w_inner[:, part(c)])

        @pl.when(step == steps - 1)
        def _():
            theirs = pl.multiple_of(c * CHUNK + (1 - core_here) * half, 128)
            send_inner[c] = a_inner[:, pl.ds(theirs, half)].astype(jnp.bfloat16)
            send_outer[c] = a_outer[part(c), pl.ds(pl.multiple_of((1 - core_here) * half, 128), half)].astype(jnp.bfloat16)
            for move in exchange(c):
                move.start()

        return 0

    lax.fori_loop(0, chunks, backward, 0)
    grad_first = work[...]
    add_sum(3, grad_first * normed[...])
    add_sum(4, grad_first)
    scaled = grad_first * vector(1)
    pre_first = first_recip * (scaled - row_mean(scaled) - normed[...] * row_mean(scaled * normed[...]))
    pre_first_ref[...] = pre_first
    grad_attended = pre_first.astype(jnp.bfloat16)
    add_sum(5, grad_attended.astype(jnp.float32))
    a_output[...] += dot_nn(context[...].T, grad_attended)
    context[...] = dot_nt(grad_attended, w_output[...]).astype(jnp.bfloat16)
    grad_mine_ref[...] = context[:, pl.ds(pl.multiple_of(core_here * half, 128), half)]
    grad_other_ref[...] = context[:, pl.ds(pl.multiple_of((1 - core_here) * half, 128), half)]

    @pl.when(step == steps - 1)
    def _():
        grad_output_ref[...] = a_output[...].astype(jnp.bfloat16)

        shard = width // shards
        long = hidden // shards

        def inner_out(c):
            copies = []
            for k in range(size_z):
                for column in range(size_x):
                    slot = lax.rem(z + k, size_z) * size_x + column
                    src = send_inner.at[c, pl.ds(pl.multiple_of(slot * shard, shard), shard), :]
                    copies.append(
                        pltpu.make_async_copy(src, inner_terms[k].at[column, :, pl.ds(c * half, half)], store_sem.at[0, c])
                    )
            return copies

        def outer_out(c):
            copies = []
            group = CHUNK // long // size_x
            for i in range(group):
                for j in range(size_x):
                    src = send_outer.at[c, pl.ds(pl.multiple_of((i * size_x + lax.rem(x + j, size_x)) * long, long), long), :]
                    copies.append(pltpu.make_async_copy(src, outer_terms[j].at[c * group + i], store_sem.at[1, c]))
            return copies

        for c in range(chunks):
            ours = pl.multiple_of(c * CHUNK + core_here * half, 128)
            first_move, second_move = exchange(c)
            first_move.wait()
            send_inner[c] = (a_inner[:, pl.ds(ours, half)] + recv_inner[c].astype(jnp.float32)).astype(jnp.bfloat16)
            for copy in inner_out(c):
                copy.start()
            second_move.wait()
            columns = pl.ds(pl.multiple_of(core_here * half, 128), half)
            send_outer[c] = (a_outer[part(c), columns] + recv_outer[c].astype(jnp.float32)).astype(jnp.bfloat16)
            for copy in outer_out(c):
                copy.start()
        for c in range(chunks):
            pltpu.make_async_copy(send_inner.at[c], send_inner.at[c], store_sem.at[0, c]).wait()
            pltpu.make_async_copy(send_outer.at[c], send_outer.at[c], store_sem.at[1, c]).wait()


def dense_layer(size_z, size_x, tokens, mine, other, cotangent, vectors, bias_inner, weights):
    local, half = mine.shape
    width = 2 * half
    hidden = bias_inner.shape[1]
    steps = local // TILE
    shards = size_z * size_x
    chunks = hidden // CHUNK
    low, high = jnp.bfloat16, jnp.float32
    tile = pl.BlockSpec((TILE, width), lambda t, *_: (t, 0))
    half_tile = pl.BlockSpec((TILE, half), lambda t, *_: (t, 0))
    anywhere = pl.BlockSpec(memory_space=pl.ANY)

    def whole(shape):
        return pl.BlockSpec(shape, lambda t, *_: (0, 0))

    inner_shape = jax.ShapeDtypeStruct((size_x, width // shards, hidden // 2), low)
    outer_shape = jax.ShapeDtypeStruct((size_z, hidden // shards, half), low)
    halves = pltpu.VMEM((chunks, width, half), low)
    dma = pltpu.SemaphoreType.DMA
    return pl.pallas_call(
        lambda *refs: dense_kernel(size_z, size_x, *refs),
        out_shape=(
            jax.ShapeDtypeStruct((local, width), low),
            jax.ShapeDtypeStruct((local, width), high),
            jax.ShapeDtypeStruct((local, half), low),
            jax.ShapeDtypeStruct((local, half), low),
            jax.ShapeDtypeStruct((48, width), high),
            jax.ShapeDtypeStruct((8, hidden), high),
            jax.ShapeDtypeStruct((width, width), low),
        )
        + (inner_shape,) * size_z
        + (outer_shape,) * size_x,
        grid_spec=pltpu.PrefetchScalarGridSpec(
            num_scalar_prefetch=0,
            grid=(steps,),
            in_specs=[
                tile,
                half_tile,
                half_tile,
                tile,
                whole((8, width)),
                whole((1, hidden)),
                anywhere,
            ],
            out_specs=[
                tile,
                tile,
                half_tile,
                half_tile,
                whole((48, width)),
                whole((8, hidden)),
                whole((width, width)),
            ]
            + [anywhere] * (size_z + size_x),
            scratch_shapes=[
                pltpu.VMEM((width, width), low),
                pltpu.VMEM((width, hidden), low),
                pltpu.VMEM((hidden, width), low),
                pltpu.VMEM((width, width), high),
                pltpu.VMEM((width, hidden), high),
                pltpu.VMEM((hidden, width), high),
                pltpu.VMEM((TILE, width), low),
                pltpu.VMEM((TILE, width), low),
                pltpu.VMEM((TILE, width), low),
                pltpu.VMEM((width, TILE), low),
                pltpu.VMEM((TILE, width), high),
                pltpu.VMEM((TILE, width), high),
                pltpu.VMEM((TILE, hidden), high),
                pltpu.VMEM((TILE, hidden), low),
                pltpu.VMEM((TILE, width), high),
                halves,
                halves,
                halves,
                halves,
                dma((2,)),
                dma,
                dma((2, chunks)),
                dma((2, chunks)),
                dma((2, chunks)),
            ],
        ),
        compiler_params=pltpu.CompilerParams(
            dimension_semantics=("arbitrary",), vmem_limit_bytes=67_000_000, collective_id=3, has_side_effects=True
        ),
        cost_estimate=pl.CostEstimate(flops=32_000_000_000, bytes_accessed=40_000_000, transcendentals=6_000_000),
        name="dense_layer",
    )(tokens, mine, other, cotangent, vectors, bias_inner, weights)


def lowered(piece):
    return piece.astype(jnp.bfloat16)


def widen(piece):
    return piece.astype(jnp.float32)


def matmul(left, right):
    return jnp.dot(left, right, preferred_element_type=jnp.float32)


def matmul_tn(left, right):
    return lax.dot_general(
        left, right, (((0,), (0,)), ((), ())), preferred_element_type=jnp.float32
    )


def matmul_nt(left, right):
    return lax.dot_general(
        left, right, (((1,), (1,)), ((), ())), preferred_element_type=jnp.float32
    )


def normalize(hidden, norm_gain, norm_shift):
    centred = hidden - jnp.mean(hidden, axis=-1, keepdims=True)
    reciprocal = lax.rsqrt(jnp.mean(centred * centred, axis=-1, keepdims=True) + EPS)
    normed = centred * reciprocal
    return (normed * norm_gain + norm_shift, normed, reciprocal)


def normalize_back(upstream, normed, reciprocal, norm_gain):
    scaled = upstream * norm_gain
    result = reciprocal * (
        scaled
        - jnp.mean(scaled, axis=-1, keepdims=True)
        - normed * jnp.mean(scaled * normed, axis=-1, keepdims=True)
    )
    return (result, jnp.sum(upstream * normed, axis=0), jnp.sum(upstream, axis=0))


def gelu_value(values_in):
    return 0.5 * values_in * (1.0 + lax.erf(values_in * ROOT_HALF))


def gelu_slope(values_in):
    return (
        0.5 * (1.0 + lax.erf(values_in * ROOT_HALF))
        + values_in * jnp.exp(-0.5 * values_in * values_in) * INV_ROOT_TAU
    )


def shift(piece, axis, step):
    size = lax.axis_size(axis)
    return lax.ppermute(piece, axis, [(i, (i + step) % size) for i in range(size)])


def swap(piece, axis):
    return lax.ppermute(piece, axis, [(0, 1), (1, 0)])


def pick(piece, index, axis=0):
    return lax.dynamic_index_in_dim(piece, index, axis, keepdims=False)


def in_order(first_is_zero, own, other, axis):
    return jnp.where(
        first_is_zero,
        jnp.concatenate([own, other], axis),
        jnp.concatenate([other, own], axis),
    )


def collect(piece):
    size_z, size_x = lax.axis_size("z"), lax.axis_size("x")
    z, x = lax.axis_index("z"), lax.axis_index("x")
    along_z = [piece] + [shift(piece, "z", k) for k in range(1, size_z)]
    whole = jnp.zeros((size_z, size_x) + piece.shape, piece.dtype)
    zeros = (0,) * piece.ndim
    for j in range(size_x):
        for k in range(size_z):
            arrived = along_z[k] if j == 0 else shift(along_z[k], "x", j)
            place = ((z - k) % size_z, (x - j) % size_x) + zeros
            whole = lax.dynamic_update_slice(whole, arrived[None, None], place)
    return whole.reshape((size_z * size_x,) + piece.shape)


def reduce_owned(terms):
    size_z, size_x = lax.axis_size("z"), lax.axis_size("x")
    z, x = lax.axis_index("z"), lax.axis_index("x")
    terms = terms.reshape((size_z, size_x) + terms.shape[1:])
    total = widen(pick(terms, x, 1))
    for j in range(1, size_x):
        total = total + widen(shift(pick(terms, (x + j) % size_x, 1), "x", j))
    terms = lowered(total)
    total = widen(pick(terms, z))
    for k in range(1, size_z):
        total = total + widen(shift(pick(terms, (z + k) % size_z), "z", k))
    terms = lowered(total)
    return widen(terms) + widen(swap(terms, "y"))


def plain_body(
    tokens,
    segment_ids,
    w_query,
    w_key,
    w_value,
    w_output,
    b_query,
    b_value,
    b_output,
    first_gain,
    first_shift,
    w_inner,
    b_inner,
    w_outer,
    b_outer,
    second_gain,
    second_shift,
    cotangent,
):
    core, y = lax.axis_index("core"), lax.axis_index("y")
    shards = lax.axis_size("z") * lax.axis_size("x")
    sequences, part, width = tokens.shape
    half = width // 2
    pairs = half // 128
    hidden = w_inner.shape[1]
    local = 2 * part
    own_rows = w_query.shape[0]
    unit_half = hidden // shards // 2

    def columns(matrix):
        return lowered(lax.dynamic_slice_in_dim(matrix, core * half, half, 1))

    vectors = (b_query, b_value, b_output, first_gain, first_shift, b_inner, b_outer, second_gain, second_shift)
    flat = jnp.concatenate([lowered(v) for v in vectors])
    lanes = 3 * half
    extra = -(-flat.shape[0] // lanes)
    flat = jnp.pad(flat, (0, extra * lanes - flat.shape[0])).reshape(extra, lanes)
    weights = jnp.stack([columns(w).reshape(own_rows, pairs, 128) for w in (w_query, w_key, w_value)], axis=2)
    early = collect(jnp.concatenate([weights.reshape(own_rows, lanes), flat], axis=0))

    mine = pick(tokens, y)
    arrived = swap(pick(tokens, 1 - y), "y")
    mine_other, arrived_other = swap(mine, "core"), swap(arrived, "core")
    inputs_all = jnp.concatenate([mine, arrived, mine_other, arrived_other], axis=0)
    inputs = jnp.concatenate([mine, arrived], axis=0)

    inner_piece = lowered(pick(w_inner.reshape(own_rows, shards, 2, unit_half), core, 2)).reshape(own_rows, hidden // 2)
    late = collect(jnp.concatenate([columns(w_output), inner_piece], axis=1)).reshape(width, half + hidden // 2)
    outer_own = collect(lowered(lax.dynamic_slice_in_dim(w_outer, core * unit_half, unit_half, 0))).reshape(hidden // 2, width)
    output_own, inner_own = late[:, :half], late[:, half:]
    output_other, inner_other, outer_other = swap(output_own, "core"), swap(inner_own, "core"), swap(outer_own, "core")
    full_output = in_order(core == 0, output_own, output_other, 1)
    cotangent_mine = pick(cotangent, y)
    cotangent_arrived = swap(pick(cotangent, 1 - y), "y")

    full_early = early[:, :own_rows].reshape(width, lanes)
    flat_all = early[:, own_rows:].reshape(shards, extra * lanes)
    sizes = [v.shape[0] for v in vectors]
    gathered, at = [], 0
    for size in sizes:
        gathered.append(flat_all[:, at : at + size].reshape(shards * size))
        at += size
    bias_query, bias_value, bias_output, gain_first, shift_first, bias_inner, bias_outer, gain_second, shift_second = [
        widen(v) for v in gathered
    ]
    heads_query = lax.dynamic_slice_in_dim(bias_query, core * half, half).reshape(pairs, 1, 128)
    heads_value = lax.dynamic_slice_in_dim(bias_value, core * half, half).reshape(pairs, 1, 128)
    bias_all = jnp.concatenate([heads_query, jnp.zeros_like(heads_query), heads_value], axis=1).reshape(lanes)
    scale = jnp.tile(jnp.concatenate([jnp.full((128,), HD ** (-0.5)), jnp.ones((256,))]), pairs)
    projected = lowered((matmul(inputs_all, full_early) + bias_all) * scale)

    spot = jnp.arange(5, dtype=jnp.int32)
    place = jnp.where(spot < 4, ((spot % 2 != core) * 2 + (spot // 2 != y) * 1) * part, core)
    segments = pick(segment_ids, y)
    heads_mine, heads_other, logsum = attention(place, segments, projected)
    context = in_order(core == 0, heads_mine, swap(heads_other, "core"), 1)

    attended = matmul(context, full_output) + bias_output
    first, first_normed, first_recip = normalize(widen(inputs) + attended, gain_first, shift_first)
    first_low = lowered(first)
    biases = bias_inner.reshape(shards, 2, unit_half)
    halves = ((inner_own, outer_own, pick(biases, core, 1)), (inner_other, outer_other, pick(biases, 1 - core, 1)))
    outer, kept = bias_outer, []
    for inner_weight, outer_weight, bias in halves:
        inner = matmul(first_low, inner_weight) + bias.reshape(hidden // 2)
        active = lowered(gelu_value(inner))
        outer = outer + matmul(active, outer_weight)
        kept.append((inner, active))
    mixed, second_normed, second_recip = normalize(first + outer, gain_second, shift_second)
    mixed = lowered(mixed)

    upstream = widen(jnp.concatenate([cotangent_mine, cotangent_arrived], axis=0))
    pre_second, grad_second_gain, grad_second_shift = normalize_back(upstream, second_normed, second_recip, gain_second)
    grad_outer = lowered(pre_second)
    grad_b_outer = jnp.sum(widen(grad_outer), axis=0)
    grad_first, inner_grads, outer_grads, bias_grads = pre_second, [], [], []
    for (inner, active), (inner_weight, outer_weight, _) in zip(kept, halves):
        grad_inner = lowered(matmul_nt(grad_outer, outer_weight) * gelu_slope(inner))
        outer_grads.append(lowered(matmul_tn(active, grad_outer)))
        inner_grads.append(lowered(matmul_tn(first_low, grad_inner)))
        bias_grads.append(jnp.sum(widen(grad_inner), axis=0).reshape(shards, 1, unit_half))
        grad_first = grad_first + matmul_nt(grad_inner, inner_weight)
    grad_b_inner = in_order(core == 0, bias_grads[0], bias_grads[1], 1).reshape(hidden)
    pre_first, grad_first_gain, grad_first_shift = normalize_back(grad_first, first_normed, first_recip, gain_first)
    grad_attended = lowered(pre_first)
    grad_b_output = jnp.sum(widen(grad_attended), axis=0)
    grad_w_output = lowered(matmul_tn(context, grad_attended))
    grad_context = lowered(matmul_nt(grad_attended, full_output))
    context_mine = lax.dynamic_slice_in_dim(grad_context, core * half, half, 1)
    context_other = lax.dynamic_slice_in_dim(grad_context, (1 - core) * half, half, 1)
    upstream_other = swap(context_other, "core")

    def core_sum(own, other):
        return lowered(widen(own) + widen(swap(other, "core")))

    outer_term = core_sum(*outer_grads)
    inner_term = core_sum(*inner_grads)
    output_term = core_sum(
        lax.dynamic_slice_in_dim(grad_w_output, core * half, half, 1),
        lax.dynamic_slice_in_dim(grad_w_output, (1 - core) * half, half, 1),
    )
    outer_done = reduce_owned(outer_term.reshape(shards, unit_half, width))
    late_done = reduce_owned(jnp.concatenate([output_term, inner_term], axis=1).reshape(shards, own_rows, half + hidden // 2))

    grads, sums = attention_back(place, segments, projected, heads_mine, heads_other, context_mine, upstream_other, logsum)
    grad_early = lowered(matmul_tn(inputs_all, grads))
    partial = matmul_nt(grads, full_early)
    sums = sums.reshape(pairs, 8, 3, 128)[:, 0]
    blank = jnp.zeros((width,), jnp.float32)
    grad_b_query = lax.dynamic_update_slice(blank, sums[:, 0].reshape(half), (core * half,))
    grad_b_value = lax.dynamic_update_slice(blank, sums[:, 2].reshape(half), (core * half,))
    vector_grads = (
        grad_b_query,
        grad_b_value,
        grad_b_output,
        grad_first_gain,
        grad_first_shift,
        grad_b_inner,
        grad_b_outer,
        grad_second_gain,
        grad_second_shift,
    )
    flat_grads = jnp.concatenate([v.reshape(shards, -1) for v in vector_grads], axis=1)
    flat_grads = jnp.pad(flat_grads, ((0, 0), (0, extra * lanes - flat_grads.shape[1])))
    early_term = jnp.concatenate(
        [grad_early.reshape(shards, own_rows, lanes), lowered(flat_grads).reshape(shards, extra, lanes)], axis=1
    )
    early_done = reduce_owned(early_term)

    grad_inputs = pre_first + partial[:local] + widen(swap(lowered(partial[local:]), "core"))
    returned = widen(swap(lowered(grad_inputs[part:]), "y"))
    grad_tokens = in_order(y == 0, grad_inputs[None, :part], returned[None], 0)
    mixed_out = in_order(y == 0, mixed[None, :part], swap(mixed[part:], "y")[None], 0)

    def both(piece):
        return widen(swap(lowered(piece), "core"))

    early_matrix = early_done[:own_rows]
    early_full = in_order(
        core == 0, early_matrix.reshape(own_rows, pairs, 3, 128)[None], both(early_matrix).reshape(own_rows, pairs, 3, 128)[None], 0
    )
    early_full = early_full.transpose(3, 1, 0, 2, 4).reshape(3, own_rows, width)
    late_other = both(late_done)
    output_full = in_order(core == 0, late_done[:, :half], late_other[:, :half], 1)
    inner_full = in_order(
        core == 0,
        late_done[:, half:].reshape(own_rows, shards, 1, unit_half),
        late_other[:, half:].reshape(own_rows, shards, 1, unit_half),
        2,
    ).reshape(own_rows, hidden)
    outer_full = in_order(core == 0, outer_done, both(outer_done), 0)
    vector_part = early_done[own_rows:]
    vector_sums = (vector_part + swap(vector_part, "core")).reshape(extra * lanes)
    out_vectors, at = [], 0
    for size in sizes:
        out_vectors.append(vector_sums[at : at + size])
        at += size
    (
        done_b_query,
        done_b_value,
        done_b_output,
        done_first_gain,
        done_first_shift,
        done_b_inner,
        done_b_outer,
        done_second_gain,
        done_second_shift,
    ) = out_vectors
    return (
        mixed_out,
        grad_tokens,
        early_full[0],
        early_full[1],
        early_full[2],
        output_full,
        done_b_query,
        done_b_value,
        done_b_output,
        done_first_gain,
        done_first_shift,
        inner_full,
        done_b_inner,
        outer_full,
        done_b_outer,
        done_second_gain,
        done_second_shift,
    )


def body(
    tokens,
    segment_ids,
    w_query,
    w_key,
    w_value,
    w_output,
    b_query,
    b_value,
    b_output,
    first_gain,
    first_shift,
    w_inner,
    b_inner,
    w_outer,
    b_outer,
    second_gain,
    second_shift,
    cotangent,
):
    core, y = lax.axis_index("core"), lax.axis_index("y")
    size_z, size_x = lax.axis_size("z"), lax.axis_size("x")
    shards = size_z * size_x
    everyone = ("z", "x", "core")
    sequences, part, width = tokens.shape
    half = width // 2
    pairs = half // 128
    hidden = w_inner.shape[1]
    local = 2 * part
    own_rows = w_query.shape[0]
    lanes = 3 * half

    stack = hidden // width

    def core_rows(matrix):
        rows = matrix.shape[0] // 2
        return lowered(lax.dynamic_slice_in_dim(matrix, core * rows, rows, 0))

    outer_rows = core_rows(w_outer)
    outer_rows = outer_rows.reshape(stack, own_rows // 2, width).transpose(1, 0, 2).reshape(own_rows // 2, hidden)
    pieces = (core_rows(w_inner), core_rows(w_output), outer_rows)
    dense = lax.all_gather(jnp.concatenate(pieces, axis=1), everyone, axis=0, tiled=True)

    vectors = (b_query, b_value, b_output, first_gain, first_shift, b_inner, b_outer, second_gain, second_shift)
    sizes = [v.shape[0] for v in vectors]
    tokens_all, cotangent_all, early, vectors_all = entry(size_z, size_x, tokens, cotangent, w_query, w_key, w_value, vectors)
    inputs_all = tokens_all.reshape(4 * part, width)
    full_early = early.reshape(width, lanes)
    bias_query, bias_value, bias_output, gain_first, shift_first, bias_inner, bias_outer, gain_second, shift_second = [
        vectors_all[:, i, :size].reshape(shards * size) for i, size in enumerate(sizes)
    ]
    heads_query = lax.dynamic_slice_in_dim(bias_query, core * half, half).reshape(pairs, 1, 128)
    heads_value = lax.dynamic_slice_in_dim(bias_value, core * half, half).reshape(pairs, 1, 128)
    bias_all = jnp.concatenate([heads_query, jnp.zeros_like(heads_query), heads_value], axis=1).reshape(lanes)
    scale = jnp.tile(jnp.concatenate([jnp.full((128,), HD ** (-0.5)), jnp.ones((256,))]), pairs)
    projected = lowered((matmul(inputs_all, full_early) + bias_all) * scale)

    spot = jnp.arange(5, dtype=jnp.int32)
    place = jnp.where(spot < 4, ((spot % 2 != core) * 2 + (spot // 2 != y) * 1) * part, core)
    segments = pick(segment_ids, y)
    context_mine, context_other, logsum = attention(place, segments, projected)
    norms = jnp.stack([bias_output, gain_first, shift_first, bias_outer, gain_second, shift_second])
    norms = jnp.concatenate([norms, jnp.zeros((2, width), jnp.float32)], axis=0)
    made = dense_layer(
        size_z,
        size_x,
        inputs_all,
        context_mine,
        swap(context_other, "core"),
        cotangent_all.reshape(local, width),
        norms,
        bias_inner.reshape(1, hidden),
        dense,
    )
    mixed, pre_first, upstream_mine, upstream_send, dense_sums, inner_sums, grad_w_output = made[:7]
    inner_terms = [made[7]] + [shift(made[7 + k], "z", k) for k in range(1, size_z)]
    outer_terms = [made[7 + size_z]] + [shift(made[7 + size_z + j], "x", j) for j in range(1, size_x)]
    upstream_other = swap(upstream_send, "core")
    dense_sums = jnp.sum(dense_sums.reshape(6, 8, width), axis=1)
    grad_second_gain, grad_second_shift, grad_b_outer, grad_first_gain, grad_first_shift, grad_b_output = [
        dense_sums[i] for i in range(6)
    ]
    grad_b_inner = jnp.sum(inner_sums, axis=0)
    mixed_out = in_order(y == 0, mixed[None, :part], swap(mixed[part:], "y")[None], 0)

    grads, sums = attention_back(place, segments, projected, context_mine, context_other, upstream_mine, upstream_other, logsum)
    sums = sums.reshape(pairs, 8, 3, 128)[:, 0]
    blank = jnp.zeros((width,), jnp.float32)
    grad_b_query = lax.dynamic_update_slice(blank, sums[:, 0].reshape(half), (core * half,))
    grad_b_value = lax.dynamic_update_slice(blank, sums[:, 2].reshape(half), (core * half,))
    vector_grads = (
        grad_b_query,
        grad_b_value,
        grad_b_output,
        grad_first_gain,
        grad_first_shift,
        grad_b_inner,
        grad_b_outer,
        grad_second_gain,
        grad_second_shift,
    )
    longest = vectors_all.shape[2]
    rows = [jnp.pad(v.reshape(shards, 1, -1), ((0, 0), (0, 0), (0, longest - v.shape[0] // shards))) for v in vector_grads]
    rows.append(jnp.zeros((shards, vectors_all.shape[1] - len(rows), longest), jnp.float32))
    vector_terms = jnp.concatenate(rows, axis=1)
    grad_tokens, grad_query, grad_key, grad_value, grad_output, grad_inner_full, grad_outer_full, vector_sums = exit_call(
        size_z,
        size_x,
        grads,
        inputs_all,
        full_early,
        pre_first,
        grad_w_output.reshape(shards, own_rows, width),
        vector_terms,
        inner_terms,
        outer_terms,
    )
    done = [vector_sums[i, :size] for i, size in enumerate(sizes)]
    return (
        mixed_out,
        grad_tokens,
        grad_query,
        grad_key,
        grad_value,
        grad_output,
        done[0],
        done[1],
        done[2],
        done[3],
        done[4],
        grad_inner_full,
        done[5],
        grad_outer_full,
        done[6],
        done[7],
        done[8],
    )


def layer(*arrays):
    if arrays[2].shape[0] % 32 == 0 and lax.axis_size("x") > 1:
        return body(*arrays)
    return plain_body(*arrays)


def solution(mesh):
    outer, inner = mesh.devices.shape
    size_z = 1
    while size_z * size_z < outer:
        size_z *= 2
    split = Mesh(mesh.devices.reshape(size_z, outer // size_z, inner // 2, 2), ("z", "x", "y", "core"))
    dp, seq = ("z", "x"), ("y", "core")
    activation, matrix, vector = P(dp, seq, None), P(dp, None), P(dp)
    return jax.shard_map(
        layer,
        mesh=split,
        in_specs=(
            activation,
            matrix,
            matrix,
            matrix,
            matrix,
            matrix,
            vector,
            vector,
            vector,
            vector,
            vector,
            matrix,
            vector,
            matrix,
            vector,
            vector,
            vector,
            activation,
        ),
        out_specs=(
            activation,
            activation,
            matrix,
            matrix,
            matrix,
            matrix,
            vector,
            vector,
            vector,
            vector,
            vector,
            matrix,
            vector,
            matrix,
            vector,
            vector,
            vector,
        ),
        check_vma=False,
    )
```

time: 410 us -> 353 us (0.86)
  Pallas kernels: 311 us -> 274 us
  starting transfers between devices: 0.51 us -> 21.1 us
  waiting for transfers between devices: 17.6 us -> 0.04 us
  matrix products: 25.4 us -> 7.89 us
  other arithmetic: 10.6 us -> 4.76 us
    pallas_call x3 -> x2, Pallas kernels: 154 us -> 127 us  [the longest x1 63.9 us: exit_call(): pl.pallas_call(lambda *refs: exit_kernel(size_z, size_x, shapes, *refs),...]
    ppermute x0 -> x4, starting transfers between devices: none -> 20.6 us  [shift(): lax.ppermute(piece, axis, [(i, (i + step) % size) for i in range(size)])]
    pallas_call x1, Pallas kernels: 71.8 us -> 53.9 us  [attention_back(): pl.pallas_call(backward_kernel, out_shape=(jax.ShapeDtypeStruct((length,...]
    ppermute x4 -> x3, waiting for transfers between devices: 17.6 us -> 0.01 us  [swap(): return lax.ppermute(piece, axis, [(0, 1), (1, 0)])]
    dot_general x3 -> x0, matrix products: 16.3 us -> none  [the longest x2 10.8 us: matmul_nt(): lax.dot_general(left, right, (((1,), (1,)), ((), ())), preferred_element_...]
    pallas_call x1, Pallas kernels: 41.6 us -> 49.4 us  [entry(): pl.pallas_call(lambda *refs: entry_kernel(size_z, size_x, len(vectors), *...]
    unnamed x75 -> x65, local copies, waits for them, and re-layouts: 11.3 us -> 17.4 us
    add x1 -> x0, other arithmetic: 5.06 us -> none  [body(): own_partial = pre_first + matmul_nt(grads[:local], full_early)]
  transfers between devices with their start and end apart: 6 -> 8, of which waited for: 1 -> 0; matrix products, arithmetic and copies ran while one was open for 11% -> 6% of each run, Pallas kernels for 56% -> 41%
where the time goes in v3:
time: 353 us; the launch traced here: 354 us
  Pallas kernels  274 us (78%)
  local copies, waits for them, and re-layouts  32 us (9%)
  starting transfers between devices  21.1 us (6%)
  between operations  14.5 us (4%)
  matrix products  7.89 us (2%)
  other arithmetic  4.76 us (1%)
    pallas_call x1, Pallas kernels, exit_call(): pl.pallas_call(lambda *refs: exit_kernel(size_z, size_x, shapes, *refs),...  63.9 us
    pallas_call x1, Pallas kernels, dense_layer(): pl.pallas_call(lambda *refs: dense_kernel(size_z, size_x, *refs), out_sha...  63 us
    pallas_call x1, Pallas kernels, attention_back(): pl.pallas_call(backward_kernel, out_shape=(jax.ShapeDtypeStruct((length,...  53.9 us
    pallas_call x1, Pallas kernels, entry(): pl.pallas_call(lambda *refs: entry_kernel(size_z, size_x, len(vectors), *...  49.4 us
    pallas_call x1, Pallas kernels, attention(): pl.pallas_call(forward_kernel, out_shape=(jax.ShapeDtypeStruct((rows, pai...  43.6 us
    ppermute x4, starting transfers between devices, shift(): lax.ppermute(piece, axis, [(i, (i + step) % size) for i in range(size)])  20.6 us
    unnamed x65, local copies, waits for them, and re-layouts  17.4 us
    dot_general x1, matrix products, matmul(): return jnp.dot(left, right, preferred_element_type=jnp.float32)  7.89 us
  transfers between devices with their start and end apart: 8, of which 0 were waited for; matrix products, arithmetic and copies ran while one was open for 6% of the time, Pallas kernels for 41%

profile of v3, /device:TPU:0, one launch (start us, length us, event | category | flops | bytes accessed | tf_op | source)
XLA Modules:
  0.0 354.1 jit_solution(8429127632450984990)
XLA Ops:
  7.3 1.1 dynamic-slice_convert_fusion.1
  9.3 1.1 dynamic-slice_convert_fusion
  11.8 1.4 copy-done.4
  13.2 1.4 copy-done.5
  14.6 1.0 copy-done.7
  16.5 49.4 %entry.1 = (bf16[4,512,768]{2,1,0:T(8,128)(2,1)S(1)}, bf16[2,512,768]{2,1,0:T(8,128)(2,1)S(1)}, bf16[8,96,1152]{2,1,0:T(8,128)(2,1)S(1)}, f32[8,16,384]{2,1,0:T(8,128)S(1)}) custom-call(bf16[2,512,768]{2,1,0:T(8,128)(2,1)S(1)} %copy-done.4, bf16[2,512,768]{2,1,0:T(8,128)(2,1)S(1)} %copy-done.5, f32[96,768]{1,0:T(8,128)S(1)} %copy-done.6, ...), custom_call_target="tpu_custom_call" | custom-call | tf_op jit(solution)/shard_map/entry/pallas_call | solution.py:515
  66.0 1.2 copy-done.3
  67.2 1.1 copy-done.18
  70.7 7.9 %multiply_convert_fusion.qkv_ref = bf16[2048,1152]{1,0:T(8,128)(2,1)} fusion(bf16[2048,768]{1,0:T(8,128)(2,1)S(1)} %bitcast.51, bf16[768,1152]{1,0:T(8,128)(2,1)} %bitcast.54, f32[1152]{0:T(1024)S(1)} %mul.32, f32[1152]{0:T(1024)S(1)} %add.57), kind=kOutput, calls=%fused_computation | convolution fusion | flops 3630956544 | bytes 9643008 | tf_op jit(solution)/shard_map/dot_general | solution.py:1186
  78.6 43.6 %attention_forward.1 = (bf16[1024,384]{1,0:T(8,128)(2,1)}, bf16[1024,384]{1,0:T(8,128)(2,1)}, f32[24,2048]{1,0:T(8,128)}) custom-call(s32[5]{0:T(128)} %compare_select_fusion.1.place_ref, s32[2048]{0:T(1024)} %bitcast.73, bf16[2048,1152]{1,0:T(8,128)(2,1)} %multiply_convert_fusion.qkv_ref, s32[1,2048]{1,0:T(1,128)} %constant_dynamic-slice_fusion.row_ref), custom_call_target="tpu_custom_call" | custom-call | flops 24000000000 | bytes 9000000 | tf_op jit(solution)/shard_map/attention_forward/pallas_call | solution.py:167
  122.2 1.5 slice.95
  124.8 63.0 %dense_layer.1 = (bf16[1024,768]{1,0:T(8,128)(2,1)}, f32[1024,768]{1,0:T(8,128)}, bf16[1024,384]{1,0:T(8,128)(2,1)}, bf16[1024,384]{1,0:T(8,128)(2,1)}, f32[48,7...) custom-call(bf16[2048,768]{1,0:T(8,128)(2,1)} %bitcast.52, ...), custom_call_target="tpu_custom_call" | custom-call | flops 32000000000 | bytes 40000000 | tf_op jit(solution)/shard_map/dense_layer/pallas_call | solution.py:1107
  189.8 18.2 %collective-permute-start.3 = (bf16[2,96,1536]{2,1,0:T(8,128)(2,1)}, bf16[2,96,1536]{2,1,0:T(8,128)(2,1)}, u32[]{:S(2)}, u32[]{:S(2)}) collective-permute-start(bf16[2,96,1536]{2,1,0:T(8,128)(2,1)} %get-tuple-element.64), channel_id=1, source_target_pairs={{0,8},{8,16},{16,24},{24,0},{1,9},{9,17},{17,25},{25,1},{2,10},{10... | collective-permute-start | bytes 1769480 | tf_op jit(solution)/shard_map/ppermute | solution.py:1231
  208.0 2.4 collective-permute-start.5
  211.4 1.5 slice_bitcast_fusion
  213.8 53.9 %attention_backward.1 = (bf16[2048,1152]{1,0:T(8,128)(2,1)}, f32[24,384]{1,0:T(8,128)}) custom-call(s32[5]{0:T(128)} %compare_select_fusion.1.place_ref, s32[2048]{0:T(1024)} %bitcast.74, bf16[2048,1152]{1,0:T(8,128)(2,1)} %multiply_convert_fusion.qkv_ref, bf16[1024,384]{1,0:T(8,128)(2,1)} %get-tuple-element.50.refs_1_.ctx_mine_ref, ...), custom_call_target="tpu_custom_call" | custom-call | flops 60000002048 | bytes 15000000 | tf_op jit(solution)/shard_map/attention_backward/pallas_call | solution.py:331
  268.9 1.5 concatenate.23.refs_5_
  270.4 1.4 maximum_select_fusion
  271.8 63.9 %exit.1 = (f32[2,512,768]{2,1,0:T(8,128)}, f32[96,768]{1,0:T(8,128)}, f32[96,768]{1,0:T(8,128)}, f32[96,768]{1,0:T(8,128)}, f32[96,768]{1,0:T(8,128)}, /*index=5...) custom-call(bf16[2048,1152]{1,0:T(8,128)(2,1)} %get-tuple-element.57.refs_0_, bf16[2048,768]{1,0:T(8,128)(2,1)} %bitcast.53, ...), custom_call_target="tpu_custom_call" | custom-call | tf_op jit(solution)/shard_map/exit/pallas_call | solution.py:848
  335.7 1.5 slice_bitcast_fusion.1
  337.2 1.3 slice_reduce_fusion.16
  338.5 3.8 %copy.59 = f32[2,512,768]{2,1,0:T(8,128)} copy(f32[2,512,768]{2,1,0:T(8,128)} %get-tuple-element.121) | data formatting | bytes 6291456
  345.2 1.0 copy.64
  346.2 1.0 copy.65
  (124 shorter events, 14.6 us)
Async XLA Ops:
  7.2 62.9 %copy-start = (s32[2,2048]{1,0:T(2,128)S(1)}, s32[2,2048]{1,0:T(2,128)}, u32[]{:S(2)}) copy-start(s32[2,2048]{1,0:T(2,128)} %param.19) | copy-start | bytes 49156
  7.2 117.6 %all-gather.2.cloned.1.call-start = ((), (), s32[]{:S(2)}) async-start(), calls=%async_computation | async-start | bytes 11280384 | tf_op jit(solution)/shard_map/all_gather | solution.py:1530
  10.4 1.3 copy-start.6
  10.4 1.3 copy-start.10
  10.4 1.3 copy-start.11
  10.4 1.3 copy-start.12
  11.8 1.4 copy-start.4
  13.2 1.4 copy-start.5
  16.5 53.1 %copy-start.26 = (f32[384]{0:T(512)S(1)}, f32[384]{0:T(512)}, u32[]{:S(2)}) copy-start(f32[384]{0:T(512)} %constant.62.clone.1) | copy-start | bytes 4612
  68.3 10.3 %copy-start.2 = (bf16[4,512,768]{2,1,0:T(8,128)(2,1)}, bf16[4,512,768]{2,1,0:T(8,128)(2,1)S(1)}, u32[]{:S(2)}) copy-start(bf16[4,512,768]{2,1,0:T(8,128)(2,1)S(1)} %get-tuple-element.47) | copy-start | bytes 9437188
  122.2 2.6 collective-permute-start
  187.8 25.0 %collective-permute-start.2 = (bf16[1024,384]{1,0:T(8,128)(2,1)}, bf16[1024,384]{1,0:T(8,128)(2,1)S(1)}, u32[]{:S(2)}, u32[]{:S(2)}) collective-permute-start(bf16[1024,384]{1,0:T(8,128)(2,1)} %get-tuple-element.55), channel_id=1, source_target_pairs={{0,1},{1,0},{2,3},{3,2},{4,5},{5,4},{6,7},{7,6},{8,9},{9,8},{10,11... | collective-permute-start | bytes 2359304 | tf_op jit(solution)/shard_map/ppermute | solution.py:1235
  189.8 82.0 %collective-permute-start.6 = (bf16[4,384,384]{2,1,0:T(8,128)(2,1)}, bf16[4,384,384]{2,1,0:T(8,128)(2,1)}, u32[]{:S(2)}, u32[]{:S(2)}) collective-permute-start(bf16[4,384,384]{2,1,0:T(8,128)(2,1)} %get-tuple-element.68), channel_id=1, source_target_pairs={{0,4},{4,0},{1,5},{5,1},{2,6},{6,2},{3,7},{7,3},{8,12},{12,8},{9,1... | collective-permute-start | bytes 3538952 | tf_op jit(solution)/shard_map/ppermute | solution.py:1231
  189.8 82.0 %collective-permute-start.3 = (bf16[2,96,1536]{2,1,0:T(8,128)(2,1)}, bf16[2,96,1536]{2,1,0:T(8,128)(2,1)}, u32[]{:S(2)}, u32[]{:S(2)}) collective-permute-start(bf16[2,96,1536]{2,1,0:T(8,128)(2,1)} %get-tuple-element.64), channel_id=1, source_target_pairs={{0,8},{8,16},{16,24},{24,0},{1,9},{9,17},{17,25},{25,1},{2,10},{10... | collective-permute-start | bytes 1769480 | tf_op jit(solution)/shard_map/ppermute | solution.py:1231
  208.0 63.8 %collective-permute-start.4 = (bf16[2,96,1536]{2,1,0:T(8,128)(2,1)}, bf16[2,96,1536]{2,1,0:T(8,128)(2,1)}, u32[]{:S(2)}, u32[]{:S(2)}) collective-permute-start(bf16[2,96,1536]{2,1,0:T(8,128)(2,1)} %get-tuple-element.65), channel_id=1, source_target_pairs={{0,16},{8,24},{16,0},{24,8},{1,17},{9,25},{17,1},{25,9},{2,18},{10... | collective-permute-start | bytes 1769480 | tf_op jit(solution)/shard_map/ppermute | solution.py:1231
  208.0 63.8 %collective-permute-start.5 = (bf16[2,96,1536]{2,1,0:T(8,128)(2,1)}, bf16[2,96,1536]{2,1,0:T(8,128)(2,1)}, u32[]{:S(2)}, u32[]{:S(2)}) collective-permute-start(bf16[2,96,1536]{2,1,0:T(8,128)(2,1)} %get-tuple-element.66), channel_id=1, source_target_pairs={{0,24},{8,0},{16,8},{24,16},{1,25},{9,1},{17,9},{25,17},{2,26},{10... | collective-permute-start | bytes 1769480 | tf_op jit(solution)/shard_map/ppermute | solution.py:1231
  212.9 57.5 %collective-permute-start.1 = (bf16[512,768]{1,0:T(8,128)(2,1)S(1)}, bf16[512,768]{1,0:T(8,128)(2,1)S(1)}, u32[]{:S(2)}, u32[]{:S(2)}) collective-permute-start(bf16[512,768]{1,0:T(8,128)(2,1)S(1)} %get-tuple-element.94), channel_id=1, source_target_pairs={{0,2},{2,0},{1,3},{3,1},{4,6},{6,4},{5,7},{7,5},{8,10},{10,8},{9,1... | collective-permute-start | bytes 2359304 | tf_op jit(solution)/shard_map/ppermute | solution.py:1235
  338.5 3.8 %copy-start.24 = (f32[96,768]{1,0:T(8,128)S(1)}, f32[96,768]{1,0:T(8,128)}, u32[]{:S(2)}) copy-start(f32[96,768]{1,0:T(8,128)} %get-tuple-element.122) | copy-start | bytes 884740
  338.5 4.6 %copy-start.23 = (f32[96,768]{1,0:T(8,128)S(1)}, f32[96,768]{1,0:T(8,128)}, u32[]{:S(2)}) copy-start(f32[96,768]{1,0:T(8,128)} %get-tuple-element.123) | copy-start | bytes 884740
  338.5 5.3 %copy-start.22 = (f32[96,768]{1,0:T(8,128)S(1)}, f32[96,768]{1,0:T(8,128)}, u32[]{:S(2)}) copy-start(f32[96,768]{1,0:T(8,128)} %get-tuple-element.124) | copy-start | bytes 884740
  342.3 2.2 copy-start.21
  342.3 2.9 copy-start.20
  344.5 1.7 copy-start.19
  345.2 2.0 copy-start.1
  (12 other events, 13.4 us)
Sparse Core Ops, SparseCore 0:
  11.8 109.5 all-gather.1

commit v4 on v3

--- a/solution.py
+++ b/solution.py
@@ -80,9 +80,8 @@
         mark_key[rows, :] = jnp.where(apart, BIG, 0.0).astype(jnp.bfloat16)
 
 
-def forward_kernel(
-    place_ref, segment_ref, qkv_ref, row_ref, mine_ref, other_ref, lse_ref, q2, k2, vt, acc, top, tot, keep, mark_query, mark_key, bound_ref
-):
+def forward_kernel(place_ref, segment_ref, row_ref, tokens_ref, weights_ref, bias_ref, *refs):
+    mine_ref, other_ref, lse_ref, qkv_ref, q2, k2, vt, acc, top, tot, keep, mark_query, mark_key, bound_ref = refs
     length = qkv_ref.shape[0]
     blocks = length // BLK
     part = length // 4
@@ -96,15 +95,23 @@
     for b in range(4):
         src = part_rows(place_ref, b, part)
         dst = slice(b * part, (b + 1) * part)
-        k, nohk = qkv_ref[src, 128:256], mark_key[dst, :]
-        turned = qkv_ref[src, 0:128].T
+        made = dot_nn(tokens_ref[src, :], weights_ref[...])
+        lanes = pl.ds(pl.multiple_of(place_ref[4] * (128 * pl.num_programs(0)) + pl.program_id(0) * 128, 128), 128)
+        q = ((made[:, 0:128] + bias_ref[0:1, lanes]) * 0.125).astype(jnp.bfloat16)
+        k = made[:, 128:256].astype(jnp.bfloat16)
+        v = (made[:, 256:384] + bias_ref[1:2, lanes]).astype(jnp.bfloat16)
+        qkv_ref[src, 0:128] = q
+        qkv_ref[src, 128:256] = k
+        qkv_ref[src, 256:384] = v
+        nohk = mark_key[dst, :]
+        turned = q.T
         q2[0, 0:64, dst] = turned[0:64]
         q2[0, 64:128, dst] = mark_query[64:128, dst]
         q2[1, 0:64, dst] = mark_query[0:64, dst]
         q2[1, 64:128, dst] = turned[64:128]
         k2[0, dst, :] = jnp.where(low, k, nohk)
         k2[1, dst, :] = jnp.where(low, nohk, k)
-        vt[:, dst] = qkv_ref[src, 256:384].T
+        vt[:, dst] = v.T
     lse_ref[...] = jnp.zeros_like(lse_ref)
 
     def row(qb, _):
@@ -160,8 +167,9 @@
     lax.fori_loop(0, blocks, row, 0)
 
 
-def attention(place, segments, qkv):
-    length, width = qkv.shape
+def attention(place, segments, tokens, weights, biases):
+    length, depth = tokens.shape
+    width = weights.shape[1]
     pairs = width // 384
     rows = length // 2
     return pl.pallas_call(
@@ -170,18 +178,22 @@
             jax.ShapeDtypeStruct((rows, pairs * 128), jnp.bfloat16),
             jax.ShapeDtypeStruct((rows, pairs * 128), jnp.bfloat16),
             jax.ShapeDtypeStruct((pairs * 8, length), jnp.float32),
+            jax.ShapeDtypeStruct((length, width), jnp.bfloat16),
         ),
         grid_spec=pltpu.PrefetchScalarGridSpec(
             num_scalar_prefetch=2,
             grid=(pairs,),
             in_specs=[
-                pl.BlockSpec((length, 384), lambda p, *_: (0, p)),
                 pl.BlockSpec((1, length), lambda p, *_: (0, 0)),
+                pl.BlockSpec((length, depth), lambda p, *_: (0, 0)),
+                pl.BlockSpec((depth, 384), lambda p, *_: (0, p)),
+                pl.BlockSpec(biases.shape, lambda p, *_: (0, 0)),
             ],
             out_specs=[
                 pl.BlockSpec((rows, 128), lambda p, *_: (0, p)),
                 pl.BlockSpec((rows, 128), lambda p, *_: (0, p)),
                 pl.BlockSpec((8, length), lambda p, *_: (p, 0)),
+                pl.BlockSpec((length, 384), lambda p, *_: (0, p)),
             ],
             scratch_shapes=[
                 pltpu.VMEM((2, 128, length), jnp.bfloat16),
@@ -199,7 +211,7 @@
         compiler_params=pltpu.CompilerParams(dimension_semantics=("arbitrary",), vmem_limit_bytes=60 << 20),
         cost_estimate=pl.CostEstimate(flops=pairs * 8_000_000_000, bytes_accessed=pairs * 3_000_000, transcendentals=pairs * 4_000_000),
         name="attention_forward",
-    )(place, segments, qkv, segments.reshape(1, length))
+    )(place, segments, segments.reshape(1, length), tokens, weights, biases)
 
 
 def backward_kernel(
@@ -374,6 +386,7 @@
 
 
 MESH_ID = pl.DeviceIdType.MESH
+WIDE = 5
 
 
 def place_of():
@@ -411,9 +424,11 @@
 def entry_kernel(size_z, size_x, count, *refs):
     tokens, cotangent, wq, wk, wv = refs[:5]
     vectors = refs[5 : 5 + count]
-    tokens_all, cotangent_all, weights_all, vectors_all = refs[5 + count : 9 + count]
-    raw = refs[9 + count : 9 + 2 * count]
-    stage, cot_stage, wbuf, pack, vpack, local_sem, load_sem, tsend, trecv, zsend, zrecv, xsend, xrecv = refs[9 + 2 * count :]
+    tokens_all, cotangent_all, weights_all, rows_out, inner_out = refs[5 + count : 10 + count]
+    raw = refs[10 + count : 10 + 2 * count]
+    stage, cot_stage, wbuf, pack, vpack, vectors_all, local_sem, load_sem, tsend, trecv, zsend, zrecv, xsend, xrecv = refs[
+        10 + 2 * count :
+    ]
     z, x, y, core = place_of()
     half = pack.shape[1] // 3
     pairs = half // 128
@@ -467,9 +482,8 @@
         second.start()
     beside.start()
     keep_weights = pltpu.make_async_copy(pack, weights_all.at[me], local_sem.at[1])
-    keep_vectors = pltpu.make_async_copy(vpack, vectors_all.at[me], local_sem.at[2])
     keep_weights.start()
-    keep_vectors.start()
+    vectors_all[me] = vpack[...]
     load.wait()
     keep_tokens = pltpu.make_async_copy(stage, tokens_all.at[0], local_sem.at[3])
     keep_tokens.start()
@@ -494,12 +508,16 @@
     for first, second in along:
         first.wait_send()
         second.wait_send()
+    short = min(vector.shape[1] for vector in raw)
+    longest = vpack.shape[1]
+    for s in range(size_z * size_x):
+        rows_out[:, s * short : (s + 1) * short] = vectors_all[s, :, 0:short]
+        inner_out[:, s * longest : (s + 1) * longest] = vectors_all[s, WIDE : WIDE + 1, :]
     across.wait_send()
     beside.wait()
     onward.wait()
     later.wait()
     keep_weights.wait()
-    keep_vectors.wait()
     keep_tokens.wait()
     keep_cot.wait()
 
@@ -518,10 +536,11 @@
             jax.ShapeDtypeStruct((4, part, width), tokens.dtype),
             jax.ShapeDtypeStruct((2, part, width), cotangent.dtype),
             jax.ShapeDtypeStruct((shards, rows, lanes), jnp.bfloat16),
-            jax.ShapeDtypeStruct((shards, 16, longest), jnp.float32),
+            jax.ShapeDtypeStruct((16, width), jnp.float32),
+            jax.ShapeDtypeStruct((1, shards * longest), jnp.float32),
         ),
         in_specs=[anywhere] * (5 + len(vectors)),
-        out_specs=(anywhere,) * 4,
+        out_specs=(anywhere,) * 3 + (pl.BlockSpec(memory_space=pltpu.VMEM),) * 2,
         scratch_shapes=[pltpu.VMEM((1, v.shape[0]), v.dtype) for v in vectors]
         + [
             pltpu.VMEM((part, width), tokens.dtype),
@@ -529,6 +548,7 @@
             pltpu.VMEM((3, rows, lanes // 3), wq.dtype),
             pltpu.VMEM((rows, lanes), jnp.bfloat16),
             pltpu.VMEM((16, longest), jnp.float32),
+            pltpu.VMEM((shards, 16, longest), jnp.float32),
             dma((6,)),
             dma((3 + len(vectors),)),
             dma((4,)),
@@ -538,7 +558,7 @@
             dma((2, size_z, max(size_x - 1, 1))),
             dma((2, size_z, max(size_x - 1, 1))),
         ],
-        compiler_params=pltpu.CompilerParams(collective_id=0, has_side_effects=True, vmem_limit_bytes=20 << 20),
+        compiler_params=pltpu.CompilerParams(collective_id=0, has_side_effects=True, vmem_limit_bytes=66_000_000),
         name="entry",
     )(tokens, cotangent, wq, wk, wv, *[v.reshape(1, -1) for v in vectors])
 
@@ -546,15 +566,18 @@
 def exit_kernel(size_z, size_x, shapes, *refs):
     z, x, y, core = place_of()
     names = list(shapes)
-    grads_hbm, inputs_hbm, weights_hbm, base_hbm, output_term, vector_terms = refs[:6]
-    inner_in = refs[6 : 6 + size_z]
-    outer_in = refs[6 + size_z : 6 + size_z + size_x]
-    refs = refs[6 + size_z + size_x :]
-    token_grads, grad_query, grad_key, grad_value, grad_output, grad_inner, grad_outer, vector_sums = refs[:8]
-    grads, inputs, turned, weights, base, terms, other_rows, recv_rows, send_rows, far_rows, odd = refs[8:19]
-    inner_buf, outer_buf = refs[19:21]
-    load_sem, tsend, trecv, osend, orecv = refs[21:26]
-    refs = refs[26:]
+    grads_hbm, inputs_hbm, weights_hbm, base_hbm, output_term, dense_sums, inner_sums, head_sums = refs[:8]
+    inner_in = refs[8 : 8 + size_z]
+    outer_in = refs[8 + size_z : 8 + size_z + size_x]
+    refs = refs[8 + size_z + size_x :]
+    results = refs[:8]
+    token_grads, grad_query, grad_key, grad_value, grad_output, grad_inner, grad_outer, vector_sums = refs[8:16]
+    grads, inputs, turned, weights, base, terms, other_rows, recv_rows, send_rows, far_rows, odd = refs[16:27]
+    inner_buf, outer_buf, vector_rows, vector_terms, store_sem = refs[27:32]
+    load_sem, tsend, trecv, osend, orecv = refs[32:37]
+    refs = refs[37:]
+    made = (token_grads, grad_query, grad_key, grad_value, grad_output, grad_inner, grad_outer, vector_sums)
+    stores = [pltpu.make_async_copy(a, b, store_sem.at[i]) for i, (a, b) in enumerate(zip(made, results))]
     xin, xsend, xrecv, xout = {}, {}, {}, {}
     zout, zin, zsend, zrecv = {}, {}, {}, {}
     ybuf, ysend, yrecv, cbuf, csend, crecv = {}, {}, {}, {}, {}, {}
@@ -620,6 +643,19 @@
         move.start()
         along[name, k] = move
 
+    vector_rows[...] = jnp.zeros_like(vector_rows)
+    for i, row in enumerate((7, 8, 6, 3, 4, 2)):
+        vector_rows[row : row + 1, :] = jnp.sum(dense_sums[8 * i : 8 * i + 8, :], axis=0, keepdims=True)
+    for p in range(pairs):
+        place = pl.ds(pl.multiple_of(core * half + p * 128, 128), 128)
+        vector_rows[0:1, place] = head_sums[8 * p : 8 * p + 1, 0:128]
+        vector_rows[1:2, place] = head_sums[8 * p : 8 * p + 1, 256:384]
+    inner_row = jnp.sum(inner_sums[...], axis=0, keepdims=True)
+    vector_terms[...] = jnp.zeros_like(vector_terms)
+    longest = vector_terms.shape[2]
+    for s in range(shards):
+        vector_terms[s, :, 0:rows] = vector_rows[:, s * rows : (s + 1) * rows]
+        vector_terms[s, WIDE : WIDE + 1, :] = inner_row[:, s * longest : (s + 1) * longest]
     for k in order:
         for j in range(1, size_x):
             send_x("vec", 0, k, j, vector_terms.at[slot_of(k, j)], xin["vec"].at[j - 1, k])
@@ -761,6 +797,7 @@
     finish_z("out")
     back.wait()
     token_grads[1 - y] = far_rows[...].astype(high)
+    stores[0].start()
     step_core("vec")
 
     def finish_core(name):
@@ -774,14 +811,17 @@
         for c in range(chunks):
             place = pl.ds(pl.multiple_of(c * CHUNK + owner * half, 128), half)
             grad_inner[:, place] = buf[i, :, c * half : (c + 1) * half]
+    stores[5].start()
     buf = finish_core("outer")
     for i in range(2):
         owner = core if i == 0 else 1 - core
         grad_outer[:, pl.ds(pl.multiple_of(owner * half, 128), half)] = buf[i]
+    stores[6].start()
     step_core("qkv")
     step_core("out")
     buf = finish_core("vec")
     vector_sums[...] = buf[0] + buf[1]
+    stores[7].start()
     buf = finish_core("qkv")
     for i in range(2):
         owner = core if i == 0 else 1 - core
@@ -789,13 +829,44 @@
             place = pl.ds(pl.multiple_of(owner * half + p * 128, 128), 128)
             for n, out in enumerate((grad_query, grad_key, grad_value)):
                 out[:, place] = buf[i, :, (3 * p + n) * 128 : (3 * p + n + 1) * 128]
+    for i in (1, 2, 3):
+        stores[i].start()
     buf = finish_core("out")
     for i in range(2):
         owner = core if i == 0 else 1 - core
         grad_output[:, pl.ds(pl.multiple_of(owner * half, 128), half)] = buf[i]
-
-
-def exit_call(size_z, size_x, grads, inputs, weights, base, output_term, vector_terms, inner_terms, outer_terms):
+    stores[4].start()
+    for store in stores:
+        store.wait()
+
+
+def deliver_kernel(count, *refs):
+    sources, vectors, outs, sem = refs[:count], refs[count], refs[count + 1 : -1], refs[-1]
+    copies = [pltpu.make_async_copy(src, dst, sem.at[i]) for i, (src, dst) in enumerate(zip(sources, outs))]
+    for copy in copies:
+        copy.start()
+    for i, out in enumerate(outs[count:]):
+        out[...] = vectors[i : i + 1, 0 : out.shape[1]]
+    for copy in copies:
+        copy.wait()
+
+
+def deliver(matrices, vectors, sizes):
+    count = len(matrices)
+    vmem, anywhere = pl.BlockSpec(memory_space=pltpu.VMEM), pl.BlockSpec(memory_space=pl.ANY)
+    return pl.pallas_call(
+        lambda *refs: deliver_kernel(count, *refs),
+        out_shape=tuple(jax.ShapeDtypeStruct(m.shape, m.dtype) for m in matrices)
+        + tuple(jax.ShapeDtypeStruct((1, size), jnp.float32) for size in sizes),
+        in_specs=[vmem] * (count + 1),
+        out_specs=(anywhere,) * count + (vmem,) * len(sizes),
+        scratch_shapes=[pltpu.SemaphoreType.DMA((count,))],
+        compiler_params=pltpu.CompilerParams(vmem_limit_bytes=60_000_000),
+        name="deliver",
+    )(*matrices, vectors)
+
+
+def exit_call(size_z, size_x, grads, inputs, weights, base, output_term, dense_sums, inner_sums, head_sums, inner_terms, outer_terms):
     shards, rows, width = output_term.shape
     lanes = grads.shape[1]
     half = width // 2
@@ -809,14 +880,26 @@
     dma = pltpu.SemaphoreType.DMA
     side = size_x - 1
     low, high = jnp.bfloat16, jnp.float32
+    vector_shape = (16, hidden // shards)
     shapes = {
-        "vec": (vector_terms.shape[1:], high, 1),
+        "vec": (vector_shape, high, 1),
         "qkv": ((rows, lanes), low, pairs),
         "out": ((rows, half), low, 1),
         "inner": ((rows, hidden // 2), low, 1),
         "outer": ((long, half), low, 1),
     }
-    scratch = [
+    matrix = jax.ShapeDtypeStruct((rows, width), high)
+    results = (
+        jax.ShapeDtypeStruct((2, part, width), high),
+        matrix,
+        matrix,
+        matrix,
+        matrix,
+        jax.ShapeDtypeStruct((rows, hidden), high),
+        jax.ShapeDtypeStruct((long, width), high),
+        jax.ShapeDtypeStruct(vector_shape, high),
+    )
+    scratch = [pltpu.VMEM(r.shape, r.dtype) for r in results] + [
         pltpu.VMEM((length, lanes), low),
         pltpu.VMEM((length, width), low),
         pltpu.VMEM((width, length), low),
@@ -830,6 +913,9 @@
         pltpu.VMEM((shards, rows, half), low),
         pltpu.VMEM((size_z,) + inner_terms[0].shape, low),
         pltpu.VMEM((size_x,) + outer_terms[0].shape, low),
+        pltpu.VMEM((16, width), high),
+        pltpu.VMEM((shards,) + vector_shape, high),
+        dma((len(results),)),
         dma((size_z + size_x + 4,)),
         dma((2,)),
         dma((2,)),
@@ -844,25 +930,15 @@
         if name != "inner":
             scratch += [pltpu.VMEM((size_z - 1,) + shape, kind)] * 2 + [dma((size_z - 1,))] * 2
     scratch.append(pltpu.VMEM((side, rows, hidden // 2), low))
-    matrix = jax.ShapeDtypeStruct((rows, width), high)
     return pl.pallas_call(
         lambda *refs: exit_kernel(size_z, size_x, shapes, *refs),
-        out_shape=(
-            jax.ShapeDtypeStruct((2, part, width), high),
-            matrix,
-            matrix,
-            matrix,
-            matrix,
-            jax.ShapeDtypeStruct((rows, hidden), high),
-            jax.ShapeDtypeStruct((long, width), high),
-            jax.ShapeDtypeStruct(vector_terms.shape[1:], high),
-        ),
-        in_specs=[anywhere] * 4 + [vmem] * 2 + [anywhere] * (size_z + size_x),
-        out_specs=(vmem,) * 8,
+        out_shape=results,
+        in_specs=[anywhere] * 4 + [vmem] * 4 + [anywhere] * (size_z + size_x),
+        out_specs=(anywhere,) * len(results),
         scratch_shapes=scratch,
         compiler_params=pltpu.CompilerParams(collective_id=1, has_side_effects=True, vmem_limit_bytes=67_000_000),
         name="exit",
-    )(grads, inputs, weights, base, output_term, vector_terms, *inner_terms, *outer_terms)
+    )(grads, inputs, weights, base, output_term, dense_sums, inner_sums, head_sums, *inner_terms, *outer_terms)
 
 
 TILE = 256
@@ -954,7 +1030,8 @@
         inner_sum_ref[...] = jnp.zeros_like(inner_sum_ref)
 
     def vector(i):
-        return vectors_ref[i : i + 1, :]
+        row = (2, 3, 4, 6, 7, 8)[i]
+        return vectors_ref[row : row + 1, :]
 
     def add_sum(i, value):
         sums_ref[8 * i : 8 * i + 8, :] += column_sum(value)
@@ -1125,7 +1202,7 @@
                 half_tile,
                 half_tile,
                 tile,
-                whole((8, width)),
+                whole((16, width)),
                 whole((1, hidden)),
                 anywhere,
             ],
@@ -1342,16 +1419,11 @@
     bias_query, bias_value, bias_output, gain_first, shift_first, bias_inner, bias_outer, gain_second, shift_second = [
         widen(v) for v in gathered
     ]
-    heads_query = lax.dynamic_slice_in_dim(bias_query, core * half, half).reshape(pairs, 1, 128)
-    heads_value = lax.dynamic_slice_in_dim(bias_value, core * half, half).reshape(pairs, 1, 128)
-    bias_all = jnp.concatenate([heads_query, jnp.zeros_like(heads_query), heads_value], axis=1).reshape(lanes)
-    scale = jnp.tile(jnp.concatenate([jnp.full((128,), HD ** (-0.5)), jnp.ones((256,))]), pairs)
-    projected = lowered((matmul(inputs_all, full_early) + bias_all) * scale)
-
     spot = jnp.arange(5, dtype=jnp.int32)
     place = jnp.where(spot < 4, ((spot % 2 != core) * 2 + (spot // 2 != y) * 1) * part, core)
     segments = pick(segment_ids, y)
-    heads_mine, heads_other, logsum = attention(place, segments, projected)
+    biases = jnp.concatenate([bias_query[None], bias_value[None], jnp.zeros((14, width), jnp.float32)], axis=0)
+    heads_mine, heads_other, logsum, projected = attention(place, segments, inputs_all, full_early, biases)
     context = in_order(core == 0, heads_mine, swap(heads_other, "core"), 1)
 
     attended = matmul(context, full_output) + bias_output
@@ -1531,24 +1603,13 @@
 
     vectors = (b_query, b_value, b_output, first_gain, first_shift, b_inner, b_outer, second_gain, second_shift)
     sizes = [v.shape[0] for v in vectors]
-    tokens_all, cotangent_all, early, vectors_all = entry(size_z, size_x, tokens, cotangent, w_query, w_key, w_value, vectors)
+    tokens_all, cotangent_all, early, rows, inner_row = entry(size_z, size_x, tokens, cotangent, w_query, w_key, w_value, vectors)
     inputs_all = tokens_all.reshape(4 * part, width)
     full_early = early.reshape(width, lanes)
-    bias_query, bias_value, bias_output, gain_first, shift_first, bias_inner, bias_outer, gain_second, shift_second = [
-        vectors_all[:, i, :size].reshape(shards * size) for i, size in enumerate(sizes)
-    ]
-    heads_query = lax.dynamic_slice_in_dim(bias_query, core * half, half).reshape(pairs, 1, 128)
-    heads_value = lax.dynamic_slice_in_dim(bias_value, core * half, half).reshape(pairs, 1, 128)
-    bias_all = jnp.concatenate([heads_query, jnp.zeros_like(heads_query), heads_value], axis=1).reshape(lanes)
-    scale = jnp.tile(jnp.concatenate([jnp.full((128,), HD ** (-0.5)), jnp.ones((256,))]), pairs)
-    projected = lowered((matmul(inputs_all, full_early) + bias_all) * scale)
-
     spot = jnp.arange(5, dtype=jnp.int32)
     place = jnp.where(spot < 4, ((spot % 2 != core) * 2 + (spot // 2 != y) * 1) * part, core)
     segments = pick(segment_ids, y)
-    context_mine, context_other, logsum = attention(place, segments, projected)
-    norms = jnp.stack([bias_output, gain_first, shift_first, bias_outer, gain_second, shift_second])
-    norms = jnp.concatenate([norms, jnp.zeros((2, width), jnp.float32)], axis=0)
+    context_mine, context_other, logsum, projected = attention(place, segments, inputs_all, full_early, rows)
     made = dense_layer(
         size_z,
         size_x,
@@ -1556,42 +1617,18 @@
         context_mine,
         swap(context_other, "core"),
         cotangent_all.reshape(local, width),
-        norms,
-        bias_inner.reshape(1, hidden),
+        rows,
+        inner_row,
         dense,
     )
     mixed, pre_first, upstream_mine, upstream_send, dense_sums, inner_sums, grad_w_output = made[:7]
     inner_terms = [made[7]] + [shift(made[7 + k], "z", k) for k in range(1, size_z)]
     outer_terms = [made[7 + size_z]] + [shift(made[7 + size_z + j], "x", j) for j in range(1, size_x)]
     upstream_other = swap(upstream_send, "core")
-    dense_sums = jnp.sum(dense_sums.reshape(6, 8, width), axis=1)
-    grad_second_gain, grad_second_shift, grad_b_outer, grad_first_gain, grad_first_shift, grad_b_output = [
-        dense_sums[i] for i in range(6)
-    ]
-    grad_b_inner = jnp.sum(inner_sums, axis=0)
     mixed_out = in_order(y == 0, mixed[None, :part], swap(mixed[part:], "y")[None], 0)
 
     grads, sums = attention_back(place, segments, projected, context_mine, context_other, upstream_mine, upstream_other, logsum)
-    sums = sums.reshape(pairs, 8, 3, 128)[:, 0]
-    blank = jnp.zeros((width,), jnp.float32)
-    grad_b_query = lax.dynamic_update_slice(blank, sums[:, 0].reshape(half), (core * half,))
-    grad_b_value = lax.dynamic_update_slice(blank, sums[:, 2].reshape(half), (core * half,))
-    vector_grads = (
-        grad_b_query,
-        grad_b_value,
-        grad_b_output,
-        grad_first_gain,
-        grad_first_shift,
-        grad_b_inner,
-        grad_b_outer,
-        grad_second_gain,
-        grad_second_shift,
-    )
-    longest = vectors_all.shape[2]
-    rows = [jnp.pad(v.reshape(shards, 1, -1), ((0, 0), (0, 0), (0, longest - v.shape[0] // shards))) for v in vector_grads]
-    rows.append(jnp.zeros((shards, vectors_all.shape[1] - len(rows), longest), jnp.float32))
-    vector_terms = jnp.concatenate(rows, axis=1)
-    grad_tokens, grad_query, grad_key, grad_value, grad_output, grad_inner_full, grad_outer_full, vector_sums = exit_call(
+    made = exit_call(
         size_z,
         size_x,
         grads,
@@ -1599,11 +1636,16 @@
         full_early,
         pre_first,
         grad_w_output.reshape(shards, own_rows, width),
-        vector_terms,
+        dense_sums,
+        inner_sums,
+        sums,
         inner_terms,
         outer_terms,
     )
-    done = [vector_sums[i, :size] for i, size in enumerate(sizes)]
+    grad_tokens, grad_query, grad_key, grad_value, grad_output, grad_inner_full, grad_outer_full, *done = deliver(
+        made[:7], made[7], sizes
+    )
+    done = [v.reshape(size) for v, size in zip(done, sizes)]
     return (
         mixed_out,
         grad_tokens,
@@ -1611,17 +1653,11 @@
         grad_key,
         grad_value,
         grad_output,
-        done[0],
-        done[1],
-        done[2],
-        done[3],
-        done[4],
+        *done[:5],
         grad_inner_full,
         done[5],
         grad_outer_full,
-        done[6],
-        done[7],
-        done[8],
+        *done[6:],
     )
 
 

time: 353 us -> 331 us (0.938)
  local copies, waits for them, and re-layouts: 32 us -> 6.16 us
  waiting for transfers between devices: 0.04 us -> 13.1 us
  matrix products: 7.89 us -> 0 us
  starting transfers between devices: 21.1 us -> 15.7 us
    unnamed x65 -> x9, local copies, waits for them, and re-layouts: 17.4 us -> 0.14 us
    all_gather x1, waiting for transfers between devices: 0.01 us -> 10.4 us  [body(): lax.all_gather(jnp.concatenate(pieces, axis=1), everyone, axis=0, tiled=T...]
    pallas_call x1, Pallas kernels: 53.9 us -> 43.5 us  [attention_back(): pl.pallas_call(backward_kernel, out_shape=(jax.ShapeDtypeStruct((length,...]
    pallas_call x1, Pallas kernels: 63.9 us -> 72.1 us  [exit_call(): pl.pallas_call(lambda *refs: exit_kernel(size_z, size_x, shapes, *refs),...]
    dot_general x1 -> x0, matrix products: 7.89 us -> none  [matmul(): return jnp.dot(left, right, preferred_element_type=jnp.float32)]
    pallas_call x0 -> x1, Pallas kernels: none -> 6.41 us  [deliver(): pl.pallas_call(lambda *refs: deliver_kernel(count, *refs), out_shape=tupl...]
    ppermute x4, starting transfers between devices: 20.6 us -> 15.3 us  [shift(): lax.ppermute(piece, axis, [(i, (i + step) % size) for i in range(size)])]
    slice x6 -> x0, local copies, waits for them, and re-layouts: 3.74 us -> none  [the longest x2 1.6 us: body(): vectors_all[:, i, :size].reshape(shards * size)]
  transfers between devices with their start and end apart: 8 -> 8, of which waited for: 0 -> 2; matrix products, arithmetic and copies ran while one was open for 6% -> 1% of each run, Pallas kernels for 41% -> 41%
where the time goes in v4:
time: 331 us; the launch traced here: 330 us
  Pallas kernels  277 us (84%)
  starting transfers between devices  15.7 us (5%)
  between operations  14.2 us (4%)
  waiting for transfers between devices  13.1 us (4%)
  local copies, waits for them, and re-layouts  6.16 us (2%)
  other arithmetic  4.06 us (1%)
    pallas_call x1, Pallas kernels, exit_call(): pl.pallas_call(lambda *refs: exit_kernel(size_z, size_x, shapes, *refs),...  72.1 us
    pallas_call x1, Pallas kernels, dense_layer(): pl.pallas_call(lambda *refs: dense_kernel(size_z, size_x, *refs), out_sha...  62.9 us
    pallas_call x1, Pallas kernels, entry(): pl.pallas_call(lambda *refs: entry_kernel(size_z, size_x, len(vectors), *...  51.5 us
    pallas_call x1, Pallas kernels, attention_back(): pl.pallas_call(backward_kernel, out_shape=(jax.ShapeDtypeStruct((length,...  43.5 us
    pallas_call x1, Pallas kernels, attention(): pl.pallas_call(forward_kernel, out_shape=(jax.ShapeDtypeStruct((rows, pai...  40.2 us
    ppermute x4, starting transfers between devices, shift(): lax.ppermute(piece, axis, [(i, (i + step) % size) for i in range(size)])  15.3 us
    all_gather x1, waiting for transfers between devices, body(): lax.all_gather(jnp.concatenate(pieces, axis=1), everyone, axis=0, tiled=T...  10.4 us
  transfers between devices with their start and end apart: 8, of which 2 were waited for; matrix products, arithmetic and copies ran while one was open for 1% of the time, Pallas kernels for 41%

profile of v4, /device:TPU:0, one launch (start us, length us, event | category | flops | bytes accessed | tf_op | source)
XLA Modules:
  0.0 329.9 jit_solution(10928108287375333244)
XLA Ops:
  7.3 0.9 dynamic-slice_convert_fusion.2
  8.2 1.1 dynamic-slice_convert_fusion.1
  9.3 1.1 dynamic-slice_convert_fusion
  10.4 0.2 copy.35
  10.6 0.9 pad_maximum_fusion
  11.5 0.6 reshape.113.refs_10_
  12.1 51.5 %entry.1 = (bf16[4,512,768]{2,1,0:T(8,128)(2,1)}, bf16[2,512,768]{2,1,0:T(8,128)(2,1)}, bf16[8,96,1152]{2,1,0:T(8,128)(2,1)}, f32[16,768]{1,0:T(8,128)}, f32[1,3072]{1,0:T(1,128)}) custom-call(bf16[2,512,768]{2,1,0:T(8,128)(2,1)} %refs_0_.1, bf16[2,512,768]{2,1,0:T(8,128)(2,1)} %refs_1_.1, f32[96,768]{1,0:T(8,128)} %refs_2_.1, f32[96,768]{1,0:T(8,128)} %refs_3_.1, ...), custom_call_target="tpu_custom_call" | custom-call | tf_op jit(solution)/shard_map/entry/pallas_call | solution.py:533
  63.6 0.5 compare_select_fusion.1.place_ref
  64.1 0.6 constant_dynamic-slice_fusion.row_ref
  64.7 40.2 %attention_forward.1 = (bf16[1024,384]{1,0:T(8,128)(2,1)}, bf16[1024,384]{1,0:T(8,128)(2,1)}, f32[24,2048]{1,0:T(8,128)}, bf16[2048,1152]{1,0:T(8,128)(2,1)}) custom-call(s32[5]{0:T(128)} %compare_select_fusion.1.place_ref, s32[2048]{0:T(1024)} %bitcast.38, s32[1,2048]{1,0:T(1,128)} %constant_dynamic-slice_fusion.row_ref, bf16[2048,768]{1,0:T(8,128)(2,1)} %bitcast.28, ...), custom_call_target="tpu_custom_call" | custom-call | flops 24000000000 | bytes 9000000 | tf_op jit(solution)/shard_map/attention_forward/pallas_call | solution.py:175
  104.9 2.6 collective-permute-done.refs_2_
  107.5 10.4 %all-gather.2.cloned.1.call-done.refs_6_ = bf16[768,6912]{1,0:T(8,128)(2,1)} async-done(((bf16[48,6912]{1,0:T(8,128)(2,1)}), bf16[768,6912]{1,0:T(8,128)(2,1)}) %all-gather.2.cloned.1.call-update) | async-done | bytes 10616848 | tf_op jit(solution)/shard_map/all_gather | solution.py:1602
  117.9 62.9 %dense_layer.1 = (bf16[1024,768]{1,0:T(8,128)(2,1)}, f32[1024,768]{1,0:T(8,128)}, bf16[1024,384]{1,0:T(8,128)(2,1)}, bf16[1024,384]{1,0:T(8,128)(2,1)}, f32[48,7...) custom-call(bf16[2048,768]{1,0:T(8,128)(2,1)} %bitcast.29, ...), custom_call_target="tpu_custom_call" | custom-call | flops 32000000000 | bytes 40000000 | tf_op jit(solution)/shard_map/dense_layer/pallas_call | solution.py:1184
  180.9 0.3 collective-permute-start.2
  181.2 9.5 %collective-permute-start.3 = (bf16[2,96,1536]{2,1,0:T(8,128)(2,1)}, bf16[2,96,1536]{2,1,0:T(8,128)(2,1)}, u32[]{:S(2)}, u32[]{:S(2)}) collective-permute-start(bf16[2,96,1536]{2,1,0:T(8,128)(2,1)} %get-tuple-element.84), channel_id=1, source_target_pairs={{0,8},{8,16},{16,24},{24,0},{1,9},{9,17},{17,25},{25,1},{2,10},{10... | collective-permute-start | bytes 1769480 | tf_op jit(solution)/shard_map/ppermute | solution.py:1308
  190.7 2.4 collective-permute-start.5
  193.2 1.6 slice_bitcast_fusion
  194.8 0.1 copy-done.3
  194.9 3.4 %collective-permute-start.6 = (bf16[4,384,384]{2,1,0:T(8,128)(2,1)S(1)}, bf16[4,384,384]{2,1,0:T(8,128)(2,1)}, u32[]{:S(2)}, u32[]{:S(2)}) collective-permute-start(bf16[4,384,384]{2,1,0:T(8,128)(2,1)S(1)} %copy-done.3), channel_id=1, source_target_pairs={{0,4},{4,0},{1,5},{5,1},{2,6},{6,2},{3,7},{7,3},{8,12},{12,8},{9,1... | collective-permute-start | bytes 3538952 | tf_op jit(solution)/shard_map/ppermute | solution.py:1308
  198.3 43.5 %attention_backward.1 = (bf16[2048,1152]{1,0:T(8,128)(2,1)}, f32[24,384]{1,0:T(8,128)}) custom-call(s32[5]{0:T(128)} %compare_select_fusion.1.place_ref, s32[2048]{0:T(1024)} %bitcast.39, bf16[2048,1152]{1,0:T(8,128)(2,1)} %get-tuple-element.73.qkv_ref, bf16[1024,384]{1,0:T(8,128)(2,1)} %get-tuple-element.68.refs_1_.ctx_mine_ref, ...), custom_call_target="tpu_custom_call" | custom-call | flops 60000002048 | bytes 15000000 | tf_op jit(solution)/shard_map/attention_backward/pallas_call | solution.py:343
  241.8 1.4 maximum_select_fusion
  243.2 72.1 %exit.1 = (f32[2,512,768]{2,1,0:T(8,128)}, f32[96,768]{1,0:T(8,128)}, f32[96,768]{1,0:T(8,128)}, f32[96,768]{1,0:T(8,128)}, f32[96,768]{1,0:T(8,128)}, /*index=5...) custom-call(bf16[2048,1152]{1,0:T(8,128)(2,1)} %get-tuple-element.77.refs_0_, bf16[2048,768]{1,0:T(8,128)(2,1)} %bitcast.30, ...), custom_call_target="tpu_custom_call" | custom-call | tf_op jit(solution)/shard_map/exit/pallas_call | solution.py:933
  315.4 6.4 %deliver.1 = (f32[2,512,768]{2,1,0:T(8,128)}, f32[96,768]{1,0:T(8,128)}, f32[96,768]{1,0:T(8,128)}, f32[96,768]{1,0:T(8,128)}, f32[96,768]{1,0:T(8,128)}, /*inde...) custom-call(f32[2,512,768]{2,1,0:T(8,128)} %get-tuple-element.89.ref, ...), custom_call_target="tpu_custom_call" | custom-call | tf_op jit(solution)/shard_map/deliver/pallas_call | solution.py:857
  321.8 1.3 reduce
  (19 shorter events, 0.2 us)
Async XLA Ops:
  7.2 56.9 %copy-start = (s32[2,2048]{1,0:T(2,128)S(1)}, s32[2,2048]{1,0:T(2,128)}, u32[]{:S(2)}) copy-start(s32[2,2048]{1,0:T(2,128)} %param.19) | copy-start | bytes 49156
  7.2 110.7 %all-gather.2.cloned.1.call-start = ((), (), s32[]{:S(2)}) async-start(), calls=%async_computation | async-start | bytes 11280384 | tf_op jit(solution)/shard_map/all_gather | solution.py:1602
  10.4 1.1 copy-start.2
  104.9 2.6 collective-permute-start
  180.9 13.9 %collective-permute-start.2 = (bf16[1024,384]{1,0:T(8,128)(2,1)}, bf16[1024,384]{1,0:T(8,128)(2,1)}, u32[]{:S(2)}, u32[]{:S(2)}) collective-permute-start(bf16[1024,384]{1,0:T(8,128)(2,1)} %get-tuple-element.75), channel_id=1, source_target_pairs={{0,1},{1,0},{2,3},{3,2},{4,5},{5,4},{6,7},{7,6},{8,9},{9,8},{10,11... | collective-permute-start | bytes 2359304 | tf_op jit(solution)/shard_map/ppermute | solution.py:1312
  181.2 62.0 %collective-permute-start.3 = (bf16[2,96,1536]{2,1,0:T(8,128)(2,1)}, bf16[2,96,1536]{2,1,0:T(8,128)(2,1)}, u32[]{:S(2)}, u32[]{:S(2)}) collective-permute-start(bf16[2,96,1536]{2,1,0:T(8,128)(2,1)} %get-tuple-element.84), channel_id=1, source_target_pairs={{0,8},{8,16},{16,24},{24,0},{1,9},{9,17},{17,25},{25,1},{2,10},{10... | collective-permute-start | bytes 1769480 | tf_op jit(solution)/shard_map/ppermute | solution.py:1308
  190.7 52.5 %collective-permute-start.4 = (bf16[2,96,1536]{2,1,0:T(8,128)(2,1)}, bf16[2,96,1536]{2,1,0:T(8,128)(2,1)}, u32[]{:S(2)}, u32[]{:S(2)}) collective-permute-start(bf16[2,96,1536]{2,1,0:T(8,128)(2,1)} %get-tuple-element.85), channel_id=1, source_target_pairs={{0,16},{8,24},{16,0},{24,8},{1,17},{9,25},{17,1},{25,9},{2,18},{10... | collective-permute-start | bytes 1769480 | tf_op jit(solution)/shard_map/ppermute | solution.py:1308
  190.7 52.5 %collective-permute-start.5 = (bf16[2,96,1536]{2,1,0:T(8,128)(2,1)}, bf16[2,96,1536]{2,1,0:T(8,128)(2,1)}, u32[]{:S(2)}, u32[]{:S(2)}) collective-permute-start(bf16[2,96,1536]{2,1,0:T(8,128)(2,1)} %get-tuple-element.86), channel_id=1, source_target_pairs={{0,24},{8,0},{16,8},{24,16},{1,25},{9,1},{17,9},{25,17},{2,26},{10... | collective-permute-start | bytes 1769480 | tf_op jit(solution)/shard_map/ppermute | solution.py:1308
  193.1 1.7 copy-start.3
  194.7 47.1 %collective-permute-start.1 = (bf16[512,768]{1,0:T(8,128)(2,1)S(1)}, bf16[512,768]{1,0:T(8,128)(2,1)S(1)}, u32[]{:S(2)}, u32[]{:S(2)}) collective-permute-start(bf16[512,768]{1,0:T(8,128)(2,1)S(1)} %get-tuple-element.114), channel_id=1, source_target_pairs={{0,2},{2,0},{1,3},{3,1},{4,6},{6,4},{5,7},{7,5},{8,10},{10,8},{9,1... | collective-permute-start | bytes 2359304 | tf_op jit(solution)/shard_map/ppermute | solution.py:1312
  194.9 48.3 %collective-permute-start.6 = (bf16[4,384,384]{2,1,0:T(8,128)(2,1)S(1)}, bf16[4,384,384]{2,1,0:T(8,128)(2,1)}, u32[]{:S(2)}, u32[]{:S(2)}) collective-permute-start(bf16[4,384,384]{2,1,0:T(8,128)(2,1)S(1)} %copy-done.3), channel_id=1, source_target_pairs={{0,4},{4,0},{1,5},{5,1},{2,6},{6,2},{3,7},{7,3},{8,12},{12,8},{9,1... | collective-permute-start | bytes 3538952 | tf_op jit(solution)/shard_map/ppermute | solution.py:1308
  315.4 7.7 %copy-start.1 = (s32[2,2048]{1,0:T(2,128)S(1)}, s32[2,2048]{1,0:T(2,128)}, u32[]{:S(2)}) copy-start(s32[2,2048]{1,0:T(2,128)} %param.19) | copy-start | bytes 49156
Sparse Core Ops, SparseCore 0:
  11.6 106.2 all-gather.1

commit v5 on v4

--- a/solution.py
+++ b/solution.py
@@ -422,27 +422,36 @@
 
 
 def entry_kernel(size_z, size_x, count, *refs):
-    tokens, cotangent, wq, wk, wv = refs[:5]
-    vectors = refs[5 : 5 + count]
-    tokens_all, cotangent_all, weights_all, rows_out, inner_out = refs[5 + count : 10 + count]
-    raw = refs[10 + count : 10 + 2 * count]
-    stage, cot_stage, wbuf, pack, vpack, vectors_all, local_sem, load_sem, tsend, trecv, zsend, zrecv, xsend, xrecv = refs[
-        10 + 2 * count :
-    ]
+    tokens, cotangent, wq, wk, wv, w_inner, w_output, w_outer = refs[:8]
+    vectors = refs[8 : 8 + count]
+    tokens_all, cotangent_all, weights_all, inner_all, outer_all, rows_out, inner_out = refs[8 + count : 15 + count]
+    raw = refs[15 + count : 15 + 2 * count]
+    stage, cot_stage, wbuf, ibuf, obuf, pack, ipack, opack, vpack, vectors_all = refs[15 + 2 * count : 25 + 2 * count]
+    local_sem, load_sem, tsend, trecv, zsend, zrecv, xsend, xrecv, osend, orecv = refs[25 + 2 * count :]
     z, x, y, core = place_of()
     half = pack.shape[1] // 3
     pairs = half // 128
+    chunks = w_inner.shape[1] // CHUNK
     me = z * size_x + x
+    columns = [lax.rem(x + j, size_x) for j in range(size_x)]
 
     mine = pl.ds(pl.multiple_of(core * half, 128), half)
     loads = [pltpu.make_async_copy(w.at[:, mine], wbuf.at[i], load_sem.at[i]) for i, w in enumerate((wq, wk, wv))]
     loads += [pltpu.make_async_copy(v, r, load_sem.at[3 + i]) for i, (v, r) in enumerate(zip(vectors, raw))]
-    for load in loads:
-        load.start()
+    late = [
+        pltpu.make_async_copy(
+            w_inner.at[:, pl.ds(pl.multiple_of(c * CHUNK + core * half, 128), half)],
+            ibuf.at[:, pl.ds(c * half, half)],
+            load_sem.at[3 + count + c],
+        )
+        for c in range(chunks)
+    ]
+    late.append(pltpu.make_async_copy(w_output.at[:, mine], ibuf.at[:, pl.ds(chunks * half, half)], load_sem.at[3 + count + chunks]))
+    late.append(pltpu.make_async_copy(w_outer.at[:, mine], obuf, load_sem.at[4 + count + chunks]))
     load = pltpu.make_async_copy(tokens.at[y], stage, local_sem.at[0])
-    load.start()
     cot_load = pltpu.make_async_copy(cotangent.at[y], cot_stage, local_sem.at[4])
-    cot_load.start()
+    for copy in loads + late + [load, cot_load]:
+        copy.start()
     vpack[...] = jnp.zeros_like(vpack)
     for copy in loads:
         copy.wait()
@@ -451,116 +460,203 @@
     for i in range(3):
         for p in range(pairs):
             pack[:, (3 * p + i) * 128 : (3 * p + i + 1) * 128] = wbuf[i, :, p * 128 : (p + 1) * 128].astype(jnp.bfloat16)
+    vectors_all[me] = vpack[...]
     greet(True)
+
     across = remote(tokens.at[1 - y], tokens_all.at[1], tsend.at[0], trecv.at[0], partner(y=1 - y))
     across.start()
-    along = []
-    for k in range(1, size_z):
-        peer = partner(z=lax.rem(z + k, size_z))
-        along.append(
-            (
-                remote(pack, weights_all.at[me], zsend.at[0, k - 1], zrecv.at[0, k - 1], peer),
-                remote(vpack, vectors_all.at[me], zsend.at[1, k - 1], zrecv.at[1, k - 1], peer),
-            )
-        )
     beside = remote(tokens.at[y], tokens_all.at[2], tsend.at[1], trecv.at[1], partner(core=1 - core))
-    sideways = []
-
-    def forward(k, weights_src, vectors_src):
-        slot = lax.rem(z - k + size_z, size_z) * size_x + x
+
+    packs = (pack, vpack, ipack)
+
+    def home(stream, origin):
+        if stream == 2:
+            return inner_all.at[origin]
+        return (weights_all, vectors_all)[stream].at[origin * size_x + x]
+
+    def z_move(stream, way, t):
+        step = 1 - 2 * way
+        origin = z - step * (t - 1)
+        src = packs[stream] if t == 1 else home(stream, origin)
+        peer = partner(z=lax.rem(z + step + size_z, size_z))
+        return remote(src, home(stream, origin), zsend.at[stream, way, t - 1], zrecv.at[stream, way, t - 1], peer)
+
+    def sends(way, t):
+        step = 1 - 2 * way
+        origin, target = z - step * (t - 1), z + step
+        inside = lambda v: jnp.logical_and(v >= 0, v < size_z)
+        return jnp.logical_and(inside(origin), inside(target))
+
+    def receives(way, t):
+        origin = z - (1 - 2 * way) * t
+        return jnp.logical_and(origin >= 0, origin < size_z)
+
+    def x_moves(index, origin, own):
+        moves = []
         for j in range(1, size_x):
-            peer = partner(x=lax.rem(x + j, size_x))
-            first = remote(weights_src, weights_all.at[slot], xsend.at[0, k, j - 1], xrecv.at[0, k, j - 1], peer)
-            second = remote(vectors_src, vectors_all.at[slot], xsend.at[1, k, j - 1], xrecv.at[1, k, j - 1], peer)
-            first.start()
-            second.start()
-            sideways.append((first, second))
-
-    forward(0, pack, vpack)
-    for first, second in along:
-        first.start()
-        second.start()
+            for stream in range(2):
+                src = packs[stream] if own else home(stream, origin)
+                moves.append(
+                    remote(
+                        src,
+                        home(stream, origin),
+                        xsend.at[stream, index, j - 1],
+                        xrecv.at[stream, index, j - 1],
+                        partner(x=columns[j]),
+                    )
+                )
+        return moves
+
+    def start_z(streams, t):
+        for way in range(2):
+
+            @pl.when(sends(way, t))
+            def _():
+                for stream in streams:
+                    z_move(stream, way, t).start()
+
+    for move in x_moves(0, z, True):
+        move.start()
+    start_z((0, 1), 1)
     beside.start()
-    keep_weights = pltpu.make_async_copy(pack, weights_all.at[me], local_sem.at[1])
-    keep_weights.start()
-    vectors_all[me] = vpack[...]
+    for copy in late:
+        copy.wait()
+    ipack[...] = ibuf[...].astype(jnp.bfloat16)
+    opack[...] = obuf[...].astype(jnp.bfloat16)
+    start_z((2,), 1)
+    outer_moves = [
+        remote(opack, outer_all.at[x], osend.at[j - 1], orecv.at[j - 1], partner(x=columns[j])) for j in range(1, size_x)
+    ]
+    keeps = [
+        pltpu.make_async_copy(pack, weights_all.at[me], local_sem.at[1]),
+        pltpu.make_async_copy(ipack, inner_all.at[z], local_sem.at[2]),
+        pltpu.make_async_copy(opack, outer_all.at[x], local_sem.at[6]),
+    ]
     load.wait()
-    keep_tokens = pltpu.make_async_copy(stage, tokens_all.at[0], local_sem.at[3])
-    keep_tokens.start()
+    keeps.append(pltpu.make_async_copy(stage, tokens_all.at[0], local_sem.at[3]))
     cot_load.wait()
-    keep_cot = pltpu.make_async_copy(cot_stage, cotangent_all.at[0], local_sem.at[5])
-    keep_cot.start()
-    order = sorted(range(1, size_z), key=lambda k: min(k, size_z - k))
-    for k in order:
-        first, second = along[k - 1]
-        first.wait_recv()
-        second.wait_recv()
-        slot = lax.rem(z - k + size_z, size_z) * size_x + x
-        forward(k, weights_all.at[slot], vectors_all.at[slot])
-    across.wait_recv()
+    keeps.append(pltpu.make_async_copy(cot_stage, cotangent_all.at[0], local_sem.at[5]))
+    for keep in keeps:
+        keep.start()
+
+    def arrive(streams, t, sideways):
+        for way in range(2):
+
+            @pl.when(receives(way, t))
+            def _():
+                origin = z - (1 - 2 * way) * t
+                for stream in streams:
+                    slot = home(stream, origin)
+                    remote(
+                        slot, slot, zsend.at[stream, way, t - 1], zrecv.at[stream, way, t - 1], partner(core=1 - core)
+                    ).wait_recv()
+                if sideways:
+                    for move in x_moves(1 + way * (size_z - 1) + t - 1, origin, False):
+                        move.start()
+
     onward = remote(tokens_all.at[1], tokens_all.at[3], tsend.at[2], trecv.at[2], partner(core=1 - core))
-    onward.start()
     later = remote(cotangent.at[1 - y], cotangent_all.at[1], tsend.at[3], trecv.at[3], partner(y=1 - y))
-    later.start()
-    for first, second in sideways:
-        first.wait()
-        second.wait()
-    for first, second in along:
-        first.wait_send()
-        second.wait_send()
+    for t in range(1, size_z):
+        arrive((0, 1), t, True)
+        if t < size_z - 1:
+            start_z((0, 1), t + 1)
+        if t == 1:
+            for move in outer_moves:
+                move.start()
+        arrive((2,), t, False)
+        if t < size_z - 1:
+            start_z((2,), t + 1)
+        if t == min(2, size_z - 1):
+            across.wait_recv()
+            onward.start()
+            later.start()
+
+    for move in x_moves(0, z, True):
+        move.wait()
+    for t in range(1, size_z):
+        for way in range(2):
+
+            @pl.when(receives(way, t))
+            def _():
+                origin = z - (1 - 2 * way) * t
+                for move in x_moves(1 + way * (size_z - 1) + t - 1, origin, False):
+                    move.wait()
+
+            @pl.when(sends(way, t))
+            def _():
+                for stream in range(3):
+                    z_move(stream, way, t).wait_send()
+
     short = min(vector.shape[1] for vector in raw)
     longest = vpack.shape[1]
     for s in range(size_z * size_x):
         rows_out[:, s * short : (s + 1) * short] = vectors_all[s, :, 0:short]
         inner_out[:, s * longest : (s + 1) * longest] = vectors_all[s, WIDE : WIDE + 1, :]
+    for move in outer_moves:
+        move.wait()
     across.wait_send()
     beside.wait()
     onward.wait()
     later.wait()
-    keep_weights.wait()
-    keep_tokens.wait()
-    keep_cot.wait()
-
-
-def entry(size_z, size_x, tokens, cotangent, wq, wk, wv, vectors):
+    for keep in keeps:
+        keep.wait()
+
+
+def entry(size_z, size_x, tokens, cotangent, wq, wk, wv, w_inner, w_output, w_outer, vectors):
     _, part, width = tokens.shape
     rows = wq.shape[0]
-    lanes = wq.shape[1] // 2 * 3
+    half = width // 2
+    lanes = 3 * half
+    hidden = w_inner.shape[1]
+    long = w_outer.shape[0]
+    mixed_lanes = hidden // 2 + half
+    chunks = hidden // CHUNK
     longest = max(v.shape[0] for v in vectors)
     shards = size_z * size_x
-    anywhere = pl.BlockSpec(memory_space=pl.ANY)
+    count = len(vectors)
+    anywhere, vmem = pl.BlockSpec(memory_space=pl.ANY), pl.BlockSpec(memory_space=pltpu.VMEM)
     dma = pltpu.SemaphoreType.DMA
+    low, high = jnp.bfloat16, jnp.float32
+    side = size_x - 1
     return pl.pallas_call(
-        lambda *refs: entry_kernel(size_z, size_x, len(vectors), *refs),
+        lambda *refs: entry_kernel(size_z, size_x, count, *refs),
         out_shape=(
-            jax.ShapeDtypeStruct((4, part, width), tokens.dtype),
-            jax.ShapeDtypeStruct((2, part, width), cotangent.dtype),
-            jax.ShapeDtypeStruct((shards, rows, lanes), jnp.bfloat16),
-            jax.ShapeDtypeStruct((16, width), jnp.float32),
-            jax.ShapeDtypeStruct((1, shards * longest), jnp.float32),
+            jax.ShapeDtypeStruct((4, part, width), low),
+            jax.ShapeDtypeStruct((2, part, width), low),
+            jax.ShapeDtypeStruct((shards, rows, lanes), low),
+            jax.ShapeDtypeStruct((size_z, rows, mixed_lanes), low),
+            jax.ShapeDtypeStruct((size_x, long, half), low),
+            jax.ShapeDtypeStruct((16, width), high),
+            jax.ShapeDtypeStruct((1, shards * longest), high),
         ),
-        in_specs=[anywhere] * (5 + len(vectors)),
-        out_specs=(anywhere,) * 3 + (pl.BlockSpec(memory_space=pltpu.VMEM),) * 2,
+        in_specs=[anywhere] * (8 + count),
+        out_specs=(anywhere,) * 5 + (vmem,) * 2,
         scratch_shapes=[pltpu.VMEM((1, v.shape[0]), v.dtype) for v in vectors]
         + [
-            pltpu.VMEM((part, width), tokens.dtype),
-            pltpu.VMEM((part, width), cotangent.dtype),
-            pltpu.VMEM((3, rows, lanes // 3), wq.dtype),
-            pltpu.VMEM((rows, lanes), jnp.bfloat16),
-            pltpu.VMEM((16, longest), jnp.float32),
-            pltpu.VMEM((shards, 16, longest), jnp.float32),
-            dma((6,)),
-            dma((3 + len(vectors),)),
+            pltpu.VMEM((part, width), low),
+            pltpu.VMEM((part, width), low),
+            pltpu.VMEM((3, rows, half), high),
+            pltpu.VMEM((rows, mixed_lanes), high),
+            pltpu.VMEM((long, half), high),
+            pltpu.VMEM((rows, lanes), low),
+            pltpu.VMEM((rows, mixed_lanes), low),
+            pltpu.VMEM((long, half), low),
+            pltpu.VMEM((16, longest), high),
+            pltpu.VMEM((shards, 16, longest), high),
+            dma((7,)),
+            dma((5 + count + chunks,)),
             dma((4,)),
             dma((4,)),
-            dma((2, size_z - 1)),
-            dma((2, size_z - 1)),
-            dma((2, size_z, max(size_x - 1, 1))),
-            dma((2, size_z, max(size_x - 1, 1))),
+            dma((3, 2, size_z - 1)),
+            dma((3, 2, size_z - 1)),
+            dma((2, 2 * size_z - 1, side)),
+            dma((2, 2 * size_z - 1, side)),
+            dma((side,)),
+            dma((side,)),
         ],
         compiler_params=pltpu.CompilerParams(collective_id=0, has_side_effects=True, vmem_limit_bytes=66_000_000),
         name="entry",
-    )(tokens, cotangent, wq, wk, wv, *[v.reshape(1, -1) for v in vectors])
+    )(tokens, cotangent, wq, wk, wv, w_inner, w_output, w_outer, *[v.reshape(1, -1) for v in vectors])
 
 
 def exit_kernel(size_z, size_x, shapes, *refs):
@@ -972,57 +1068,69 @@
     cot_ref,
     vectors_ref,
     bias_inner_ref,
-    weights_hbm,
     *refs,
 ):
+    inner_parts, outer_parts = refs[:size_x], refs[size_x : size_x + size_z]
+    refs = refs[size_x + size_z :]
     mixed_ref, pre_first_ref, grad_mine_ref, grad_other_ref, sums_ref, inner_sum_ref, grad_output_ref = refs[:7]
     inner_terms = refs[7 : 7 + size_z]
     outer_terms = refs[7 + size_z : 7 + size_z + size_x]
     refs = refs[7 + size_z + size_x :]
     w_output, w_inner, w_outer, a_output, a_inner, a_outer, grad_out_buf = refs[:7]
     context, first_low, turned_low, normed, first, slope, active, work = refs[7:15]
-    send_inner, send_outer, recv_inner, recv_outer, load_sem, outer_sem, send_sem, recv_sem, store_sem = refs[15:]
+    send_inner, send_outer, recv_inner, recv_outer = refs[15:19]
+    load_sem, share_send, share_recv, send_sem, recv_sem, store_sem = refs[19:]
     step, steps = pl.program_id(0), pl.num_programs(0)
     core_here = lax.axis_index("core")
     width, hidden = w_inner.shape
     half = width // 2
     chunks = hidden // CHUNK
     shards = size_z * size_x
-    pieces = 2 * shards
-    rows = width // pieces
-    ratio = hidden // width
     z, x, y, _ = place_of()
     twin = partner(core=1 - lax.axis_index("core"))
 
-    def load_outer(start):
-        if not start:
-            pltpu.make_async_copy(w_outer, w_outer, outer_sem).wait()
-            return
-
-        def piece(s, _):
-            for q in range(ratio):
-                src = weights_hbm.at[
-                    pl.ds(pl.multiple_of(s * rows, rows), rows), pl.ds(hidden + width + q * width, width)
-                ]
-                dst = w_outer.at[pl.ds(pl.multiple_of((s * ratio + q) * rows, rows), rows), :]
-                pltpu.make_async_copy(src, dst, outer_sem).start()
-            return 0
-
-        lax.fori_loop(0, pieces, piece, 0)
-
-    loads = (
-        pltpu.make_async_copy(weights_hbm.at[:, pl.ds(hidden, width)], w_output, load_sem.at[0]),
-        pltpu.make_async_copy(weights_hbm.at[:, pl.ds(0, hidden)], w_inner, load_sem.at[1]),
-    )
+    shard = width // shards
+    long = hidden // shards
+    group = CHUNK // long // size_x
+
+    def columns_of(first, owner):
+        return pl.ds(pl.multiple_of(first + owner * half, 128), half)
+
+    def start_piece(i, src, dst):
+        pltpu.make_async_copy(src, dst, load_sem.at[i]).start()
+        remote(src, dst, share_send.at[i], share_recv.at[i], twin).start()
+
+    def start_rows(i, lane, ref, first):
+        for j in range(size_x):
+            for at in range(size_z):
+                slot = at * size_x + lax.rem(x - j + size_x, size_x)
+                rows = pl.ds(pl.multiple_of(slot * shard, shard), shard)
+                start_piece(i, inner_parts[j].at[at, :, pl.ds(lane, half)], ref.at[rows, columns_of(first, core_here)])
+
+    def start_loads():
+        start_rows(0, hidden // 2, w_output, 0)
+        for c in range(chunks):
+            start_rows(1 + 2 * c, c * half, w_inner, c * CHUNK)
+            for at in range(c * group, (c + 1) * group):
+                for k in range(size_z):
+
+                    @pl.when(lax.rem(z - k + size_z, size_z) == at)
+                    def _():
+                        for column in range(size_x):
+                            rows = pl.ds((at * size_x + column) * long, long)
+                            start_piece(2 + 2 * c, outer_parts[k].at[column], w_outer.at[rows, columns_of(0, core_here)])
+
+    def wait_load(i, ref, rows, first):
+        own, far = ref.at[rows, columns_of(first, core_here)], ref.at[rows, columns_of(first, 1 - core_here)]
+        pltpu.make_async_copy(own, own, load_sem.at[i]).wait()
+        remote(own, far, share_send.at[i], share_recv.at[i], twin).wait()
 
     @pl.when(step == 0)
     def _():
         barrier = pltpu.get_barrier_semaphore()
         pl.semaphore_signal(barrier, inc=1, device_id=twin, device_id_type=MESH_ID)
         pl.semaphore_wait(barrier, 1)
-        for load in loads:
-            load.start()
-        load_outer(True)
+        start_loads()
         a_output[...] = jnp.zeros_like(a_output)
         a_inner[...] = jnp.zeros_like(a_inner)
         a_outer[...] = jnp.zeros_like(a_outer)
@@ -1041,7 +1149,7 @@
 
     @pl.when(step == 0)
     def _():
-        loads[0].wait()
+        wait_load(0, w_output, slice(None), 0)
 
     hidden_rows = tokens_ref[...].astype(jnp.float32) + (dot_nn(context[...], w_output[...]) + vector(0))
     normed[...], first_recip = standardize(hidden_rows)
@@ -1050,11 +1158,6 @@
     turned_low[...] = first_low[...].T
     work[...] = jnp.broadcast_to(vector(3), work.shape)
 
-    @pl.when(step == 0)
-    def _():
-        loads[1].wait()
-        load_outer(False)
-
     def part(c):
         return pl.ds(pl.multiple_of(c * CHUNK, CHUNK), CHUNK)
 
@@ -1064,15 +1167,24 @@
             remote(send_outer.at[c], recv_outer.at[c], send_sem.at[1, c], recv_sem.at[1, c], twin),
         )
 
-    def forward(c, _):
+    def forward(c):
+        @pl.when(step == 0)
+        def _():
+            wait_load(1 + 2 * c, w_inner, slice(None), c * CHUNK)
+
         u = dot_nn(first_low[...], w_inner[:, part(c)]) + bias_inner_ref[0:1, part(c)]
         cdf = 0.5 * (1.0 + lax.erf(u * ROOT_HALF))
         slope[:, part(c)] = cdf + u * jnp.exp(-0.5 * u * u) * INV_ROOT_TAU
         active[:, part(c)] = (u * cdf).astype(jnp.bfloat16)
+
+        @pl.when(step == 0)
+        def _():
+            wait_load(2 + 2 * c, w_outer, part(c), 0)
+
         work[...] += dot_nn(active[:, part(c)], w_outer[part(c), :])
-        return 0
-
-    lax.fori_loop(0, chunks, forward, 0)
+
+    for c in range(chunks):
+        forward(c)
     second, second_recip = standardize(first[...] + work[...])
     mixed_ref[...] = (second * vector(4) + vector(5)).astype(jnp.bfloat16)
     upstream = cot_ref[...].astype(jnp.float32)
@@ -1122,9 +1234,6 @@
     def _():
         grad_output_ref[...] = a_output[...].astype(jnp.bfloat16)
 
-        shard = width // shards
-        long = hidden // shards
-
         def inner_out(c):
             copies = []
             for k in range(size_z):
@@ -1138,7 +1247,6 @@
 
         def outer_out(c):
             copies = []
-            group = CHUNK // long // size_x
             for i in range(group):
                 for j in range(size_x):
                     src = send_outer.at[c, pl.ds(pl.multiple_of((i * size_x + lax.rem(x + j, size_x)) * long, long), long), :]
@@ -1162,7 +1270,7 @@
             pltpu.make_async_copy(send_outer.at[c], send_outer.at[c], store_sem.at[1, c]).wait()
 
 
-def dense_layer(size_z, size_x, tokens, mine, other, cotangent, vectors, bias_inner, weights):
+def dense_layer(size_z, size_x, tokens, mine, other, cotangent, vectors, bias_inner, inner_parts, outer_parts):
     local, half = mine.shape
     width = 2 * half
     hidden = bias_inner.shape[1]
@@ -1204,8 +1312,8 @@
                 tile,
                 whole((16, width)),
                 whole((1, hidden)),
-                anywhere,
-            ],
+            ]
+            + [anywhere] * (size_x + size_z),
             out_specs=[
                 tile,
                 tile,
@@ -1236,8 +1344,9 @@
                 halves,
                 halves,
                 halves,
-                dma((2,)),
-                dma,
+                dma((1 + 2 * chunks,)),
+                dma((1 + 2 * chunks,)),
+                dma((1 + 2 * chunks,)),
                 dma((2, chunks)),
                 dma((2, chunks)),
                 dma((2, chunks)),
@@ -1248,7 +1357,7 @@
         ),
         cost_estimate=pl.CostEstimate(flops=32_000_000_000, bytes_accessed=40_000_000, transcendentals=6_000_000),
         name="dense_layer",
-    )(tokens, mine, other, cotangent, vectors, bias_inner, weights)
+    )(tokens, mine, other, cotangent, vectors, bias_inner, *inner_parts, *outer_parts)
 
 
 def lowered(piece):
@@ -1581,7 +1690,6 @@
     core, y = lax.axis_index("core"), lax.axis_index("y")
     size_z, size_x = lax.axis_size("z"), lax.axis_size("x")
     shards = size_z * size_x
-    everyone = ("z", "x", "core")
     sequences, part, width = tokens.shape
     half = width // 2
     pairs = half // 128
@@ -1590,20 +1698,13 @@
     own_rows = w_query.shape[0]
     lanes = 3 * half
 
-    stack = hidden // width
-
-    def core_rows(matrix):
-        rows = matrix.shape[0] // 2
-        return lowered(lax.dynamic_slice_in_dim(matrix, core * rows, rows, 0))
-
-    outer_rows = core_rows(w_outer)
-    outer_rows = outer_rows.reshape(stack, own_rows // 2, width).transpose(1, 0, 2).reshape(own_rows // 2, hidden)
-    pieces = (core_rows(w_inner), core_rows(w_output), outer_rows)
-    dense = lax.all_gather(jnp.concatenate(pieces, axis=1), everyone, axis=0, tiled=True)
-
     vectors = (b_query, b_value, b_output, first_gain, first_shift, b_inner, b_outer, second_gain, second_shift)
     sizes = [v.shape[0] for v in vectors]
-    tokens_all, cotangent_all, early, rows, inner_row = entry(size_z, size_x, tokens, cotangent, w_query, w_key, w_value, vectors)
+    tokens_all, cotangent_all, early, inner_own, outer_own, rows, inner_row = entry(
+        size_z, size_x, tokens, cotangent, w_query, w_key, w_value, w_inner, w_output, w_outer, vectors
+    )
+    inner_parts = [inner_own] + [shift(inner_own, "x", j) for j in range(1, size_x)]
+    outer_parts = [outer_own] + [shift(outer_own, "z", k) for k in range(1, size_z)]
     inputs_all = tokens_all.reshape(4 * part, width)
     full_early = early.reshape(width, lanes)
     spot = jnp.arange(5, dtype=jnp.int32)
@@ -1619,7 +1720,8 @@
         cotangent_all.reshape(local, width),
         rows,
         inner_row,
-        dense,
+        inner_parts,
+        outer_parts,
     )
     mixed, pre_first, upstream_mine, upstream_send, dense_sums, inner_sums, grad_w_output = made[:7]
     inner_terms = [made[7]] + [shift(made[7 + k], "z", k) for k in range(1, size_z)]

time: 331 us -> 361 us (1.091)
  waiting for transfers between devices: 13.1 us -> 51.5 us
  between operations: 14.2 us -> 0.75 us
  Pallas kernels: 277 us -> 281 us
    ppermute x4 -> x8, waiting for transfers between devices: 0.01 us -> 51.5 us  [shift(): lax.ppermute(piece, axis, [(i, (i + step) % size) for i in range(size)])]
    all_gather x1 -> x0, waiting for transfers between devices: 10.4 us -> none  [body(): lax.all_gather(jnp.concatenate(pieces, axis=1), everyone, axis=0, tiled=T...]
    ppermute x4 -> x8, starting transfers between devices: 15.3 us -> 17.8 us  [shift(): lax.ppermute(piece, axis, [(i, (i + step) % size) for i in range(size)])]
  transfers between devices with their start and end apart: 8 -> 11, of which waited for: 2 -> 2; matrix products, arithmetic and copies ran while one was open for 1% -> 1% of each run, Pallas kernels for 41% -> 23%
where the time goes in v5:
time: 361 us; the launch traced here: 360 us
  Pallas kernels  281 us (78%)
  waiting for transfers between devices  51.5 us (14%)
  starting transfers between devices  18.5 us (5%)
  local copies, waits for them, and re-layouts  4.42 us (1%)
    pallas_call x1, Pallas kernels, exit_call(): pl.pallas_call(lambda *refs: exit_kernel(size_z, size_x, shapes, *refs),...  73.6 us
    pallas_call x1, Pallas kernels, dense_layer(): pl.pallas_call(lambda *refs: dense_kernel(size_z, size_x, *refs), out_sha...  64 us
    pallas_call x1, Pallas kernels, entry(): pl.pallas_call(lambda *refs: entry_kernel(size_z, size_x, count, *refs),...  53.6 us
    ppermute x8, waiting for transfers between devices, shift(): lax.ppermute(piece, axis, [(i, (i + step) % size) for i in range(size)])  51.5 us
    pallas_call x1, Pallas kernels, attention_back(): pl.pallas_call(backward_kernel, out_shape=(jax.ShapeDtypeStruct((length,...  43.5 us
    pallas_call x1, Pallas kernels, attention(): pl.pallas_call(forward_kernel, out_shape=(jax.ShapeDtypeStruct((rows, pai...  40.3 us
    ppermute x8, starting transfers between devices, shift(): lax.ppermute(piece, axis, [(i, (i + step) % size) for i in range(size)])  17.8 us
  transfers between devices with their start and end apart: 11, of which 2 were waited for; matrix products, arithmetic and copies ran while one was open for 1% of the time, Pallas kernels for 23%

profile of v5, /device:TPU:0, one launch (start us, length us, event | category | flops | bytes accessed | tf_op | source)
XLA Modules:
  0.0 359.6 jit_solution(5257589486823548858)
XLA Ops:
  0.7 1.3 reshape.107.refs_13_
  1.9 53.6 %entry.1 = (bf16[4,512,768]{2,1,0:T(8,128)(2,1)}, bf16[2,512,768]{2,1,0:T(8,128)(2,1)}, bf16[8,96,1152]{2,1,0:T(8,128)(2,1)}, bf16[4,96,1920]{2,1,0:T(8,128)(2,1...) custom-call(bf16[2,512,768]{2,1,0:T(8,128)(2,1)} %refs_0_.1, bf16[2,512,768]{2,1,0:T(8,128)(2,1)} %refs_1_.1, ...), custom_call_target="tpu_custom_call" | custom-call | tf_op jit(solution)/shard_map/entry/pallas_call | solution.py:621
  55.5 1.6 collective-permute-start.1
  57.1 0.5 compare_select_fusion.1.place_ref
  57.6 0.6 constant_dynamic-slice_fusion.row_ref
  58.2 40.3 %attention_forward.1 = (bf16[1024,384]{1,0:T(8,128)(2,1)}, bf16[1024,384]{1,0:T(8,128)(2,1)}, f32[24,2048]{1,0:T(8,128)}, bf16[2048,1152]{1,0:T(8,128)(2,1)}) custom-call(s32[5]{0:T(128)} %compare_select_fusion.1.place_ref, s32[2048]{0:T(1024)} %bitcast.31, s32[1,2048]{1,0:T(1,128)} %constant_dynamic-slice_fusion.row_ref, bf16[2048,768]{1,0:T(8,128)(2,1)} %bitcast.24, ...), custom_call_target="tpu_custom_call" | custom-call | flops 24000000000 | bytes 9000000 | tf_op jit(solution)/shard_map/attention_forward/pallas_call | solution.py:175
  98.5 10.5 %collective-permute-start.4 = (bf16[2,384,384]{2,1,0:T(8,128)(2,1)S(1)}, bf16[2,384,384]{2,1,0:T(8,128)(2,1)S(1)}, u32[]{:S(2)}, u32[]{:S(2)}) collective-permute-start(bf16[2,384,384]{2,1,0:T(8,128)(2,1)S(1)} %copy-done.2), channel_id=1, source_target_pairs={{0,24},{8,0},{16,8},{24,16},{1,25},{9,1},{17,9},{25,17},{2,26},{10... | collective-permute-start | bytes 1769480 | tf_op jit(solution)/shard_map/ppermute | solution.py:1417
  109.0 0.5 collective-permute-start.3
  109.7 13.1 %collective-permute-done.4.refs_11_ = bf16[2,384,384]{2,1,0:T(8,128)(2,1)S(1)} collective-permute-done((bf16[2,384,384]{2,1,0:T(8,128)(2,1)S(1)}, bf16[2,384,384]{2,1,0:T(8,128)(2,1)S(1)}, u32[]{:S(2)}, u32[]{:S(2)}) %collective-permute-start.4) | collective-permute-done | bytes 589856 | tf_op jit(solution)/shard_map/ppermute | solution.py:1417
  122.8 38.4 %collective-permute-done.3.refs_10_ = bf16[2,384,384]{2,1,0:T(8,128)(2,1)S(1)} collective-permute-done((bf16[2,384,384]{2,1,0:T(8,128)(2,1)S(1)}, bf16[2,384,384]{2,1,0:T(8,128)(2,1)S(1)}, u32[]{:S(2)}, u32[]{:S(2)}) %collective-permute-start.3) | collective-permute-done | bytes 589856 | tf_op jit(solution)/shard_map/ppermute | solution.py:1417
  161.2 0.8 copy-done.4
  162.0 0.2 copy-done.5
  162.1 64.0 %dense_layer.1 = (bf16[1024,768]{1,0:T(8,128)(2,1)}, f32[1024,768]{1,0:T(8,128)}, bf16[1024,384]{1,0:T(8,128)(2,1)}, bf16[1024,384]{1,0:T(8,128)(2,1)}, f32[48,7...) custom-call(bf16[2048,768]{1,0:T(8,128)(2,1)} %bitcast.25, ...), custom_call_target="tpu_custom_call" | custom-call | flops 32000000000 | bytes 40000000 | tf_op jit(solution)/shard_map/dense_layer/pallas_call | solution.py:1292
  226.1 0.4 collective-permute-start.6
  226.5 1.3 collective-permute-start.8
  227.9 2.9 collective-permute-start.9
  230.8 1.6 slice_bitcast_fusion
  232.4 0.3 collective-permute-start.5
  232.7 0.8 collective-permute-start.10
  233.5 43.5 %attention_backward.1 = (bf16[2048,1152]{1,0:T(8,128)(2,1)}, f32[24,384]{1,0:T(8,128)}) custom-call(s32[5]{0:T(128)} %compare_select_fusion.1.place_ref, s32[2048]{0:T(1024)} %bitcast.32, bf16[2048,1152]{1,0:T(8,128)(2,1)} %get-tuple-element.77.qkv_ref, bf16[1024,384]{1,0:T(8,128)(2,1)} %get-tuple-element.70.refs_1_.ctx_mine_ref, ...), custom_call_target="tpu_custom_call" | custom-call | flops 60000002048 | bytes 15000000 | tf_op jit(solution)/shard_map/attention_backward/pallas_call | solution.py:343
  277.0 1.4 maximum_select_fusion
  278.4 73.6 %exit.1 = (f32[2,512,768]{2,1,0:T(8,128)}, f32[96,768]{1,0:T(8,128)}, f32[96,768]{1,0:T(8,128)}, f32[96,768]{1,0:T(8,128)}, f32[96,768]{1,0:T(8,128)}, /*index=5...) custom-call(bf16[2048,1152]{1,0:T(8,128)(2,1)} %get-tuple-element.81.refs_0_, bf16[2048,768]{1,0:T(8,128)(2,1)} %bitcast.26, ...), custom_call_target="tpu_custom_call" | custom-call | tf_op jit(solution)/shard_map/exit/pallas_call | solution.py:1029
  352.0 6.4 %deliver.1 = (f32[2,512,768]{2,1,0:T(8,128)}, f32[96,768]{1,0:T(8,128)}, f32[96,768]{1,0:T(8,128)}, f32[96,768]{1,0:T(8,128)}, f32[96,768]{1,0:T(8,128)}, /*inde...) custom-call(f32[2,512,768]{2,1,0:T(8,128)} %get-tuple-element.93.ref, ...), custom_call_target="tpu_custom_call" | custom-call | tf_op jit(solution)/shard_map/deliver/pallas_call | solution.py:953
  358.4 1.2 reduce
  (22 shorter events, 0.2 us)
Async XLA Ops:
  0.7 56.9 %copy-start = (s32[2,2048]{1,0:T(2,128)S(1)}, s32[2,2048]{1,0:T(2,128)}, u32[]{:S(2)}) copy-start(s32[2,2048]{1,0:T(2,128)} %param.19) | copy-start | bytes 49156
  55.5 106.4 %collective-permute-start.1 = (bf16[4,96,1920]{2,1,0:T(8,128)(2,1)}, bf16[4,96,1920]{2,1,0:T(8,128)(2,1)}, u32[]{:S(2)}, u32[]{:S(2)}) collective-permute-start(bf16[4,96,1920]{2,1,0:T(8,128)(2,1)} %get-tuple-element.74.refs_6_), channel_id=1, source_target_pairs={{0,4},{4,0},{1,5},{5,1},{2,6},{6,2},{3,7},{7,3},{8,12},{12,8},{9,1... | collective-permute-start | bytes 4423688 | tf_op jit(solution)/shard_map/ppermute | solution.py:1417
  58.2 40.3 %copy-start.2 = (bf16[2,384,384]{2,1,0:T(8,128)(2,1)S(1)}, bf16[2,384,384]{2,1,0:T(8,128)(2,1)}, u32[]{:S(2)}) copy-start(bf16[2,384,384]{2,1,0:T(8,128)(2,1)} %get-tuple-element.75.refs_8_) | copy-start | bytes 1769476
  98.5 62.6 %collective-permute-start = (bf16[1024,384]{1,0:T(8,128)(2,1)}, bf16[1024,384]{1,0:T(8,128)(2,1)}, u32[]{:S(2)}, u32[]{:S(2)}) collective-permute-start(bf16[1024,384]{1,0:T(8,128)(2,1)} %get-tuple-element.71.ctx_other_ref), channel_id=1, source_target_pairs={{0,1},{1,0},{2,3},{3,2},{4,5},{5,4},{6,7},{7,6},{8,9},{9,8},{10,11... | collective-permute-start | bytes 2359304 | tf_op jit(solution)/shard_map/ppermute | solution.py:1421
  98.5 24.2 %collective-permute-start.4 = (bf16[2,384,384]{2,1,0:T(8,128)(2,1)S(1)}, bf16[2,384,384]{2,1,0:T(8,128)(2,1)S(1)}, u32[]{:S(2)}, u32[]{:S(2)}) collective-permute-start(bf16[2,384,384]{2,1,0:T(8,128)(2,1)S(1)} %copy-done.2), channel_id=1, source_target_pairs={{0,24},{8,0},{16,8},{24,16},{1,25},{9,1},{17,9},{25,17},{2,26},{10... | collective-permute-start | bytes 1769480 | tf_op jit(solution)/shard_map/ppermute | solution.py:1417
  109.0 52.1 %collective-permute-start.3 = (bf16[2,384,384]{2,1,0:T(8,128)(2,1)S(1)}, bf16[2,384,384]{2,1,0:T(8,128)(2,1)S(1)}, u32[]{:S(2)}, u32[]{:S(2)}) collective-permute-start(bf16[2,384,384]{2,1,0:T(8,128)(2,1)S(1)} %copy-done.2), channel_id=1, source_target_pairs={{0,16},{8,24},{16,0},{24,8},{1,17},{9,25},{17,1},{25,9},{2,18},{10... | collective-permute-start | bytes 1769480 | tf_op jit(solution)/shard_map/ppermute | solution.py:1417
  109.6 51.6 %collective-permute-start.2 = (bf16[2,384,384]{2,1,0:T(8,128)(2,1)S(1)}, bf16[2,384,384]{2,1,0:T(8,128)(2,1)S(1)}, u32[]{:S(2)}, u32[]{:S(2)}) collective-permute-start(bf16[2,384,384]{2,1,0:T(8,128)(2,1)S(1)} %copy-done.2), channel_id=1, source_target_pairs={{0,8},{8,16},{16,24},{24,0},{1,9},{9,17},{17,25},{25,1},{2,10},{10... | collective-permute-start | bytes 1769480 | tf_op jit(solution)/shard_map/ppermute | solution.py:1417
  122.8 38.4 %copy-start.3 = (bf16[2,384,384]{2,1,0:T(8,128)(2,1)}, bf16[2,384,384]{2,1,0:T(8,128)(2,1)S(1)}, u32[]{:S(2)}) copy-start(bf16[2,384,384]{2,1,0:T(8,128)(2,1)S(1)} %collective-permute-done.4.refs_11_) | copy-start | bytes 1769476
  161.1 0.8 copy-start.4
  161.1 1.0 copy-start.5
  226.1 6.5 %collective-permute-start.6 = (bf16[1024,384]{1,0:T(8,128)(2,1)}, bf16[1024,384]{1,0:T(8,128)(2,1)}, u32[]{:S(2)}, u32[]{:S(2)}) collective-permute-start(bf16[1024,384]{1,0:T(8,128)(2,1)} %get-tuple-element.79), channel_id=1, source_target_pairs={{0,1},{1,0},{2,3},{3,2},{4,5},{5,4},{6,7},{7,6},{8,9},{9,8},{10,11... | collective-permute-start | bytes 2359304 | tf_op jit(solution)/shard_map/ppermute | solution.py:1421
  226.5 51.8 %collective-permute-start.7 = (bf16[2,96,1536]{2,1,0:T(8,128)(2,1)}, bf16[2,96,1536]{2,1,0:T(8,128)(2,1)}, u32[]{:S(2)}, u32[]{:S(2)}) collective-permute-start(bf16[2,96,1536]{2,1,0:T(8,128)(2,1)} %get-tuple-element.88), channel_id=1, source_target_pairs={{0,8},{8,16},{16,24},{24,0},{1,9},{9,17},{17,25},{25,1},{2,10},{10... | collective-permute-start | bytes 1769480 | tf_op jit(solution)/shard_map/ppermute | solution.py:1417
  226.5 51.8 %collective-permute-start.8 = (bf16[2,96,1536]{2,1,0:T(8,128)(2,1)}, bf16[2,96,1536]{2,1,0:T(8,128)(2,1)}, u32[]{:S(2)}, u32[]{:S(2)}) collective-permute-start(bf16[2,96,1536]{2,1,0:T(8,128)(2,1)} %get-tuple-element.89), channel_id=1, source_target_pairs={{0,16},{8,24},{16,0},{24,8},{1,17},{9,25},{17,1},{25,9},{2,18},{10... | collective-permute-start | bytes 1769480 | tf_op jit(solution)/shard_map/ppermute | solution.py:1417
  227.9 50.5 %collective-permute-start.9 = (bf16[2,96,1536]{2,1,0:T(8,128)(2,1)}, bf16[2,96,1536]{2,1,0:T(8,128)(2,1)}, u32[]{:S(2)}, u32[]{:S(2)}) collective-permute-start(bf16[2,96,1536]{2,1,0:T(8,128)(2,1)} %get-tuple-element.90), channel_id=1, source_target_pairs={{0,24},{8,0},{16,8},{24,16},{1,25},{9,1},{17,9},{25,17},{2,26},{10... | collective-permute-start | bytes 1769480 | tf_op jit(solution)/shard_map/ppermute | solution.py:1417
  230.8 1.8 copy-start.1
  232.4 44.6 %collective-permute-start.5 = (bf16[512,768]{1,0:T(8,128)(2,1)S(1)}, bf16[512,768]{1,0:T(8,128)(2,1)S(1)}, u32[]{:S(2)}, u32[]{:S(2)}) collective-permute-start(bf16[512,768]{1,0:T(8,128)(2,1)S(1)} %get-tuple-element.118), channel_id=1, source_target_pairs={{0,2},{2,0},{1,3},{3,1},{4,6},{6,4},{5,7},{7,5},{8,10},{10,8},{9,1... | collective-permute-start | bytes 2359304 | tf_op jit(solution)/shard_map/ppermute | solution.py:1421
  232.7 45.7 %collective-permute-start.10 = (bf16[4,384,384]{2,1,0:T(8,128)(2,1)S(1)}, bf16[4,384,384]{2,1,0:T(8,128)(2,1)}, u32[]{:S(2)}, u32[]{:S(2)}) collective-permute-start(bf16[4,384,384]{2,1,0:T(8,128)(2,1)S(1)} %copy-done.1), channel_id=1, source_target_pairs={{0,4},{4,0},{1,5},{5,1},{2,6},{6,2},{3,7},{7,3},{8,12},{12,8},{9,1... | collective-permute-start | bytes 3538952 | tf_op jit(solution)/shard_map/ppermute | solution.py:1417

commit v6 on v5

--- a/solution.py
+++ b/solution.py
@@ -209,7 +209,7 @@
             ],
         ),
         compiler_params=pltpu.CompilerParams(dimension_semantics=("arbitrary",), vmem_limit_bytes=60 << 20),
-        cost_estimate=pl.CostEstimate(flops=pairs * 8_000_000_000, bytes_accessed=pairs * 3_000_000, transcendentals=pairs * 4_000_000),
+        cost_estimate=pl.CostEstimate(flops=pairs * 40_000_000_000, bytes_accessed=pairs * 3_000_000, transcendentals=pairs * 4_000_000),
         name="attention_forward",
     )(place, segments, segments.reshape(1, length), tokens, weights, biases)
 
@@ -1064,7 +1064,7 @@
     size_x,
     tokens_ref,
     mine_ref,
-    other_ref,
+    other_hbm,
     cot_ref,
     vectors_ref,
     bias_inner_ref,
@@ -1072,14 +1072,15 @@
 ):
     inner_parts, outer_parts = refs[:size_x], refs[size_x : size_x + size_z]
     refs = refs[size_x + size_z :]
-    mixed_ref, pre_first_ref, grad_mine_ref, grad_other_ref, sums_ref, inner_sum_ref, grad_output_ref = refs[:7]
+    mixed_ref, pre_first_ref, grad_mine_ref, grad_far_hbm, sums_ref, inner_sum_ref, grad_output_ref = refs[:7]
     inner_terms = refs[7 : 7 + size_z]
     outer_terms = refs[7 + size_z : 7 + size_z + size_x]
     refs = refs[7 + size_z + size_x :]
     w_output, w_inner, w_outer, a_output, a_inner, a_outer, grad_out_buf = refs[:7]
     context, first_low, turned_low, normed, first, slope, active, work = refs[7:15]
     send_inner, send_outer, recv_inner, recv_outer = refs[15:19]
-    load_sem, share_send, share_recv, send_sem, recv_sem, store_sem = refs[19:]
+    far_rows, grad_send, swap_send, swap_recv = refs[19:23]
+    load_sem, share_send, share_recv, send_sem, recv_sem, store_sem = refs[23:]
     step, steps = pl.program_id(0), pl.num_programs(0)
     core_here = lax.axis_index("core")
     width, hidden = w_inner.shape
@@ -1130,6 +1131,7 @@
         barrier = pltpu.get_barrier_semaphore()
         pl.semaphore_signal(barrier, inc=1, device_id=twin, device_id_type=MESH_ID)
         pl.semaphore_wait(barrier, 1)
+        remote(other_hbm, far_rows, swap_send.at[0], swap_recv.at[0], twin).start()
         start_loads()
         a_output[...] = jnp.zeros_like(a_output)
         a_inner[...] = jnp.zeros_like(a_inner)
@@ -1145,7 +1147,15 @@
         sums_ref[8 * i : 8 * i + 8, :] += column_sum(value)
 
     context[:, pl.ds(pl.multiple_of(core_here * half, 128), half)] = mine_ref[...]
-    context[:, pl.ds(pl.multiple_of((1 - core_here) * half, 128), half)] = other_ref[...]
+
+    context_move = remote(other_hbm, far_rows, swap_send.at[0], swap_recv.at[0], twin)
+
+    @pl.when(step == 0)
+    def _():
+        context_move.wait()
+
+    here = pl.ds(pl.multiple_of(step * TILE, TILE), TILE)
+    context[:, pl.ds(pl.multiple_of((1 - core_here) * half, 128), half)] = far_rows[here, :]
 
     @pl.when(step == 0)
     def _():
@@ -1228,7 +1238,13 @@
     a_output[...] += dot_nn(context[...].T, grad_attended)
     context[...] = dot_nt(grad_attended, w_output[...]).astype(jnp.bfloat16)
     grad_mine_ref[...] = context[:, pl.ds(pl.multiple_of(core_here * half, 128), half)]
-    grad_other_ref[...] = context[:, pl.ds(pl.multiple_of((1 - core_here) * half, 128), half)]
+
+    def grad_move(t):
+        rows = pl.ds(pl.multiple_of(t * TILE, TILE), TILE)
+        return remote(grad_send.at[t], grad_far_hbm.at[rows, :], swap_send.at[1 + t], swap_recv.at[1 + t], twin)
+
+    grad_send[step] = context[:, pl.ds(pl.multiple_of((1 - core_here) * half, 128), half)]
+    grad_move(step).start()
 
     @pl.when(step == steps - 1)
     def _():
@@ -1265,6 +1281,8 @@
             send_outer[c] = (a_outer[part(c), columns] + recv_outer[c].astype(jnp.float32)).astype(jnp.bfloat16)
             for copy in outer_out(c):
                 copy.start()
+        for t in range(grad_send.shape[0]):
+            grad_move(t).wait()
         for c in range(chunks):
             pltpu.make_async_copy(send_inner.at[c], send_inner.at[c], store_sem.at[0, c]).wait()
             pltpu.make_async_copy(send_outer.at[c], send_outer.at[c], store_sem.at[1, c]).wait()
@@ -1308,7 +1326,7 @@
             in_specs=[
                 tile,
                 half_tile,
-                half_tile,
+                anywhere,
                 tile,
                 whole((16, width)),
                 whole((1, hidden)),
@@ -1318,7 +1336,7 @@
                 tile,
                 tile,
                 half_tile,
-                half_tile,
+                anywhere,
                 whole((48, width)),
                 whole((8, hidden)),
                 whole((width, width)),
@@ -1344,6 +1362,10 @@
                 halves,
                 halves,
                 halves,
+                pltpu.VMEM((local, half), low),
+                pltpu.VMEM((steps, TILE, half), low),
+                dma((1 + steps,)),
+                dma((1 + steps,)),
                 dma((1 + 2 * chunks,)),
                 dma((1 + 2 * chunks,)),
                 dma((1 + 2 * chunks,)),
@@ -1716,17 +1738,16 @@
         size_x,
         inputs_all,
         context_mine,
-        swap(context_other, "core"),
+        context_other,
         cotangent_all.reshape(local, width),
         rows,
         inner_row,
         inner_parts,
         outer_parts,
     )
-    mixed, pre_first, upstream_mine, upstream_send, dense_sums, inner_sums, grad_w_output = made[:7]
+    mixed, pre_first, upstream_mine, upstream_other, dense_sums, inner_sums, grad_w_output = made[:7]
     inner_terms = [made[7]] + [shift(made[7 + k], "z", k) for k in range(1, size_z)]
     outer_terms = [made[7 + size_z]] + [shift(made[7 + size_z + j], "x", j) for j in range(1, size_x)]
-    upstream_other = swap(upstream_send, "core")
     mixed_out = in_order(y == 0, mixed[None, :part], swap(mixed[part:], "y")[None], 0)
 
     grads, sums = attention_back(place, segments, projected, context_mine, context_other, upstream_mine, upstream_other, logsum)

time: 361 us -> 310 us (0.86)
  waiting for transfers between devices: 51.5 us -> 0.02 us
  Pallas kernels: 281 us -> 292 us
  starting transfers between devices: 18.5 us -> 10.2 us
    ppermute x8, waiting for transfers between devices: 51.5 us -> 0.02 us  [shift(): lax.ppermute(piece, axis, [(i, (i + step) % size) for i in range(size)])]
    pallas_call x1, Pallas kernels: 43.5 us -> 54.2 us  [attention_back(): pl.pallas_call(backward_kernel, out_shape=(jax.ShapeDtypeStruct((length,...]
    pallas_call x1, Pallas kernels: 73.6 us -> 63.9 us  [exit_call(): pl.pallas_call(lambda *refs: exit_kernel(size_z, size_x, shapes, *refs),...]
    ppermute x8, starting transfers between devices: 17.8 us -> 8.97 us  [shift(): lax.ppermute(piece, axis, [(i, (i + step) % size) for i in range(size)])]
    pallas_call x1, Pallas kernels: 40.3 us -> 49 us  [attention(): pl.pallas_call(forward_kernel, out_shape=(jax.ShapeDtypeStruct((rows, pai...]
  transfers between devices with their start and end apart: 11 -> 9, of which waited for: 2 -> 0; matrix products, arithmetic and copies ran while one was open for 1% -> 1% of each run, Pallas kernels for 23% -> 33%
where the time goes in v6:
time: 310 us
  Pallas kernels  292 us (94%)
  starting transfers between devices  10.2 us (3%)
  local copies, waits for them, and re-layouts  3.44 us (1%)
  other arithmetic  3.16 us (1%)
    pallas_call x1, Pallas kernels, dense_layer(): pl.pallas_call(lambda *refs: dense_kernel(size_z, size_x, *refs), out_sha...  65.2 us
    pallas_call x1, Pallas kernels, exit_call(): pl.pallas_call(lambda *refs: exit_kernel(size_z, size_x, shapes, *refs),...  63.9 us
    pallas_call x1, Pallas kernels, attention_back(): pl.pallas_call(backward_kernel, out_shape=(jax.ShapeDtypeStruct((length,...  54.2 us
    pallas_call x1, Pallas kernels, entry(): pl.pallas_call(lambda *refs: entry_kernel(size_z, size_x, count, *refs),...  53.6 us
    pallas_call x1, Pallas kernels, attention(): pl.pallas_call(forward_kernel, out_shape=(jax.ShapeDtypeStruct((rows, pai...  49 us
    ppermute x8, starting transfers between devices, shift(): lax.ppermute(piece, axis, [(i, (i + step) % size) for i in range(size)])  8.97 us
    pallas_call x1, Pallas kernels, deliver(): pl.pallas_call(lambda *refs: deliver_kernel(count, *refs), out_shape=tupl...  6.39 us
  transfers between devices with their start and end apart: 9, of which 0 were waited for; matrix products, arithmetic and copies ran while one was open for 1% of the time, Pallas kernels for 33%

profile of v6, /device:TPU:0, one launch (start us, length us, event | category | flops | bytes accessed | tf_op | source)
XLA Modules:
  0.0 309.8 jit_solution(470040309399376906)
XLA Ops:
  0.7 0.0 copy-start
  0.7 1.3 reshape.107.refs_13_
  1.9 53.6 %entry.1 = (bf16[4,512,768]{2,1,0:T(8,128)(2,1)}, bf16[2,512,768]{2,1,0:T(8,128)(2,1)}, bf16[8,96,1152]{2,1,0:T(8,128)(2,1)}, bf16[4,96,1920]{2,1,0:T(8,128)(2,1...) custom-call(bf16[2,512,768]{2,1,0:T(8,128)(2,1)} %refs_0_.1, bf16[2,512,768]{2,1,0:T(8,128)(2,1)} %refs_1_.1, ...), custom_call_target="tpu_custom_call" | custom-call | tf_op jit(solution)/shard_map/entry/pallas_call | solution.py:621
  55.5 1.5 collective-permute-start.3
  57.0 0.6 collective-permute-start.2
  57.6 1.5 collective-permute-start.1
  59.1 1.5 collective-permute-start
  60.6 0.5 compare_select_fusion.1.place_ref
  61.1 0.6 constant_dynamic-slice_fusion.row_ref
  61.7 49.0 %attention_forward.1 = (bf16[1024,384]{1,0:T(8,128)(2,1)}, bf16[1024,384]{1,0:T(8,128)(2,1)}, f32[24,2048]{1,0:T(8,128)}, bf16[2048,1152]{1,0:T(8,128)(2,1)}) custom-call(s32[5]{0:T(128)} %compare_select_fusion.1.place_ref, s32[2048]{0:T(1024)} %bitcast.31, s32[1,2048]{1,0:T(1,128)} %constant_dynamic-slice_fusion.row_ref, bf16[2048,768]{1,0:T(8,128)(2,1)} %bitcast.24, ...), custom_call_target="tpu_custom_call" | custom-call | flops 120000004096 | bytes 9000000 | tf_op jit(solution)/shard_map/attention_forward/pallas_call | solution.py:175
  110.6 0.0 collective-permute-done.3.refs_11_
  110.6 0.0 collective-permute-done.1.refs_9_
  110.7 65.2 %dense_layer.1 = (bf16[1024,768]{1,0:T(8,128)(2,1)}, f32[1024,768]{1,0:T(8,128)}, bf16[1024,384]{1,0:T(8,128)(2,1)}, bf16[1024,384]{1,0:T(8,128)(2,1)}, f32[48,7...) custom-call(bf16[2048,768]{1,0:T(8,128)(2,1)} %bitcast.25, ...), custom_call_target="tpu_custom_call" | custom-call | flops 32000000000 | bytes 40000000 | tf_op jit(solution)/shard_map/dense_layer/pallas_call | solution.py:1310
  175.9 1.6 slice_bitcast_fusion
  177.5 0.1 collective-permute-start.5
  177.5 0.4 collective-permute-start.6
  177.9 3.4 %collective-permute-start.7 = (bf16[2,96,1536]{2,1,0:T(8,128)(2,1)}, bf16[2,96,1536]{2,1,0:T(8,128)(2,1)}, u32[]{:S(2)}, u32[]{:S(2)}) collective-permute-start(bf16[2,96,1536]{2,1,0:T(8,128)(2,1)} %get-tuple-element.90), channel_id=1, source_target_pairs={{0,24},{8,0},{16,8},{24,16},{1,25},{9,1},{17,9},{25,17},{2,26},{10... | collective-permute-start | bytes 1769480 | tf_op jit(solution)/shard_map/ppermute | solution.py:1439
  181.4 1.2 collective-permute-start.4
  182.6 0.0 collective-permute-start.8
  182.6 54.2 %attention_backward.1 = (bf16[2048,1152]{1,0:T(8,128)(2,1)}, f32[24,384]{1,0:T(8,128)}) custom-call(s32[5]{0:T(128)} %compare_select_fusion.1.place_ref, s32[2048]{0:T(1024)} %bitcast.32, bf16[2048,1152]{1,0:T(8,128)(2,1)} %get-tuple-element.77.qkv_ref, bf16[1024,384]{1,0:T(8,128)(2,1)} %get-tuple-element.70.refs_1_.ctx_mine_ref, ...), custom_call_target="tpu_custom_call" | custom-call | flops 60000002048 | bytes 15000000 | tf_op jit(solution)/shard_map/attention_backward/pallas_call | solution.py:343
  236.9 1.4 maximum_select_fusion
  238.3 63.9 %exit.1 = (f32[2,512,768]{2,1,0:T(8,128)}, f32[96,768]{1,0:T(8,128)}, f32[96,768]{1,0:T(8,128)}, f32[96,768]{1,0:T(8,128)}, f32[96,768]{1,0:T(8,128)}, /*index=5...) custom-call(bf16[2048,1152]{1,0:T(8,128)(2,1)} %get-tuple-element.81.refs_0_, bf16[2048,768]{1,0:T(8,128)(2,1)} %bitcast.26, ...), custom_call_target="tpu_custom_call" | custom-call | tf_op jit(solution)/shard_map/exit/pallas_call | solution.py:1029
  302.1 6.4 %deliver.1 = (f32[2,512,768]{2,1,0:T(8,128)}, f32[96,768]{1,0:T(8,128)}, f32[96,768]{1,0:T(8,128)}, f32[96,768]{1,0:T(8,128)}, f32[96,768]{1,0:T(8,128)}, /*inde...) custom-call(f32[2,512,768]{2,1,0:T(8,128)} %get-tuple-element.93.ref, ...), custom_call_target="tpu_custom_call" | custom-call | tf_op jit(solution)/shard_map/deliver/pallas_call | solution.py:953
  308.5 1.3 reduce
  (10 shorter events, 0.0 us)
Async XLA Ops:
  0.7 60.4 %copy-start = (s32[2,2048]{1,0:T(2,128)S(1)}, s32[2,2048]{1,0:T(2,128)}, u32[]{:S(2)}) copy-start(s32[2,2048]{1,0:T(2,128)} %param.19) | copy-start | bytes 49156
  55.5 55.1 %collective-permute-start.3 = (bf16[2,384,384]{2,1,0:T(8,128)(2,1)}, bf16[2,384,384]{2,1,0:T(8,128)(2,1)}, u32[]{:S(2)}, u32[]{:S(2)}) collective-permute-start(bf16[2,384,384]{2,1,0:T(8,128)(2,1)} %get-tuple-element.75.refs_8_), channel_id=1, source_target_pairs={{0,24},{8,0},{16,8},{24,16},{1,25},{9,1},{17,9},{25,17},{2,26},{10... | collective-permute-start | bytes 1769480 | tf_op jit(solution)/shard_map/ppermute | solution.py:1439
  57.0 53.6 %collective-permute-start.2 = (bf16[2,384,384]{2,1,0:T(8,128)(2,1)}, bf16[2,384,384]{2,1,0:T(8,128)(2,1)}, u32[]{:S(2)}, u32[]{:S(2)}) collective-permute-start(bf16[2,384,384]{2,1,0:T(8,128)(2,1)} %get-tuple-element.75.refs_8_), channel_id=1, source_target_pairs={{0,16},{8,24},{16,0},{24,8},{1,17},{9,25},{17,1},{25,9},{2,18},{10... | collective-permute-start | bytes 1769480 | tf_op jit(solution)/shard_map/ppermute | solution.py:1439
  57.6 53.0 %collective-permute-start.1 = (bf16[2,384,384]{2,1,0:T(8,128)(2,1)}, bf16[2,384,384]{2,1,0:T(8,128)(2,1)}, u32[]{:S(2)}, u32[]{:S(2)}) collective-permute-start(bf16[2,384,384]{2,1,0:T(8,128)(2,1)} %get-tuple-element.75.refs_8_), channel_id=1, source_target_pairs={{0,8},{8,16},{16,24},{24,0},{1,9},{9,17},{17,25},{25,1},{2,10},{10... | collective-permute-start | bytes 1769480 | tf_op jit(solution)/shard_map/ppermute | solution.py:1439
  59.1 51.6 %collective-permute-start = (bf16[4,96,1920]{2,1,0:T(8,128)(2,1)}, bf16[4,96,1920]{2,1,0:T(8,128)(2,1)}, u32[]{:S(2)}, u32[]{:S(2)}) collective-permute-start(bf16[4,96,1920]{2,1,0:T(8,128)(2,1)} %get-tuple-element.74.refs_6_), channel_id=1, source_target_pairs={{0,4},{4,0},{1,5},{5,1},{2,6},{6,2},{3,7},{7,3},{8,12},{12,8},{9,1... | collective-permute-start | bytes 4423688 | tf_op jit(solution)/shard_map/ppermute | solution.py:1439
  175.9 6.7 %copy-start.1 = (bf16[4,384,384]{2,1,0:T(8,128)(2,1)S(1)}, bf16[4,384,384]{2,1,0:T(8,128)(2,1)}, u32[]{:S(2)}) copy-start(bf16[4,384,384]{2,1,0:T(8,128)(2,1)} %get-tuple-element.92) | copy-start | bytes 3538948
  177.5 60.8 %collective-permute-start.5 = (bf16[2,96,1536]{2,1,0:T(8,128)(2,1)}, bf16[2,96,1536]{2,1,0:T(8,128)(2,1)}, u32[]{:S(2)}, u32[]{:S(2)}) collective-permute-start(bf16[2,96,1536]{2,1,0:T(8,128)(2,1)} %get-tuple-element.88), channel_id=1, source_target_pairs={{0,8},{8,16},{16,24},{24,0},{1,9},{9,17},{17,25},{25,1},{2,10},{10... | collective-permute-start | bytes 1769480 | tf_op jit(solution)/shard_map/ppermute | solution.py:1439
  177.5 60.7 %collective-permute-start.6 = (bf16[2,96,1536]{2,1,0:T(8,128)(2,1)}, bf16[2,96,1536]{2,1,0:T(8,128)(2,1)}, u32[]{:S(2)}, u32[]{:S(2)}) collective-permute-start(bf16[2,96,1536]{2,1,0:T(8,128)(2,1)} %get-tuple-element.89), channel_id=1, source_target_pairs={{0,16},{8,24},{16,0},{24,8},{1,17},{9,25},{17,1},{25,9},{2,18},{10... | collective-permute-start | bytes 1769480 | tf_op jit(solution)/shard_map/ppermute | solution.py:1439
  177.9 60.3 %collective-permute-start.7 = (bf16[2,96,1536]{2,1,0:T(8,128)(2,1)}, bf16[2,96,1536]{2,1,0:T(8,128)(2,1)}, u32[]{:S(2)}, u32[]{:S(2)}) collective-permute-start(bf16[2,96,1536]{2,1,0:T(8,128)(2,1)} %get-tuple-element.90), channel_id=1, source_target_pairs={{0,24},{8,0},{16,8},{24,16},{1,25},{9,1},{17,9},{25,17},{2,26},{10... | collective-permute-start | bytes 1769480 | tf_op jit(solution)/shard_map/ppermute | solution.py:1439
  181.4 55.5 %collective-permute-start.4 = (bf16[512,768]{1,0:T(8,128)(2,1)S(1)}, bf16[512,768]{1,0:T(8,128)(2,1)S(1)}, u32[]{:S(2)}, u32[]{:S(2)}) collective-permute-start(bf16[512,768]{1,0:T(8,128)(2,1)S(1)} %get-tuple-element.118), channel_id=1, source_target_pairs={{0,2},{2,0},{1,3},{3,1},{4,6},{6,4},{5,7},{7,5},{8,10},{10,8},{9,1... | collective-permute-start | bytes 2359304 | tf_op jit(solution)/shard_map/ppermute | solution.py:1443
  182.6 55.7 %collective-permute-start.8 = (bf16[4,384,384]{2,1,0:T(8,128)(2,1)S(1)}, bf16[4,384,384]{2,1,0:T(8,128)(2,1)}, u32[]{:S(2)}, u32[]{:S(2)}) collective-permute-start(bf16[4,384,384]{2,1,0:T(8,128)(2,1)S(1)} %copy-done.1), channel_id=1, source_target_pairs={{0,4},{4,0},{1,5},{5,1},{2,6},{6,2},{3,7},{7,3},{8,12},{12,8},{9,1... | collective-permute-start | bytes 3538952 | tf_op jit(solution)/shard_map/ppermute | solution.py:1439

commit v7 on v6

--- a/solution.py
+++ b/solution.py
@@ -21,12 +21,18 @@
     return jnp.dot(a, b, preferred_element_type=jnp.float32)
 
 
-def part_rows(place_ref, part, rows):
-    return pl.ds(pl.multiple_of(place_ref[part], 128), rows)
+def local_start(b, part):
+    core, y = lax.axis_index("core"), lax.axis_index("y")
+    return (jnp.where(b % 2 == core, 0, 2) + jnp.where(b // 2 == y, 0, 1)) * part
+
+
+def part_rows(b, part):
+    return pl.ds(pl.multiple_of(local_start(b, part), 128), part)
 
 
 def find_bounds(segment_ref, bound_ref):
-    length = segment_ref.shape[0]
+    length = segment_ref.shape[1]
+    y = lax.axis_index("y")
     bound_ref[0] = 0
     bound_ref[DOCUMENTS] = length
     for d in range(1, DOCUMENTS):
@@ -34,7 +40,7 @@
         def halve(_, span):
             low, high = span
             middle = (low + high) // 2
-            below = segment_ref[jnp.minimum(middle, length - 1)] < d
+            below = segment_ref[y, jnp.minimum(middle, length - 1)] < d
             inside = low < high
             return (
                 jnp.where(jnp.logical_and(inside, below), middle + 1, low),
@@ -46,9 +52,10 @@
 
 
 def find_window(segment_ref, bound_ref, qb):
-    length = segment_ref.shape[0]
-    first = segment_ref[qb * BLK]
-    last = segment_ref[qb * BLK + BLK - 1]
+    length = segment_ref.shape[1]
+    y = lax.axis_index("y")
+    first = segment_ref[y, qb * BLK]
+    last = segment_ref[y, qb * BLK + BLK - 1]
     start = bound_ref[first] // 128 * 128
     count = (bound_ref[last + 1] - start + BLK - 1) // BLK
     return jnp.minimum(start, length - count * BLK), count
@@ -68,19 +75,20 @@
 
 def make_marks(row_ref, mark_query, mark_key):
     length = mark_key.shape[0]
+    y = lax.axis_index("y")
     step = 512
     for b in range(length // step):
         rows = slice(b * step, (b + 1) * step)
-        column = jnp.broadcast_to(row_ref[0:1, rows], (128, step)).T
+        column = jnp.broadcast_to(row_ref[pl.ds(y, 1), rows], (128, step)).T
         lane = lax.broadcasted_iota(jnp.int32, (step, 128), 1) % 64
         same = lane == column
         line = lax.broadcasted_iota(jnp.int32, (128, step), 0) % 64
-        mark_query[:, rows] = jnp.where(line == row_ref[0:1, rows], 1.0, 0.0).astype(jnp.bfloat16)
+        mark_query[:, rows] = jnp.where(line == row_ref[pl.ds(y, 1), rows], 1.0, 0.0).astype(jnp.bfloat16)
         apart = jnp.logical_and(lane < DOCUMENTS, jnp.logical_not(same))
         mark_key[rows, :] = jnp.where(apart, BIG, 0.0).astype(jnp.bfloat16)
 
 
-def forward_kernel(place_ref, segment_ref, row_ref, tokens_ref, weights_ref, bias_ref, *refs):
+def forward_kernel(segment_ref, row_ref, tokens_ref, weights_ref, bias_ref, *refs):
     mine_ref, other_ref, lse_ref, qkv_ref, q2, k2, vt, acc, top, tot, keep, mark_query, mark_key, bound_ref = refs
     length = qkv_ref.shape[0]
     blocks = length // BLK
@@ -93,10 +101,10 @@
 
     low = lax.broadcasted_iota(jnp.int32, (part, 128), 1) < 64
     for b in range(4):
-        src = part_rows(place_ref, b, part)
+        src = part_rows(b, part)
         dst = slice(b * part, (b + 1) * part)
         made = dot_nn(tokens_ref[src, :], weights_ref[...])
-        lanes = pl.ds(pl.multiple_of(place_ref[4] * (128 * pl.num_programs(0)) + pl.program_id(0) * 128, 128), 128)
+        lanes = pl.ds(pl.multiple_of(lax.axis_index("core") * (128 * pl.num_programs(0)) + pl.program_id(0) * 128, 128), 128)
         q = ((made[:, 0:128] + bias_ref[0:1, lanes]) * 0.125).astype(jnp.bfloat16)
         k = made[:, 128:256].astype(jnp.bfloat16)
         v = (made[:, 256:384] + bias_ref[1:2, lanes]).astype(jnp.bfloat16)
@@ -151,7 +159,7 @@
             total = jnp.sum(tot[h], axis=0, keepdims=True)
             acc[rows, :] = acc[rows, :] / total
             lse_ref[h : h + 1, qs] = largest[h] + jnp.log(total)
-        where = place_ref[qb * BLK // part] + qb * BLK % part
+        where = local_start(qb * BLK // part, part) + qb * BLK % part
         result = acc[...].T.astype(jnp.bfloat16)
 
         @pl.when(where < 2 * part)
@@ -167,7 +175,7 @@
     lax.fori_loop(0, blocks, row, 0)
 
 
-def attention(place, segments, tokens, weights, biases):
+def attention(segments, tokens, weights, biases):
     length, depth = tokens.shape
     width = weights.shape[1]
     pairs = width // 384
@@ -181,10 +189,10 @@
             jax.ShapeDtypeStruct((length, width), jnp.bfloat16),
         ),
         grid_spec=pltpu.PrefetchScalarGridSpec(
-            num_scalar_prefetch=2,
+            num_scalar_prefetch=1,
             grid=(pairs,),
             in_specs=[
-                pl.BlockSpec((1, length), lambda p, *_: (0, 0)),
+                pl.BlockSpec(segments.shape, lambda p, *_: (0, 0)),
                 pl.BlockSpec((length, depth), lambda p, *_: (0, 0)),
                 pl.BlockSpec((depth, 384), lambda p, *_: (0, p)),
                 pl.BlockSpec(biases.shape, lambda p, *_: (0, 0)),
@@ -211,11 +219,10 @@
         compiler_params=pltpu.CompilerParams(dimension_semantics=("arbitrary",), vmem_limit_bytes=60 << 20),
         cost_estimate=pl.CostEstimate(flops=pairs * 40_000_000_000, bytes_accessed=pairs * 3_000_000, transcendentals=pairs * 4_000_000),
         name="attention_forward",
-    )(place, segments, segments.reshape(1, length), tokens, weights, biases)
+    )(segments, segments, tokens, weights, biases)
 
 
 def backward_kernel(
-    place_ref,
     segment_ref,
     qkv_ref,
     ctx_mine_ref,
@@ -253,7 +260,7 @@
     low = lax.broadcasted_iota(jnp.int32, (part, 128), 1) < 64
 
     def prepare(b, do, ctx):
-        src = part_rows(place_ref, b, part)
+        src = part_rows(b, part)
         dst = slice(b * part, (b + 1) * part)
         q, k = qkv_ref[src, 0:128], qkv_ref[src, 128:256]
         zero = jnp.zeros_like(q)
@@ -283,14 +290,14 @@
 
     for b in range(4):
 
-        @pl.when(place_ref[b] < 2 * part)
+        @pl.when(local_start(b, part) < 2 * part)
         def _():
-            rows = part_rows(place_ref, b, part)
+            rows = part_rows(b, part)
             prepare(b, do_mine_ref[rows, :], ctx_mine_ref[rows, :])
 
-        @pl.when(place_ref[b] >= 2 * part)
+        @pl.when(local_start(b, part) >= 2 * part)
         def _():
-            rows = pl.ds(pl.multiple_of(place_ref[b] - 2 * part, 128), part)
+            rows = pl.ds(pl.multiple_of(local_start(b, part) - 2 * part, 128), part)
             prepare(b, do_other_ref[rows, :], ctx_other_ref[rows, :])
 
     dk[...] = jnp.zeros_like(dk)
@@ -322,7 +329,7 @@
     lax.fori_loop(0, blocks, row, 0)
     sums = [jnp.zeros((1, 128), jnp.float32) for _ in range(3)]
     for b in range(4):
-        dst = part_rows(place_ref, b, part)
+        dst = part_rows(b, part)
         src = slice(b * part, (b + 1) * part)
         pieces = ((dqt[:, src].T * 0.125).astype(jnp.bfloat16), dk[src, :].astype(jnp.bfloat16), dv[src, :].astype(jnp.bfloat16))
         for i, piece in enumerate(pieces):
@@ -333,7 +340,7 @@
         sum_ref[0:1, 128 * i : 128 * i + 128] = sums[i]
 
 
-def attention_back(place, segments, qkv, ctx_mine, ctx_other, do_mine, do_other, lse):
+def attention_back(segments, qkv, ctx_mine, ctx_other, do_mine, do_other, lse):
     length, width = qkv.shape
     pairs = width // 384
     rows = length // 2
@@ -347,7 +354,7 @@
             jax.ShapeDtypeStruct((pairs * 8, 384), jnp.float32),
         ),
         grid_spec=pltpu.PrefetchScalarGridSpec(
-            num_scalar_prefetch=2,
+            num_scalar_prefetch=1,
             grid=(pairs,),
             in_specs=[
                 pl.BlockSpec((length, 384), lambda p, *_: (0, p)),
@@ -356,7 +363,7 @@
                 column,
                 column,
                 pl.BlockSpec((8, length), lambda p, *_: (p, 0)),
-                pl.BlockSpec((1, length), lambda p, *_: (0, 0)),
+                pl.BlockSpec(segments.shape, lambda p, *_: (0, 0)),
             ],
             out_specs=[
                 pl.BlockSpec((length, 384), lambda p, *_: (0, p)),
@@ -382,7 +389,7 @@
         compiler_params=pltpu.CompilerParams(dimension_semantics=("arbitrary",), vmem_limit_bytes=60 << 20),
         cost_estimate=pl.CostEstimate(flops=pairs * 20_000_000_000, bytes_accessed=pairs * 5_000_000, transcendentals=pairs * 4_000_000),
         name="attention_backward",
-    )(place, segments, qkv, ctx_mine, ctx_other, do_mine, do_other, lse, segments.reshape(1, length))
+    )(segments, qkv, ctx_mine, ctx_other, do_mine, do_other, lse, segments)
 
 
 MESH_ID = pl.DeviceIdType.MESH
@@ -424,10 +431,10 @@
 def entry_kernel(size_z, size_x, count, *refs):
     tokens, cotangent, wq, wk, wv, w_inner, w_output, w_outer = refs[:8]
     vectors = refs[8 : 8 + count]
-    tokens_all, cotangent_all, weights_all, inner_all, outer_all, rows_out, inner_out = refs[8 + count : 15 + count]
+    tokens_all, cotangent_send, weights_all, inner_all, outer_all, rows_out, inner_out = refs[8 + count : 15 + count]
     raw = refs[15 + count : 15 + 2 * count]
     stage, cot_stage, wbuf, ibuf, obuf, pack, ipack, opack, vpack, vectors_all = refs[15 + 2 * count : 25 + 2 * count]
-    local_sem, load_sem, tsend, trecv, zsend, zrecv, xsend, xrecv, osend, orecv = refs[25 + 2 * count :]
+    local_sem, load_sem, tsend, trecv, zsend, zrecv, xsend, xrecv, ysend, yrecv, osend, orecv = refs[25 + 2 * count :]
     z, x, y, core = place_of()
     half = pack.shape[1] // 3
     pairs = half // 128
@@ -449,7 +456,7 @@
     late.append(pltpu.make_async_copy(w_output.at[:, mine], ibuf.at[:, pl.ds(chunks * half, half)], load_sem.at[3 + count + chunks]))
     late.append(pltpu.make_async_copy(w_outer.at[:, mine], obuf, load_sem.at[4 + count + chunks]))
     load = pltpu.make_async_copy(tokens.at[y], stage, local_sem.at[0])
-    cot_load = pltpu.make_async_copy(cotangent.at[y], cot_stage, local_sem.at[4])
+    cot_load = pltpu.make_async_copy(cotangent.at[1 - y], cot_stage, local_sem.at[4])
     for copy in loads + late + [load, cot_load]:
         copy.start()
     vpack[...] = jnp.zeros_like(vpack)
@@ -467,11 +474,20 @@
     across.start()
     beside = remote(tokens.at[y], tokens_all.at[2], tsend.at[1], trecv.at[1], partner(core=1 - core))
 
-    packs = (pack, vpack, ipack)
+    rows = ipack.shape[0]
+
+    def share(owner):
+        return pl.ds(pl.multiple_of(owner * (rows // 2), rows // 2), rows // 2)
+
+    packs = (pack, vpack, ipack.at[share(y), :])
+
+    def y_move(index, origin):
+        slot = home(2, origin)
+        return remote(slot, slot, ysend.at[index], yrecv.at[index], partner(y=1 - y))
 
     def home(stream, origin):
         if stream == 2:
-            return inner_all.at[origin]
+            return inner_all.at[origin, share(y), :]
         return (weights_all, vectors_all)[stream].at[origin * size_x + x]
 
     def z_move(stream, way, t):
@@ -535,7 +551,7 @@
     load.wait()
     keeps.append(pltpu.make_async_copy(stage, tokens_all.at[0], local_sem.at[3]))
     cot_load.wait()
-    keeps.append(pltpu.make_async_copy(cot_stage, cotangent_all.at[0], local_sem.at[5]))
+    keeps.append(pltpu.make_async_copy(cot_stage, cotangent_send, local_sem.at[5]))
     for keep in keeps:
         keep.start()
 
@@ -553,9 +569,10 @@
                 if sideways:
                     for move in x_moves(1 + way * (size_z - 1) + t - 1, origin, False):
                         move.start()
+                else:
+                    y_move(way * (size_z - 1) + t - 1, origin).start()
 
     onward = remote(tokens_all.at[1], tokens_all.at[3], tsend.at[2], trecv.at[2], partner(core=1 - core))
-    later = remote(cotangent.at[1 - y], cotangent_all.at[1], tsend.at[3], trecv.at[3], partner(y=1 - y))
     for t in range(1, size_z):
         arrive((0, 1), t, True)
         if t < size_z - 1:
@@ -569,7 +586,6 @@
         if t == min(2, size_z - 1):
             across.wait_recv()
             onward.start()
-            later.start()
 
     for move in x_moves(0, z, True):
         move.wait()
@@ -581,6 +597,7 @@
                 origin = z - (1 - 2 * way) * t
                 for move in x_moves(1 + way * (size_z - 1) + t - 1, origin, False):
                     move.wait()
+                y_move(way * (size_z - 1) + t - 1, origin).wait()
 
             @pl.when(sends(way, t))
             def _():
@@ -597,7 +614,6 @@
     across.wait_send()
     beside.wait()
     onward.wait()
-    later.wait()
     for keep in keeps:
         keep.wait()
 
@@ -622,7 +638,7 @@
         lambda *refs: entry_kernel(size_z, size_x, count, *refs),
         out_shape=(
             jax.ShapeDtypeStruct((4, part, width), low),
-            jax.ShapeDtypeStruct((2, part, width), low),
+            jax.ShapeDtypeStruct((part, width), low),
             jax.ShapeDtypeStruct((shards, rows, lanes), low),
             jax.ShapeDtypeStruct((size_z, rows, mixed_lanes), low),
             jax.ShapeDtypeStruct((size_x, long, half), low),
@@ -651,6 +667,8 @@
             dma((3, 2, size_z - 1)),
             dma((2, 2 * size_z - 1, side)),
             dma((2, 2 * size_z - 1, side)),
+            dma((2 * size_z - 2,)),
+            dma((2 * size_z - 2,)),
             dma((side,)),
             dma((side,)),
         ],
@@ -661,34 +679,31 @@
 
 def exit_kernel(size_z, size_x, shapes, *refs):
     z, x, y, core = place_of()
-    names = list(shapes)
     grads_hbm, inputs_hbm, weights_hbm, base_hbm, output_term, dense_sums, inner_sums, head_sums = refs[:8]
     inner_in = refs[8 : 8 + size_z]
     outer_in = refs[8 + size_z : 8 + size_z + size_x]
     refs = refs[8 + size_z + size_x :]
     results = refs[:8]
-    token_grads, grad_query, grad_key, grad_value, grad_output, grad_inner, grad_outer, vector_sums = refs[8:16]
+    made = refs[8:16]
+    token_grads, grad_query, grad_key, grad_value, grad_output, grad_inner, grad_outer, vector_sums = made
     grads, inputs, turned, weights, base, terms, other_rows, recv_rows, send_rows, far_rows, odd = refs[16:27]
-    inner_buf, outer_buf, vector_rows, vector_terms, store_sem = refs[27:32]
-    load_sem, tsend, trecv, osend, orecv = refs[32:37]
-    refs = refs[37:]
-    made = (token_grads, grad_query, grad_key, grad_value, grad_output, grad_inner, grad_outer, vector_sums)
+    inner_buf, outer_buf, vector_rows, vector_terms, inner_send, store_sem = refs[27:33]
+    load_sem, tsend, trecv, osend, orecv = refs[33:38]
+    refs = list(refs[38:])
     stores = [pltpu.make_async_copy(a, b, store_sem.at[i]) for i, (a, b) in enumerate(zip(made, results))]
-    xin, xsend, xrecv, xout = {}, {}, {}, {}
+    xin, xsend, xrecv = {}, {}, {}
     zout, zin, zsend, zrecv = {}, {}, {}, {}
     ybuf, ysend, yrecv, cbuf, csend, crecv = {}, {}, {}, {}, {}, {}
-    refs = list(refs)
-    for name in names:
+    for name in shapes:
         ybuf[name], ysend[name], yrecv[name], cbuf[name], csend[name], crecv[name] = [refs.pop(0) for _ in range(6)]
         if name != "outer":
             xin[name], xsend[name], xrecv[name] = [refs.pop(0) for _ in range(3)]
         if name != "inner":
             zout[name], zin[name], zsend[name], zrecv[name] = [refs.pop(0) for _ in range(4)]
-    xout["inner"] = refs.pop(0)
-
-    shards, rows, lanes = terms.shape
-    half = lanes // 3
-    width = 2 * half
+
+    shards, rows, full = terms.shape
+    half = full // 4
+    lanes = 3 * half
     pairs = half // 128
     hidden = grad_inner.shape[1]
     part = token_grads.shape[1]
@@ -696,12 +711,9 @@
     low, high = jnp.bfloat16, jnp.float32
     mine = pl.ds(pl.multiple_of(core * half, 128), half)
     theirs = pl.ds(pl.multiple_of((1 - core) * half, 128), half)
-    order = sorted(range(size_z), key=lambda k: -min(k, size_z - k))
-    far_order = [k for k in order if k > 0]
     columns = [lax.rem(x + j, size_x) for j in range(size_x)]
-
-    def slot_of(k, j):
-        return lax.rem(z + k, size_z) * size_x + columns[j]
+    steps = [(t, way) for t in range(1, size_z) for way in range(2)]
+    core_peer, y_peer = partner(core=1 - core), partner(y=1 - y)
 
     loads = {}
     for i, src in enumerate(inner_in):
@@ -714,30 +726,113 @@
         loads[name] = pltpu.make_async_copy(src, dst, load_sem.at[size_z + size_x + i])
     for load in loads.values():
         load.start()
-    greet(True)
-
-    core_peer, y_peer = partner(core=1 - core), partner(y=1 - y)
-    outputs = remote(output_term.at[:, :, theirs], odd, osend, orecv, core_peer)
-    outputs.start()
-    sideways = {}
-    along = {}
-    kept = {}
-
-    def send_x(name, n, k, j, src, dst):
-        move = remote(src, dst, xsend[name].at[n, k, j - 1], xrecv[name].at[n, k, j - 1], partner(x=columns[j]))
-        move.start()
-        sideways.setdefault((name, k, j), []).append(move)
-
-    def send_z(name, k):
-        move = remote(
-            zout[name].at[k - 1],
-            zin[name].at[k - 1],
-            zsend[name].at[k - 1],
-            zrecv[name].at[k - 1],
-            partner(z=lax.rem(z + k, size_z)),
+
+    def inside(v):
+        return jnp.logical_and(v >= 0, v < size_z)
+
+    def target_of(t, way):
+        return z + (1 - 2 * way) * (size_z - t)
+
+    def fed(way):
+        return inside(z - (1 - 2 * way))
+
+    def x_move(name, n, at, j, src, dst):
+        return remote(src, dst, xsend[name].at[n, at, j - 1], xrecv[name].at[n, at, j - 1], partner(x=columns[j]))
+
+    def x_pieces(name, at):
+        source = vector_terms if name == "vec" else terms
+        return [
+            x_move(name, 0, at, j, source.at[at * size_x + columns[j]], xin[name].at[j - 1, at]) for j in range(1, size_x)
+        ]
+
+    def send_x(name):
+        for t, way in steps:
+
+            @pl.when(inside(target_of(t, way)))
+            def _():
+                for move in x_pieces(name, target_of(t, way)):
+                    move.start()
+
+        for move in x_pieces(name, z):
+            move.start()
+
+    def own_part(name, at):
+        if name == "outer":
+            total = outer_buf[0, at].astype(high)
+            for i in range(1, size_x):
+                total = total + outer_buf[i, at].astype(high)
+            return [(slice(None), total)]
+        slot = at * size_x + x
+        if name == "vec":
+            total = vector_terms[slot]
+            for move in x_pieces("vec", at):
+                move.wait()
+            for j in range(1, size_x):
+                total = total + xin["vec"][j - 1, at]
+            return [(slice(None), total)]
+        for move in x_pieces(name, at):
+            move.wait()
+        total = terms[slot].astype(high)
+        for j in range(1, size_x):
+            total = total + xin[name][j - 1, at].astype(high)
+        return [(slice(None), total)]
+
+    def z_move(name, t, way):
+        peer = partner(z=lax.rem(z + 1 - 2 * way + size_z, size_z))
+        return remote(
+            zout[name].at[way, t - 1], zin[name].at[way, t - 1], zsend[name].at[way, t - 1], zrecv[name].at[way, t - 1], peer
         )
-        move.start()
-        along[name, k] = move
+
+    def step_z(name, t):
+        for way in range(2):
+
+            @pl.when(inside(target_of(t, way)))
+            def _():
+                pieces = own_part(name, target_of(t, way))
+                if t > 1:
+
+                    @pl.when(fed(way))
+                    def _():
+                        z_move(name, t - 1, way).wait_recv()
+
+                for span, total in pieces:
+                    if t > 1:
+                        before = zin[name][way, t - 2, :, span].astype(high)
+                        total = total + jnp.where(fed(way), before, 0.0)
+                    zout[name][way, t - 1, :, span] = total.astype(zout[name].dtype)
+                z_move(name, t, way).start()
+
+    across, swapped = {}, {}
+
+    def step_y(name):
+        across[name] = remote(ybuf[name].at[0], ybuf[name].at[1], ysend[name], yrecv[name], y_peer)
+        across[name].start()
+
+    def finish_z(name):
+        pieces = own_part(name, z)
+        last = size_z - 1
+        for way in range(2):
+
+            @pl.when(fed(way))
+            def _():
+                z_move(name, last, way).wait_recv()
+
+        for span, total in pieces:
+            for way in range(2):
+                before = zin[name][way, last - 1, :, span].astype(high)
+                total = total + jnp.where(fed(way), before, 0.0)
+            ybuf[name][0, :, span] = total.astype(ybuf[name].dtype)
+        step_y(name)
+
+    def step_core(name):
+        across[name].wait()
+        cbuf[name][0] = ybuf[name][0].astype(high) + ybuf[name][1].astype(high)
+        swapped[name] = remote(cbuf[name].at[0], cbuf[name].at[1], csend[name], crecv[name], core_peer)
+        swapped[name].start()
+
+    def finish_core(name):
+        swapped[name].wait()
+        return cbuf[name]
 
     vector_rows[...] = jnp.zeros_like(vector_rows)
     for i, row in enumerate((7, 8, 6, 3, 4, 2)):
@@ -748,44 +843,62 @@
         vector_rows[1:2, place] = head_sums[8 * p : 8 * p + 1, 256:384]
     inner_row = jnp.sum(inner_sums[...], axis=0, keepdims=True)
     vector_terms[...] = jnp.zeros_like(vector_terms)
+    for name in zin:
+        if name == "vec":
+            zin[name][...] = jnp.zeros_like(zin[name])
     longest = vector_terms.shape[2]
     for s in range(shards):
         vector_terms[s, :, 0:rows] = vector_rows[:, s * rows : (s + 1) * rows]
         vector_terms[s, WIDE : WIDE + 1, :] = inner_row[:, s * longest : (s + 1) * longest]
-    for k in order:
-        for j in range(1, size_x):
-            send_x("vec", 0, k, j, vector_terms.at[slot_of(k, j)], xin["vec"].at[j - 1, k])
-
+    greet(True)
+
+    outputs = remote(output_term.at[:, :, theirs], odd, osend, orecv, core_peer)
+    outputs.start()
+    send_x("vec")
     for i in range(size_z):
         loads["inner", i].wait()
-    for j in range(size_x):
+    inner_moves = []
+    for j in range(1, size_x):
         total = inner_buf[0, columns[j]].astype(high)
         for i in range(1, size_z):
             total = total + inner_buf[i, columns[j]].astype(high)
-        if j == 0:
-            kept["inner"] = total
-        else:
-            xout["inner"][j - 1] = total.astype(low)
-            send_x("inner", 0, 0, j, xout["inner"].at[j - 1], xin["inner"].at[j - 1, 0])
-
+        inner_send[j - 1] = total.astype(low)
+        move = x_move("inner", 0, 0, j, inner_send.at[j - 1], xin["inner"].at[j - 1, 0])
+        move.start()
+        inner_moves.append(move)
     for i in range(size_x):
         loads["outer", i].wait()
-    for k in order:
-        target = lax.rem(z + k, size_z)
-        total = outer_buf[0, target].astype(high)
-        for i in range(1, size_x):
-            total = total + outer_buf[i, target].astype(high)
-        if k == 0:
-            kept["outer"] = total
-        else:
-            zout["outer"][k - 1] = total.astype(low)
-            send_z("outer", k)
+    step_z("outer", 1)
+
+    strip = 256
+
+    def product(first):
+        at = pl.ds(pl.multiple_of(first, strip), strip)
+        return dot_nt(grads[at, :], weights[...])
+
+    def token_rows(first):
+        def other_strip(i, _):
+            at = pl.ds(pl.multiple_of(first + i * strip, strip), strip)
+            other_rows[at, :] = product(local + first + i * strip).astype(low)
+            return 0
+
+        def own_strip(i, _):
+            at = pl.ds(pl.multiple_of(first + i * strip, strip), strip)
+            base[at, :] = base[at, :] + product(first + i * strip)
+            return 0
+
+        lax.fori_loop(0, part // strip, other_strip, 0)
+        span = pl.ds(first, part)
+        move = remote(other_rows.at[span, :], recv_rows.at[span, :], tsend.at[first // part], trecv.at[first // part], core_peer)
+        move.start()
+        lax.fori_loop(0, part // strip, own_strip, 0)
+        return move
 
     loads["inputs"].wait()
     for b in range(4):
         turned[:, b * part : (b + 1) * part] = inputs[b * part : (b + 1) * part, :].T
+    group = 4
     loads["grads"].wait()
-    group = 4
     for p in range(pairs):
         block = slice(p * 384, (p + 1) * 384)
 
@@ -795,113 +908,48 @@
             return 0
 
         lax.fori_loop(0, shards // group, some, 0)
-        for k in order:
-            for j in range(1, size_x):
-                send_x("qkv", p, k, j, terms.at[slot_of(k, j), :, block], xin["qkv"].at[j - 1, k, :, block])
-
-    loads["weights"].wait()
-    strip = 256
-
-    def product(first):
-        at = pl.ds(pl.multiple_of(first, strip), strip)
-        return dot_nt(grads[at, :], weights[...])
-
-    def other_strip(i, _):
-        other_rows[pl.ds(pl.multiple_of(i * strip, strip), strip), :] = product(local + i * strip).astype(low)
-        return 0
-
-    lax.fori_loop(0, local // strip, other_strip, 0)
-    halves = remote(other_rows, recv_rows, tsend.at[0], trecv.at[0], core_peer)
-    halves.start()
     outputs.wait()
-    for k in order:
-        for j in range(1, size_x):
-            slot = slot_of(k, j)
-            odd[slot] = (odd[slot].astype(high) + output_term[slot, :, mine].astype(high)).astype(low)
-            send_x("out", 0, k, j, odd.at[slot], xin["out"].at[j - 1, k])
-    loads["base"].wait()
-
-    def own_strip(i, _):
-        at = pl.ds(pl.multiple_of(i * strip, strip), strip)
-        base[at, :] = base[at, :] + product(i * strip)
-        return 0
-
-    lax.fori_loop(0, local // strip, own_strip, 0)
+    terms[:, :, lanes : lanes + half] = (odd[...].astype(high) + output_term[:, :, mine].astype(high)).astype(low)
+    send_x("qkvo")
+    for name in ("weights", "base"):
+        loads[name].wait()
+    halves = token_rows(part)
     halves.wait()
     send_rows[...] = (base[part:local, :] + recv_rows[part:local, :].astype(high)).astype(low)
-    back = remote(send_rows, far_rows, tsend.at[1], trecv.at[1], y_peer)
+    back = remote(send_rows, far_rows, tsend.at[2], trecv.at[2], y_peer)
     back.start()
-    token_grads[y] = base[0:part, :] + recv_rows[0:part, :].astype(high)
-
-    across = {}
-    swapped = {}
-
-    def step_y(name):
-        move = remote(ybuf[name].at[0], ybuf[name].at[1], ysend[name], yrecv[name], y_peer)
-        move.start()
-        across[name] = move
-
-    def step_core(name):
-        across[name].wait()
-        cbuf[name][0] = ybuf[name][0].astype(high) + ybuf[name][1].astype(high)
-        move = remote(cbuf[name].at[0], cbuf[name].at[1], csend[name], crecv[name], core_peer)
-        move.start()
-        swapped[name] = move
-
-    def finish_x(name):
-        for k in order:
-            slot = slot_of(k, 0)
-            if name == "qkv":
-                total = terms[slot].astype(high)
-            elif name == "out":
-                total = odd[slot].astype(high) + output_term[slot, :, mine].astype(high)
-            else:
-                total = vector_terms[slot]
-            for j in range(1, size_x):
-                for move in sideways[name, k, j]:
-                    move.wait()
-                total = total + xin[name][j - 1, k].astype(high)
-            if k == 0:
-                kept[name] = total
-            else:
-                zout[name][k - 1] = total.astype(zout[name].dtype)
-                send_z(name, k)
-
-    def finish_z(name):
-        total = kept[name]
-        for k in far_order:
-            along[name, k].wait()
-            total = total + zin[name][k - 1].astype(high)
-        ybuf[name][0] = total.astype(ybuf[name].dtype)
-        step_y(name)
-
-    total = kept["inner"]
+
+    step_z("outer", 2)
+    halves = token_rows(0)
+    for t in range(3, size_z):
+        step_z("outer", t)
+    step_z("vec", 1)
+    step_z("qkvo", 1)
+
+    total = inner_buf[0, x].astype(high)
+    for i in range(1, size_z):
+        total = total + inner_buf[i, x].astype(high)
     for j in range(1, size_x):
-        for move in sideways["inner", 0, j]:
-            move.wait()
+        inner_moves[j - 1].wait()
         total = total + xin["inner"][j - 1, 0].astype(high)
     ybuf["inner"][0] = total.astype(low)
     step_y("inner")
-    finish_x("vec")
-    finish_x("qkv")
     finish_z("outer")
+    step_z("vec", 2)
+    step_z("qkvo", 2)
+    halves.wait()
+    token_grads[y] = base[0:part, :] + recv_rows[0:part, :].astype(high)
     step_core("inner")
-    finish_x("out")
+    for t in range(3, size_z):
+        step_z("vec", t)
+        step_z("qkvo", t)
+    step_core("outer")
     finish_z("vec")
-    step_core("outer")
-    finish_z("qkv")
-    finish_z("out")
     back.wait()
     token_grads[1 - y] = far_rows[...].astype(high)
     stores[0].start()
-    step_core("vec")
-
-    def finish_core(name):
-        swapped[name].wait()
-        return cbuf[name]
-
+    chunks = hidden // CHUNK
     buf = finish_core("inner")
-    chunks = hidden // CHUNK
     for i in range(2):
         owner = core if i == 0 else 1 - core
         for c in range(chunks):
@@ -913,53 +961,76 @@
         owner = core if i == 0 else 1 - core
         grad_outer[:, pl.ds(pl.multiple_of(owner * half, 128), half)] = buf[i]
     stores[6].start()
-    step_core("qkv")
-    step_core("out")
+    finish_z("qkvo")
+    step_core("vec")
+    step_core("qkvo")
+    for name in zout:
+        for t, way in steps:
+
+            @pl.when(inside(target_of(t, way)))
+            def _():
+                z_move(name, t, way).wait_send()
+
     buf = finish_core("vec")
     vector_sums[...] = buf[0] + buf[1]
     stores[7].start()
-    buf = finish_core("qkv")
+    buf = finish_core("qkvo")
     for i in range(2):
         owner = core if i == 0 else 1 - core
         for p in range(pairs):
             place = pl.ds(pl.multiple_of(owner * half + p * 128, 128), 128)
             for n, out in enumerate((grad_query, grad_key, grad_value)):
                 out[:, place] = buf[i, :, (3 * p + n) * 128 : (3 * p + n + 1) * 128]
-    for i in (1, 2, 3):
+        grad_output[:, pl.ds(pl.multiple_of(owner * half, 128), half)] = buf[i, :, lanes : lanes + half]
+    for i in range(1, 5):
         stores[i].start()
-    buf = finish_core("out")
-    for i in range(2):
-        owner = core if i == 0 else 1 - core
-        grad_output[:, pl.ds(pl.multiple_of(owner * half, 128), half)] = buf[i]
-    stores[4].start()
     for store in stores:
         store.wait()
 
 
-def deliver_kernel(count, *refs):
-    sources, vectors, outs, sem = refs[:count], refs[count], refs[count + 1 : -1], refs[-1]
-    copies = [pltpu.make_async_copy(src, dst, sem.at[i]) for i, (src, dst) in enumerate(zip(sources, outs))]
-    for copy in copies:
+def deliver_kernel(count, mixed_mine, mixed_far, *refs):
+    matrices, vectors = refs[:count], refs[count]
+    mixed = refs[count + 1]
+    outs = refs[count + 2 : 2 * count + 2]
+    smalls = refs[2 * count + 2 : -(count + 4)]
+    stage, bufs, in_sem, out_sem = refs[-(count + 4) : -(count + 2)], refs[-(count + 2) : -2], refs[-2], refs[-1]
+    y = lax.axis_index("y")
+    moves = [(mixed_mine, stage[0], mixed.at[y]), (mixed_far, stage[1], mixed.at[1 - y])]
+    for src, buf, dst in zip(matrices, bufs, outs):
+        if len(src.shape) == 3:
+            moves += [(src.at[i], buf.at[i], dst.at[i]) for i in range(src.shape[0])]
+        else:
+            moves.append((src, buf, dst))
+    first = [pltpu.make_async_copy(src, buf, in_sem.at[i]) for i, (src, buf, _) in enumerate(moves)]
+    second = [pltpu.make_async_copy(buf, dst, out_sem.at[i]) for i, (_, buf, dst) in enumerate(moves)]
+    for copy in first:
         copy.start()
-    for i, out in enumerate(outs[count:]):
-        out[...] = vectors[i : i + 1, 0 : out.shape[1]]
-    for copy in copies:
+    for i, small in enumerate(smalls):
+        small[...] = vectors[i : i + 1, 0 : small.shape[1]]
+    for arrived, leaving in zip(first, second):
+        arrived.wait()
+        leaving.start()
+    for copy in second:
         copy.wait()
 
 
-def deliver(matrices, vectors, sizes):
+def deliver(mixed_mine, mixed_far, matrices, vectors, sizes):
     count = len(matrices)
     vmem, anywhere = pl.BlockSpec(memory_space=pltpu.VMEM), pl.BlockSpec(memory_space=pl.ANY)
+    moves = count + 4
     return pl.pallas_call(
         lambda *refs: deliver_kernel(count, *refs),
-        out_shape=tuple(jax.ShapeDtypeStruct(m.shape, m.dtype) for m in matrices)
+        out_shape=(jax.ShapeDtypeStruct((2,) + mixed_mine.shape, mixed_mine.dtype),)
+        + tuple(jax.ShapeDtypeStruct(m.shape, m.dtype) for m in matrices)
         + tuple(jax.ShapeDtypeStruct((1, size), jnp.float32) for size in sizes),
-        in_specs=[vmem] * (count + 1),
-        out_specs=(anywhere,) * count + (vmem,) * len(sizes),
-        scratch_shapes=[pltpu.SemaphoreType.DMA((count,))],
+        in_specs=[anywhere] * (2 + count) + [vmem],
+        out_specs=(anywhere,) * (count + 1) + (vmem,) * len(sizes),
+        scratch_shapes=[pltpu.VMEM(mixed_mine.shape, mixed_mine.dtype)] * 2
+        + [pltpu.VMEM(m.shape, m.dtype) for m in matrices]
+        + [pltpu.SemaphoreType.DMA((moves,))] * 2,
         compiler_params=pltpu.CompilerParams(vmem_limit_bytes=60_000_000),
         name="deliver",
-    )(*matrices, vectors)
+    )(mixed_mine, mixed_far, *matrices, vectors)
 
 
 def exit_call(size_z, size_x, grads, inputs, weights, base, output_term, dense_sums, inner_sums, head_sums, inner_terms, outer_terms):
@@ -975,12 +1046,12 @@
     vmem, anywhere = pl.BlockSpec(memory_space=pltpu.VMEM), pl.BlockSpec(memory_space=pl.ANY)
     dma = pltpu.SemaphoreType.DMA
     side = size_x - 1
+    full = lanes + half
     low, high = jnp.bfloat16, jnp.float32
     vector_shape = (16, hidden // shards)
     shapes = {
         "vec": (vector_shape, high, 1),
-        "qkv": ((rows, lanes), low, pairs),
-        "out": ((rows, half), low, 1),
+        "qkvo": ((rows, full), low, 1),
         "inner": ((rows, hidden // 2), low, 1),
         "outer": ((long, half), low, 1),
     }
@@ -1001,7 +1072,7 @@
         pltpu.VMEM((width, length), low),
         pltpu.VMEM((width, lanes), low),
         pltpu.VMEM((local, width), high),
-        pltpu.VMEM((shards, rows, lanes), low),
+        pltpu.VMEM((shards, rows, full), low),
         pltpu.VMEM((local, width), low),
         pltpu.VMEM((local, width), low),
         pltpu.VMEM((part, width), low),
@@ -1011,10 +1082,11 @@
         pltpu.VMEM((size_x,) + outer_terms[0].shape, low),
         pltpu.VMEM((16, width), high),
         pltpu.VMEM((shards,) + vector_shape, high),
+        pltpu.VMEM((side, rows, hidden // 2), low),
         dma((len(results),)),
         dma((size_z + size_x + 4,)),
-        dma((2,)),
-        dma((2,)),
+        dma((3,)),
+        dma((3,)),
         dma,
         dma,
     ]
@@ -1024,8 +1096,7 @@
         if name != "outer":
             scratch += [pltpu.VMEM((side, stages) + shape, kind), dma((sends, stages, side)), dma((sends, stages, side))]
         if name != "inner":
-            scratch += [pltpu.VMEM((size_z - 1,) + shape, kind)] * 2 + [dma((size_z - 1,))] * 2
-    scratch.append(pltpu.VMEM((side, rows, hidden // 2), low))
+            scratch += [pltpu.VMEM((2, size_z - 1) + shape, kind)] * 2 + [dma((2, size_z - 1))] * 2
     return pl.pallas_call(
         lambda *refs: exit_kernel(size_z, size_x, shapes, *refs),
         out_shape=results,
@@ -1065,22 +1136,23 @@
     tokens_ref,
     mine_ref,
     other_hbm,
-    cot_ref,
+    cot_hbm,
+    cot_far_hbm,
     vectors_ref,
     bias_inner_ref,
     *refs,
 ):
     inner_parts, outer_parts = refs[:size_x], refs[size_x : size_x + size_z]
     refs = refs[size_x + size_z :]
-    mixed_ref, pre_first_ref, grad_mine_ref, grad_far_hbm, sums_ref, inner_sum_ref, grad_output_ref = refs[:7]
-    inner_terms = refs[7 : 7 + size_z]
-    outer_terms = refs[7 + size_z : 7 + size_z + size_x]
-    refs = refs[7 + size_z + size_x :]
+    mixed_ref, mixed_send_ref, pre_first_ref, grad_mine_ref, grad_far_hbm, sums_ref, inner_sum_ref, grad_output_ref = refs[:8]
+    inner_terms = refs[8 : 8 + size_z]
+    outer_terms = refs[8 + size_z : 8 + size_z + size_x]
+    refs = refs[8 + size_z + size_x :]
     w_output, w_inner, w_outer, a_output, a_inner, a_outer, grad_out_buf = refs[:7]
     context, first_low, turned_low, normed, first, slope, active, work = refs[7:15]
     send_inner, send_outer, recv_inner, recv_outer = refs[15:19]
-    far_rows, grad_send, swap_send, swap_recv = refs[19:23]
-    load_sem, share_send, share_recv, send_sem, recv_sem, store_sem = refs[23:]
+    far_rows, grad_send, ready, cotangent, cot_sem, swap_send, swap_recv = refs[19:26]
+    load_sem, share_send, share_recv, send_sem, recv_sem, store_sem = refs[26:]
     step, steps = pl.program_id(0), pl.num_programs(0)
     core_here = lax.axis_index("core")
     width, hidden = w_inner.shape
@@ -1089,6 +1161,11 @@
     shards = size_z * size_x
     z, x, y, _ = place_of()
     twin = partner(core=1 - lax.axis_index("core"))
+    near = cotangent.shape[0] // 2
+    cot_loads = (
+        pltpu.make_async_copy(cot_hbm.at[y], cotangent.at[pl.ds(0, near), :], cot_sem.at[0]),
+        pltpu.make_async_copy(cot_far_hbm, cotangent.at[pl.ds(near, near), :], cot_sem.at[1]),
+    )
 
     shard = width // shards
     long = hidden // shards
@@ -1133,6 +1210,8 @@
         pl.semaphore_wait(barrier, 1)
         remote(other_hbm, far_rows, swap_send.at[0], swap_recv.at[0], twin).start()
         start_loads()
+        for load in cot_loads:
+            load.start()
         a_output[...] = jnp.zeros_like(a_output)
         a_inner[...] = jnp.zeros_like(a_inner)
         a_outer[...] = jnp.zeros_like(a_outer)
@@ -1169,7 +1248,7 @@
     work[...] = jnp.broadcast_to(vector(3), work.shape)
 
     def part(c):
-        return pl.ds(pl.multiple_of(c * CHUNK, CHUNK), CHUNK)
+        return pl.ds(c * CHUNK, CHUNK)
 
     def exchange(c):
         return (
@@ -1177,27 +1256,51 @@
             remote(send_outer.at[c], recv_outer.at[c], send_sem.at[1, c], recv_sem.at[1, c], twin),
         )
 
-    def forward(c):
+    def wait_inner(c):
         @pl.when(step == 0)
         def _():
             wait_load(1 + 2 * c, w_inner, slice(None), c * CHUNK)
 
-        u = dot_nn(first_low[...], w_inner[:, part(c)]) + bias_inner_ref[0:1, part(c)]
-        cdf = 0.5 * (1.0 + lax.erf(u * ROOT_HALF))
-        slope[:, part(c)] = cdf + u * jnp.exp(-0.5 * u * u) * INV_ROOT_TAU
-        active[:, part(c)] = (u * cdf).astype(jnp.bfloat16)
+    def ahead(c):
+        ready[c % 2] = dot_nn(first_low[...], w_inner[:, part(c)])
+
+    wait_inner(0)
+    ahead(0)
+    for c in range(chunks):
+        if c + 1 < chunks:
+            wait_inner(c + 1)
 
         @pl.when(step == 0)
         def _():
             wait_load(2 + 2 * c, w_outer, part(c), 0)
 
-        work[...] += dot_nn(active[:, part(c)], w_outer[part(c), :])
-
-    for c in range(chunks):
-        forward(c)
+        if c + 1 < chunks:
+            ahead(c + 1)
+        u = ready[c % 2] + bias_inner_ref[0:1, part(c)]
+        cdf = 0.5 * (1.0 + lax.erf(u * ROOT_HALF))
+        slope[:, part(c)] = cdf + u * jnp.exp(-0.5 * u * u) * INV_ROOT_TAU
+        acted = (u * cdf).astype(jnp.bfloat16)
+        active[:, part(c)] = acted
+        work[...] += dot_nn(acted, w_outer[part(c), :])
+
     second, second_recip = standardize(first[...] + work[...])
-    mixed_ref[...] = (second * vector(4) + vector(5)).astype(jnp.bfloat16)
-    upstream = cot_ref[...].astype(jnp.float32)
+    mixed = (second * vector(4) + vector(5)).astype(jnp.bfloat16)
+
+    @pl.when(step < steps // 2)
+    def _():
+        mixed_ref[...] = mixed
+
+    @pl.when(step >= steps // 2)
+    def _():
+        mixed_send_ref[...] = mixed
+
+
+    @pl.when(step == 0)
+    def _():
+        for load in cot_loads:
+            load.wait()
+
+    upstream = cotangent[pl.ds(pl.multiple_of(step * TILE, TILE), TILE), :].astype(jnp.float32)
     add_sum(0, upstream * second)
     add_sum(1, upstream)
     scaled = upstream * vector(4)
@@ -1207,12 +1310,16 @@
     work[...] = pre_second
     grad_out_buf[...] = grad_outer
 
-    def backward(c, _):
-        grad_out = grad_out_buf[...]
-        grad = dot_nt(grad_out, w_outer[part(c), :])
-        grad_inner = (grad * slope[:, part(c)]).astype(jnp.bfloat16)
+    def behind(c):
+        ready[c % 2] = dot_nt(grad_out_buf[...], w_outer[part(c), :])
+
+    behind(0)
+    for c in range(chunks):
+        if c + 1 < chunks:
+            behind(c + 1)
+        grad_inner = (ready[c % 2] * slope[:, part(c)]).astype(jnp.bfloat16)
         inner_sum_ref[:, part(c)] += column_sum(grad_inner.astype(jnp.float32))
-        a_outer[part(c), :] += dot_nn(active[:, part(c)].T, grad_out)
+        a_outer[part(c), :] += dot_nn(active[:, part(c)].T, grad_out_buf[...])
         a_inner[:, part(c)] += dot_nn(turned_low[...], grad_inner)
         work[...] += dot_nt(grad_inner, w_inner[:, part(c)])
 
@@ -1224,9 +1331,6 @@
             for move in exchange(c):
                 move.start()
 
-        return 0
-
-    lax.fori_loop(0, chunks, backward, 0)
     grad_first = work[...]
     add_sum(3, grad_first * normed[...])
     add_sum(4, grad_first)
@@ -1288,7 +1392,7 @@
             pltpu.make_async_copy(send_outer.at[c], send_outer.at[c], store_sem.at[1, c]).wait()
 
 
-def dense_layer(size_z, size_x, tokens, mine, other, cotangent, vectors, bias_inner, inner_parts, outer_parts):
+def dense_layer(size_z, size_x, tokens, mine, other, cotangent, cotangent_far, vectors, bias_inner, inner_parts, outer_parts):
     local, half = mine.shape
     width = 2 * half
     hidden = bias_inner.shape[1]
@@ -1310,7 +1414,8 @@
     return pl.pallas_call(
         lambda *refs: dense_kernel(size_z, size_x, *refs),
         out_shape=(
-            jax.ShapeDtypeStruct((local, width), low),
+            jax.ShapeDtypeStruct((local // 2, width), low),
+            jax.ShapeDtypeStruct((local // 2, width), low),
             jax.ShapeDtypeStruct((local, width), high),
             jax.ShapeDtypeStruct((local, half), low),
             jax.ShapeDtypeStruct((local, half), low),
@@ -1327,13 +1432,15 @@
                 tile,
                 half_tile,
                 anywhere,
-                tile,
+                anywhere,
+                anywhere,
                 whole((16, width)),
                 whole((1, hidden)),
             ]
             + [anywhere] * (size_x + size_z),
             out_specs=[
-                tile,
+                pl.BlockSpec((TILE, width), lambda t: (jnp.minimum(t, steps // 2 - 1), 0)),
+                pl.BlockSpec((TILE, width), lambda t: (jnp.maximum(t - steps // 2, 0), 0)),
                 tile,
                 half_tile,
                 anywhere,
@@ -1364,6 +1471,9 @@
                 halves,
                 pltpu.VMEM((local, half), low),
                 pltpu.VMEM((steps, TILE, half), low),
+                pltpu.VMEM((2, TILE, CHUNK), high),
+                pltpu.VMEM((local, width), low),
+                dma((2,)),
                 dma((1 + steps,)),
                 dma((1 + steps,)),
                 dma((1 + 2 * chunks,)),
@@ -1379,7 +1489,7 @@
         ),
         cost_estimate=pl.CostEstimate(flops=32_000_000_000, bytes_accessed=40_000_000, transcendentals=6_000_000),
         name="dense_layer",
-    )(tokens, mine, other, cotangent, vectors, bias_inner, *inner_parts, *outer_parts)
+    )(tokens, mine, other, cotangent, cotangent_far, vectors, bias_inner, *inner_parts, *outer_parts)
 
 
 def lowered(piece):
@@ -1550,11 +1660,8 @@
     bias_query, bias_value, bias_output, gain_first, shift_first, bias_inner, bias_outer, gain_second, shift_second = [
         widen(v) for v in gathered
     ]
-    spot = jnp.arange(5, dtype=jnp.int32)
-    place = jnp.where(spot < 4, ((spot % 2 != core) * 2 + (spot // 2 != y) * 1) * part, core)
-    segments = pick(segment_ids, y)
     biases = jnp.concatenate([bias_query[None], bias_value[None], jnp.zeros((14, width), jnp.float32)], axis=0)
-    heads_mine, heads_other, logsum, projected = attention(place, segments, inputs_all, full_early, biases)
+    heads_mine, heads_other, logsum, projected = attention(segment_ids, inputs_all, full_early, biases)
     context = in_order(core == 0, heads_mine, swap(heads_other, "core"), 1)
 
     attended = matmul(context, full_output) + bias_output
@@ -1604,7 +1711,7 @@
     outer_done = reduce_owned(outer_term.reshape(shards, unit_half, width))
     late_done = reduce_owned(jnp.concatenate([output_term, inner_term], axis=1).reshape(shards, own_rows, half + hidden // 2))
 
-    grads, sums = attention_back(place, segments, projected, heads_mine, heads_other, context_mine, upstream_other, logsum)
+    grads, sums = attention_back(segment_ids, projected, heads_mine, heads_other, context_mine, upstream_other, logsum)
     grad_early = lowered(matmul_tn(inputs_all, grads))
     partial = matmul_nt(grads, full_early)
     sums = sums.reshape(pairs, 8, 3, 128)[:, 0]
@@ -1722,35 +1829,33 @@
 
     vectors = (b_query, b_value, b_output, first_gain, first_shift, b_inner, b_outer, second_gain, second_shift)
     sizes = [v.shape[0] for v in vectors]
-    tokens_all, cotangent_all, early, inner_own, outer_own, rows, inner_row = entry(
+    tokens_all, cotangent_send, early, inner_own, outer_own, rows, inner_row = entry(
         size_z, size_x, tokens, cotangent, w_query, w_key, w_value, w_inner, w_output, w_outer, vectors
     )
+    cotangent_far = swap(cotangent_send, "y")
     inner_parts = [inner_own] + [shift(inner_own, "x", j) for j in range(1, size_x)]
     outer_parts = [outer_own] + [shift(outer_own, "z", k) for k in range(1, size_z)]
     inputs_all = tokens_all.reshape(4 * part, width)
     full_early = early.reshape(width, lanes)
-    spot = jnp.arange(5, dtype=jnp.int32)
-    place = jnp.where(spot < 4, ((spot % 2 != core) * 2 + (spot // 2 != y) * 1) * part, core)
-    segments = pick(segment_ids, y)
-    context_mine, context_other, logsum, projected = attention(place, segments, inputs_all, full_early, rows)
+    context_mine, context_other, logsum, projected = attention(segment_ids, inputs_all, full_early, rows)
     made = dense_layer(
         size_z,
         size_x,
         inputs_all,
         context_mine,
         context_other,
-        cotangent_all.reshape(local, width),
+        cotangent,
+        cotangent_far,
         rows,
         inner_row,
         inner_parts,
         outer_parts,
     )
-    mixed, pre_first, upstream_mine, upstream_other, dense_sums, inner_sums, grad_w_output = made[:7]
-    inner_terms = [made[7]] + [shift(made[7 + k], "z", k) for k in range(1, size_z)]
-    outer_terms = [made[7 + size_z]] + [shift(made[7 + size_z + j], "x", j) for j in range(1, size_x)]
-    mixed_out = in_order(y == 0, mixed[None, :part], swap(mixed[part:], "y")[None], 0)
-
-    grads, sums = attention_back(place, segments, projected, context_mine, context_other, upstream_mine, upstream_other, logsum)
+    mixed, mixed_send, pre_first, upstream_mine, upstream_other, dense_sums, inner_sums, grad_w_output = made[:8]
+    inner_terms = [made[8]] + [shift(made[8 + k], "z", k) for k in range(1, size_z)]
+    outer_terms = [made[8 + size_z]] + [shift(made[8 + size_z + j], "x", j) for j in range(1, size_x)]
+    mixed_far = swap(mixed_send, "y")
+    grads, sums = attention_back(segment_ids, projected, context_mine, context_other, upstream_mine, upstream_other, logsum)
     made = exit_call(
         size_z,
         size_x,
@@ -1765,8 +1870,8 @@
         inner_terms,
         outer_terms,
     )
-    grad_tokens, grad_query, grad_key, grad_value, grad_output, grad_inner_full, grad_outer_full, *done = deliver(
-        made[:7], made[7], sizes
+    mixed_out, grad_tokens, grad_query, grad_key, grad_value, grad_output, grad_inner_full, grad_outer_full, *done = deliver(
+        mixed, mixed_far, made[:7], made[7], sizes
     )
     done = [v.reshape(size) for v, size in zip(done, sizes)]
     return (

time: 310 us -> 292 us (0.942)
  Pallas kernels: 292 us -> 270 us
  starting transfers between devices: 10.2 us -> 15.7 us
  waiting for transfers between devices: 0.02 us -> 4.74 us
    pallas_call x1, Pallas kernels: 53.6 us -> 42.2 us  [entry(): pl.pallas_call(lambda *refs: entry_kernel(size_z, size_x, count, *refs),...]
    pallas_call x1, Pallas kernels: 63.9 us -> 74.4 us  [exit_call(): pl.pallas_call(lambda *refs: exit_kernel(size_z, size_x, shapes, *refs),...]
    pallas_call x1, Pallas kernels: 54.2 us -> 43.7 us  [attention_back(): pl.pallas_call(backward_kernel, out_shape=(jax.ShapeDtypeStruct((length,...]
    pallas_call x1, Pallas kernels: 49 us -> 40.2 us  [attention(): pl.pallas_call(forward_kernel, out_shape=(jax.ShapeDtypeStruct((rows, pai...]
    ppermute x8, waiting for transfers between devices: 0.02 us -> 4.74 us  [shift(): lax.ppermute(piece, axis, [(i, (i + step) % size) for i in range(size)])]
    ppermute x8, starting transfers between devices: 8.97 us -> 12.8 us  [shift(): lax.ppermute(piece, axis, [(i, (i + step) % size) for i in range(size)])]
    pallas_call x1, Pallas kernels: 65.2 us -> 61.7 us  [dense_layer(): pl.pallas_call(lambda *refs: dense_kernel(size_z, size_x, *refs), out_sha...]
  transfers between devices with their start and end apart: 9 -> 10, of which waited for: 0 -> 1; matrix products, arithmetic and copies ran while one was open for 1% -> 0% of each run, Pallas kernels for 33% -> 54%
where the time goes in v7:
time: 292 us; the launch traced here: 294 us
  Pallas kernels  270 us (92%)
  starting transfers between devices  15.7 us (5%)
  waiting for transfers between devices  4.74 us (2%)
    pallas_call x1, Pallas kernels, exit_call(): pl.pallas_call(lambda *refs: exit_kernel(size_z, size_x, shapes, *refs),...  74.4 us
    pallas_call x1, Pallas kernels, dense_layer(): pl.pallas_call(lambda *refs: dense_kernel(size_z, size_x, *refs), out_sha...  61.7 us
    pallas_call x1, Pallas kernels, attention_back(): pl.pallas_call(backward_kernel, out_shape=(jax.ShapeDtypeStruct((length,...  43.7 us
    pallas_call x1, Pallas kernels, entry(): pl.pallas_call(lambda *refs: entry_kernel(size_z, size_x, count, *refs),...  42.2 us
    pallas_call x1, Pallas kernels, attention(): pl.pallas_call(forward_kernel, out_shape=(jax.ShapeDtypeStruct((rows, pai...  40.2 us
    ppermute x8, starting transfers between devices, shift(): lax.ppermute(piece, axis, [(i, (i + step) % size) for i in range(size)])  12.8 us
    pallas_call x1, Pallas kernels, deliver(): pl.pallas_call(lambda *refs: deliver_kernel(count, *refs), out_shape=(jax...  8.01 us
  transfers between devices with their start and end apart: 10, of which 1 were waited for; matrix products, arithmetic and copies ran while one was open for 0% of the time, Pallas kernels for 54%

profile of v7, /device:TPU:0, one launch (start us, length us, event | category | flops | bytes accessed | tf_op | source)
XLA Modules:
  0.0 294.0 jit_solution(15135554414113227963)
XLA Ops:
  0.7 1.2 reshape.102.refs_13_
  1.9 42.2 %entry.1 = (bf16[4,512,768]{2,1,0:T(8,128)(2,1)}, bf16[512,768]{1,0:T(8,128)(2,1)}, bf16[8,96,1152]{2,1,0:T(8,128)(2,1)}, bf16[4,96,1920]{2,1,0:T(8,128)(2,1)}, ...) custom-call(bf16[2,512,768]{2,1,0:T(8,128)(2,1)} %refs_0_.1, bf16[2,512,768]{2,1,0:T(8,128)(2,1)} %refs_3_.3, ...), custom_call_target="tpu_custom_call" | custom-call | tf_op jit(solution)/shard_map/entry/pallas_call | solution.py:637
  44.1 1.5 collective-permute-start.4
  45.6 0.0 collective-permute-start.3
  45.6 0.6 collective-permute-start.2
  46.3 0.5 collective-permute-start
  46.8 1.5 collective-permute-start.1
  48.3 40.2 %attention_forward.1 = (bf16[1024,384]{1,0:T(8,128)(2,1)}, bf16[1024,384]{1,0:T(8,128)(2,1)}, f32[24,2048]{1,0:T(8,128)}, bf16[2048,1152]{1,0:T(8,128)(2,1)}) custom-call(s32[2,2048]{1,0:T(2,128)} %row_ref.3, s32[2,2048]{1,0:T(2,128)} %row_ref.3, bf16[2048,768]{1,0:T(8,128)(2,1)} %bitcast.19, bf16[768,1152]{1,0:T(8,128)(2,1)} %bitcast.22, ...), custom_call_target="tpu_custom_call" | custom-call | flops 120000004096 | bytes 9000000 | tf_op jit(solution)/shard_map/attention_forward/pallas_call | solution.py:183
  88.5 0.0 collective-permute-done.4.refs_12_
  88.5 4.7 %collective-permute-done.3.refs_11_ = bf16[2,384,384]{2,1,0:T(8,128)(2,1)} collective-permute-done((bf16[2,384,384]{2,1,0:T(8,128)(2,1)}, bf16[2,384,384]{2,1,0:T(8,128)(2,1)}, u32[]{:S(2)}, u32[]{:S(2)}) %collective-permute-start.3) | collective-permute-done | bytes 589856 | tf_op jit(solution)/shard_map/ppermute | solution.py:1549
  93.2 0.0 collective-permute-done.2.refs_10_
  93.2 0.0 collective-permute-done.refs_4_
  93.2 0.0 collective-permute-done.1.refs_8_
  93.2 61.7 %dense_layer.1 = (bf16[512,768]{1,0:T(8,128)(2,1)}, bf16[512,768]{1,0:T(8,128)(2,1)}, f32[1024,768]{1,0:T(8,128)}, bf16[1024,384]{1,0:T(8,128)(2,1)}, bf16[1024,...) custom-call(bf16[2048,768]{1,0:T(8,128)(2,1)} %bitcast.20, ...), custom_call_target="tpu_custom_call" | custom-call | flops 32000000000 | bytes 40000000 | tf_op jit(solution)/shard_map/dense_layer/pallas_call | solution.py:1414
  155.0 2.4 collective-permute-start.6
  157.4 2.0 collective-permute-start.7
  159.4 2.8 collective-permute-start.8
  162.2 2.4 collective-permute-start.5
  164.7 1.9 collective-permute-start.9
  166.5 43.7 %attention_backward.1 = (bf16[2048,1152]{1,0:T(8,128)(2,1)}, f32[24,384]{1,0:T(8,128)}) custom-call(s32[2,2048]{1,0:T(2,128)} %row_ref.3, bf16[2048,1152]{1,0:T(8,128)(2,1)} %get-tuple-element.80.qkv_ref, bf16[1024,384]{1,0:T(8,128)(2,1)} %get-tuple-element.72.refs_1_.ctx_mine_ref, bf16[1024,384]{1,0:T(8,128)(2,1)} %get-tuple-element.73.refs_2_.ctx_other_ref, ...), custom_call_target="tpu_custom_call" | custom-call | flops 60000002048 | bytes 15000000 | tf_op jit(solution)/shard_map/attention_backward/pallas_call | solution.py:350
  210.3 0.0 collective-permute-done.6.refs_9_
  210.3 74.4 %exit.1 = (f32[2,512,768]{2,1,0:T(8,128)}, f32[96,768]{1,0:T(8,128)}, f32[96,768]{1,0:T(8,128)}, f32[96,768]{1,0:T(8,128)}, f32[96,768]{1,0:T(8,128)}, /*index=5...) custom-call(bf16[2048,1152]{1,0:T(8,128)(2,1)} %get-tuple-element.84.refs_0_, bf16[2048,768]{1,0:T(8,128)(2,1)} %bitcast.21, ...), custom_call_target="tpu_custom_call" | custom-call | tf_op jit(solution)/shard_map/exit/pallas_call | solution.py:1100
  284.7 8.0 %deliver.1 = (bf16[2,512,768]{2,1,0:T(8,128)(2,1)}, f32[2,512,768]{2,1,0:T(8,128)}, f32[96,768]{1,0:T(8,128)}, f32[96,768]{1,0:T(8,128)}, f32[96,768]{1,0:T(8,12...) custom-call(bf16[512,768]{1,0:T(8,128)(2,1)} %get-tuple-element.78.r, ...), custom_call_target="tpu_custom_call" | custom-call | tf_op jit(solution)/shard_map/deliver/pallas_call | solution.py:1021
  292.7 1.2 reduce
  (4 shorter events, 0.0 us)
Async XLA Ops:
  44.1 44.4 %collective-permute-start.4 = (bf16[2,384,384]{2,1,0:T(8,128)(2,1)}, bf16[2,384,384]{2,1,0:T(8,128)(2,1)}, u32[]{:S(2)}, u32[]{:S(2)}) collective-permute-start(bf16[2,384,384]{2,1,0:T(8,128)(2,1)} %get-tuple-element.77.refs_9_), channel_id=1, source_target_pairs={{0,24},{8,0},{16,8},{24,16},{1,25},{9,1},{17,9},{25,17},{2,26},{10... | collective-permute-start | bytes 1769480 | tf_op jit(solution)/shard_map/ppermute | solution.py:1549
  45.6 47.6 %collective-permute-start.3 = (bf16[2,384,384]{2,1,0:T(8,128)(2,1)}, bf16[2,384,384]{2,1,0:T(8,128)(2,1)}, u32[]{:S(2)}, u32[]{:S(2)}) collective-permute-start(bf16[2,384,384]{2,1,0:T(8,128)(2,1)} %get-tuple-element.77.refs_9_), channel_id=1, source_target_pairs={{0,16},{8,24},{16,0},{24,8},{1,17},{9,25},{17,1},{25,9},{2,18},{10... | collective-permute-start | bytes 1769480 | tf_op jit(solution)/shard_map/ppermute | solution.py:1549
  45.6 47.6 %collective-permute-start.2 = (bf16[2,384,384]{2,1,0:T(8,128)(2,1)}, bf16[2,384,384]{2,1,0:T(8,128)(2,1)}, u32[]{:S(2)}, u32[]{:S(2)}) collective-permute-start(bf16[2,384,384]{2,1,0:T(8,128)(2,1)} %get-tuple-element.77.refs_9_), channel_id=1, source_target_pairs={{0,8},{8,16},{16,24},{24,0},{1,9},{9,17},{17,25},{25,1},{2,10},{10... | collective-permute-start | bytes 1769480 | tf_op jit(solution)/shard_map/ppermute | solution.py:1549
  46.3 47.0 %collective-permute-start = (bf16[512,768]{1,0:T(8,128)(2,1)}, bf16[512,768]{1,0:T(8,128)(2,1)}, u32[]{:S(2)}, u32[]{:S(2)}) collective-permute-start(bf16[512,768]{1,0:T(8,128)(2,1)} %get-tuple-element.74), channel_id=1, source_target_pairs={{0,2},{2,0},{1,3},{3,1},{4,6},{6,4},{5,7},{7,5},{8,10},{10,8},{9,1... | collective-permute-start | bytes 2359304 | tf_op jit(solution)/shard_map/ppermute | solution.py:1553
  46.8 46.4 %collective-permute-start.1 = (bf16[4,96,1920]{2,1,0:T(8,128)(2,1)}, bf16[4,96,1920]{2,1,0:T(8,128)(2,1)}, u32[]{:S(2)}, u32[]{:S(2)}) collective-permute-start(bf16[4,96,1920]{2,1,0:T(8,128)(2,1)} %get-tuple-element.76.refs_7_), channel_id=1, source_target_pairs={{0,4},{4,0},{1,5},{5,1},{2,6},{6,2},{3,7},{7,3},{8,12},{12,8},{9,1... | collective-permute-start | bytes 4423688 | tf_op jit(solution)/shard_map/ppermute | solution.py:1549
  155.0 55.3 %collective-permute-start.6 = (bf16[2,96,1536]{2,1,0:T(8,128)(2,1)}, bf16[2,96,1536]{2,1,0:T(8,128)(2,1)}, u32[]{:S(2)}, u32[]{:S(2)}) collective-permute-start(bf16[2,96,1536]{2,1,0:T(8,128)(2,1)} %get-tuple-element.91), channel_id=1, source_target_pairs={{0,8},{8,16},{16,24},{24,0},{1,9},{9,17},{17,25},{25,1},{2,10},{10... | collective-permute-start | bytes 1769480 | tf_op jit(solution)/shard_map/ppermute | solution.py:1549
  157.4 52.9 %collective-permute-start.7 = (bf16[2,96,1536]{2,1,0:T(8,128)(2,1)}, bf16[2,96,1536]{2,1,0:T(8,128)(2,1)}, u32[]{:S(2)}, u32[]{:S(2)}) collective-permute-start(bf16[2,96,1536]{2,1,0:T(8,128)(2,1)} %get-tuple-element.92), channel_id=1, source_target_pairs={{0,16},{8,24},{16,0},{24,8},{1,17},{9,25},{17,1},{25,9},{2,18},{10... | collective-permute-start | bytes 1769480 | tf_op jit(solution)/shard_map/ppermute | solution.py:1549
  159.4 50.9 %collective-permute-start.8 = (bf16[2,96,1536]{2,1,0:T(8,128)(2,1)}, bf16[2,96,1536]{2,1,0:T(8,128)(2,1)}, u32[]{:S(2)}, u32[]{:S(2)}) collective-permute-start(bf16[2,96,1536]{2,1,0:T(8,128)(2,1)} %get-tuple-element.93), channel_id=1, source_target_pairs={{0,24},{8,0},{16,8},{24,16},{1,25},{9,1},{17,9},{25,17},{2,26},{10... | collective-permute-start | bytes 1769480 | tf_op jit(solution)/shard_map/ppermute | solution.py:1549
  162.2 122.4 %collective-permute-start.5 = (bf16[512,768]{1,0:T(8,128)(2,1)}, bf16[512,768]{1,0:T(8,128)(2,1)}, u32[]{:S(2)}, u32[]{:S(2)}) collective-permute-start(bf16[512,768]{1,0:T(8,128)(2,1)} %get-tuple-element.79), channel_id=1, source_target_pairs={{0,2},{2,0},{1,3},{3,1},{4,6},{6,4},{5,7},{7,5},{8,10},{10,8},{9,1... | collective-permute-start | bytes 2359304 | tf_op jit(solution)/shard_map/ppermute | solution.py:1553
  164.7 45.6 %collective-permute-start.9 = (bf16[4,384,384]{2,1,0:T(8,128)(2,1)}, bf16[4,384,384]{2,1,0:T(8,128)(2,1)}, u32[]{:S(2)}, u32[]{:S(2)}) collective-permute-start(bf16[4,384,384]{2,1,0:T(8,128)(2,1)} %get-tuple-element.95), channel_id=1, source_target_pairs={{0,4},{4,0},{1,5},{5,1},{2,6},{6,2},{3,7},{7,3},{8,12},{12,8},{9,1... | collective-permute-start | bytes 3538952 | tf_op jit(solution)/shard_map/ppermute | solution.py:1549

commit v8 on v7

--- a/solution.py
+++ b/solution.py
@@ -463,7 +463,8 @@
     for copy in loads:
         copy.wait()
     for i, vector in enumerate(raw):
-        vpack[i : i + 1, 0 : vector.shape[1]] = vector[...].astype(jnp.bfloat16).astype(jnp.float32)
+        size = vector.shape[0]
+        vpack[i : i + 1, 0:size] = vector[...].reshape(1, size).astype(jnp.bfloat16).astype(jnp.float32)
     for i in range(3):
         for p in range(pairs):
             pack[:, (3 * p + i) * 128 : (3 * p + i + 1) * 128] = wbuf[i, :, p * 128 : (p + 1) * 128].astype(jnp.bfloat16)
@@ -604,7 +605,7 @@
                 for stream in range(3):
                     z_move(stream, way, t).wait_send()
 
-    short = min(vector.shape[1] for vector in raw)
+    short = min(vector.shape[0] for vector in raw)
     longest = vpack.shape[1]
     for s in range(size_z * size_x):
         rows_out[:, s * short : (s + 1) * short] = vectors_all[s, :, 0:short]
@@ -647,7 +648,7 @@
         ),
         in_specs=[anywhere] * (8 + count),
         out_specs=(anywhere,) * 5 + (vmem,) * 2,
-        scratch_shapes=[pltpu.VMEM((1, v.shape[0]), v.dtype) for v in vectors]
+        scratch_shapes=[pltpu.VMEM(v.shape, v.dtype) for v in vectors]
         + [
             pltpu.VMEM((part, width), low),
             pltpu.VMEM((part, width), low),
@@ -674,7 +675,7 @@
         ],
         compiler_params=pltpu.CompilerParams(collective_id=0, has_side_effects=True, vmem_limit_bytes=66_000_000),
         name="entry",
-    )(tokens, cotangent, wq, wk, wv, w_inner, w_output, w_outer, *[v.reshape(1, -1) for v in vectors])
+    )(tokens, cotangent, wq, wk, wv, w_inner, w_output, w_outer, *vectors)
 
 
 def exit_kernel(size_z, size_x, shapes, *refs):
@@ -683,14 +684,13 @@
     inner_in = refs[8 : 8 + size_z]
     outer_in = refs[8 + size_z : 8 + size_z + size_x]
     refs = refs[8 + size_z + size_x :]
-    results = refs[:8]
-    made = refs[8:16]
+    made = refs[:8]
     token_grads, grad_query, grad_key, grad_value, grad_output, grad_inner, grad_outer, vector_sums = made
-    grads, inputs, turned, weights, base, terms, other_rows, recv_rows, send_rows, far_rows, odd = refs[16:27]
-    inner_buf, outer_buf, vector_rows, vector_terms, inner_send, store_sem = refs[27:33]
-    load_sem, tsend, trecv, osend, orecv = refs[33:38]
-    refs = list(refs[38:])
-    stores = [pltpu.make_async_copy(a, b, store_sem.at[i]) for i, (a, b) in enumerate(zip(made, results))]
+    grads, inputs, turned, weights, base, terms_a, terms_b, other_rows, recv_rows, send_rows, far_rows, odd = refs[8:20]
+    inner_buf, outer_buf, vector_rows, vector_terms, inner_send = refs[20:25]
+    load_sem, tsend, trecv, osend, orecv = refs[25:30]
+    refs = list(refs[30:])
+    terms = {"qa": terms_a, "qb": terms_b}
     xin, xsend, xrecv = {}, {}, {}
     zout, zin, zsend, zrecv = {}, {}, {}, {}
     ybuf, ysend, yrecv, cbuf, csend, crecv = {}, {}, {}, {}, {}, {}
@@ -701,8 +701,7 @@
         if name != "inner":
             zout[name], zin[name], zsend[name], zrecv[name] = [refs.pop(0) for _ in range(4)]
 
-    shards, rows, full = terms.shape
-    half = full // 4
+    shards, rows, half = odd.shape
     lanes = 3 * half
     pairs = half // 128
     hidden = grad_inner.shape[1]
@@ -740,7 +739,7 @@
         return remote(src, dst, xsend[name].at[n, at, j - 1], xrecv[name].at[n, at, j - 1], partner(x=columns[j]))
 
     def x_pieces(name, at):
-        source = vector_terms if name == "vec" else terms
+        source = vector_terms if name == "vec" else terms[name]
         return [
             x_move(name, 0, at, j, source.at[at * size_x + columns[j]], xin[name].at[j - 1, at]) for j in range(1, size_x)
         ]
@@ -772,7 +771,7 @@
             return [(slice(None), total)]
         for move in x_pieces(name, at):
             move.wait()
-        total = terms[slot].astype(high)
+        total = terms[name][slot].astype(high)
         for j in range(1, size_x):
             total = total + xin[name][j - 1, at].astype(high)
         return [(slice(None), total)]
@@ -901,16 +900,20 @@
     loads["grads"].wait()
     for p in range(pairs):
         block = slice(p * 384, (p + 1) * 384)
+        where = slice(p % 2 * 384, p % 2 * 384 + 384)
+        goal = terms_a if p < 2 else terms_b
 
         def some(m, _):
             value = dot_nn(turned[pl.ds(pl.multiple_of(m * group * rows, group * rows), group * rows), :], grads[:, block])
-            terms[pl.ds(m * group, group), :, block] = value.reshape(group, rows, 384).astype(low)
+            goal[pl.ds(m * group, group), :, where] = value.reshape(group, rows, 384).astype(low)
             return 0
 
         lax.fori_loop(0, shards // group, some, 0)
+        if p == 1:
+            send_x("qa")
     outputs.wait()
-    terms[:, :, lanes : lanes + half] = (odd[...].astype(high) + output_term[:, :, mine].astype(high)).astype(low)
-    send_x("qkvo")
+    terms_b[:, :, half : 2 * half] = (odd[...].astype(high) + output_term[:, :, mine].astype(high)).astype(low)
+    send_x("qb")
     for name in ("weights", "base"):
         loads[name].wait()
     halves = token_rows(part)
@@ -920,12 +923,6 @@
     back.start()
 
     step_z("outer", 2)
-    halves = token_rows(0)
-    for t in range(3, size_z):
-        step_z("outer", t)
-    step_z("vec", 1)
-    step_z("qkvo", 1)
-
     total = inner_buf[0, x].astype(high)
     for i in range(1, size_z):
         total = total + inner_buf[i, x].astype(high)
@@ -934,20 +931,29 @@
         total = total + xin["inner"][j - 1, 0].astype(high)
     ybuf["inner"][0] = total.astype(low)
     step_y("inner")
+    for t in range(3, size_z):
+        step_z("outer", t)
+    step_z("vec", 1)
+    step_z("qa", 1)
+    halves = token_rows(0)
+    step_z("vec", 2)
+    step_z("qa", 2)
     finish_z("outer")
-    step_z("vec", 2)
-    step_z("qkvo", 2)
+    for t in range(3, size_z):
+        step_z("vec", t)
+        step_z("qa", t)
+    step_z("qb", 1)
     halves.wait()
     token_grads[y] = base[0:part, :] + recv_rows[0:part, :].astype(high)
     step_core("inner")
+    step_z("qb", 2)
+    finish_z("qa")
+    finish_z("vec")
     for t in range(3, size_z):
-        step_z("vec", t)
-        step_z("qkvo", t)
+        step_z("qb", t)
     step_core("outer")
-    finish_z("vec")
     back.wait()
     token_grads[1 - y] = far_rows[...].astype(high)
-    stores[0].start()
     chunks = hidden // CHUNK
     buf = finish_core("inner")
     for i in range(2):
@@ -955,15 +961,26 @@
         for c in range(chunks):
             place = pl.ds(pl.multiple_of(c * CHUNK + owner * half, 128), half)
             grad_inner[:, place] = buf[i, :, c * half : (c + 1) * half]
-    stores[5].start()
     buf = finish_core("outer")
     for i in range(2):
         owner = core if i == 0 else 1 - core
         grad_outer[:, pl.ds(pl.multiple_of(owner * half, 128), half)] = buf[i]
-    stores[6].start()
-    finish_z("qkvo")
+    finish_z("qb")
     step_core("vec")
-    step_core("qkvo")
+    step_core("qa")
+
+    def spread(name):
+        buf = finish_core(name)
+        for i in range(2):
+            owner = core if i == 0 else 1 - core
+            for p in (0, 1) if name == "qa" else (2,):
+                place = pl.ds(pl.multiple_of(owner * half + p * 128, 128), 128)
+                for n, out in enumerate((grad_query, grad_key, grad_value)):
+                    at = (3 * (p % 2) + n) * 128
+                    out[:, place] = buf[i, :, at : at + 128]
+            if name == "qb":
+                grad_output[:, pl.ds(pl.multiple_of(owner * half, 128), half)] = buf[i, :, half : 2 * half]
+
     for name in zout:
         for t, way in steps:
 
@@ -973,62 +990,44 @@
 
     buf = finish_core("vec")
     vector_sums[...] = buf[0] + buf[1]
-    stores[7].start()
-    buf = finish_core("qkvo")
-    for i in range(2):
-        owner = core if i == 0 else 1 - core
-        for p in range(pairs):
-            place = pl.ds(pl.multiple_of(owner * half + p * 128, 128), 128)
-            for n, out in enumerate((grad_query, grad_key, grad_value)):
-                out[:, place] = buf[i, :, (3 * p + n) * 128 : (3 * p + n + 1) * 128]
-        grad_output[:, pl.ds(pl.multiple_of(owner * half, 128), half)] = buf[i, :, lanes : lanes + half]
-    for i in range(1, 5):
-        stores[i].start()
-    for store in stores:
-        store.wait()
+    spread("qa")
+    step_core("qb")
+    spread("qb")
 
 
 def deliver_kernel(count, mixed_mine, mixed_far, *refs):
-    matrices, vectors = refs[:count], refs[count]
-    mixed = refs[count + 1]
+    matrices, vectors, mixed = refs[:count], refs[count], refs[count + 1]
     outs = refs[count + 2 : 2 * count + 2]
-    smalls = refs[2 * count + 2 : -(count + 4)]
-    stage, bufs, in_sem, out_sem = refs[-(count + 4) : -(count + 2)], refs[-(count + 2) : -2], refs[-2], refs[-1]
+    smalls = refs[2 * count + 2 : -4]
+    stage, in_sem, out_sem = refs[-4:-2], refs[-2], refs[-1]
     y = lax.axis_index("y")
-    moves = [(mixed_mine, stage[0], mixed.at[y]), (mixed_far, stage[1], mixed.at[1 - y])]
-    for src, buf, dst in zip(matrices, bufs, outs):
-        if len(src.shape) == 3:
-            moves += [(src.at[i], buf.at[i], dst.at[i]) for i in range(src.shape[0])]
-        else:
-            moves.append((src, buf, dst))
-    first = [pltpu.make_async_copy(src, buf, in_sem.at[i]) for i, (src, buf, _) in enumerate(moves)]
-    second = [pltpu.make_async_copy(buf, dst, out_sem.at[i]) for i, (_, buf, dst) in enumerate(moves)]
-    for copy in first:
+    loads = [pltpu.make_async_copy(src, stage[i], in_sem.at[i]) for i, src in enumerate((mixed_mine, mixed_far))]
+    copies = [pltpu.make_async_copy(src, dst, out_sem.at[i]) for i, (src, dst) in enumerate(zip(matrices, outs))]
+    for copy in loads + copies:
         copy.start()
     for i, small in enumerate(smalls):
-        small[...] = vectors[i : i + 1, 0 : small.shape[1]]
-    for arrived, leaving in zip(first, second):
-        arrived.wait()
-        leaving.start()
-    for copy in second:
+        small[...] = vectors[i : i + 1, 0 : small.shape[0]].reshape(small.shape)
+    for i, place in enumerate((y, 1 - y)):
+        loads[i].wait()
+        copies.append(pltpu.make_async_copy(stage[i], mixed.at[place], out_sem.at[count + i]))
+        copies[-1].start()
+    for copy in copies:
         copy.wait()
 
 
 def deliver(mixed_mine, mixed_far, matrices, vectors, sizes):
     count = len(matrices)
     vmem, anywhere = pl.BlockSpec(memory_space=pltpu.VMEM), pl.BlockSpec(memory_space=pl.ANY)
-    moves = count + 4
     return pl.pallas_call(
         lambda *refs: deliver_kernel(count, *refs),
         out_shape=(jax.ShapeDtypeStruct((2,) + mixed_mine.shape, mixed_mine.dtype),)
         + tuple(jax.ShapeDtypeStruct(m.shape, m.dtype) for m in matrices)
-        + tuple(jax.ShapeDtypeStruct((1, size), jnp.float32) for size in sizes),
-        in_specs=[anywhere] * (2 + count) + [vmem],
+        + tuple(jax.ShapeDtypeStruct((size,), jnp.float32) for size in sizes),
+        in_specs=[anywhere] * 2 + [vmem] * (count + 1),
         out_specs=(anywhere,) * (count + 1) + (vmem,) * len(sizes),
         scratch_shapes=[pltpu.VMEM(mixed_mine.shape, mixed_mine.dtype)] * 2
-        + [pltpu.VMEM(m.shape, m.dtype) for m in matrices]
-        + [pltpu.SemaphoreType.DMA((moves,))] * 2,
-        compiler_params=pltpu.CompilerParams(vmem_limit_bytes=60_000_000),
+        + [pltpu.SemaphoreType.DMA((2,)), pltpu.SemaphoreType.DMA((count + 2,))],
+        compiler_params=pltpu.CompilerParams(vmem_limit_bytes=40_000_000),
         name="deliver",
     )(mixed_mine, mixed_far, *matrices, vectors)
 
@@ -1051,7 +1050,8 @@
     vector_shape = (16, hidden // shards)
     shapes = {
         "vec": (vector_shape, high, 1),
-        "qkvo": ((rows, full), low, 1),
+        "qa": ((rows, width), low, 1),
+        "qb": ((rows, width), low, 1),
         "inner": ((rows, hidden // 2), low, 1),
         "outer": ((long, half), low, 1),
     }
@@ -1066,13 +1066,14 @@
         jax.ShapeDtypeStruct((long, width), high),
         jax.ShapeDtypeStruct(vector_shape, high),
     )
-    scratch = [pltpu.VMEM(r.shape, r.dtype) for r in results] + [
+    scratch = [
         pltpu.VMEM((length, lanes), low),
         pltpu.VMEM((length, width), low),
         pltpu.VMEM((width, length), low),
         pltpu.VMEM((width, lanes), low),
         pltpu.VMEM((local, width), high),
-        pltpu.VMEM((shards, rows, full), low),
+        pltpu.VMEM((shards, rows, width), low),
+        pltpu.VMEM((shards, rows, width), low),
         pltpu.VMEM((local, width), low),
         pltpu.VMEM((local, width), low),
         pltpu.VMEM((part, width), low),
@@ -1083,7 +1084,6 @@
         pltpu.VMEM((16, width), high),
         pltpu.VMEM((shards,) + vector_shape, high),
         pltpu.VMEM((side, rows, hidden // 2), low),
-        dma((len(results),)),
         dma((size_z + size_x + 4,)),
         dma((3,)),
         dma((3,)),
@@ -1099,11 +1099,11 @@
             scratch += [pltpu.VMEM((2, size_z - 1) + shape, kind)] * 2 + [dma((2, size_z - 1))] * 2
     return pl.pallas_call(
         lambda *refs: exit_kernel(size_z, size_x, shapes, *refs),
-        out_shape=results,
+        out_shape=tuple(pltpu.VMEM(r.shape, r.dtype) for r in results),
         in_specs=[anywhere] * 4 + [vmem] * 4 + [anywhere] * (size_z + size_x),
-        out_specs=(anywhere,) * len(results),
+        out_specs=(vmem,) * len(results),
         scratch_shapes=scratch,
-        compiler_params=pltpu.CompilerParams(collective_id=1, has_side_effects=True, vmem_limit_bytes=67_000_000),
+        compiler_params=pltpu.CompilerParams(collective_id=1, has_side_effects=True, vmem_limit_bytes=56_000_000),
         name="exit",
     )(grads, inputs, weights, base, output_term, dense_sums, inner_sums, head_sums, *inner_terms, *outer_terms)
 
@@ -1873,7 +1873,6 @@
     mixed_out, grad_tokens, grad_query, grad_key, grad_value, grad_output, grad_inner_full, grad_outer_full, *done = deliver(
         mixed, mixed_far, made[:7], made[7], sizes
     )
-    done = [v.reshape(size) for v, size in zip(done, sizes)]
     return (
         mixed_out,
         grad_tokens,

time: 292 us -> 285 us (0.976); the launches traced: 294 us -> 283 us
  Pallas kernels: 270 us -> 260 us
    pallas_call x1, Pallas kernels: 8.01 us -> 4.05 us  [deliver(): pl.pallas_call(lambda *refs: deliver_kernel(count, *refs), out_shape=(jax...]
where the time goes in v8:
time: 285 us; the launch traced here: 283 us
  Pallas kernels  260 us (91%)
  starting transfers between devices  14.3 us (5%)
  waiting for transfers between devices  6.54 us (2%)
    pallas_call x1, Pallas kernels, exit_call(): pl.pallas_call(lambda *refs: exit_kernel(size_z, size_x, shapes, *refs),...  71.6 us
    pallas_call x1, Pallas kernels, dense_layer(): pl.pallas_call(lambda *refs: dense_kernel(size_z, size_x, *refs), out_sha...  61.8 us
    pallas_call x1, Pallas kernels, entry(): pl.pallas_call(lambda *refs: entry_kernel(size_z, size_x, count, *refs),...  42.3 us
    pallas_call x1, Pallas kernels, attention_back(): pl.pallas_call(backward_kernel, out_shape=(jax.ShapeDtypeStruct((length,...  41.5 us
    pallas_call x1, Pallas kernels, attention(): pl.pallas_call(forward_kernel, out_shape=(jax.ShapeDtypeStruct((rows, pai...  38.4 us
    ppermute x8, starting transfers between devices, shift(): lax.ppermute(piece, axis, [(i, (i + step) % size) for i in range(size)])  13.8 us
    ppermute x8, waiting for transfers between devices, shift(): lax.ppermute(piece, axis, [(i, (i + step) % size) for i in range(size)])  6.54 us
  transfers between devices with their start and end apart: 10, of which 1 were waited for; matrix products, arithmetic and copies ran while one was open for 0% of the time, Pallas kernels for 54%

profile of v8, /device:TPU:0, one launch (start us, length us, event | category | flops | bytes accessed | tf_op | source)
XLA Modules:
  0.0 282.8 jit_solution(17737275548049497656)
XLA Ops:
  0.7 42.3 %entry.1 = (bf16[4,512,768]{2,1,0:T(8,128)(2,1)}, bf16[512,768]{1,0:T(8,128)(2,1)}, bf16[8,96,1152]{2,1,0:T(8,128)(2,1)}, bf16[4,96,1920]{2,1,0:T(8,128)(2,1)}, ...) custom-call(bf16[2,512,768]{2,1,0:T(8,128)(2,1)} %refs_0_.1, bf16[2,512,768]{2,1,0:T(8,128)(2,1)} %refs_3_.3, ...), custom_call_target="tpu_custom_call" | custom-call | tf_op jit(solution)/shard_map/entry/pallas_call | solution.py:638
  42.9 1.5 collective-permute-start.4
  44.5 0.6 collective-permute-start.2
  45.1 0.5 collective-permute-start
  45.6 1.5 collective-permute-start.1
  47.1 38.4 %attention_forward.1 = (bf16[1024,384]{1,0:T(8,128)(2,1)}, bf16[1024,384]{1,0:T(8,128)(2,1)}, f32[24,2048]{1,0:T(8,128)}, bf16[2048,1152]{1,0:T(8,128)(2,1)}) custom-call(s32[2,2048]{1,0:T(2,128)} %row_ref.3, s32[2,2048]{1,0:T(2,128)} %row_ref.3, bf16[2048,768]{1,0:T(8,128)(2,1)} %bitcast.3, bf16[768,1152]{1,0:T(8,128)(2,1)} %bitcast.6, ...), custom_call_target="tpu_custom_call" | custom-call | flops 120000004096 | bytes 9000000 | tf_op jit(solution)/shard_map/attention_forward/pallas_call | solution.py:183
  85.5 0.0 collective-permute-done.4.refs_12_
  85.5 6.5 %collective-permute-done.3.refs_11_ = bf16[2,384,384]{2,1,0:T(8,128)(2,1)} collective-permute-done((bf16[2,384,384]{2,1,0:T(8,128)(2,1)}, bf16[2,384,384]{2,1,0:T(8,128)(2,1)}, u32[]{:S(2)}, u32[]{:S(2)}) %collective-permute-start.3) | collective-permute-done | bytes 589856 | tf_op jit(solution)/shard_map/ppermute | solution.py:1549
  92.1 61.8 %dense_layer.1 = (bf16[512,768]{1,0:T(8,128)(2,1)}, bf16[512,768]{1,0:T(8,128)(2,1)}, f32[1024,768]{1,0:T(8,128)}, bf16[1024,384]{1,0:T(8,128)(2,1)}, bf16[1024,...) custom-call(bf16[2048,768]{1,0:T(8,128)(2,1)} %bitcast.4, ...), custom_call_target="tpu_custom_call" | custom-call | flops 32000000000 | bytes 40000000 | tf_op jit(solution)/shard_map/dense_layer/pallas_call | solution.py:1414
  153.9 7.1 %collective-permute-start.6 = (bf16[2,96,1536]{2,1,0:T(8,128)(2,1)}, bf16[2,96,1536]{2,1,0:T(8,128)(2,1)S(1)}, u32[]{:S(2)}, u32[]{:S(2)}) collective-permute-start(bf16[2,96,1536]{2,1,0:T(8,128)(2,1)} %get-tuple-element.91), channel_id=1, source_target_pairs={{0,8},{8,16},{16,24},{24,0},{1,9},{9,17},{17,25},{25,1},{2,10},{10... | collective-permute-start | bytes 1769480 | tf_op jit(solution)/shard_map/ppermute | solution.py:1549
  161.0 0.0 collective-permute-start.7
  161.0 2.4 collective-permute-start.8
  163.4 0.0 collective-permute-start.5
  163.4 0.6 collective-permute-start.9
  164.0 41.5 %attention_backward.1 = (bf16[2048,1152]{1,0:T(8,128)(2,1)}, f32[24,384]{1,0:T(8,128)}) custom-call(s32[2,2048]{1,0:T(2,128)} %row_ref.3, bf16[2048,1152]{1,0:T(8,128)(2,1)} %get-tuple-element.80.qkv_ref, bf16[1024,384]{1,0:T(8,128)(2,1)} %get-tuple-element.72.refs_1_.ctx_mine_ref, bf16[1024,384]{1,0:T(8,128)(2,1)} %get-tuple-element.73.refs_2_.ctx_other_ref, ...), custom_call_target="tpu_custom_call" | custom-call | flops 60000002048 | bytes 15000000 | tf_op jit(solution)/shard_map/attention_backward/pallas_call | solution.py:350
  205.5 0.0 copy-start.2
  205.5 0.0 copy-start.3
  205.6 0.0 collective-permute-done.8.refs_11_
  205.6 0.0 copy-start.1
  205.6 0.7 copy-done.2
  206.3 0.2 copy-done.3
  206.5 0.4 copy-done.1
  206.9 71.6 %exit.1 = (f32[2,512,768]{2,1,0:T(8,128)S(1)}, f32[96,768]{1,0:T(8,128)S(1)}, f32[96,768]{1,0:T(8,128)S(1)}, f32[96,768]{1,0:T(8,128)S(1)}, f32[96,768]{1,0:T(8,...) custom-call(bf16[2048,1152]{1,0:T(8,128)(2,1)} %get-tuple-element.84.refs_0_, ...), custom_call_target="tpu_custom_call" | custom-call | tf_op jit(solution)/shard_map/exit/pallas_call | solution.py:1100
  278.5 4.1 %deliver.1 = (bf16[2,512,768]{2,1,0:T(8,128)(2,1)}, f32[2,512,768]{2,1,0:T(8,128)}, f32[96,768]{1,0:T(8,128)}, f32[96,768]{1,0:T(8,128)}, f32[96,768]{1,0:T(8,12...) custom-call(bf16[512,768]{1,0:T(8,128)(2,1)S(1)} %copy-done, ...), custom_call_target="tpu_custom_call" | custom-call | tf_op jit(solution)/shard_map/deliver/pallas_call | solution.py:1021
  (10 shorter events, 0.0 us)
Async XLA Ops:
  42.9 42.6 %collective-permute-start.4 = (bf16[2,384,384]{2,1,0:T(8,128)(2,1)}, bf16[2,384,384]{2,1,0:T(8,128)(2,1)}, u32[]{:S(2)}, u32[]{:S(2)}) collective-permute-start(bf16[2,384,384]{2,1,0:T(8,128)(2,1)} %get-tuple-element.77.refs_9_), channel_id=1, source_target_pairs={{0,24},{8,0},{16,8},{24,16},{1,25},{9,1},{17,9},{25,17},{2,26},{10... | collective-permute-start | bytes 1769480 | tf_op jit(solution)/shard_map/ppermute | solution.py:1549
  44.4 47.6 %collective-permute-start.3 = (bf16[2,384,384]{2,1,0:T(8,128)(2,1)}, bf16[2,384,384]{2,1,0:T(8,128)(2,1)}, u32[]{:S(2)}, u32[]{:S(2)}) collective-permute-start(bf16[2,384,384]{2,1,0:T(8,128)(2,1)} %get-tuple-element.77.refs_9_), channel_id=1, source_target_pairs={{0,16},{8,24},{16,0},{24,8},{1,17},{9,25},{17,1},{25,9},{2,18},{10... | collective-permute-start | bytes 1769480 | tf_op jit(solution)/shard_map/ppermute | solution.py:1549
  44.5 47.6 %collective-permute-start.2 = (bf16[2,384,384]{2,1,0:T(8,128)(2,1)}, bf16[2,384,384]{2,1,0:T(8,128)(2,1)}, u32[]{:S(2)}, u32[]{:S(2)}) collective-permute-start(bf16[2,384,384]{2,1,0:T(8,128)(2,1)} %get-tuple-element.77.refs_9_), channel_id=1, source_target_pairs={{0,8},{8,16},{16,24},{24,0},{1,9},{9,17},{17,25},{25,1},{2,10},{10... | collective-permute-start | bytes 1769480 | tf_op jit(solution)/shard_map/ppermute | solution.py:1549
  45.1 47.0 %collective-permute-start = (bf16[512,768]{1,0:T(8,128)(2,1)}, bf16[512,768]{1,0:T(8,128)(2,1)}, u32[]{:S(2)}, u32[]{:S(2)}) collective-permute-start(bf16[512,768]{1,0:T(8,128)(2,1)} %get-tuple-element.74), channel_id=1, source_target_pairs={{0,2},{2,0},{1,3},{3,1},{4,6},{6,4},{5,7},{7,5},{8,10},{10,8},{9,1... | collective-permute-start | bytes 2359304 | tf_op jit(solution)/shard_map/ppermute | solution.py:1553
  45.6 46.4 %collective-permute-start.1 = (bf16[4,96,1920]{2,1,0:T(8,128)(2,1)}, bf16[4,96,1920]{2,1,0:T(8,128)(2,1)}, u32[]{:S(2)}, u32[]{:S(2)}) collective-permute-start(bf16[4,96,1920]{2,1,0:T(8,128)(2,1)} %get-tuple-element.76.refs_7_), channel_id=1, source_target_pairs={{0,4},{4,0},{1,5},{5,1},{2,6},{6,2},{3,7},{7,3},{8,12},{12,8},{9,1... | collective-permute-start | bytes 4423688 | tf_op jit(solution)/shard_map/ppermute | solution.py:1549
  153.9 51.6 %collective-permute-start.6 = (bf16[2,96,1536]{2,1,0:T(8,128)(2,1)}, bf16[2,96,1536]{2,1,0:T(8,128)(2,1)S(1)}, u32[]{:S(2)}, u32[]{:S(2)}) collective-permute-start(bf16[2,96,1536]{2,1,0:T(8,128)(2,1)} %get-tuple-element.91), channel_id=1, source_target_pairs={{0,8},{8,16},{16,24},{24,0},{1,9},{9,17},{17,25},{25,1},{2,10},{10... | collective-permute-start | bytes 1769480 | tf_op jit(solution)/shard_map/ppermute | solution.py:1549
  161.0 44.6 %collective-permute-start.7 = (bf16[2,96,1536]{2,1,0:T(8,128)(2,1)}, bf16[2,96,1536]{2,1,0:T(8,128)(2,1)S(1)}, u32[]{:S(2)}, u32[]{:S(2)}) collective-permute-start(bf16[2,96,1536]{2,1,0:T(8,128)(2,1)} %get-tuple-element.92), channel_id=1, source_target_pairs={{0,16},{8,24},{16,0},{24,8},{1,17},{9,25},{17,1},{25,9},{2,18},{10... | collective-permute-start | bytes 1769480 | tf_op jit(solution)/shard_map/ppermute | solution.py:1549
  161.0 44.6 %collective-permute-start.8 = (bf16[2,96,1536]{2,1,0:T(8,128)(2,1)}, bf16[2,96,1536]{2,1,0:T(8,128)(2,1)}, u32[]{:S(2)}, u32[]{:S(2)}) collective-permute-start(bf16[2,96,1536]{2,1,0:T(8,128)(2,1)} %get-tuple-element.93), channel_id=1, source_target_pairs={{0,24},{8,0},{16,8},{24,16},{1,25},{9,1},{17,9},{25,17},{2,26},{10... | collective-permute-start | bytes 1769480 | tf_op jit(solution)/shard_map/ppermute | solution.py:1549
  163.4 115.1 %collective-permute-start.5 = (bf16[512,768]{1,0:T(8,128)(2,1)}, bf16[512,768]{1,0:T(8,128)(2,1)S(1)}, u32[]{:S(2)}, u32[]{:S(2)}) collective-permute-start(bf16[512,768]{1,0:T(8,128)(2,1)} %get-tuple-element.79), channel_id=1, source_target_pairs={{0,2},{2,0},{1,3},{3,1},{4,6},{6,4},{5,7},{7,5},{8,10},{10,8},{9,1... | collective-permute-start | bytes 2359304 | tf_op jit(solution)/shard_map/ppermute | solution.py:1553
  163.4 42.1 %collective-permute-start.9 = (bf16[4,384,384]{2,1,0:T(8,128)(2,1)}, bf16[4,384,384]{2,1,0:T(8,128)(2,1)S(1)}, u32[]{:S(2)}, u32[]{:S(2)}) collective-permute-start(bf16[4,384,384]{2,1,0:T(8,128)(2,1)} %get-tuple-element.95), channel_id=1, source_target_pairs={{0,4},{4,0},{1,5},{5,1},{2,6},{6,2},{3,7},{7,3},{8,12},{12,8},{9,1... | collective-permute-start | bytes 3538952 | tf_op jit(solution)/shard_map/ppermute | solution.py:1549
  205.5 0.8 copy-start.2
  205.5 1.0 copy-start.3
  205.6 1.3 copy-start.1
  206.9 71.6 %copy-start = (bf16[512,768]{1,0:T(8,128)(2,1)S(1)}, bf16[512,768]{1,0:T(8,128)(2,1)}, u32[]{:S(2)}) copy-start(bf16[512,768]{1,0:T(8,128)(2,1)} %get-tuple-element.78.refs_0_) | copy-start | bytes 2359300

commit v9 on v8

--- a/solution.py
+++ b/solution.py
@@ -720,7 +720,7 @@
     for i, src in enumerate(outer_in):
         loads["outer", i] = pltpu.make_async_copy(src, outer_buf.at[i], load_sem.at[size_z + i])
     for i, (name, src, dst) in enumerate(
-        (("inputs", inputs_hbm, inputs), ("grads", grads_hbm, grads), ("weights", weights_hbm, weights), ("base", base_hbm, base))
+        (("grads", grads_hbm, grads), ("weights", weights_hbm, weights), ("base", base_hbm, base), ("inputs", inputs_hbm, inputs))
     ):
         loads[name] = pltpu.make_async_copy(src, dst, load_sem.at[size_z + size_x + i])
     for load in loads.values():
@@ -744,16 +744,17 @@
             x_move(name, 0, at, j, source.at[at * size_x + columns[j]], xin[name].at[j - 1, at]) for j in range(1, size_x)
         ]
 
-    def send_x(name):
+    def send_own(name):
+        for move in x_pieces(name, z):
+            move.start()
+
+    def send_far(name):
         for t, way in steps:
 
             @pl.when(inside(target_of(t, way)))
             def _():
                 for move in x_pieces(name, target_of(t, way)):
                     move.start()
-
-        for move in x_pieces(name, z):
-            move.start()
 
     def own_part(name, at):
         if name == "outer":
@@ -853,7 +854,8 @@
 
     outputs = remote(output_term.at[:, :, theirs], odd, osend, orecv, core_peer)
     outputs.start()
-    send_x("vec")
+    send_far("vec")
+    send_own("vec")
     for i in range(size_z):
         loads["inner", i].wait()
     inner_moves = []
@@ -893,28 +895,7 @@
         lax.fori_loop(0, part // strip, own_strip, 0)
         return move
 
-    loads["inputs"].wait()
-    for b in range(4):
-        turned[:, b * part : (b + 1) * part] = inputs[b * part : (b + 1) * part, :].T
-    group = 4
-    loads["grads"].wait()
-    for p in range(pairs):
-        block = slice(p * 384, (p + 1) * 384)
-        where = slice(p % 2 * 384, p % 2 * 384 + 384)
-        goal = terms_a if p < 2 else terms_b
-
-        def some(m, _):
-            value = dot_nn(turned[pl.ds(pl.multiple_of(m * group * rows, group * rows), group * rows), :], grads[:, block])
-            goal[pl.ds(m * group, group), :, where] = value.reshape(group, rows, 384).astype(low)
-            return 0
-
-        lax.fori_loop(0, shards // group, some, 0)
-        if p == 1:
-            send_x("qa")
-    outputs.wait()
-    terms_b[:, :, half : 2 * half] = (odd[...].astype(high) + output_term[:, :, mine].astype(high)).astype(low)
-    send_x("qb")
-    for name in ("weights", "base"):
+    for name in ("grads", "weights", "base"):
         loads[name].wait()
     halves = token_rows(part)
     halves.wait()
@@ -923,6 +904,28 @@
     back.start()
 
     step_z("outer", 2)
+    loads["inputs"].wait()
+    for b in range(4):
+        turned[:, b * part : (b + 1) * part] = inputs[b * part : (b + 1) * part, :].T
+    group = 4
+    for p in range(pairs):
+        block = slice(p * 384, (p + 1) * 384)
+        where = slice(p % 2 * 384, p % 2 * 384 + 384)
+        goal = terms_a if p < 2 else terms_b
+
+        def some(m, _):
+            value = dot_nn(turned[pl.ds(pl.multiple_of(m * group * rows, group * rows), group * rows), :], grads[:, block])
+            goal[pl.ds(m * group, group), :, where] = value.reshape(group, rows, 384).astype(low)
+            return 0
+
+        lax.fori_loop(0, shards // group, some, 0)
+        if p == 1:
+            send_far("qa")
+    outputs.wait()
+    terms_b[:, :, half : 2 * half] = (odd[...].astype(high) + output_term[:, :, mine].astype(high)).astype(low)
+    send_far("qb")
+    send_own("qa")
+    send_own("qb")
     total = inner_buf[0, x].astype(high)
     for i in range(1, size_z):
         total = total + inner_buf[i, x].astype(high)
@@ -947,10 +950,10 @@
     token_grads[y] = base[0:part, :] + recv_rows[0:part, :].astype(high)
     step_core("inner")
     step_z("qb", 2)
+    for t in range(3, size_z):
+        step_z("qb", t)
     finish_z("qa")
     finish_z("vec")
-    for t in range(3, size_z):
-        step_z("qb", t)
     step_core("outer")
     back.wait()
     token_grads[1 - y] = far_rows[...].astype(high)

time: 285 us -> 281 us (0.986)
  Pallas kernels: 260 us -> 252 us
    pallas_call x1, Pallas kernels: 71.6 us -> 64.3 us  [exit_call(): pl.pallas_call(lambda *refs: exit_kernel(size_z, size_x, shapes, *refs),...]
    ppermute x2, starting transfers between devices: 0.51 us -> 4.84 us  [swap(): return lax.ppermute(piece, axis, [(0, 1), (1, 0)])]
    ppermute x8, starting transfers between devices: 13.8 us -> 10.9 us  [shift(): lax.ppermute(piece, axis, [(i, (i + step) % size) for i in range(size)])]
  transfers between devices with their start and end apart: 10 -> 10, of which waited for: 1 -> 1; matrix products, arithmetic and copies ran while one was open for 0% -> 0% of each run, Pallas kernels for 54% -> 52%
where the time goes in v9:
time: 281 us; the launch traced here: 277 us
  Pallas kernels  252 us (90%)
  starting transfers between devices  15.8 us (6%)
  waiting for transfers between devices  6.54 us (2%)
    pallas_call x1, Pallas kernels, exit_call(): pl.pallas_call(lambda *refs: exit_kernel(size_z, size_x, shapes, *refs),...  64.3 us
    pallas_call x1, Pallas kernels, dense_layer(): pl.pallas_call(lambda *refs: dense_kernel(size_z, size_x, *refs), out_sha...  61.8 us
    pallas_call x1, Pallas kernels, entry(): pl.pallas_call(lambda *refs: entry_kernel(size_z, size_x, count, *refs),...  42.3 us
    pallas_call x1, Pallas kernels, attention_back(): pl.pallas_call(backward_kernel, out_shape=(jax.ShapeDtypeStruct((length,...  41.5 us
    pallas_call x1, Pallas kernels, attention(): pl.pallas_call(forward_kernel, out_shape=(jax.ShapeDtypeStruct((rows, pai...  38.4 us
    ppermute x8, starting transfers between devices, shift(): lax.ppermute(piece, axis, [(i, (i + step) % size) for i in range(size)])  10.9 us
    ppermute x8, waiting for transfers between devices, shift(): lax.ppermute(piece, axis, [(i, (i + step) % size) for i in range(size)])  6.54 us
  transfers between devices with their start and end apart: 10, of which 1 were waited for; matrix products, arithmetic and copies ran while one was open for 0% of the time, Pallas kernels for 52%

profile of v9, /device:TPU:0, one launch (start us, length us, event | category | flops | bytes accessed | tf_op | source)
XLA Modules:
  0.0 277.0 jit_solution(16125761669478597720)
XLA Ops:
  0.7 42.3 %entry.1 = (bf16[4,512,768]{2,1,0:T(8,128)(2,1)}, bf16[512,768]{1,0:T(8,128)(2,1)}, bf16[8,96,1152]{2,1,0:T(8,128)(2,1)}, bf16[4,96,1920]{2,1,0:T(8,128)(2,1)}, ...) custom-call(bf16[2,512,768]{2,1,0:T(8,128)(2,1)} %refs_0_.1, bf16[2,512,768]{2,1,0:T(8,128)(2,1)} %refs_3_.3, ...), custom_call_target="tpu_custom_call" | custom-call | tf_op jit(solution)/shard_map/entry/pallas_call | solution.py:638
  42.9 1.5 collective-permute-start.4
  44.5 0.6 collective-permute-start.2
  45.1 0.5 collective-permute-start
  45.6 1.5 collective-permute-start.1
  47.1 38.4 %attention_forward.1 = (bf16[1024,384]{1,0:T(8,128)(2,1)}, bf16[1024,384]{1,0:T(8,128)(2,1)}, f32[24,2048]{1,0:T(8,128)}, bf16[2048,1152]{1,0:T(8,128)(2,1)}) custom-call(s32[2,2048]{1,0:T(2,128)} %row_ref.3, s32[2,2048]{1,0:T(2,128)} %row_ref.3, bf16[2048,768]{1,0:T(8,128)(2,1)} %bitcast.3, bf16[768,1152]{1,0:T(8,128)(2,1)} %bitcast.6, ...), custom_call_target="tpu_custom_call" | custom-call | flops 120000004096 | bytes 9000000 | tf_op jit(solution)/shard_map/attention_forward/pallas_call | solution.py:183
  85.5 6.5 %collective-permute-done.3.refs_11_ = bf16[2,384,384]{2,1,0:T(8,128)(2,1)} collective-permute-done((bf16[2,384,384]{2,1,0:T(8,128)(2,1)}, bf16[2,384,384]{2,1,0:T(8,128)(2,1)}, u32[]{:S(2)}, u32[]{:S(2)}) %collective-permute-start.3) | collective-permute-done | bytes 589856 | tf_op jit(solution)/shard_map/ppermute | solution.py:1552
  92.0 0.0 collective-permute-done.2.refs_10_
  92.0 0.0 collective-permute-done.refs_4_
  92.0 0.0 collective-permute-done.1.refs_8_
  92.1 61.8 %dense_layer.1 = (bf16[512,768]{1,0:T(8,128)(2,1)}, bf16[512,768]{1,0:T(8,128)(2,1)}, f32[1024,768]{1,0:T(8,128)}, bf16[1024,384]{1,0:T(8,128)(2,1)}, bf16[1024,...) custom-call(bf16[2048,768]{1,0:T(8,128)(2,1)} %bitcast.4, ...), custom_call_target="tpu_custom_call" | custom-call | flops 32000000000 | bytes 40000000 | tf_op jit(solution)/shard_map/dense_layer/pallas_call | solution.py:1417
  153.9 4.5 %collective-permute-start.6 = (bf16[2,96,1536]{2,1,0:T(8,128)(2,1)}, bf16[2,96,1536]{2,1,0:T(8,128)(2,1)S(1)}, u32[]{:S(2)}, u32[]{:S(2)}) collective-permute-start(bf16[2,96,1536]{2,1,0:T(8,128)(2,1)} %get-tuple-element.91), channel_id=1, source_target_pairs={{0,8},{8,16},{16,24},{24,0},{1,9},{9,17},{17,25},{25,1},{2,10},{10... | collective-permute-start | bytes 1769480 | tf_op jit(solution)/shard_map/ppermute | solution.py:1552
  158.4 0.9 collective-permute-start.7
  159.3 1.9 collective-permute-start.8
  161.1 4.3 %collective-permute-start.5 = (bf16[512,768]{1,0:T(8,128)(2,1)}, bf16[512,768]{1,0:T(8,128)(2,1)S(1)}, u32[]{:S(2)}, u32[]{:S(2)}) collective-permute-start(bf16[512,768]{1,0:T(8,128)(2,1)} %get-tuple-element.79), channel_id=1, source_target_pairs={{0,2},{2,0},{1,3},{3,1},{4,6},{6,4},{5,7},{7,5},{8,10},{10,8},{9,1... | collective-permute-start | bytes 2359304 | tf_op jit(solution)/shard_map/ppermute | solution.py:1556
  165.5 41.5 %attention_backward.1 = (bf16[2048,1152]{1,0:T(8,128)(2,1)}, f32[24,384]{1,0:T(8,128)}) custom-call(s32[2,2048]{1,0:T(2,128)} %row_ref.3, bf16[2048,1152]{1,0:T(8,128)(2,1)} %get-tuple-element.80.qkv_ref, bf16[1024,384]{1,0:T(8,128)(2,1)} %get-tuple-element.72.refs_1_.ctx_mine_ref, bf16[1024,384]{1,0:T(8,128)(2,1)} %get-tuple-element.73.refs_2_.ctx_other_ref, ...), custom_call_target="tpu_custom_call" | custom-call | flops 60000002048 | bytes 15000000 | tf_op jit(solution)/shard_map/attention_backward/pallas_call | solution.py:350
  207.0 0.0 copy-start.2
  207.0 0.0 copy-start.3
  207.0 0.0 copy-start.1
  207.1 0.7 copy-done.2
  207.8 0.2 copy-done.3
  208.0 0.4 copy-done.1
  208.4 64.3 %exit.1 = (f32[2,512,768]{2,1,0:T(8,128)S(1)}, f32[96,768]{1,0:T(8,128)S(1)}, f32[96,768]{1,0:T(8,128)S(1)}, f32[96,768]{1,0:T(8,128)S(1)}, f32[96,768]{1,0:T(8,...) custom-call(bf16[2048,1152]{1,0:T(8,128)(2,1)} %get-tuple-element.84.refs_0_, ...), custom_call_target="tpu_custom_call" | custom-call | tf_op jit(solution)/shard_map/exit/pallas_call | solution.py:1103
  272.7 4.1 %deliver.1 = (bf16[2,512,768]{2,1,0:T(8,128)(2,1)}, f32[2,512,768]{2,1,0:T(8,128)}, f32[96,768]{1,0:T(8,128)}, f32[96,768]{1,0:T(8,128)}, f32[96,768]{1,0:T(8,12...) custom-call(bf16[512,768]{1,0:T(8,128)(2,1)S(1)} %copy-done, ...), custom_call_target="tpu_custom_call" | custom-call | tf_op jit(solution)/shard_map/deliver/pallas_call | solution.py:1024
  (10 shorter events, 0.0 us)
Async XLA Ops:
  42.9 42.6 %collective-permute-start.4 = (bf16[2,384,384]{2,1,0:T(8,128)(2,1)}, bf16[2,384,384]{2,1,0:T(8,128)(2,1)}, u32[]{:S(2)}, u32[]{:S(2)}) collective-permute-start(bf16[2,384,384]{2,1,0:T(8,128)(2,1)} %get-tuple-element.77.refs_9_), channel_id=1, source_target_pairs={{0,24},{8,0},{16,8},{24,16},{1,25},{9,1},{17,9},{25,17},{2,26},{10... | collective-permute-start | bytes 1769480 | tf_op jit(solution)/shard_map/ppermute | solution.py:1552
  44.4 47.6 %collective-permute-start.3 = (bf16[2,384,384]{2,1,0:T(8,128)(2,1)}, bf16[2,384,384]{2,1,0:T(8,128)(2,1)}, u32[]{:S(2)}, u32[]{:S(2)}) collective-permute-start(bf16[2,384,384]{2,1,0:T(8,128)(2,1)} %get-tuple-element.77.refs_9_), channel_id=1, source_target_pairs={{0,16},{8,24},{16,0},{24,8},{1,17},{9,25},{17,1},{25,9},{2,18},{10... | collective-permute-start | bytes 1769480 | tf_op jit(solution)/shard_map/ppermute | solution.py:1552
  44.5 47.6 %collective-permute-start.2 = (bf16[2,384,384]{2,1,0:T(8,128)(2,1)}, bf16[2,384,384]{2,1,0:T(8,128)(2,1)}, u32[]{:S(2)}, u32[]{:S(2)}) collective-permute-start(bf16[2,384,384]{2,1,0:T(8,128)(2,1)} %get-tuple-element.77.refs_9_), channel_id=1, source_target_pairs={{0,8},{8,16},{16,24},{24,0},{1,9},{9,17},{17,25},{25,1},{2,10},{10... | collective-permute-start | bytes 1769480 | tf_op jit(solution)/shard_map/ppermute | solution.py:1552
  45.1 47.0 %collective-permute-start = (bf16[512,768]{1,0:T(8,128)(2,1)}, bf16[512,768]{1,0:T(8,128)(2,1)}, u32[]{:S(2)}, u32[]{:S(2)}) collective-permute-start(bf16[512,768]{1,0:T(8,128)(2,1)} %get-tuple-element.74), channel_id=1, source_target_pairs={{0,2},{2,0},{1,3},{3,1},{4,6},{6,4},{5,7},{7,5},{8,10},{10,8},{9,1... | collective-permute-start | bytes 2359304 | tf_op jit(solution)/shard_map/ppermute | solution.py:1556
  45.6 46.4 %collective-permute-start.1 = (bf16[4,96,1920]{2,1,0:T(8,128)(2,1)}, bf16[4,96,1920]{2,1,0:T(8,128)(2,1)}, u32[]{:S(2)}, u32[]{:S(2)}) collective-permute-start(bf16[4,96,1920]{2,1,0:T(8,128)(2,1)} %get-tuple-element.76.refs_7_), channel_id=1, source_target_pairs={{0,4},{4,0},{1,5},{5,1},{2,6},{6,2},{3,7},{7,3},{8,12},{12,8},{9,1... | collective-permute-start | bytes 4423688 | tf_op jit(solution)/shard_map/ppermute | solution.py:1552
  153.9 53.1 %collective-permute-start.6 = (bf16[2,96,1536]{2,1,0:T(8,128)(2,1)}, bf16[2,96,1536]{2,1,0:T(8,128)(2,1)S(1)}, u32[]{:S(2)}, u32[]{:S(2)}) collective-permute-start(bf16[2,96,1536]{2,1,0:T(8,128)(2,1)} %get-tuple-element.91), channel_id=1, source_target_pairs={{0,8},{8,16},{16,24},{24,0},{1,9},{9,17},{17,25},{25,1},{2,10},{10... | collective-permute-start | bytes 1769480 | tf_op jit(solution)/shard_map/ppermute | solution.py:1552
  158.4 48.6 %collective-permute-start.7 = (bf16[2,96,1536]{2,1,0:T(8,128)(2,1)}, bf16[2,96,1536]{2,1,0:T(8,128)(2,1)S(1)}, u32[]{:S(2)}, u32[]{:S(2)}) collective-permute-start(bf16[2,96,1536]{2,1,0:T(8,128)(2,1)} %get-tuple-element.92), channel_id=1, source_target_pairs={{0,16},{8,24},{16,0},{24,8},{1,17},{9,25},{17,1},{25,9},{2,18},{10... | collective-permute-start | bytes 1769480 | tf_op jit(solution)/shard_map/ppermute | solution.py:1552
  159.3 47.7 %collective-permute-start.8 = (bf16[2,96,1536]{2,1,0:T(8,128)(2,1)}, bf16[2,96,1536]{2,1,0:T(8,128)(2,1)}, u32[]{:S(2)}, u32[]{:S(2)}) collective-permute-start(bf16[2,96,1536]{2,1,0:T(8,128)(2,1)} %get-tuple-element.93), channel_id=1, source_target_pairs={{0,24},{8,0},{16,8},{24,16},{1,25},{9,1},{17,9},{25,17},{2,26},{10... | collective-permute-start | bytes 1769480 | tf_op jit(solution)/shard_map/ppermute | solution.py:1552
  161.1 111.6 %collective-permute-start.5 = (bf16[512,768]{1,0:T(8,128)(2,1)}, bf16[512,768]{1,0:T(8,128)(2,1)S(1)}, u32[]{:S(2)}, u32[]{:S(2)}) collective-permute-start(bf16[512,768]{1,0:T(8,128)(2,1)} %get-tuple-element.79), channel_id=1, source_target_pairs={{0,2},{2,0},{1,3},{3,1},{4,6},{6,4},{5,7},{7,5},{8,10},{10,8},{9,1... | collective-permute-start | bytes 2359304 | tf_op jit(solution)/shard_map/ppermute | solution.py:1556
  165.5 41.6 %collective-permute-start.9 = (bf16[4,384,384]{2,1,0:T(8,128)(2,1)}, bf16[4,384,384]{2,1,0:T(8,128)(2,1)S(1)}, u32[]{:S(2)}, u32[]{:S(2)}) collective-permute-start(bf16[4,384,384]{2,1,0:T(8,128)(2,1)} %get-tuple-element.95), channel_id=1, source_target_pairs={{0,4},{4,0},{1,5},{5,1},{2,6},{6,2},{3,7},{7,3},{8,12},{12,8},{9,1... | collective-permute-start | bytes 3538952 | tf_op jit(solution)/shard_map/ppermute | solution.py:1552
  207.0 0.8 copy-start.2
  207.0 1.0 copy-start.3
  207.0 1.3 copy-start.1
  208.4 64.4 %copy-start = (bf16[512,768]{1,0:T(8,128)(2,1)S(1)}, bf16[512,768]{1,0:T(8,128)(2,1)}, u32[]{:S(2)}) copy-start(bf16[512,768]{1,0:T(8,128)(2,1)} %get-tuple-element.78.refs_0_) | copy-start | bytes 2359300

commit v10 on v9

--- a/solution.py
+++ b/solution.py
@@ -834,28 +834,10 @@
         swapped[name].wait()
         return cbuf[name]
 
-    vector_rows[...] = jnp.zeros_like(vector_rows)
-    for i, row in enumerate((7, 8, 6, 3, 4, 2)):
-        vector_rows[row : row + 1, :] = jnp.sum(dense_sums[8 * i : 8 * i + 8, :], axis=0, keepdims=True)
-    for p in range(pairs):
-        place = pl.ds(pl.multiple_of(core * half + p * 128, 128), 128)
-        vector_rows[0:1, place] = head_sums[8 * p : 8 * p + 1, 0:128]
-        vector_rows[1:2, place] = head_sums[8 * p : 8 * p + 1, 256:384]
-    inner_row = jnp.sum(inner_sums[...], axis=0, keepdims=True)
-    vector_terms[...] = jnp.zeros_like(vector_terms)
-    for name in zin:
-        if name == "vec":
-            zin[name][...] = jnp.zeros_like(zin[name])
-    longest = vector_terms.shape[2]
-    for s in range(shards):
-        vector_terms[s, :, 0:rows] = vector_rows[:, s * rows : (s + 1) * rows]
-        vector_terms[s, WIDE : WIDE + 1, :] = inner_row[:, s * longest : (s + 1) * longest]
     greet(True)
 
     outputs = remote(output_term.at[:, :, theirs], odd, osend, orecv, core_peer)
     outputs.start()
-    send_far("vec")
-    send_own("vec")
     for i in range(size_z):
         loads["inner", i].wait()
     inner_moves = []
@@ -877,32 +859,55 @@
         at = pl.ds(pl.multiple_of(first, strip), strip)
         return dot_nt(grads[at, :], weights[...])
 
+    def token_move(first):
+        at = pl.ds(pl.multiple_of(first, strip), strip)
+        n = first // strip
+        return remote(other_rows.at[at, :], recv_rows.at[at, :], tsend.at[n], trecv.at[n], core_peer)
+
+    def back_move(i):
+        at = pl.ds(pl.multiple_of(i * strip, strip), strip)
+        n = local // strip + i
+        return remote(send_rows.at[at, :], far_rows.at[at, :], tsend.at[n], trecv.at[n], y_peer)
+
     def token_rows(first):
         def other_strip(i, _):
             at = pl.ds(pl.multiple_of(first + i * strip, strip), strip)
             other_rows[at, :] = product(local + first + i * strip).astype(low)
+            token_move(first + i * strip).start()
             return 0
 
         def own_strip(i, _):
             at = pl.ds(pl.multiple_of(first + i * strip, strip), strip)
             base[at, :] = base[at, :] + product(first + i * strip)
+            if first == part:
+                token_move(first + i * strip).wait()
+                rows_out = pl.ds(pl.multiple_of(i * strip, strip), strip)
+                send_rows[rows_out, :] = (base[at, :] + recv_rows[at, :].astype(high)).astype(low)
+                back_move(i).start()
             return 0
 
         lax.fori_loop(0, part // strip, other_strip, 0)
-        span = pl.ds(first, part)
-        move = remote(other_rows.at[span, :], recv_rows.at[span, :], tsend.at[first // part], trecv.at[first // part], core_peer)
-        move.start()
         lax.fori_loop(0, part // strip, own_strip, 0)
-        return move
 
     for name in ("grads", "weights", "base"):
         loads[name].wait()
-    halves = token_rows(part)
-    halves.wait()
-    send_rows[...] = (base[part:local, :] + recv_rows[part:local, :].astype(high)).astype(low)
-    back = remote(send_rows, far_rows, tsend.at[2], trecv.at[2], y_peer)
-    back.start()
-
+    token_rows(part)
+
+    vector_rows[...] = jnp.zeros_like(vector_rows)
+    for i, row in enumerate((7, 8, 6, 3, 4, 2)):
+        vector_rows[row : row + 1, :] = jnp.sum(dense_sums[8 * i : 8 * i + 8, :], axis=0, keepdims=True)
+    for p in range(pairs):
+        place = pl.ds(pl.multiple_of(core * half + p * 128, 128), 128)
+        vector_rows[0:1, place] = head_sums[8 * p : 8 * p + 1, 0:128]
+        vector_rows[1:2, place] = head_sums[8 * p : 8 * p + 1, 256:384]
+    inner_row = jnp.sum(inner_sums[...], axis=0, keepdims=True)
+    vector_terms[...] = jnp.zeros_like(vector_terms)
+    longest = vector_terms.shape[2]
+    for s in range(shards):
+        vector_terms[s, :, 0:rows] = vector_rows[:, s * rows : (s + 1) * rows]
+        vector_terms[s, WIDE : WIDE + 1, :] = inner_row[:, s * longest : (s + 1) * longest]
+    send_far("vec")
+    send_own("vec")
     step_z("outer", 2)
     loads["inputs"].wait()
     for b in range(4):
@@ -938,7 +943,7 @@
         step_z("outer", t)
     step_z("vec", 1)
     step_z("qa", 1)
-    halves = token_rows(0)
+    token_rows(0)
     step_z("vec", 2)
     step_z("qa", 2)
     finish_z("outer")
@@ -946,7 +951,8 @@
         step_z("vec", t)
         step_z("qa", t)
     step_z("qb", 1)
-    halves.wait()
+    for i in range(part // strip):
+        token_move(i * strip).wait()
     token_grads[y] = base[0:part, :] + recv_rows[0:part, :].astype(high)
     step_core("inner")
     step_z("qb", 2)
@@ -955,7 +961,8 @@
     finish_z("qa")
     finish_z("vec")
     step_core("outer")
-    back.wait()
+    for i in range(part // strip):
+        back_move(i).wait()
     token_grads[1 - y] = far_rows[...].astype(high)
     chunks = hidden // CHUNK
     buf = finish_core("inner")
@@ -1088,8 +1095,8 @@
         pltpu.VMEM((shards,) + vector_shape, high),
         pltpu.VMEM((side, rows, hidden // 2), low),
         dma((size_z + size_x + 4,)),
-        dma((3,)),
-        dma((3,)),
+        dma((local // 256 + part // 256,)),
+        dma((local // 256 + part // 256,)),
         dma,
         dma,
     ]

time: 281 us -> 280 us (level)
    ppermute x8, starting transfers between devices: 10.9 us -> 15.7 us  [shift(): lax.ppermute(piece, axis, [(i, (i + step) % size) for i in range(size)])]
    ppermute x2, starting transfers between devices: 4.84 us -> 0.51 us  [swap(): return lax.ppermute(piece, axis, [(0, 1), (1, 0)])]
where the time goes in v10:
time: 280 us; the launch traced here: 275 us
  Pallas kernels  250 us (89%)
  starting transfers between devices  16.2 us (6%)
  waiting for transfers between devices  6.54 us (2%)
    pallas_call x1, Pallas kernels, exit_call(): pl.pallas_call(lambda *refs: exit_kernel(size_z, size_x, shapes, *refs),...  62.3 us
    pallas_call x1, Pallas kernels, dense_layer(): pl.pallas_call(lambda *refs: dense_kernel(size_z, size_x, *refs), out_sha...  61.8 us
    pallas_call x1, Pallas kernels, entry(): pl.pallas_call(lambda *refs: entry_kernel(size_z, size_x, count, *refs),...  42.3 us
    pallas_call x1, Pallas kernels, attention_back(): pl.pallas_call(backward_kernel, out_shape=(jax.ShapeDtypeStruct((length,...  41.5 us
    pallas_call x1, Pallas kernels, attention(): pl.pallas_call(forward_kernel, out_shape=(jax.ShapeDtypeStruct((rows, pai...  38.4 us
    ppermute x8, starting transfers between devices, shift(): lax.ppermute(piece, axis, [(i, (i + step) % size) for i in range(size)])  15.7 us
    ppermute x8, waiting for transfers between devices, shift(): lax.ppermute(piece, axis, [(i, (i + step) % size) for i in range(size)])  6.54 us
  transfers between devices with their start and end apart: 10, of which 1 were waited for; matrix products, arithmetic and copies ran while one was open for 0% of the time, Pallas kernels for 52%

profile of v10, /device:TPU:0, one launch (start us, length us, event | category | flops | bytes accessed | tf_op | source)
XLA Modules:
  0.0 275.4 jit_solution(2147693550608025124)
XLA Ops:
  0.7 42.3 %entry.1 = (bf16[4,512,768]{2,1,0:T(8,128)(2,1)}, bf16[512,768]{1,0:T(8,128)(2,1)}, bf16[8,96,1152]{2,1,0:T(8,128)(2,1)}, bf16[4,96,1920]{2,1,0:T(8,128)(2,1)}, ...) custom-call(bf16[2,512,768]{2,1,0:T(8,128)(2,1)} %refs_0_.1, bf16[2,512,768]{2,1,0:T(8,128)(2,1)} %refs_3_.3, ...), custom_call_target="tpu_custom_call" | custom-call | tf_op jit(solution)/shard_map/entry/pallas_call | solution.py:638
  42.9 1.5 collective-permute-start.4
  44.4 0.0 collective-permute-start.3
  44.5 0.6 collective-permute-start.2
  45.1 0.5 collective-permute-start
  45.6 1.5 collective-permute-start.1
  47.1 38.4 %attention_forward.1 = (bf16[1024,384]{1,0:T(8,128)(2,1)}, bf16[1024,384]{1,0:T(8,128)(2,1)}, f32[24,2048]{1,0:T(8,128)}, bf16[2048,1152]{1,0:T(8,128)(2,1)}) custom-call(s32[2,2048]{1,0:T(2,128)} %row_ref.3, s32[2,2048]{1,0:T(2,128)} %row_ref.3, bf16[2048,768]{1,0:T(8,128)(2,1)} %bitcast.3, bf16[768,1152]{1,0:T(8,128)(2,1)} %bitcast.6, ...), custom_call_target="tpu_custom_call" | custom-call | flops 120000004096 | bytes 9000000 | tf_op jit(solution)/shard_map/attention_forward/pallas_call | solution.py:183
  85.5 6.5 %collective-permute-done.3.refs_11_ = bf16[2,384,384]{2,1,0:T(8,128)(2,1)} collective-permute-done((bf16[2,384,384]{2,1,0:T(8,128)(2,1)}, bf16[2,384,384]{2,1,0:T(8,128)(2,1)}, u32[]{:S(2)}, u32[]{:S(2)}) %collective-permute-start.3) | collective-permute-done | bytes 589856 | tf_op jit(solution)/shard_map/ppermute | solution.py:1559
  92.0 0.0 collective-permute-done.2.refs_10_
  92.0 0.0 collective-permute-done.refs_4_
  92.1 61.8 %dense_layer.1 = (bf16[512,768]{1,0:T(8,128)(2,1)}, bf16[512,768]{1,0:T(8,128)(2,1)}, f32[1024,768]{1,0:T(8,128)}, bf16[1024,384]{1,0:T(8,128)(2,1)}, bf16[1024,...) custom-call(bf16[2048,768]{1,0:T(8,128)(2,1)} %bitcast.4, ...), custom_call_target="tpu_custom_call" | custom-call | flops 32000000000 | bytes 40000000 | tf_op jit(solution)/shard_map/dense_layer/pallas_call | solution.py:1424
  153.9 2.4 collective-permute-start.6
  156.3 4.8 %collective-permute-start.7 = (bf16[2,96,1536]{2,1,0:T(8,128)(2,1)}, bf16[2,96,1536]{2,1,0:T(8,128)(2,1)S(1)}, u32[]{:S(2)}, u32[]{:S(2)}) collective-permute-start(bf16[2,96,1536]{2,1,0:T(8,128)(2,1)} %get-tuple-element.92), channel_id=1, source_target_pairs={{0,16},{8,24},{16,0},{24,8},{1,17},{9,25},{17,1},{25,9},{2,18},{10... | collective-permute-start | bytes 1769480 | tf_op jit(solution)/shard_map/ppermute | solution.py:1559
  161.1 2.8 %collective-permute-start.8 = (bf16[2,96,1536]{2,1,0:T(8,128)(2,1)}, bf16[2,96,1536]{2,1,0:T(8,128)(2,1)}, u32[]{:S(2)}, u32[]{:S(2)}) collective-permute-start(bf16[2,96,1536]{2,1,0:T(8,128)(2,1)} %get-tuple-element.93), channel_id=1, source_target_pairs={{0,24},{8,0},{16,8},{24,16},{1,25},{9,1},{17,9},{25,17},{2,26},{10... | collective-permute-start | bytes 1769480 | tf_op jit(solution)/shard_map/ppermute | solution.py:1559
  164.0 2.0 collective-permute-start.9
  166.0 41.5 %attention_backward.1 = (bf16[2048,1152]{1,0:T(8,128)(2,1)}, f32[24,384]{1,0:T(8,128)}) custom-call(s32[2,2048]{1,0:T(2,128)} %row_ref.3, bf16[2048,1152]{1,0:T(8,128)(2,1)} %get-tuple-element.80.qkv_ref, bf16[1024,384]{1,0:T(8,128)(2,1)} %get-tuple-element.72.refs_1_.ctx_mine_ref, bf16[1024,384]{1,0:T(8,128)(2,1)} %get-tuple-element.73.refs_2_.ctx_other_ref, ...), custom_call_target="tpu_custom_call" | custom-call | flops 60000002048 | bytes 15000000 | tf_op jit(solution)/shard_map/attention_backward/pallas_call | solution.py:350
  207.5 0.0 copy-start.2
  207.5 0.0 copy-start.3
  207.5 0.0 copy-start.1
  207.5 0.7 copy-done.2
  208.3 0.2 copy-done.3
  208.5 0.4 copy-done.1
  208.9 62.3 %exit.1 = (f32[2,512,768]{2,1,0:T(8,128)S(1)}, f32[96,768]{1,0:T(8,128)S(1)}, f32[96,768]{1,0:T(8,128)S(1)}, f32[96,768]{1,0:T(8,128)S(1)}, f32[96,768]{1,0:T(8,...) custom-call(bf16[2048,1152]{1,0:T(8,128)(2,1)} %get-tuple-element.84.refs_0_, ...), custom_call_target="tpu_custom_call" | custom-call | tf_op jit(solution)/shard_map/exit/pallas_call | solution.py:1110
  271.2 4.1 %deliver.1 = (bf16[2,512,768]{2,1,0:T(8,128)(2,1)}, f32[2,512,768]{2,1,0:T(8,128)}, f32[96,768]{1,0:T(8,128)}, f32[96,768]{1,0:T(8,128)}, f32[96,768]{1,0:T(8,12...) custom-call(bf16[512,768]{1,0:T(8,128)(2,1)S(1)} %copy-done, ...), custom_call_target="tpu_custom_call" | custom-call | tf_op jit(solution)/shard_map/deliver/pallas_call | solution.py:1031
  (10 shorter events, 0.0 us)
Async XLA Ops:
  42.9 42.6 %collective-permute-start.4 = (bf16[2,384,384]{2,1,0:T(8,128)(2,1)}, bf16[2,384,384]{2,1,0:T(8,128)(2,1)}, u32[]{:S(2)}, u32[]{:S(2)}) collective-permute-start(bf16[2,384,384]{2,1,0:T(8,128)(2,1)} %get-tuple-element.77.refs_9_), channel_id=1, source_target_pairs={{0,24},{8,0},{16,8},{24,16},{1,25},{9,1},{17,9},{25,17},{2,26},{10... | collective-permute-start | bytes 1769480 | tf_op jit(solution)/shard_map/ppermute | solution.py:1559
  44.4 47.6 %collective-permute-start.3 = (bf16[2,384,384]{2,1,0:T(8,128)(2,1)}, bf16[2,384,384]{2,1,0:T(8,128)(2,1)}, u32[]{:S(2)}, u32[]{:S(2)}) collective-permute-start(bf16[2,384,384]{2,1,0:T(8,128)(2,1)} %get-tuple-element.77.refs_9_), channel_id=1, source_target_pairs={{0,16},{8,24},{16,0},{24,8},{1,17},{9,25},{17,1},{25,9},{2,18},{10... | collective-permute-start | bytes 1769480 | tf_op jit(solution)/shard_map/ppermute | solution.py:1559
  44.5 47.6 %collective-permute-start.2 = (bf16[2,384,384]{2,1,0:T(8,128)(2,1)}, bf16[2,384,384]{2,1,0:T(8,128)(2,1)}, u32[]{:S(2)}, u32[]{:S(2)}) collective-permute-start(bf16[2,384,384]{2,1,0:T(8,128)(2,1)} %get-tuple-element.77.refs_9_), channel_id=1, source_target_pairs={{0,8},{8,16},{16,24},{24,0},{1,9},{9,17},{17,25},{25,1},{2,10},{10... | collective-permute-start | bytes 1769480 | tf_op jit(solution)/shard_map/ppermute | solution.py:1559
  45.1 47.0 %collective-permute-start = (bf16[512,768]{1,0:T(8,128)(2,1)}, bf16[512,768]{1,0:T(8,128)(2,1)}, u32[]{:S(2)}, u32[]{:S(2)}) collective-permute-start(bf16[512,768]{1,0:T(8,128)(2,1)} %get-tuple-element.74), channel_id=1, source_target_pairs={{0,2},{2,0},{1,3},{3,1},{4,6},{6,4},{5,7},{7,5},{8,10},{10,8},{9,1... | collective-permute-start | bytes 2359304 | tf_op jit(solution)/shard_map/ppermute | solution.py:1563
  45.6 46.4 %collective-permute-start.1 = (bf16[4,96,1920]{2,1,0:T(8,128)(2,1)}, bf16[4,96,1920]{2,1,0:T(8,128)(2,1)}, u32[]{:S(2)}, u32[]{:S(2)}) collective-permute-start(bf16[4,96,1920]{2,1,0:T(8,128)(2,1)} %get-tuple-element.76.refs_7_), channel_id=1, source_target_pairs={{0,4},{4,0},{1,5},{5,1},{2,6},{6,2},{3,7},{7,3},{8,12},{12,8},{9,1... | collective-permute-start | bytes 4423688 | tf_op jit(solution)/shard_map/ppermute | solution.py:1559
  153.9 53.6 %collective-permute-start.6 = (bf16[2,96,1536]{2,1,0:T(8,128)(2,1)}, bf16[2,96,1536]{2,1,0:T(8,128)(2,1)S(1)}, u32[]{:S(2)}, u32[]{:S(2)}) collective-permute-start(bf16[2,96,1536]{2,1,0:T(8,128)(2,1)} %get-tuple-element.91), channel_id=1, source_target_pairs={{0,8},{8,16},{16,24},{24,0},{1,9},{9,17},{17,25},{25,1},{2,10},{10... | collective-permute-start | bytes 1769480 | tf_op jit(solution)/shard_map/ppermute | solution.py:1559
  156.3 51.2 %collective-permute-start.7 = (bf16[2,96,1536]{2,1,0:T(8,128)(2,1)}, bf16[2,96,1536]{2,1,0:T(8,128)(2,1)S(1)}, u32[]{:S(2)}, u32[]{:S(2)}) collective-permute-start(bf16[2,96,1536]{2,1,0:T(8,128)(2,1)} %get-tuple-element.92), channel_id=1, source_target_pairs={{0,16},{8,24},{16,0},{24,8},{1,17},{9,25},{17,1},{25,9},{2,18},{10... | collective-permute-start | bytes 1769480 | tf_op jit(solution)/shard_map/ppermute | solution.py:1559
  161.1 46.4 %collective-permute-start.8 = (bf16[2,96,1536]{2,1,0:T(8,128)(2,1)}, bf16[2,96,1536]{2,1,0:T(8,128)(2,1)}, u32[]{:S(2)}, u32[]{:S(2)}) collective-permute-start(bf16[2,96,1536]{2,1,0:T(8,128)(2,1)} %get-tuple-element.93), channel_id=1, source_target_pairs={{0,24},{8,0},{16,8},{24,16},{1,25},{9,1},{17,9},{25,17},{2,26},{10... | collective-permute-start | bytes 1769480 | tf_op jit(solution)/shard_map/ppermute | solution.py:1559
  163.9 107.2 %collective-permute-start.5 = (bf16[512,768]{1,0:T(8,128)(2,1)}, bf16[512,768]{1,0:T(8,128)(2,1)S(1)}, u32[]{:S(2)}, u32[]{:S(2)}) collective-permute-start(bf16[512,768]{1,0:T(8,128)(2,1)} %get-tuple-element.79), channel_id=1, source_target_pairs={{0,2},{2,0},{1,3},{3,1},{4,6},{6,4},{5,7},{7,5},{8,10},{10,8},{9,1... | collective-permute-start | bytes 2359304 | tf_op jit(solution)/shard_map/ppermute | solution.py:1563
  164.0 43.6 %collective-permute-start.9 = (bf16[4,384,384]{2,1,0:T(8,128)(2,1)}, bf16[4,384,384]{2,1,0:T(8,128)(2,1)S(1)}, u32[]{:S(2)}, u32[]{:S(2)}) collective-permute-start(bf16[4,384,384]{2,1,0:T(8,128)(2,1)} %get-tuple-element.95), channel_id=1, source_target_pairs={{0,4},{4,0},{1,5},{5,1},{2,6},{6,2},{3,7},{7,3},{8,12},{12,8},{9,1... | collective-permute-start | bytes 3538952 | tf_op jit(solution)/shard_map/ppermute | solution.py:1559
  207.5 0.8 copy-start.2
  207.5 1.0 copy-start.3
  207.5 1.3 copy-start.1
  208.9 62.3 %copy-start = (bf16[512,768]{1,0:T(8,128)(2,1)S(1)}, bf16[512,768]{1,0:T(8,128)(2,1)}, u32[]{:S(2)}) copy-start(bf16[512,768]{1,0:T(8,128)(2,1)} %get-tuple-element.78.refs_0_) | copy-start | bytes 2359300
